TPU v7x, 256 devices: a whole 4x4x8 slice. The times are simulated.
256 devices in a mesh: frames: 64 (over y, x, z_lo), pix: 4 (over z_hi, core).
Axes of the slice: x: 4, y: 4, z: 8 (z_hi: 2, z_lo: 4; z = z_hi * 4 + z_lo), core: 2. Of those that a mesh axis runs over, the one named last changes fastest.
Arguments:
- edge_frames: int32 [2, 12288], P(None, 'frames'), may hold values from 0 to 1023, as said below
- rotvec: float32 [3, 1024], replicated, may hold values from -0.06 to 0.06
- trans: float32 [3, 1024], replicated, may hold values from -0.15 to 0.15
- inv_depth: float32 [1024, 3072], P('frames', 'pix'), may hold values from 0.2 to 1
- depth_damping: float32 [1024, 3072], P('frames', 'pix'), may hold values from 0.01 to 0.1
- flow: float32 [12288, 2, 3072], P('frames', None, 'pix'), may hold values from -0.3 to 0.3
- weight: float32 [12288, 2, 3072], P('frames', None, 'pix'), may hold values from 0.02 to 1
- mask: int32 [12288, 3072], P('frames', 'pix'), may hold values 0 or 1
Outputs:
- pose_step: float32 [6, 1024], P(None, 'frames')
- depth_step: float32 [1024, 3072], P('frames', 'pix')
Inputs may be any that keep to these rules, and one draw needn't show every extreme that they name: Edge e of the block of 192 edges held by one index of frames has its target edge_frames[1, e] among that index's 16 keyframes; its source edge_frames[0, e] differs from the target by 1 to 8, and in every block some source lies exactly 8 away.
All inputs are finite; a program needn't handle non-finite values. No bound on the sum of `mask` on one device may be relied on, other than what follows from the above.
Results may differ from a plain program's by a relative error of at most 0.00015.
Values sent between devices are 32-bit elements; how exact they have to be, the bound alone decides.
No kernel may reach another device: no remote copies, remote signals or barrier semaphores. Data moves between devices by JAX's collectives and lax.ppermute only.
A program may use at most 64 MiB of HBM per device.

v0:
```python
import jax
import jax.numpy as jnp
from jax import lax
from jax.sharding import PartitionSpec as P

ROWS = 48
COLS = 64
RADIUS = 8
ITERS = 6


exact = lax.Precision.HIGHEST
pose_regularizer = 100.0


def padded(block, sides, width):
    for axis, dim in sides:
        count = lax.axis_size(axis)
        forward = [(i, i + 1) for i in range(count - 1)]
        backward = [(target, source) for source, target in forward]
        low = lax.ppermute(
            lax.slice_in_dim(block, block.shape[dim] - width, None, axis=dim), axis, forward
        )
        high = lax.ppermute(lax.slice_in_dim(block, 0, width, axis=dim), axis, backward)
        block = jnp.concatenate([low, block, high], axis=dim)
    return block


def from_behind(block, axis, distance):
    devices = range(lax.axis_size(axis))
    route = [(i - distance, i) for i in devices if i - distance in devices]
    return lax.ppermute(block, axis, route)


def total_of_pieces(shard, axis):
    tiles = lax.all_gather(shard, axis)
    return tiles.sum(axis=0)


def from_everyone(shard, axis):
    count = lax.axis_size(axis)
    return lax.all_to_all(
        jnp.broadcast_to(shard[None], (count, *shard.shape)), axis, 0, 0, tiled=True
    )


def over_copies(shard, axis):
    return from_everyone(shard, axis).sum(axis=0)


def in_one(arrays, axis):
    ends = [0]
    for a in arrays:
        ends.append(ends[-1] + a.size)
    running = over_copies(jnp.concatenate([a.ravel() for a in arrays]), axis)
    return tuple((running[b:e].reshape(a.shape) for a, b, e in zip(arrays, ends, ends[1:])))


def pixel_coords(pixel):
    row = pixel // COLS
    column = pixel % COLS
    col_coord = (column.astype(jnp.float32) - 0.5 * (COLS - 1)) / COLS
    row_coord = (row.astype(jnp.float32) - 0.5 * (ROWS - 1)) / COLS
    return (col_coord, row_coord)


def rotations(rotvec):
    omega_x, omega_y, omega_z = (rotvec[0], rotvec[1], rotvec[2])
    zero = jnp.zeros_like(omega_x)
    cross = [[zero, -omega_z, omega_y], [omega_z, zero, -omega_x], [-omega_y, omega_x, zero]]
    theta_sq = omega_x * omega_x + omega_y * omega_y + omega_z * omega_z
    first_coef = 1.0 - theta_sq / 6.0 + theta_sq * theta_sq / 120.0
    second_coef = 0.5 - theta_sq / 24.0 + theta_sq * theta_sq / 720.0
    lines = []
    for row in range(3):
        entries = []
        for column in range(3):
            square = (
                cross[row][0] * cross[0][column]
                + cross[row][1] * cross[1][column]
                + cross[row][2] * cross[2][column]
            )
            entries.append(
                float(row == column) + first_coef * cross[row][column] + second_coef * square
            )
        lines.append(jnp.stack(entries))
    return jnp.stack(lines)


def relative(rot, trans, source, target):
    rot_source = jnp.take(rot, source, axis=2)
    rot_target = jnp.take(rot, target, axis=2)
    rel_rot = jnp.einsum("ike,jke->ije", rot_target, rot_source, precision=exact)
    rel_trans = jnp.take(trans, target, axis=1) - jnp.einsum(
        "ije,je->ie", rel_rot, jnp.take(trans, source, axis=1), precision=exact
    )
    zero = jnp.zeros_like(rel_trans[0])
    skew = jnp.stack(
        [
            jnp.stack([zero, -rel_trans[2], rel_trans[1]]),
            jnp.stack([rel_trans[2], zero, -rel_trans[0]]),
            jnp.stack([-rel_trans[1], rel_trans[0], zero]),
        ]
    )
    corner = jnp.einsum("ike,kje->ije", skew, rel_rot, precision=exact)
    upper = jnp.concatenate([rel_rot, corner], axis=1)
    lower = jnp.concatenate([jnp.zeros_like(rel_rot), rel_rot], axis=1)
    return (rel_rot, rel_trans, jnp.concatenate([upper, lower], axis=0))


def geometry(rel_rot, rel_trans, depth, flow, weight, mask, col_coord, row_coord):

    def coordinate(line):
        return (
            rel_rot[line, 0][:, None] * col_coord
            + rel_rot[line, 1][:, None] * row_coord
            + rel_rot[line, 2][:, None]
            + depth * rel_trans[line][:, None]
        )

    inverse_z = 1.0 / coordinate(2)
    proj_u = coordinate(0) * inverse_z
    proj_v = coordinate(1) * inverse_z
    depth_scale = depth * inverse_z
    slope_u = inverse_z * (rel_trans[0][:, None] - proj_u * rel_trans[2][:, None])
    slope_v = inverse_z * (rel_trans[1][:, None] - proj_v * rel_trans[2][:, None])
    live = mask.astype(jnp.float32)
    conf_u = weight[:, 0] * live
    conf_v = weight[:, 1] * live
    error_u = col_coord + flow[:, 0] - proj_u
    error_v = row_coord + flow[:, 1] - proj_v
    return (proj_u, proj_v, depth_scale, slope_u, slope_v, conf_u, conf_v, error_u, error_v)


def apply_pose(geo, motion):
    proj_u, proj_v, depth_scale = (geo[0], geo[1], geo[2])
    part = [motion[index][:, None] for index in range(6)]
    cross_uv = proj_u * proj_v
    lin_u = (
        depth_scale * (part[0] - proj_u * part[2])
        - cross_uv * part[3]
        + (1.0 + proj_u * proj_u) * part[4]
        - proj_v * part[5]
    )
    lin_v = (
        depth_scale * (part[1] - proj_v * part[2])
        - (1.0 + proj_v * proj_v) * part[3]
        + cross_uv * part[4]
        + proj_u * part[5]
    )
    return (lin_u, lin_v)


def pose_terms(geo, part_u, part_v):
    proj_u, proj_v, depth_scale = (geo[0], geo[1], geo[2])
    heavy_u = geo[5] * part_u
    heavy_v = geo[6] * part_v
    cross_uv = proj_u * proj_v
    entries = [
        depth_scale * heavy_u,
        depth_scale * heavy_v,
        -depth_scale * (proj_u * heavy_u + proj_v * heavy_v),
        -cross_uv * heavy_u - (1.0 + proj_v * proj_v) * heavy_v,
        (1.0 + proj_u * proj_u) * heavy_u + cross_uv * heavy_v,
        -proj_v * heavy_u + proj_u * heavy_v,
    ]
    return jnp.stack([jnp.sum(entry, axis=1) for entry in entries])


def margins(extended, radius, own_count, axis):
    lower = lax.slice_in_dim(extended, 0, radius, axis=axis)
    own = lax.slice_in_dim(extended, radius, radius + own_count, axis=axis)
    upper = lax.slice_in_dim(extended, radius + own_count, 2 * radius + own_count, axis=axis)
    return (lower, own, upper)


def settle(own, from_below, from_above, axis):
    count = own.shape[axis]
    width = from_below.shape[axis]
    pads_low = [(0, 0)] * own.ndim
    pads_high = [(0, 0)] * own.ndim
    pads_low[axis] = (0, count - width)
    pads_high[axis] = (count - width, 0)
    return own + jnp.pad(from_below, pads_low) + jnp.pad(from_above, pads_high)


def per_device(edge_frames, rotvec, trans, inv_depth, depth_damping, flow, weight, mask):
    f_dev = inv_depth.shape[0]
    plocal = inv_depth.shape[1]
    radius = RADIUS
    start = lax.axis_index("frames") * f_dev
    pixel = lax.axis_index("pix") * plocal + jnp.arange(plocal, dtype=jnp.int32)
    col_coord, row_coord = pixel_coords(pixel)
    source = edge_frames[0]
    target = edge_frames[1]
    source_ext = source - start + radius
    target_ext = target - start + radius
    slots = jnp.arange(f_dev + 2 * radius, dtype=jnp.int32)
    pick_source = (slots[:, None] == source_ext[None, :]).astype(jnp.float32)
    pick_target = (slots[:, None] == target_ext[None, :]).astype(jnp.float32)
    rot = rotations(rotvec)
    rel_rot, rel_trans, adjoint = relative(rot, trans, source, target)
    depth_table = padded(inv_depth, (("frames", 0),), radius)
    depth_edges = jnp.take(depth_table, source_ext, axis=0)
    geo = geometry(rel_rot, rel_trans, depth_edges, flow, weight, mask, col_coord, row_coord)
    slope_u, slope_v, conf_u, conf_v, error_u, error_v = (
        geo[3],
        geo[4],
        geo[5],
        geo[6],
        geo[7],
        geo[8],
    )

    def fetch_image(values):
        table = padded(values, (("frames", 0),), radius)
        return jnp.take(table, source_ext, axis=0)

    def fetch_step(motion):
        table = padded(motion, (("frames", 1),), radius)
        at_source = jnp.take(table, source_ext, axis=1)
        at_target = jnp.take(table, target_ext, axis=1)
        return at_target - jnp.einsum("jke,ke->je", adjoint, at_source, precision=exact)

    def collect_depth(terms):
        extended = jnp.einsum("fe,ep->fp", pick_source, terms, precision=exact)
        lower, own, upper = margins(extended, radius, f_dev, 0)
        from_above = from_behind(lower, "frames", -1)
        from_below = from_behind(upper, "frames", 1)
        return settle(own, from_below, from_above, 0)

    def pass_rims(extended):
        lower, own, upper = margins(extended, radius, f_dev, 1)
        from_above = from_behind(lower, "frames", -1)
        from_below = from_behind(upper, "frames", 1)
        return settle(own, from_below, from_above, 1)

    def collect_pose(part_u, part_v):
        target_terms = pose_terms(geo, part_u, part_v)
        source_terms = -jnp.einsum("jke,je->ke", adjoint, target_terms, precision=exact)
        extended = jnp.einsum("ke,fe->kf", target_terms, pick_target, precision=exact) + jnp.einsum(
            "ke,fe->kf", source_terms, pick_source, precision=exact
        )
        return pass_rims(total_of_pieces(extended, "pix"))

    terms = jnp.stack(
        [
            conf_u * slope_u * slope_u + conf_v * slope_v * slope_v,
            -(slope_u * conf_u * error_u + slope_v * conf_v * error_v),
        ]
    )
    extended = jnp.einsum("fe,kep->kfp", pick_source, terms, precision=exact)
    lower, own, upper = margins(extended, radius, f_dev, 1)
    from_above = from_behind(lower, "frames", -1)
    from_below = from_behind(upper, "frames", 1)
    totals = settle(own, from_below, from_above, 1)
    curvature = totals[0] + depth_damping
    base_step = totals[1] / curvature
    base_edges = fetch_image(base_step)
    rhs = collect_pose(-error_u - slope_u * base_edges, -error_v - slope_v * base_edges)

    def reduced(motion):
        lin_u, lin_v = apply_pose(geo, fetch_step(motion))
        image = collect_depth(slope_u * conf_u * lin_u + slope_v * conf_v * lin_v) / curvature
        image_edges = fetch_image(image)
        return (
            collect_pose(lin_u - slope_u * image_edges, lin_v - slope_v * image_edges)
            + pose_regularizer * motion
        )

    solution = jnp.zeros_like(rhs)
    residual = rhs

    def two_products(values, image):
        return in_one((jnp.sum(values * values), jnp.sum(values * image)), "frames")

    image = reduced(residual)
    norm_now, product = two_products(residual, image)
    alpha = norm_now / product
    direction, along = (residual, image)
    for step in range(ITERS):
        solution = solution + alpha * direction
        residual = residual - alpha * along
        if step + 1 < ITERS:
            image = reduced(residual)
            norm_next, product = two_products(residual, image)
            ratio = norm_next / norm_now
            alpha = norm_next / (product - ratio * norm_next / alpha)
            direction = residual + ratio * direction
            along = image + ratio * along
            norm_now = norm_next
    lin_u, lin_v = apply_pose(geo, fetch_step(solution))
    depth_step = (
        base_step - collect_depth(slope_u * conf_u * lin_u + slope_v * conf_v * lin_v) / curvature
    )
    return (solution, depth_step)


def solution(mesh):
    return jax.shard_map(
        per_device,
        mesh=mesh,
        in_specs=(
            P(None, "frames"),
            P(),
            P(),
            P("frames", "pix"),
            P("frames", "pix"),
            P("frames", None, "pix"),
            P("frames", None, "pix"),
            P("frames", "pix"),
        ),
        out_specs=(P(None, "frames"), P("frames", "pix")),
        check_vma=False,
    )
```

profile of v0, /device:TPU:8, one launch (start us, length us, event | category | flops | bytes accessed | tf_op | source)
XLA Modules:
  0.0 715.7 jit_solution(11499175933534023825)
XLA Ops:
  1.4 3.8 collective-permute-start
  5.2 6.8 collective-permute-start.1
  22.6 3.8 fusion.165
  26.3 1.9 fusion.166
  28.4 2.2 convolution_bitcast_fusion.1
  30.6 6.0 slice_reduce_fusion.44
  40.6 3.3 add_bitcast_fusion
  48.1 8.7 %collective-permute-start.3 = (f32[2,8,768]{2,1,0:T(8,128)}, f32[2,8,768]{2,1,0:T(8,128)}, u32[]{:S(2)}, u32[]{:S(2)}) collective-permute-start(f32[2,8,768]{2,1,0:T(8,128)} %get-tuple-element.170), channel_id=1, source_target_pairs={{4,0},{8,4},{12,8},{16,12},{20,16},{24,20},{28,24},{32,28},{36,32}... | collective-permute-start | bytes 147464 | tf_op jit(solution)/shard_map/ppermute | solution.py:32
  63.7 9.2 %collective-permute-start.5 = (f32[8,768]{1,0:T(8,128)S(1)}, f32[8,768]{1,0:T(8,128)S(1)}, u32[]{:S(2)}, u32[]{:S(2)}) collective-permute-start(f32[8,768]{1,0:T(8,128)S(1)} %get-tuple-element.198), channel_id=1, source_target_pairs={{4,0},{8,4},{12,8},{16,12},{20,16},{24,20},{28,24},{32,28},{36,32}... | collective-permute-start | bytes 73736 | tf_op jit(solution)/shard_map/ppermute | solution.py:24
  72.9 3.2 convolution_bitcast_fusion
  77.4 1.9 gather_fusion.5
  79.4 2.0 subtract_multiply_fusion.13
  83.4 10.5 %all-gather.7 = f32[4,6,32]{2,1,0:T(8,128)S(1)} all-gather(f32[1,6,32]{2,1,0:T(8,128)S(1)} %fusion.13), channel_id=2, replica_groups=mesh['frames'=64,'pix'=4] {'pix'}, dimensions={0}, use_global_device_ids=true | all-gather | bytes 3840 | tf_op jit(solution)/shard_map/all_gather | solution.py:36
  95.8 8.7 %collective-permute-start.7 = (f32[6,8]{1,0:T(8,128)S(1)}, f32[6,8]{1,0:T(8,128)S(1)}, u32[]{:S(2)}, u32[]{:S(2)}) collective-permute-start(f32[6,8]{1,0:T(8,128)S(1)} %get-tuple-element.236), channel_id=1, source_target_pairs={{4,0},{8,4},{12,8},{16,12},{20,16},{24,20},{28,24},{32,28},{36,32}... | collective-permute-start | bytes 584 | tf_op jit(solution)/shard_map/ppermute | solution.py:32
  108.0 9.0 %collective-permute-start.9 = (f32[6,8]{1,0:T(8,128)S(1)}, f32[6,8]{1,0:T(8,128)S(1)}, u32[]{:S(2)}, u32[]{:S(2)}) collective-permute-start(f32[6,8]{1,0:T(8,128)S(1)} %get-tuple-element.234), channel_id=1, source_target_pairs={{4,0},{8,4},{12,8},{16,12},{20,16},{24,20},{28,24},{32,28},{36,32}... | collective-permute-start | bytes 584 | tf_op jit(solution)/shard_map/ppermute | solution.py:24
  125.5 9.0 %collective-permute-start.11 = (f32[8,768]{1,0:T(8,128)S(1)}, f32[8,768]{1,0:T(8,128)S(1)}, u32[]{:S(2)}, u32[]{:S(2)}) collective-permute-start(f32[8,768]{1,0:T(8,128)S(1)} %get-tuple-element.184), channel_id=1, source_target_pairs={{4,0},{8,4},{12,8},{16,12},{20,16},{24,20},{28,24},{32,28},{36,32}... | collective-permute-start | bytes 73736 | tf_op jit(solution)/shard_map/ppermute | solution.py:32
  138.0 9.1 %collective-permute-start.13 = (f32[8,768]{1,0:T(8,128)S(1)}, f32[8,768]{1,0:T(8,128)S(1)}, u32[]{:S(2)}, u32[]{:S(2)}) collective-permute-start(f32[8,768]{1,0:T(8,128)S(1)} %get-tuple-element.196), channel_id=1, source_target_pairs={{4,0},{8,4},{12,8},{16,12},{20,16},{24,20},{28,24},{32,28},{36,32}... | collective-permute-start | bytes 73736 | tf_op jit(solution)/shard_map/ppermute | solution.py:24
  150.3 2.4 subtract_multiply_fusion.11
  154.1 9.1 %all-gather.8 = f32[4,6,32]{2,1,0:T(8,128)S(1)} all-gather(f32[1,6,32]{2,1,0:T(8,128)S(1)} %fusion.12), channel_id=3, replica_groups=mesh['frames'=64,'pix'=4] {'pix'}, dimensions={0}, use_global_device_ids=true | all-gather | bytes 3840 | tf_op jit(solution)/shard_map/all_gather | solution.py:36
  165.2 9.1 %collective-permute-start.15 = (f32[6,8]{1,0:T(8,128)S(1)}, f32[6,8]{1,0:T(8,128)S(1)}, u32[]{:S(2)}, u32[]{:S(2)}) collective-permute-start(f32[6,8]{1,0:T(8,128)S(1)} %get-tuple-element.232), channel_id=1, source_target_pairs={{4,0},{8,4},{12,8},{16,12},{20,16},{24,20},{28,24},{32,28},{36,32}... | collective-permute-start | bytes 584 | tf_op jit(solution)/shard_map/ppermute | solution.py:32
  177.5 20.5 %all_to_all.36 = f32[64,1,2]{2,1,0:T(1,128)S(1)} all-to-all(f32[64,1,2]{2,1,0:T(1,128)S(1)} %broadcast_in_dim.51), channel_id=1, replica_groups=mesh['frames'=64,'pix'=4] {'frames'}, dimensions={0} | all-to-all | bytes 1024 | tf_op jit(solution)/shard_map/all_to_all | solution.py:42
  200.2 2.5 collective-permute-start.16
  202.7 8.1 %collective-permute-start.17 = (f32[6,8]{1,0:T(8,128)S(1)}, f32[6,8]{1,0:T(8,128)S(1)}, u32[]{:S(2)}, u32[]{:S(2)}) collective-permute-start(f32[6,8]{1,0:T(8,128)S(1)} %get-tuple-element.230), channel_id=1, source_target_pairs={{4,0},{8,4},{12,8},{16,12},{20,16},{24,20},{28,24},{32,28},{36,32}... | collective-permute-start | bytes 584 | tf_op jit(solution)/shard_map/ppermute | solution.py:24
  220.8 9.0 %collective-permute-start.19 = (f32[8,768]{1,0:T(8,128)S(1)}, f32[8,768]{1,0:T(8,128)S(1)}, u32[]{:S(2)}, u32[]{:S(2)}) collective-permute-start(f32[8,768]{1,0:T(8,128)S(1)} %get-tuple-element.182), channel_id=1, source_target_pairs={{4,0},{8,4},{12,8},{16,12},{20,16},{24,20},{28,24},{32,28},{36,32}... | collective-permute-start | bytes 73736 | tf_op jit(solution)/shard_map/ppermute | solution.py:32
  233.2 9.0 %collective-permute-start.21 = (f32[8,768]{1,0:T(8,128)S(1)}, f32[8,768]{1,0:T(8,128)S(1)}, u32[]{:S(2)}, u32[]{:S(2)}) collective-permute-start(f32[8,768]{1,0:T(8,128)S(1)} %get-tuple-element.194), channel_id=1, source_target_pairs={{4,0},{8,4},{12,8},{16,12},{20,16},{24,20},{28,24},{32,28},{36,32}... | collective-permute-start | bytes 73736 | tf_op jit(solution)/shard_map/ppermute | solution.py:24
  245.5 2.4 subtract_multiply_fusion.9
  249.3 9.1 %all-gather.9 = f32[4,6,32]{2,1,0:T(8,128)S(1)} all-gather(f32[1,6,32]{2,1,0:T(8,128)S(1)} %fusion.11), channel_id=4, replica_groups=mesh['frames'=64,'pix'=4] {'pix'}, dimensions={0}, use_global_device_ids=true | all-gather | bytes 3840 | tf_op jit(solution)/shard_map/all_gather | solution.py:36
  260.4 9.0 %collective-permute-start.23 = (f32[6,8]{1,0:T(8,128)S(1)}, f32[6,8]{1,0:T(8,128)S(1)}, u32[]{:S(2)}, u32[]{:S(2)}) collective-permute-start(f32[6,8]{1,0:T(8,128)S(1)} %get-tuple-element.228), channel_id=1, source_target_pairs={{4,0},{8,4},{12,8},{16,12},{20,16},{24,20},{28,24},{32,28},{36,32}... | collective-permute-start | bytes 584 | tf_op jit(solution)/shard_map/ppermute | solution.py:32
  272.8 19.4 %all_to_all.37 = f32[64,1,2]{2,1,0:T(1,128)S(1)} all-to-all(f32[64,1,2]{2,1,0:T(1,128)S(1)} %broadcast_in_dim.52), channel_id=1, replica_groups=mesh['frames'=64,'pix'=4] {'frames'}, dimensions={0} | all-to-all | bytes 1024 | tf_op jit(solution)/shard_map/all_to_all | solution.py:42
  297.3 2.5 collective-permute-start.24
  299.8 8.1 %collective-permute-start.25 = (f32[6,8]{1,0:T(8,128)S(1)}, f32[6,8]{1,0:T(8,128)S(1)}, u32[]{:S(2)}, u32[]{:S(2)}) collective-permute-start(f32[6,8]{1,0:T(8,128)S(1)} %get-tuple-element.226), channel_id=1, source_target_pairs={{4,0},{8,4},{12,8},{16,12},{20,16},{24,20},{28,24},{32,28},{36,32}... | collective-permute-start | bytes 584 | tf_op jit(solution)/shard_map/ppermute | solution.py:24
  317.8 9.0 %collective-permute-start.27 = (f32[8,768]{1,0:T(8,128)S(1)}, f32[8,768]{1,0:T(8,128)S(1)}, u32[]{:S(2)}, u32[]{:S(2)}) collective-permute-start(f32[8,768]{1,0:T(8,128)S(1)} %get-tuple-element.180), channel_id=1, source_target_pairs={{4,0},{8,4},{12,8},{16,12},{20,16},{24,20},{28,24},{32,28},{36,32}... | collective-permute-start | bytes 73736 | tf_op jit(solution)/shard_map/ppermute | solution.py:32
  330.3 9.2 %collective-permute-start.29 = (f32[8,768]{1,0:T(8,128)S(1)}, f32[8,768]{1,0:T(8,128)S(1)}, u32[]{:S(2)}, u32[]{:S(2)}) collective-permute-start(f32[8,768]{1,0:T(8,128)S(1)} %get-tuple-element.192), channel_id=1, source_target_pairs={{4,0},{8,4},{12,8},{16,12},{20,16},{24,20},{28,24},{32,28},{36,32}... | collective-permute-start | bytes 73736 | tf_op jit(solution)/shard_map/ppermute | solution.py:24
  342.6 2.4 subtract_multiply_fusion.7
  346.5 9.1 %all-gather.10 = f32[4,6,32]{2,1,0:T(8,128)S(1)} all-gather(f32[1,6,32]{2,1,0:T(8,128)S(1)} %fusion.10), channel_id=5, replica_groups=mesh['frames'=64,'pix'=4] {'pix'}, dimensions={0}, use_global_device_ids=true | all-gather | bytes 3840 | tf_op jit(solution)/shard_map/all_gather | solution.py:36
  357.6 9.0 %collective-permute-start.31 = (f32[6,8]{1,0:T(8,128)S(1)}, f32[6,8]{1,0:T(8,128)S(1)}, u32[]{:S(2)}, u32[]{:S(2)}) collective-permute-start(f32[6,8]{1,0:T(8,128)S(1)} %get-tuple-element.224), channel_id=1, source_target_pairs={{4,0},{8,4},{12,8},{16,12},{20,16},{24,20},{28,24},{32,28},{36,32}... | collective-permute-start | bytes 584 | tf_op jit(solution)/shard_map/ppermute | solution.py:32
  370.1 19.4 %all_to_all.38 = f32[64,1,2]{2,1,0:T(1,128)S(1)} all-to-all(f32[64,1,2]{2,1,0:T(1,128)S(1)} %broadcast_in_dim.53), channel_id=1, replica_groups=mesh['frames'=64,'pix'=4] {'frames'}, dimensions={0} | all-to-all | bytes 1024 | tf_op jit(solution)/shard_map/all_to_all | solution.py:42
  394.8 2.5 collective-permute-start.32
  397.3 8.1 %collective-permute-start.33 = (f32[6,8]{1,0:T(8,128)S(1)}, f32[6,8]{1,0:T(8,128)S(1)}, u32[]{:S(2)}, u32[]{:S(2)}) collective-permute-start(f32[6,8]{1,0:T(8,128)S(1)} %get-tuple-element.222), channel_id=1, source_target_pairs={{4,0},{8,4},{12,8},{16,12},{20,16},{24,20},{28,24},{32,28},{36,32}... | collective-permute-start | bytes 584 | tf_op jit(solution)/shard_map/ppermute | solution.py:24
  415.4 9.0 %collective-permute-start.35 = (f32[8,768]{1,0:T(8,128)S(1)}, f32[8,768]{1,0:T(8,128)S(1)}, u32[]{:S(2)}, u32[]{:S(2)}) collective-permute-start(f32[8,768]{1,0:T(8,128)S(1)} %get-tuple-element.178), channel_id=1, source_target_pairs={{4,0},{8,4},{12,8},{16,12},{20,16},{24,20},{28,24},{32,28},{36,32}... | collective-permute-start | bytes 73736 | tf_op jit(solution)/shard_map/ppermute | solution.py:32
  427.8 9.0 %collective-permute-start.37 = (f32[8,768]{1,0:T(8,128)S(1)}, f32[8,768]{1,0:T(8,128)S(1)}, u32[]{:S(2)}, u32[]{:S(2)}) collective-permute-start(f32[8,768]{1,0:T(8,128)S(1)} %get-tuple-element.190), channel_id=1, source_target_pairs={{4,0},{8,4},{12,8},{16,12},{20,16},{24,20},{28,24},{32,28},{36,32}... | collective-permute-start | bytes 73736 | tf_op jit(solution)/shard_map/ppermute | solution.py:24
  440.1 2.4 subtract_multiply_fusion.5
  444.0 9.1 %all-gather.11 = f32[4,6,32]{2,1,0:T(8,128)S(1)} all-gather(f32[1,6,32]{2,1,0:T(8,128)S(1)} %fusion.9), channel_id=6, replica_groups=mesh['frames'=64,'pix'=4] {'pix'}, dimensions={0}, use_global_device_ids=true | all-gather | bytes 3840 | tf_op jit(solution)/shard_map/all_gather | solution.py:36
  455.1 9.0 %collective-permute-start.39 = (f32[6,8]{1,0:T(8,128)S(1)}, f32[6,8]{1,0:T(8,128)S(1)}, u32[]{:S(2)}, u32[]{:S(2)}) collective-permute-start(f32[6,8]{1,0:T(8,128)S(1)} %get-tuple-element.220), channel_id=1, source_target_pairs={{4,0},{8,4},{12,8},{16,12},{20,16},{24,20},{28,24},{32,28},{36,32}... | collective-permute-start | bytes 584 | tf_op jit(solution)/shard_map/ppermute | solution.py:32
  467.5 19.4 %all_to_all.39 = f32[64,1,2]{2,1,0:T(1,128)S(1)} all-to-all(f32[64,1,2]{2,1,0:T(1,128)S(1)} %broadcast_in_dim.54), channel_id=1, replica_groups=mesh['frames'=64,'pix'=4] {'frames'}, dimensions={0} | all-to-all | bytes 1024 | tf_op jit(solution)/shard_map/all_to_all | solution.py:42
  491.4 2.5 collective-permute-start.40
  493.9 8.4 %collective-permute-start.41 = (f32[6,8]{1,0:T(8,128)S(1)}, f32[6,8]{1,0:T(8,128)S(1)}, u32[]{:S(2)}, u32[]{:S(2)}) collective-permute-start(f32[6,8]{1,0:T(8,128)S(1)} %get-tuple-element.218), channel_id=1, source_target_pairs={{4,0},{8,4},{12,8},{16,12},{20,16},{24,20},{28,24},{32,28},{36,32}... | collective-permute-start | bytes 584 | tf_op jit(solution)/shard_map/ppermute | solution.py:24
  512.0 9.0 %collective-permute-start.43 = (f32[8,768]{1,0:T(8,128)S(1)}, f32[8,768]{1,0:T(8,128)S(1)}, u32[]{:S(2)}, u32[]{:S(2)}) collective-permute-start(f32[8,768]{1,0:T(8,128)S(1)} %get-tuple-element.176), channel_id=1, source_target_pairs={{4,0},{8,4},{12,8},{16,12},{20,16},{24,20},{28,24},{32,28},{36,32}... | collective-permute-start | bytes 73736 | tf_op jit(solution)/shard_map/ppermute | solution.py:32
  524.5 9.0 %collective-permute-start.45 = (f32[8,768]{1,0:T(8,128)S(1)}, f32[8,768]{1,0:T(8,128)S(1)}, u32[]{:S(2)}, u32[]{:S(2)}) collective-permute-start(f32[8,768]{1,0:T(8,128)S(1)} %get-tuple-element.188), channel_id=1, source_target_pairs={{4,0},{8,4},{12,8},{16,12},{20,16},{24,20},{28,24},{32,28},{36,32}... | collective-permute-start | bytes 73736 | tf_op jit(solution)/shard_map/ppermute | solution.py:24
  536.8 2.4 subtract_multiply_fusion.3
  540.6 9.1 %all-gather.12 = f32[4,6,32]{2,1,0:T(8,128)S(1)} all-gather(f32[1,6,32]{2,1,0:T(8,128)S(1)} %fusion.8), channel_id=7, replica_groups=mesh['frames'=64,'pix'=4] {'pix'}, dimensions={0}, use_global_device_ids=true | all-gather | bytes 3840 | tf_op jit(solution)/shard_map/all_gather | solution.py:36
  551.7 9.0 %collective-permute-start.47 = (f32[6,8]{1,0:T(8,128)S(1)}, f32[6,8]{1,0:T(8,128)S(1)}, u32[]{:S(2)}, u32[]{:S(2)}) collective-permute-start(f32[6,8]{1,0:T(8,128)S(1)} %get-tuple-element.216), channel_id=1, source_target_pairs={{4,0},{8,4},{12,8},{16,12},{20,16},{24,20},{28,24},{32,28},{36,32}... | collective-permute-start | bytes 584 | tf_op jit(solution)/shard_map/ppermute | solution.py:32
  564.2 19.4 %all_to_all.40 = f32[64,1,2]{2,1,0:T(1,128)S(1)} all-to-all(f32[64,1,2]{2,1,0:T(1,128)S(1)} %broadcast_in_dim.55), channel_id=1, replica_groups=mesh['frames'=64,'pix'=4] {'frames'}, dimensions={0} | all-to-all | bytes 1024 | tf_op jit(solution)/shard_map/all_to_all | solution.py:42
  588.4 2.5 collective-permute-start.48
  590.9 8.1 %collective-permute-start.49 = (f32[6,8]{1,0:T(8,128)S(1)}, f32[6,8]{1,0:T(8,128)S(1)}, u32[]{:S(2)}, u32[]{:S(2)}) collective-permute-start(f32[6,8]{1,0:T(8,128)S(1)} %get-tuple-element.214), channel_id=1, source_target_pairs={{4,0},{8,4},{12,8},{16,12},{20,16},{24,20},{28,24},{32,28},{36,32}... | collective-permute-start | bytes 584 | tf_op jit(solution)/shard_map/ppermute | solution.py:24
  608.9 9.0 %collective-permute-start.51 = (f32[8,768]{1,0:T(8,128)S(1)}, f32[8,768]{1,0:T(8,128)S(1)}, u32[]{:S(2)}, u32[]{:S(2)}) collective-permute-start(f32[8,768]{1,0:T(8,128)S(1)} %get-tuple-element.174), channel_id=1, source_target_pairs={{4,0},{8,4},{12,8},{16,12},{20,16},{24,20},{28,24},{32,28},{36,32}... | collective-permute-start | bytes 73736 | tf_op jit(solution)/shard_map/ppermute | solution.py:32
  621.4 9.0 %collective-permute-start.53 = (f32[8,768]{1,0:T(8,128)S(1)}, f32[8,768]{1,0:T(8,128)S(1)}, u32[]{:S(2)}, u32[]{:S(2)}) collective-permute-start(f32[8,768]{1,0:T(8,128)S(1)} %get-tuple-element.186), channel_id=1, source_target_pairs={{4,0},{8,4},{12,8},{16,12},{20,16},{24,20},{28,24},{32,28},{36,32}... | collective-permute-start | bytes 73736 | tf_op jit(solution)/shard_map/ppermute | solution.py:24
  633.7 2.4 subtract_multiply_fusion.1
  637.5 9.1 %all-gather.13 = f32[4,6,32]{2,1,0:T(8,128)S(1)} all-gather(f32[1,6,32]{2,1,0:T(8,128)S(1)} %fusion.7), channel_id=8, replica_groups=mesh['frames'=64,'pix'=4] {'pix'}, dimensions={0}, use_global_device_ids=true | all-gather | bytes 3840 | tf_op jit(solution)/shard_map/all_gather | solution.py:36
  648.7 9.3 %collective-permute-start.55 = (f32[6,8]{1,0:T(8,128)S(1)}, f32[6,8]{1,0:T(8,128)S(1)}, u32[]{:S(2)}, u32[]{:S(2)}) collective-permute-start(f32[6,8]{1,0:T(8,128)S(1)} %get-tuple-element.212), channel_id=1, source_target_pairs={{4,0},{8,4},{12,8},{16,12},{20,16},{24,20},{28,24},{32,28},{36,32}... | collective-permute-start | bytes 584 | tf_op jit(solution)/shard_map/ppermute | solution.py:32
  661.3 19.4 %all_to_all.41 = f32[64,1,2]{2,1,0:T(1,128)S(1)} all-to-all(f32[64,1,2]{2,1,0:T(1,128)S(1)} %broadcast_in_dim.56), channel_id=1, replica_groups=mesh['frames'=64,'pix'=4] {'frames'}, dimensions={0} | all-to-all | bytes 1024 | tf_op jit(solution)/shard_map/all_to_all | solution.py:42
  685.5 2.5 collective-permute-start.56
  688.0 8.1 %collective-permute-start.57 = (f32[6,8]{1,0:T(8,128)S(1)}, f32[6,8]{1,0:T(8,128)S(1)}, u32[]{:S(2)}, u32[]{:S(2)}) collective-permute-start(f32[6,8]{1,0:T(8,128)S(1)} %get-tuple-element.210), channel_id=1, source_target_pairs={{4,0},{8,4},{12,8},{16,12},{20,16},{24,20},{28,24},{32,28},{36,32}... | collective-permute-start | bytes 584 | tf_op jit(solution)/shard_map/ppermute | solution.py:24
  704.1 9.0 %collective-permute-start.59 = (f32[8,768]{1,0:T(8,128)S(1)}, f32[8,768]{1,0:T(8,128)S(1)}, u32[]{:S(2)}, u32[]{:S(2)}) collective-permute-start(f32[8,768]{1,0:T(8,128)S(1)} %get-tuple-element.172), channel_id=1, source_target_pairs={{4,0},{8,4},{12,8},{16,12},{20,16},{24,20},{28,24},{32,28},{36,32}... | collective-permute-start | bytes 73736 | tf_op jit(solution)/shard_map/ppermute | solution.py:32
  (494 shorter events, 187.9 us)
Async XLA Ops:
  1.4 37.4 %collective-permute-start = (f32[8,768]{1,0:T(8,128)S(1)}, f32[8,768]{1,0:T(8,128)S(1)}, u32[]{:S(2)}, u32[]{:S(2)}) collective-permute-start(f32[8,768]{1,0:T(8,128)S(1)} %get-tuple-element.199), channel_id=1, source_target_pairs={{0,4},{4,8},{8,12},{12,16},{16,20},{20,24},{24,28},{28,32},{32,36}... | collective-permute-start | bytes 73736 | tf_op jit(solution)/shard_map/ppermute | solution.py:21
  5.2 33.6 %collective-permute-start.1 = (f32[8,768]{1,0:T(8,128)S(1)}, f32[8,768]{1,0:T(8,128)S(1)}, u32[]{:S(2)}, u32[]{:S(2)}) collective-permute-start(f32[8,768]{1,0:T(8,128)S(1)} %get-tuple-element.200), channel_id=1, source_target_pairs={{4,0},{8,4},{12,8},{16,12},{20,16},{24,20},{28,24},{32,28},{36,32}... | collective-permute-start | bytes 73736 | tf_op jit(solution)/shard_map/ppermute | solution.py:24
  46.2 11.7 %collective-permute-start.2 = (f32[2,8,768]{2,1,0:T(8,128)}, f32[2,8,768]{2,1,0:T(8,128)}, u32[]{:S(2)}, u32[]{:S(2)}) collective-permute-start(f32[2,8,768]{2,1,0:T(8,128)} %get-tuple-element.169), channel_id=1, source_target_pairs={{0,4},{4,8},{8,12},{12,16},{16,20},{20,24},{24,28},{28,32},{32,36}... | collective-permute-start | bytes 147464 | tf_op jit(solution)/shard_map/ppermute | solution.py:32
  48.1 10.8 %collective-permute-start.3 = (f32[2,8,768]{2,1,0:T(8,128)}, f32[2,8,768]{2,1,0:T(8,128)}, u32[]{:S(2)}, u32[]{:S(2)}) collective-permute-start(f32[2,8,768]{2,1,0:T(8,128)} %get-tuple-element.170), channel_id=1, source_target_pairs={{4,0},{8,4},{12,8},{16,12},{20,16},{24,20},{28,24},{32,28},{36,32}... | collective-permute-start | bytes 147464 | tf_op jit(solution)/shard_map/ppermute | solution.py:32
  61.8 15.6 %collective-permute-start.4 = (f32[8,768]{1,0:T(8,128)S(1)}, f32[8,768]{1,0:T(8,128)S(1)}, u32[]{:S(2)}, u32[]{:S(2)}) collective-permute-start(f32[8,768]{1,0:T(8,128)S(1)} %get-tuple-element.197), channel_id=1, source_target_pairs={{0,4},{4,8},{8,12},{12,16},{16,20},{20,24},{24,28},{28,32},{32,36}... | collective-permute-start | bytes 73736 | tf_op jit(solution)/shard_map/ppermute | solution.py:21
  63.7 13.7 %collective-permute-start.5 = (f32[8,768]{1,0:T(8,128)S(1)}, f32[8,768]{1,0:T(8,128)S(1)}, u32[]{:S(2)}, u32[]{:S(2)}) collective-permute-start(f32[8,768]{1,0:T(8,128)S(1)} %get-tuple-element.198), channel_id=1, source_target_pairs={{4,0},{8,4},{12,8},{16,12},{20,16},{24,20},{28,24},{32,28},{36,32}... | collective-permute-start | bytes 73736 | tf_op jit(solution)/shard_map/ppermute | solution.py:24
  93.9 10.7 %collective-permute-start.6 = (f32[6,8]{1,0:T(8,128)S(1)}, f32[6,8]{1,0:T(8,128)S(1)}, u32[]{:S(2)}, u32[]{:S(2)}) collective-permute-start(f32[6,8]{1,0:T(8,128)S(1)} %get-tuple-element.235), channel_id=1, source_target_pairs={{0,4},{4,8},{8,12},{12,16},{16,20},{20,24},{24,28},{28,32},{32,36}... | collective-permute-start | bytes 584 | tf_op jit(solution)/shard_map/ppermute | solution.py:32
  95.8 10.0 %collective-permute-start.7 = (f32[6,8]{1,0:T(8,128)S(1)}, f32[6,8]{1,0:T(8,128)S(1)}, u32[]{:S(2)}, u32[]{:S(2)}) collective-permute-start(f32[6,8]{1,0:T(8,128)S(1)} %get-tuple-element.236), channel_id=1, source_target_pairs={{4,0},{8,4},{12,8},{16,12},{20,16},{24,20},{28,24},{32,28},{36,32}... | collective-permute-start | bytes 584 | tf_op jit(solution)/shard_map/ppermute | solution.py:32
  106.0 11.3 %collective-permute-start.8 = (f32[6,8]{1,0:T(8,128)S(1)}, f32[6,8]{1,0:T(8,128)S(1)}, u32[]{:S(2)}, u32[]{:S(2)}) collective-permute-start(f32[6,8]{1,0:T(8,128)S(1)} %get-tuple-element.233), channel_id=1, source_target_pairs={{0,4},{4,8},{8,12},{12,16},{16,20},{20,24},{24,28},{28,32},{32,36}... | collective-permute-start | bytes 584 | tf_op jit(solution)/shard_map/ppermute | solution.py:21
  108.0 10.3 %collective-permute-start.9 = (f32[6,8]{1,0:T(8,128)S(1)}, f32[6,8]{1,0:T(8,128)S(1)}, u32[]{:S(2)}, u32[]{:S(2)}) collective-permute-start(f32[6,8]{1,0:T(8,128)S(1)} %get-tuple-element.234), channel_id=1, source_target_pairs={{4,0},{8,4},{12,8},{16,12},{20,16},{24,20},{28,24},{32,28},{36,32}... | collective-permute-start | bytes 584 | tf_op jit(solution)/shard_map/ppermute | solution.py:24
  123.6 10.9 %collective-permute-start.10 = (f32[8,768]{1,0:T(8,128)S(1)}, f32[8,768]{1,0:T(8,128)S(1)}, u32[]{:S(2)}, u32[]{:S(2)}) collective-permute-start(f32[8,768]{1,0:T(8,128)S(1)} %get-tuple-element.183), channel_id=1, source_target_pairs={{0,4},{4,8},{8,12},{12,16},{16,20},{20,24},{24,28},{28,32},{32,36}... | collective-permute-start | bytes 73736 | tf_op jit(solution)/shard_map/ppermute | solution.py:32
  125.5 10.5 %collective-permute-start.11 = (f32[8,768]{1,0:T(8,128)S(1)}, f32[8,768]{1,0:T(8,128)S(1)}, u32[]{:S(2)}, u32[]{:S(2)}) collective-permute-start(f32[8,768]{1,0:T(8,128)S(1)} %get-tuple-element.184), channel_id=1, source_target_pairs={{4,0},{8,4},{12,8},{16,12},{20,16},{24,20},{28,24},{32,28},{36,32}... | collective-permute-start | bytes 73736 | tf_op jit(solution)/shard_map/ppermute | solution.py:32
  136.0 11.0 %collective-permute-start.12 = (f32[8,768]{1,0:T(8,128)S(1)}, f32[8,768]{1,0:T(8,128)S(1)}, u32[]{:S(2)}, u32[]{:S(2)}) collective-permute-start(f32[8,768]{1,0:T(8,128)S(1)} %get-tuple-element.195), channel_id=1, source_target_pairs={{0,4},{4,8},{8,12},{12,16},{16,20},{20,24},{24,28},{28,32},{32,36}... | collective-permute-start | bytes 73736 | tf_op jit(solution)/shard_map/ppermute | solution.py:21
  138.0 10.6 %collective-permute-start.13 = (f32[8,768]{1,0:T(8,128)S(1)}, f32[8,768]{1,0:T(8,128)S(1)}, u32[]{:S(2)}, u32[]{:S(2)}) collective-permute-start(f32[8,768]{1,0:T(8,128)S(1)} %get-tuple-element.196), channel_id=1, source_target_pairs={{4,0},{8,4},{12,8},{16,12},{20,16},{24,20},{28,24},{32,28},{36,32}... | collective-permute-start | bytes 73736 | tf_op jit(solution)/shard_map/ppermute | solution.py:24
  163.3 11.0 %collective-permute-start.14 = (f32[6,8]{1,0:T(8,128)S(1)}, f32[6,8]{1,0:T(8,128)S(1)}, u32[]{:S(2)}, u32[]{:S(2)}) collective-permute-start(f32[6,8]{1,0:T(8,128)S(1)} %get-tuple-element.231), channel_id=1, source_target_pairs={{0,4},{4,8},{8,12},{12,16},{16,20},{20,24},{24,28},{28,32},{32,36}... | collective-permute-start | bytes 584 | tf_op jit(solution)/shard_map/ppermute | solution.py:32
  165.2 10.4 %collective-permute-start.15 = (f32[6,8]{1,0:T(8,128)S(1)}, f32[6,8]{1,0:T(8,128)S(1)}, u32[]{:S(2)}, u32[]{:S(2)}) collective-permute-start(f32[6,8]{1,0:T(8,128)S(1)} %get-tuple-element.232), channel_id=1, source_target_pairs={{4,0},{8,4},{12,8},{16,12},{20,16},{24,20},{28,24},{32,28},{36,32}... | collective-permute-start | bytes 584 | tf_op jit(solution)/shard_map/ppermute | solution.py:32
  176.2 120.9 %copy-start.52 = (f32[6,16]{1,0:T(8,128)}, f32[6,16]{1,0:T(8,128)S(1)}, u32[]{:S(2)}) copy-start(f32[6,16]{1,0:T(8,128)S(1)} %get-tuple-element.119) | copy-start | bytes 1156
  200.2 10.7 %collective-permute-start.16 = (f32[6,8]{1,0:T(8,128)S(1)}, f32[6,8]{1,0:T(8,128)S(1)}, u32[]{:S(2)}, u32[]{:S(2)}) collective-permute-start(f32[6,8]{1,0:T(8,128)S(1)} %get-tuple-element.229), channel_id=1, source_target_pairs={{0,4},{4,8},{8,12},{12,16},{16,20},{20,24},{24,28},{28,32},{32,36}... | collective-permute-start | bytes 584 | tf_op jit(solution)/shard_map/ppermute | solution.py:21
  202.7 9.5 %collective-permute-start.17 = (f32[6,8]{1,0:T(8,128)S(1)}, f32[6,8]{1,0:T(8,128)S(1)}, u32[]{:S(2)}, u32[]{:S(2)}) collective-permute-start(f32[6,8]{1,0:T(8,128)S(1)} %get-tuple-element.230), channel_id=1, source_target_pairs={{4,0},{8,4},{12,8},{16,12},{20,16},{24,20},{28,24},{32,28},{36,32}... | collective-permute-start | bytes 584 | tf_op jit(solution)/shard_map/ppermute | solution.py:24
  218.8 10.9 %collective-permute-start.18 = (f32[8,768]{1,0:T(8,128)S(1)}, f32[8,768]{1,0:T(8,128)S(1)}, u32[]{:S(2)}, u32[]{:S(2)}) collective-permute-start(f32[8,768]{1,0:T(8,128)S(1)} %get-tuple-element.181), channel_id=1, source_target_pairs={{0,4},{4,8},{8,12},{12,16},{16,20},{20,24},{24,28},{28,32},{32,36}... | collective-permute-start | bytes 73736 | tf_op jit(solution)/shard_map/ppermute | solution.py:32
  220.8 10.5 %collective-permute-start.19 = (f32[8,768]{1,0:T(8,128)S(1)}, f32[8,768]{1,0:T(8,128)S(1)}, u32[]{:S(2)}, u32[]{:S(2)}) collective-permute-start(f32[8,768]{1,0:T(8,128)S(1)} %get-tuple-element.182), channel_id=1, source_target_pairs={{4,0},{8,4},{12,8},{16,12},{20,16},{24,20},{28,24},{32,28},{36,32}... | collective-permute-start | bytes 73736 | tf_op jit(solution)/shard_map/ppermute | solution.py:32
  231.3 11.0 %collective-permute-start.20 = (f32[8,768]{1,0:T(8,128)S(1)}, f32[8,768]{1,0:T(8,128)S(1)}, u32[]{:S(2)}, u32[]{:S(2)}) collective-permute-start(f32[8,768]{1,0:T(8,128)S(1)} %get-tuple-element.193), channel_id=1, source_target_pairs={{0,4},{4,8},{8,12},{12,16},{16,20},{20,24},{24,28},{28,32},{32,36}... | collective-permute-start | bytes 73736 | tf_op jit(solution)/shard_map/ppermute | solution.py:21
  233.2 10.5 %collective-permute-start.21 = (f32[8,768]{1,0:T(8,128)S(1)}, f32[8,768]{1,0:T(8,128)S(1)}, u32[]{:S(2)}, u32[]{:S(2)}) collective-permute-start(f32[8,768]{1,0:T(8,128)S(1)} %get-tuple-element.194), channel_id=1, source_target_pairs={{4,0},{8,4},{12,8},{16,12},{20,16},{24,20},{28,24},{32,28},{36,32}... | collective-permute-start | bytes 73736 | tf_op jit(solution)/shard_map/ppermute | solution.py:24
  258.5 10.9 %collective-permute-start.22 = (f32[6,8]{1,0:T(8,128)S(1)}, f32[6,8]{1,0:T(8,128)S(1)}, u32[]{:S(2)}, u32[]{:S(2)}) collective-permute-start(f32[6,8]{1,0:T(8,128)S(1)} %get-tuple-element.227), channel_id=1, source_target_pairs={{0,4},{4,8},{8,12},{12,16},{16,20},{20,24},{24,28},{28,32},{32,36}... | collective-permute-start | bytes 584 | tf_op jit(solution)/shard_map/ppermute | solution.py:32
  260.4 10.3 %collective-permute-start.23 = (f32[6,8]{1,0:T(8,128)S(1)}, f32[6,8]{1,0:T(8,128)S(1)}, u32[]{:S(2)}, u32[]{:S(2)}) collective-permute-start(f32[6,8]{1,0:T(8,128)S(1)} %get-tuple-element.228), channel_id=1, source_target_pairs={{4,0},{8,4},{12,8},{16,12},{20,16},{24,20},{28,24},{32,28},{36,32}... | collective-permute-start | bytes 584 | tf_op jit(solution)/shard_map/ppermute | solution.py:32
  297.3 10.7 %collective-permute-start.24 = (f32[6,8]{1,0:T(8,128)S(1)}, f32[6,8]{1,0:T(8,128)S(1)}, u32[]{:S(2)}, u32[]{:S(2)}) collective-permute-start(f32[6,8]{1,0:T(8,128)S(1)} %get-tuple-element.225), channel_id=1, source_target_pairs={{0,4},{4,8},{8,12},{12,16},{16,20},{20,24},{24,28},{28,32},{32,36}... | collective-permute-start | bytes 584 | tf_op jit(solution)/shard_map/ppermute | solution.py:21
  299.8 9.5 %collective-permute-start.25 = (f32[6,8]{1,0:T(8,128)S(1)}, f32[6,8]{1,0:T(8,128)S(1)}, u32[]{:S(2)}, u32[]{:S(2)}) collective-permute-start(f32[6,8]{1,0:T(8,128)S(1)} %get-tuple-element.226), channel_id=1, source_target_pairs={{4,0},{8,4},{12,8},{16,12},{20,16},{24,20},{28,24},{32,28},{36,32}... | collective-permute-start | bytes 584 | tf_op jit(solution)/shard_map/ppermute | solution.py:24
  315.9 10.9 %collective-permute-start.26 = (f32[8,768]{1,0:T(8,128)S(1)}, f32[8,768]{1,0:T(8,128)S(1)}, u32[]{:S(2)}, u32[]{:S(2)}) collective-permute-start(f32[8,768]{1,0:T(8,128)S(1)} %get-tuple-element.179), channel_id=1, source_target_pairs={{0,4},{4,8},{8,12},{12,16},{16,20},{20,24},{24,28},{28,32},{32,36}... | collective-permute-start | bytes 73736 | tf_op jit(solution)/shard_map/ppermute | solution.py:32
  317.8 10.5 %collective-permute-start.27 = (f32[8,768]{1,0:T(8,128)S(1)}, f32[8,768]{1,0:T(8,128)S(1)}, u32[]{:S(2)}, u32[]{:S(2)}) collective-permute-start(f32[8,768]{1,0:T(8,128)S(1)} %get-tuple-element.180), channel_id=1, source_target_pairs={{4,0},{8,4},{12,8},{16,12},{20,16},{24,20},{28,24},{32,28},{36,32}... | collective-permute-start | bytes 73736 | tf_op jit(solution)/shard_map/ppermute | solution.py:32
  328.4 11.1 %collective-permute-start.28 = (f32[8,768]{1,0:T(8,128)S(1)}, f32[8,768]{1,0:T(8,128)S(1)}, u32[]{:S(2)}, u32[]{:S(2)}) collective-permute-start(f32[8,768]{1,0:T(8,128)S(1)} %get-tuple-element.191), channel_id=1, source_target_pairs={{0,4},{4,8},{8,12},{12,16},{16,20},{20,24},{24,28},{28,32},{32,36}... | collective-permute-start | bytes 73736 | tf_op jit(solution)/shard_map/ppermute | solution.py:21
  330.3 10.5 %collective-permute-start.29 = (f32[8,768]{1,0:T(8,128)S(1)}, f32[8,768]{1,0:T(8,128)S(1)}, u32[]{:S(2)}, u32[]{:S(2)}) collective-permute-start(f32[8,768]{1,0:T(8,128)S(1)} %get-tuple-element.192), channel_id=1, source_target_pairs={{4,0},{8,4},{12,8},{16,12},{20,16},{24,20},{28,24},{32,28},{36,32}... | collective-permute-start | bytes 73736 | tf_op jit(solution)/shard_map/ppermute | solution.py:24
  345.0 49.1 %copy-start.53 = (f32[6,16]{1,0:T(8,128)S(1)}, f32[6,16]{1,0:T(8,128)}, u32[]{:S(2)}) copy-start(f32[6,16]{1,0:T(8,128)} %copy-done.52) | copy-start | bytes 1156
  355.7 10.9 %collective-permute-start.30 = (f32[6,8]{1,0:T(8,128)S(1)}, f32[6,8]{1,0:T(8,128)S(1)}, u32[]{:S(2)}, u32[]{:S(2)}) collective-permute-start(f32[6,8]{1,0:T(8,128)S(1)} %get-tuple-element.223), channel_id=1, source_target_pairs={{0,4},{4,8},{8,12},{12,16},{16,20},{20,24},{24,28},{28,32},{32,36}... | collective-permute-start | bytes 584 | tf_op jit(solution)/shard_map/ppermute | solution.py:32
  357.6 10.3 %collective-permute-start.31 = (f32[6,8]{1,0:T(8,128)S(1)}, f32[6,8]{1,0:T(8,128)S(1)}, u32[]{:S(2)}, u32[]{:S(2)}) collective-permute-start(f32[6,8]{1,0:T(8,128)S(1)} %get-tuple-element.224), channel_id=1, source_target_pairs={{4,0},{8,4},{12,8},{16,12},{20,16},{24,20},{28,24},{32,28},{36,32}... | collective-permute-start | bytes 584 | tf_op jit(solution)/shard_map/ppermute | solution.py:32
  394.8 10.7 %collective-permute-start.32 = (f32[6,8]{1,0:T(8,128)S(1)}, f32[6,8]{1,0:T(8,128)S(1)}, u32[]{:S(2)}, u32[]{:S(2)}) collective-permute-start(f32[6,8]{1,0:T(8,128)S(1)} %get-tuple-element.221), channel_id=1, source_target_pairs={{0,4},{4,8},{8,12},{12,16},{16,20},{20,24},{24,28},{28,32},{32,36}... | collective-permute-start | bytes 584 | tf_op jit(solution)/shard_map/ppermute | solution.py:21
  397.3 9.5 %collective-permute-start.33 = (f32[6,8]{1,0:T(8,128)S(1)}, f32[6,8]{1,0:T(8,128)S(1)}, u32[]{:S(2)}, u32[]{:S(2)}) collective-permute-start(f32[6,8]{1,0:T(8,128)S(1)} %get-tuple-element.222), channel_id=1, source_target_pairs={{4,0},{8,4},{12,8},{16,12},{20,16},{24,20},{28,24},{32,28},{36,32}... | collective-permute-start | bytes 584 | tf_op jit(solution)/shard_map/ppermute | solution.py:24
  413.5 10.9 %collective-permute-start.34 = (f32[8,768]{1,0:T(8,128)S(1)}, f32[8,768]{1,0:T(8,128)S(1)}, u32[]{:S(2)}, u32[]{:S(2)}) collective-permute-start(f32[8,768]{1,0:T(8,128)S(1)} %get-tuple-element.177), channel_id=1, source_target_pairs={{0,4},{4,8},{8,12},{12,16},{16,20},{20,24},{24,28},{28,32},{32,36}... | collective-permute-start | bytes 73736 | tf_op jit(solution)/shard_map/ppermute | solution.py:32
  415.4 10.5 %collective-permute-start.35 = (f32[8,768]{1,0:T(8,128)S(1)}, f32[8,768]{1,0:T(8,128)S(1)}, u32[]{:S(2)}, u32[]{:S(2)}) collective-permute-start(f32[8,768]{1,0:T(8,128)S(1)} %get-tuple-element.178), channel_id=1, source_target_pairs={{4,0},{8,4},{12,8},{16,12},{20,16},{24,20},{28,24},{32,28},{36,32}... | collective-permute-start | bytes 73736 | tf_op jit(solution)/shard_map/ppermute | solution.py:32
  425.9 11.0 %collective-permute-start.36 = (f32[8,768]{1,0:T(8,128)S(1)}, f32[8,768]{1,0:T(8,128)S(1)}, u32[]{:S(2)}, u32[]{:S(2)}) collective-permute-start(f32[8,768]{1,0:T(8,128)S(1)} %get-tuple-element.189), channel_id=1, source_target_pairs={{0,4},{4,8},{8,12},{12,16},{16,20},{20,24},{24,28},{28,32},{32,36}... | collective-permute-start | bytes 73736 | tf_op jit(solution)/shard_map/ppermute | solution.py:21
  427.8 10.5 %collective-permute-start.37 = (f32[8,768]{1,0:T(8,128)S(1)}, f32[8,768]{1,0:T(8,128)S(1)}, u32[]{:S(2)}, u32[]{:S(2)}) collective-permute-start(f32[8,768]{1,0:T(8,128)S(1)} %get-tuple-element.190), channel_id=1, source_target_pairs={{4,0},{8,4},{12,8},{16,12},{20,16},{24,20},{28,24},{32,28},{36,32}... | collective-permute-start | bytes 73736 | tf_op jit(solution)/shard_map/ppermute | solution.py:24
  453.2 10.9 %collective-permute-start.38 = (f32[6,8]{1,0:T(8,128)S(1)}, f32[6,8]{1,0:T(8,128)S(1)}, u32[]{:S(2)}, u32[]{:S(2)}) collective-permute-start(f32[6,8]{1,0:T(8,128)S(1)} %get-tuple-element.219), channel_id=1, source_target_pairs={{0,4},{4,8},{8,12},{12,16},{16,20},{20,24},{24,28},{28,32},{32,36}... | collective-permute-start | bytes 584 | tf_op jit(solution)/shard_map/ppermute | solution.py:32
  455.1 10.3 %collective-permute-start.39 = (f32[6,8]{1,0:T(8,128)S(1)}, f32[6,8]{1,0:T(8,128)S(1)}, u32[]{:S(2)}, u32[]{:S(2)}) collective-permute-start(f32[6,8]{1,0:T(8,128)S(1)} %get-tuple-element.220), channel_id=1, source_target_pairs={{4,0},{8,4},{12,8},{16,12},{20,16},{24,20},{28,24},{32,28},{36,32}... | collective-permute-start | bytes 584 | tf_op jit(solution)/shard_map/ppermute | solution.py:32
  491.4 10.9 %collective-permute-start.40 = (f32[6,8]{1,0:T(8,128)S(1)}, f32[6,8]{1,0:T(8,128)S(1)}, u32[]{:S(2)}, u32[]{:S(2)}) collective-permute-start(f32[6,8]{1,0:T(8,128)S(1)} %get-tuple-element.217), channel_id=1, source_target_pairs={{0,4},{4,8},{8,12},{12,16},{16,20},{20,24},{24,28},{28,32},{32,36}... | collective-permute-start | bytes 584 | tf_op jit(solution)/shard_map/ppermute | solution.py:21
  493.9 9.5 %collective-permute-start.41 = (f32[6,8]{1,0:T(8,128)S(1)}, f32[6,8]{1,0:T(8,128)S(1)}, u32[]{:S(2)}, u32[]{:S(2)}) collective-permute-start(f32[6,8]{1,0:T(8,128)S(1)} %get-tuple-element.218), channel_id=1, source_target_pairs={{4,0},{8,4},{12,8},{16,12},{20,16},{24,20},{28,24},{32,28},{36,32}... | collective-permute-start | bytes 584 | tf_op jit(solution)/shard_map/ppermute | solution.py:24
  510.1 10.9 %collective-permute-start.42 = (f32[8,768]{1,0:T(8,128)S(1)}, f32[8,768]{1,0:T(8,128)S(1)}, u32[]{:S(2)}, u32[]{:S(2)}) collective-permute-start(f32[8,768]{1,0:T(8,128)S(1)} %get-tuple-element.175), channel_id=1, source_target_pairs={{0,4},{4,8},{8,12},{12,16},{16,20},{20,24},{24,28},{28,32},{32,36}... | collective-permute-start | bytes 73736 | tf_op jit(solution)/shard_map/ppermute | solution.py:32
  512.0 10.5 %collective-permute-start.43 = (f32[8,768]{1,0:T(8,128)S(1)}, f32[8,768]{1,0:T(8,128)S(1)}, u32[]{:S(2)}, u32[]{:S(2)}) collective-permute-start(f32[8,768]{1,0:T(8,128)S(1)} %get-tuple-element.176), channel_id=1, source_target_pairs={{4,0},{8,4},{12,8},{16,12},{20,16},{24,20},{28,24},{32,28},{36,32}... | collective-permute-start | bytes 73736 | tf_op jit(solution)/shard_map/ppermute | solution.py:32
  522.5 11.0 %collective-permute-start.44 = (f32[8,768]{1,0:T(8,128)S(1)}, f32[8,768]{1,0:T(8,128)S(1)}, u32[]{:S(2)}, u32[]{:S(2)}) collective-permute-start(f32[8,768]{1,0:T(8,128)S(1)} %get-tuple-element.187), channel_id=1, source_target_pairs={{0,4},{4,8},{8,12},{12,16},{16,20},{20,24},{24,28},{28,32},{32,36}... | collective-permute-start | bytes 73736 | tf_op jit(solution)/shard_map/ppermute | solution.py:21
  524.5 10.5 %collective-permute-start.45 = (f32[8,768]{1,0:T(8,128)S(1)}, f32[8,768]{1,0:T(8,128)S(1)}, u32[]{:S(2)}, u32[]{:S(2)}) collective-permute-start(f32[8,768]{1,0:T(8,128)S(1)} %get-tuple-element.188), channel_id=1, source_target_pairs={{4,0},{8,4},{12,8},{16,12},{20,16},{24,20},{28,24},{32,28},{36,32}... | collective-permute-start | bytes 73736 | tf_op jit(solution)/shard_map/ppermute | solution.py:24
  539.1 49.1 %copy-start.63 = (f32[6,16]{1,0:T(8,128)S(1)}, f32[6,16]{1,0:T(8,128)}, u32[]{:S(2)}) copy-start(f32[6,16]{1,0:T(8,128)} %get-tuple-element.117) | copy-start | bytes 1156
  549.8 10.9 %collective-permute-start.46 = (f32[6,8]{1,0:T(8,128)S(1)}, f32[6,8]{1,0:T(8,128)S(1)}, u32[]{:S(2)}, u32[]{:S(2)}) collective-permute-start(f32[6,8]{1,0:T(8,128)S(1)} %get-tuple-element.215), channel_id=1, source_target_pairs={{0,4},{4,8},{8,12},{12,16},{16,20},{20,24},{24,28},{28,32},{32,36}... | collective-permute-start | bytes 584 | tf_op jit(solution)/shard_map/ppermute | solution.py:32
  551.7 10.3 %collective-permute-start.47 = (f32[6,8]{1,0:T(8,128)S(1)}, f32[6,8]{1,0:T(8,128)S(1)}, u32[]{:S(2)}, u32[]{:S(2)}) collective-permute-start(f32[6,8]{1,0:T(8,128)S(1)} %get-tuple-element.216), channel_id=1, source_target_pairs={{4,0},{8,4},{12,8},{16,12},{20,16},{24,20},{28,24},{32,28},{36,32}... | collective-permute-start | bytes 584 | tf_op jit(solution)/shard_map/ppermute | solution.py:32
  588.4 10.7 %collective-permute-start.48 = (f32[6,8]{1,0:T(8,128)S(1)}, f32[6,8]{1,0:T(8,128)S(1)}, u32[]{:S(2)}, u32[]{:S(2)}) collective-permute-start(f32[6,8]{1,0:T(8,128)S(1)} %get-tuple-element.213), channel_id=1, source_target_pairs={{0,4},{4,8},{8,12},{12,16},{16,20},{20,24},{24,28},{28,32},{32,36}... | collective-permute-start | bytes 584 | tf_op jit(solution)/shard_map/ppermute | solution.py:21
  590.9 9.5 %collective-permute-start.49 = (f32[6,8]{1,0:T(8,128)S(1)}, f32[6,8]{1,0:T(8,128)S(1)}, u32[]{:S(2)}, u32[]{:S(2)}) collective-permute-start(f32[6,8]{1,0:T(8,128)S(1)} %get-tuple-element.214), channel_id=1, source_target_pairs={{4,0},{8,4},{12,8},{16,12},{20,16},{24,20},{28,24},{32,28},{36,32}... | collective-permute-start | bytes 584 | tf_op jit(solution)/shard_map/ppermute | solution.py:24
  607.0 10.9 %collective-permute-start.50 = (f32[8,768]{1,0:T(8,128)S(1)}, f32[8,768]{1,0:T(8,128)S(1)}, u32[]{:S(2)}, u32[]{:S(2)}) collective-permute-start(f32[8,768]{1,0:T(8,128)S(1)} %get-tuple-element.173), channel_id=1, source_target_pairs={{0,4},{4,8},{8,12},{12,16},{16,20},{20,24},{24,28},{28,32},{32,36}... | collective-permute-start | bytes 73736 | tf_op jit(solution)/shard_map/ppermute | solution.py:32
  608.9 10.5 %collective-permute-start.51 = (f32[8,768]{1,0:T(8,128)S(1)}, f32[8,768]{1,0:T(8,128)S(1)}, u32[]{:S(2)}, u32[]{:S(2)}) collective-permute-start(f32[8,768]{1,0:T(8,128)S(1)} %get-tuple-element.174), channel_id=1, source_target_pairs={{4,0},{8,4},{12,8},{16,12},{20,16},{24,20},{28,24},{32,28},{36,32}... | collective-permute-start | bytes 73736 | tf_op jit(solution)/shard_map/ppermute | solution.py:32
  619.5 11.0 %collective-permute-start.52 = (f32[8,768]{1,0:T(8,128)S(1)}, f32[8,768]{1,0:T(8,128)S(1)}, u32[]{:S(2)}, u32[]{:S(2)}) collective-permute-start(f32[8,768]{1,0:T(8,128)S(1)} %get-tuple-element.185), channel_id=1, source_target_pairs={{0,4},{4,8},{8,12},{12,16},{16,20},{20,24},{24,28},{28,32},{32,36}... | collective-permute-start | bytes 73736 | tf_op jit(solution)/shard_map/ppermute | solution.py:21
  621.4 10.5 %collective-permute-start.53 = (f32[8,768]{1,0:T(8,128)S(1)}, f32[8,768]{1,0:T(8,128)S(1)}, u32[]{:S(2)}, u32[]{:S(2)}) collective-permute-start(f32[8,768]{1,0:T(8,128)S(1)} %get-tuple-element.186), channel_id=1, source_target_pairs={{4,0},{8,4},{12,8},{16,12},{20,16},{24,20},{28,24},{32,28},{36,32}... | collective-permute-start | bytes 73736 | tf_op jit(solution)/shard_map/ppermute | solution.py:24
  637.0 63.7 %copy-start.67 = (pred[192]{0:T(512)(128)(4,1)S(1)}, pred[192]{0:T(512)(128)(4,1)}, u32[]{:S(2)}) copy-start(pred[192]{0:T(512)(128)(4,1)} %get-tuple-element.120) | copy-start | bytes 580
  646.7 11.2 %collective-permute-start.54 = (f32[6,8]{1,0:T(8,128)S(1)}, f32[6,8]{1,0:T(8,128)S(1)}, u32[]{:S(2)}, u32[]{:S(2)}) collective-permute-start(f32[6,8]{1,0:T(8,128)S(1)} %get-tuple-element.211), channel_id=1, source_target_pairs={{0,4},{4,8},{8,12},{12,16},{16,20},{20,24},{24,28},{28,32},{32,36}... | collective-permute-start | bytes 584 | tf_op jit(solution)/shard_map/ppermute | solution.py:32
  648.7 10.6 %collective-permute-start.55 = (f32[6,8]{1,0:T(8,128)S(1)}, f32[6,8]{1,0:T(8,128)S(1)}, u32[]{:S(2)}, u32[]{:S(2)}) collective-permute-start(f32[6,8]{1,0:T(8,128)S(1)} %get-tuple-element.212), channel_id=1, source_target_pairs={{4,0},{8,4},{12,8},{16,12},{20,16},{24,20},{28,24},{32,28},{36,32}... | collective-permute-start | bytes 584 | tf_op jit(solution)/shard_map/ppermute | solution.py:32
  685.5 10.7 %collective-permute-start.56 = (f32[6,8]{1,0:T(8,128)S(1)}, f32[6,8]{1,0:T(8,128)S(1)}, u32[]{:S(2)}, u32[]{:S(2)}) collective-permute-start(f32[6,8]{1,0:T(8,128)S(1)} %get-tuple-element.209), channel_id=1, source_target_pairs={{0,4},{4,8},{8,12},{12,16},{16,20},{20,24},{24,28},{28,32},{32,36}... | collective-permute-start | bytes 584 | tf_op jit(solution)/shard_map/ppermute | solution.py:21
  688.0 9.5 %collective-permute-start.57 = (f32[6,8]{1,0:T(8,128)S(1)}, f32[6,8]{1,0:T(8,128)S(1)}, u32[]{:S(2)}, u32[]{:S(2)}) collective-permute-start(f32[6,8]{1,0:T(8,128)S(1)} %get-tuple-element.210), channel_id=1, source_target_pairs={{4,0},{8,4},{12,8},{16,12},{20,16},{24,20},{28,24},{32,28},{36,32}... | collective-permute-start | bytes 584 | tf_op jit(solution)/shard_map/ppermute | solution.py:24
  702.2 10.9 %collective-permute-start.58 = (f32[8,768]{1,0:T(8,128)S(1)}, f32[8,768]{1,0:T(8,128)S(1)}, u32[]{:S(2)}, u32[]{:S(2)}) collective-permute-start(f32[8,768]{1,0:T(8,128)S(1)} %get-tuple-element.171), channel_id=1, source_target_pairs={{0,4},{4,8},{8,12},{12,16},{16,20},{20,24},{24,28},{28,32},{32,36}... | collective-permute-start | bytes 73736 | tf_op jit(solution)/shard_map/ppermute | solution.py:32
  704.1 10.5 %collective-permute-start.59 = (f32[8,768]{1,0:T(8,128)S(1)}, f32[8,768]{1,0:T(8,128)S(1)}, u32[]{:S(2)}, u32[]{:S(2)}) collective-permute-start(f32[8,768]{1,0:T(8,128)S(1)} %get-tuple-element.172), channel_id=1, source_target_pairs={{4,0},{8,4},{12,8},{16,12},{20,16},{24,20},{28,24},{32,28},{36,32}... | collective-permute-start | bytes 73736 | tf_op jit(solution)/shard_map/ppermute | solution.py:32
  (78 other events, 688.6 us)
where the time goes:
time: 730 us; the launch traced here: 716 us
  starting transfers between devices  326 us (45%)
  blocking collectives  183 us (25%)
  local copies, waits for them, and re-layouts  64.6 us (9%)
  other arithmetic  57.3 us (8%)
  waiting for transfers between devices  37.8 us (5%)
  between operations  24.5 us (3%)
  matrix products  22.6 us (3%)
    ppermute x30, starting transfers between devices, from_behind(): return lax.ppermute(block, axis, route)  164 us
    ppermute x15, starting transfers between devices, padded(): lax.ppermute(lax.slice_in_dim(block, 0, width, axis=dim), axis, backward)  128 us
    all_to_all x6, blocking collectives, from_everyone(): lax.all_to_all(jnp.broadcast_to(shard[None], (count, *shard.shape)), axis...  118 us
    all_gather x7, blocking collectives, total_of_pieces(): tiles = lax.all_gather(shard, axis)  65.1 us
    ppermute x15, starting transfers between devices, padded(): lax.ppermute(lax.slice_in_dim(block, block.shape[dim] - width, None, axis...  34.1 us
    ppermute x30, waiting for transfers between devices, from_behind(): return lax.ppermute(block, axis, route)  20.6 us
    ppermute x15, waiting for transfers between devices, padded(): lax.ppermute(lax.slice_in_dim(block, 0, width, axis=dim), axis, backward)  17.2 us
    mul x7, other arithmetic, pose_terms(): heavy_u = geo[5] * part_u  16.3 us
  transfers between devices with their start and end apart: 60, of which 28 were waited for; matrix products, arithmetic and copies ran while one was open for 5% of the time, Pallas kernels for 0%

commit v1 on v0

v1 whole, which is shorter than its diff:
```python
import functools
import jax
import jax.numpy as jnp
from jax import lax
from jax.experimental import pallas as pl
from jax.experimental.pallas import tpu as pltpu
from jax.sharding import PartitionSpec as P

ROWS = 48
COLS = 64
RADIUS = 8
ITERS = 6
HIGHEST = lax.Precision.HIGHEST
F32 = jnp.float32
BF16 = jnp.bfloat16
LANES = 128
FD = 16
SLOTS = 16
GROUP = FD * 6
SIDE = RADIUS * (RADIUS + 1) // 2
POSE_REG = 100.0


def iota(shape, dim):
    return lax.broadcasted_iota(jnp.int32, shape, dim)


def thirds(x):
    first = x.astype(BF16)
    rest = x - first.astype(F32)
    second = rest.astype(BF16)
    return first, second, (rest - second.astype(F32)).astype(BF16)


def scatter_kernel(where_ref, ef_ref, flow_ref, weight_ref, mask_ref, own_ref, down_ref, up_ref):
    edges = ef_ref.shape[1]
    start = where_ref[0]
    source = ef_ref[0:1, :] - start
    delta = ef_ref[1:2, :] - start - source
    slot = jnp.where(delta < 0, delta + 8, delta + 7)
    own_at = jnp.where((source >= 0) & (source < FD), source * SLOTS + slot, -1)
    j = source + 8
    down_at = jnp.where(source < 0, ((j * (j + 1)) >> 1) + delta - 8 + j, -1)
    j = 23 - source
    up_at = jnp.where(source >= FD, ((j * (j + 1)) >> 1) + slot, -1)
    hot = jnp.concatenate(
        [
            (iota((FD * SLOTS, edges), 0) == own_at).astype(F32),
            (iota((40, edges), 0) == down_at).astype(F32),
            (iota((40, edges), 0) == up_at).astype(F32),
        ],
        axis=0,
    ).astype(BF16)
    down_ref[0:8, :] = jnp.zeros((8, down_ref.shape[1]), F32)
    per_edge = 2 * (mask_ref.shape[1] // LANES)
    for chunk in range(mask_ref.shape[1] // LANES):
        lanes = pl.ds(chunk * LANES, LANES)
        live = mask_ref[:, lanes].astype(F32)
        parts = []
        for comp in range(2):
            rows = pl.ds(chunk * 2 + comp, edges, stride=per_edge)
            conf = weight_ref[rows, :] * live
            parts.append((conf, conf * flow_ref[rows, :]))
        values = jnp.concatenate([parts[0][0], parts[1][0], parts[0][1], parts[1][1]], axis=1)
        got = sum(
            jnp.dot(hot, piece, preferred_element_type=F32) for piece in reversed(thirds(values))
        )
        for q in range(4):
            cut = got[:, q * LANES : (q + 1) * LANES]
            own_ref[q * 256 : (q + 1) * 256, lanes] = cut[0:256]
            down_ref[8 + q * SIDE : 8 + (q + 1) * SIDE, lanes] = cut[256 : 256 + SIDE]
            up_ref[q * SIDE : (q + 1) * SIDE, lanes] = cut[296 : 296 + SIDE]


def rotation_rows(w):
    x, y, z = w
    zero = jnp.zeros_like(x)
    cross = [[zero, -z, y], [z, zero, -x], [-y, x, zero]]
    sq = x * x + y * y + z * z
    first = 1.0 - sq / 6.0 + sq * sq / 120.0
    second = 0.5 - sq / 24.0 + sq * sq / 720.0
    return [
        [
            float(i == k)
            + first * cross[i][k]
            + second * sum(cross[i][m] * cross[m][k] for m in range(3))
            for k in range(3)
        ]
        for i in range(3)
    ]


def pose_kernel(where_ref, rotvec_ref, trans_ref, tab_ref, b_ref, bt_ref):
    start = where_ref[0]
    frames = rotvec_ref.shape[1]
    pair = iota((1, FD * SLOTS), 1)
    slot = pair & 15
    delta = jnp.where(slot < 8, slot - 8, slot - 7)
    at_source = start + (pair >> 4)
    at_target = jnp.clip(at_source + delta, 0, frames - 1)
    poses = jnp.concatenate([rotvec_ref[...], trans_ref[...], jnp.zeros((2, frames), F32)], axis=0)

    def pick(at):
        hot = (iota((frames, FD * SLOTS), 0) == at).astype(F32)
        return jnp.dot(poses, hot, precision=HIGHEST, preferred_element_type=F32)

    src = pick(at_source)
    tgt = pick(at_target)
    rs = rotation_rows([src[k : k + 1] for k in range(3)])
    rt = rotation_rows([tgt[k : k + 1] for k in range(3)])
    rel = [[sum(rt[i][k] * rs[m][k] for k in range(3)) for m in range(3)] for i in range(3)]
    tr = [
        tgt[3 + i : 4 + i] - sum(rel[i][m] * src[3 + m : 4 + m] for m in range(3)) for i in range(3)
    ]
    corner = [
        [tr[1] * rel[2][m] - tr[2] * rel[1][m] for m in range(3)],
        [tr[2] * rel[0][m] - tr[0] * rel[2][m] for m in range(3)],
        [tr[0] * rel[1][m] - tr[1] * rel[0][m] for m in range(3)],
    ]
    lines = [x for row in rel for x in row] + tr + [x for row in corner for x in row]
    lines = jnp.concatenate(lines + [jnp.zeros((LANES - len(lines), FD * SLOTS), F32)], axis=0)
    tab_ref[...] = lines.T

    lane3 = iota((SLOTS, 3 * LANES), 1)
    row3 = iota((SLOTS, 3 * LANES), 0)
    off3 = jnp.where(row3 < 8, row3 - 8, row3 - 7)

    def build(f, carry):
        frame = f + off3 + FD
        home = (frame >> 4) * LANES + (frame & 15) * 6
        tab = tab_ref[pl.ds(pl.multiple_of(f * SLOTS, SLOTS), SLOTS), :]
        for c in range(6):
            block = jnp.where(lane3 == home + c, 1.0, 0.0)
            for d in range(6):
                if c < 3:
                    at = c * 3 + d if d < 3 else 12 + c * 3 + d - 3
                elif d >= 3:
                    at = (c - 3) * 3 + d - 3
                else:
                    continue
                block = block - jnp.where(
                    lane3 == LANES + f * 6 + d, jnp.broadcast_to(tab[:, at : at + 1], lane3.shape), 0.0
                )
            b_ref[pl.ds(pl.multiple_of(f * GROUP + c * SLOTS, SLOTS), SLOTS), :] = block
        return carry

    lax.fori_loop(0, FD, build, 0)
    for g in range(4):
        cols = slice(g * 384, (g + 1) * 384)
        below = b_ref[cols, 0:LANES].T
        own = b_ref[cols, LANES : 2 * LANES].T
        above = b_ref[cols, 2 * LANES : 3 * LANES].T
        bt_ref[0:48, cols] = below[48:96]
        bt_ref[48:144, cols] = own[0:96]
        bt_ref[144:192, cols] = above[0:48]


def main_kernel(
    where_ref, own_ref, rdown_ref, rup_ref, depth_ref, damp_ref, tab_ref, b_ref, bt_ref,
    keep_ref, send_ref, g_ref, base_ref, scale_ref,
    half_ref, geo_ref, hi_ref, in_ref, q_ref, w_ref, t_ref,
):
    core = where_ref[2]
    plocal = depth_ref.shape[1]
    chunks = plocal // LANES
    row8 = iota((8, plocal), 0)
    for f in range(FD):
        j = 7 - f if f < 8 else f - 8
        base = j * (j + 1) // 2
        for q in range(4):
            if f < 8:
                extra = jnp.where(row8 <= j, rup_ref[q * SIDE + base : q * SIDE + base + 8, :], 0.0)
                at = q * 256 + f * SLOTS
            else:
                first = 8 + q * SIDE + base - 7 + j
                extra = jnp.where(row8 >= 7 - j, rdown_ref[first : first + 8, :], 0.0)
                at = q * 256 + f * SLOTS + 8
            half_ref[(q * FD + f) * 8 : (q * FD + f + 1) * 8, :] = own_ref[at : at + 8, :] + extra
        in_ref[f * 8 : f * 8 + 8, :] = jnp.broadcast_to(depth_ref[f : f + 1, :], (8, plocal))
        in_ref[128 + f * 8 : 136 + f * 8, :] = jnp.broadcast_to(damp_ref[f : f + 1, :], (8, plocal))
    lane = iota((8, LANES), 1)
    row = iota((8, LANES), 0)

    def frame(f, carry, merged):
        eight = pl.ds(pl.multiple_of(f * 8, 8), 8)
        def conf(q, h, lanes):
            if h == merged:
                at = (q * FD + f) * 8
                return half_ref[pl.ds(pl.multiple_of(at, 8), 8), lanes]
            at = q * 256 + f * SLOTS + 8 * h
            return own_ref[pl.ds(pl.multiple_of(at, 8), 8), lanes]

        params = []
        for h in range(2):
            tab = tab_ref[pl.ds(pl.multiple_of(f * SLOTS + 8 * h, 8), 8), :]
            params.append([jnp.broadcast_to(tab[:, k : k + 1], (8, LANES)) for k in range(12)])
        base_all = []
        scale_all = []
        for c in range(chunks):
            lanes = pl.ds(c * LANES, LANES)
            pixel = where_ref[1] + c * LANES + lane
            col = ((pixel & (COLS - 1)).astype(F32) - 0.5 * (COLS - 1)) / COLS
            line = ((pixel >> 6).astype(F32) - 0.5 * (ROWS - 1)) / COLS
            depth = in_ref[eight, lanes]
            curv = 0.0
            grad = 0.0
            for h in range(2):
                r = params[h]
                z = r[6] * col + r[7] * line + r[8] + depth * r[11]
                inv = 1.0 / z
                u = (r[0] * col + r[1] * line + r[2] + depth * r[9]) * inv
                v = (r[3] * col + r[4] * line + r[5] + depth * r[10]) * inv
                s = depth * inv
                su = inv * (r[9] - u * r[11])
                sv = inv * (r[10] - v * r[11])
                cu = conf(0, h, lanes)
                cv = conf(1, h, lanes)
                eu = cu * (col - u) + conf(2, h, lanes)
                ev = cv * (line - v) + conf(3, h, lanes)
                au = cu * su
                av = cv * sv
                curv = curv + au * su + av * sv
                grad = grad - (su * eu + sv * ev)
                for k, x in enumerate((u, v, s, au, av, eu, ev)):
                    geo_ref[k * 16 + 8 * h : k * 16 + 8 * h + 8, lanes] = x
            damp = in_ref[pl.ds(pl.multiple_of(128 + f * 8, 8), 8), lanes]
            total = damp + jnp.sum(curv, axis=0, keepdims=True)
            base = jnp.sum(grad, axis=0, keepdims=True) / total
            scale = 1.0 / jnp.sqrt(total)
            base_ref[eight, lanes] = base
            scale_ref[eight, lanes] = scale
            base_all.append(base)
            scale_all.append(scale)
        cols = {}
        for h in range(2):
            acc = [0.0] * 27
            for c in range(chunks):
                lanes = pl.ds(c * LANES, LANES)
                u, v, s, au, av, eu, ev = [
                    geo_ref[k * 16 + 8 * h : k * 16 + 8 * h + 8, lanes] for k in range(7)
                ]
                cu = conf(0, h, lanes)
                cv = conf(1, h, lanes)
                base = base_all[c]
                scale = scale_all[c]
                hu = -eu - au * base
                hv = -ev - av * base
                uv = u * v
                u1 = 1.0 + u * u
                v1 = 1.0 + v * v

                def pull(pu, pv):
                    spu = s * pu
                    spv = s * pv
                    return (
                        spu,
                        spv,
                        -(u * spu + v * spv),
                        -(uv * pu) - v1 * pv,
                        u1 * pu + uv * pv,
                        u * pv - v * pu,
                    )

                for k, x in enumerate(pull(au * scale, av * scale)):
                    at = pl.ds(pl.multiple_of(f * GROUP + k * SLOTS + 8 * h, 8), 8)
                    g_ref[at, lanes] = x
                    hi_ref[k * SLOTS + 8 * h : k * SLOTS + 8 * h + 8, lanes] = x
                su_ = cu * s
                sv_ = cv * s
                ju = (None, None, None, -uv, u1, -v)
                jv = (None, None, None, -v1, uv, u)
                terms = list(pull(hu, hv))
                a00 = su_ * s
                a11 = sv_ * s
                a02 = -(a00 * u)
                a12 = -(a11 * v)
                a22 = -(a02 * u + a12 * v)
                terms += [a00, a11, a02, a12, a22]
                tu = [su_ * ju[k] for k in (3, 4, 5)]
                tv = [sv_ * jv[k] for k in (3, 4, 5)]
                terms += tu + tv
                terms += [-(u * tu[k] + v * tv[k]) for k in range(3)]
                wu = [cu * ju[k] for k in (3, 4, 5)]
                wv = [cv * jv[k] for k in (3, 4, 5)]
                for a in range(3):
                    for b in range(a, 3):
                        terms.append(wu[a] * ju[3 + b] + wv[a] * jv[3 + b])
                acc = [x + y for x, y in zip(acc, terms)]
            assert len(acc) == len(terms)
            sums = [jnp.sum(x, axis=1, keepdims=True) for x in acc]
            a = {(0, 0): sums[6], (1, 1): sums[7], (0, 2): sums[8], (1, 2): sums[9], (2, 2): sums[10]}
            for k in range(3):
                a[(0, 3 + k)] = sums[11 + k]
                a[(1, 3 + k)] = sums[14 + k]
                a[(2, 3 + k)] = sums[17 + k]
            at = 20
            for x in range(3):
                for y in range(x, 3):
                    a[(3 + x, 3 + y)] = sums[at]
                    at += 1
            for c in range(6):
                block = jnp.zeros((8, LANES), F32)
                for d in range(6):
                    key = (min(c, d), max(c, d))
                    if key == (0, 1):
                        continue
                    block = jnp.where(
                        lane == d * SLOTS + 8 * h + row, jnp.broadcast_to(a[key], (8, LANES)), block
                    )
                q_ref[c * SLOTS + 8 * h : c * SLOTS + 8 * h + 8, :] = block
                cols[(c, h)] = sums[c]
        g = hi_ref[...]
        top = g.astype(BF16)
        low = (g - top.astype(F32)).astype(BF16)
        left = jnp.concatenate([top, low, top], axis=1)
        right = jnp.concatenate([top, top, low], axis=1)
        m = lax.dot_general(left, right, (((1,), (1,)), ((), ())), preferred_element_type=F32)
        q = q_ref[:, 0:GROUP] - m
        rows = pl.ds(pl.multiple_of(f * GROUP, 8), GROUP)
        w_ref[rows, :] = jnp.dot(q, b_ref[rows, :], precision=HIGHEST, preferred_element_type=F32)
        for c in range(6):
            for h in range(2):
                at = pl.ds(pl.multiple_of(f * GROUP + c * SLOTS + 8 * h, 8), 8)
                w_ref[at, 0:LANES] = jnp.where(
                    lane == LANES - 1, jnp.broadcast_to(cols[(c, h)], (8, LANES)), w_ref[at, 0:LANES]
                )
        return carry

    lax.fori_loop(0, 8, functools.partial(frame, merged=0), 0)
    lax.fori_loop(8, 16, functools.partial(frame, merged=1), 0)
    t_ref[...] = jnp.dot(bt_ref[...], w_ref[...], precision=HIGHEST, preferred_element_type=F32)
    keep_ref[0:48, :] = t_ref[pl.ds(pl.multiple_of(48 + 48 * core, 8), 48), :]
    keep_ref[48:96, :] = t_ref[pl.ds(pl.multiple_of(144 - 144 * core, 8), 48), :]
    send_ref[0:48, :] = t_ref[pl.ds(pl.multiple_of(96 - 48 * core, 8), 48), :]
    send_ref[48:96, :] = t_ref[pl.ds(pl.multiple_of(144 * core, 8), 48), :]


def rows_kernel(where_ref, own_ref, own2_ref, rim_ref, rim2_ref, out_ref):
    core = where_ref[2]
    own = own_ref[...] + own2_ref[...]
    rim = rim_ref[...] + rim2_ref[...]
    lane = iota((48, LANES), 1)
    below = rim[:, 0:LANES]
    mid = rim[:, LANES : 2 * LANES]
    above = rim[:, 2 * LANES :]
    vec = jnp.where(lane == LANES - 1, below, 0.0)
    below = jnp.where(lane == LANES - 1, 0.0, below)
    low = core == 0
    out_ref[:, 0:LANES] = own[:, 0:LANES] + vec + jnp.where(low, mid, 0.0)
    out_ref[:, LANES : 2 * LANES] = own[:, LANES : 2 * LANES] + jnp.where(low, above, below)
    out_ref[:, 2 * LANES :] = own[:, 2 * LANES :] + jnp.where(low, 0.0, mid)


def to_row(column):
    return jnp.sum(
        jnp.where(iota((GROUP, LANES), 0) == iota((GROUP, LANES), 1), column, 0.0),
        axis=0,
        keepdims=True,
    )


def full_kernel(where_ref, mine_ref, other_ref, s_ref, r_ref):
    core = where_ref[2]
    mine = mine_ref[...]
    other = other_ref[...]
    low = core == 0
    s = jnp.concatenate([jnp.where(low, mine, other), jnp.where(low, other, mine)], axis=0)
    r_ref[...] = jnp.zeros((8, LANES), F32)
    r_ref[0:1, :] = to_row(s[:, LANES - 1 : LANES])
    r = iota((GROUP, 3 * LANES), 0)
    l = iota((GROUP, 3 * LANES), 1)
    s = jnp.where(l == LANES - 1, 0.0, s)
    s_ref[...] = s + jnp.where(l == LANES + r, POSE_REG, 0.0)


def mv_kernel(s_ref, below_ref, own_ref, above_ref, out_ref, dots_ref):
    own = own_ref[0:1, :]
    s = s_ref[...]
    prod = (
        s[:, 0:LANES] * below_ref[0:1, :]
        + s[:, LANES : 2 * LANES] * own
        + s[:, 2 * LANES :] * above_ref[0:1, :]
    )
    y = to_row(jnp.sum(prod, axis=1, keepdims=True))
    out_ref[...] = jnp.zeros((8, LANES), F32)
    out_ref[0:1, :] = y
    rr = jnp.sum(own * own, axis=1, keepdims=True)
    ry = jnp.sum(own * y, axis=1, keepdims=True)
    row = iota((8, LANES), 0)
    dots_ref[...] = jnp.where(row == 0, jnp.broadcast_to(rr, (8, LANES)), jnp.broadcast_to(ry, (8, LANES)))


def final_kernel(below_ref, own_ref, above_ref, b_ref, g_ref, base_ref, scale_ref, out_ref, sum_ref):
    x0 = below_ref[0:1, :]
    x1 = own_ref[0:1, :]
    x2 = above_ref[0:1, :]

    def frame(f, carry):
        rows = pl.ds(pl.multiple_of(f * GROUP, 8), GROUP)
        prod = (
            b_ref[rows, 0:LANES] * x0
            + b_ref[rows, LANES : 2 * LANES] * x1
            + b_ref[rows, 2 * LANES : 3 * LANES] * x2
        )
        x = jnp.sum(prod, axis=1, keepdims=True)
        image = jnp.sum(g_ref[rows, :] * x, axis=0, keepdims=True)
        at = pl.ds(pl.multiple_of(f * 8, 8), 8)
        sum_ref[at, :] = base_ref[at, :] - scale_ref[at, :] * image
        return carry

    lax.fori_loop(0, FD, frame, 0)
    for f in range(FD):
        out_ref[f : f + 1, :] = sum_ref[f * 8 : f * 8 + 1, :]


SMEM = pl.BlockSpec(memory_space=pltpu.SMEM)
VMEM = pl.BlockSpec(memory_space=pltpu.VMEM)


def call(kernel, name, outs, smem, *args, scratch=()):
    return pl.pallas_call(
        kernel,
        name=name,
        out_shape=[jax.ShapeDtypeStruct(s, F32) for s in outs],
        in_specs=[SMEM] * smem + [VMEM] * (len(args) - smem),
        out_specs=[VMEM] * len(outs),
        scratch_shapes=list(scratch),
    )(*args)


def per_device(edge_frames, rotvec, trans, inv_depth, depth_damping, flow, weight, mask):
    f_dev, plocal = inv_depth.shape
    edges = mask.shape[0]
    count = lax.axis_size("frames")
    pixes = lax.axis_size("pix")
    fi = lax.axis_index("frames")
    pi = lax.axis_index("pix")
    spot = jnp.stack([fi * f_dev, pi * plocal, pi % 2]).astype(jnp.int32)

    def shift(block, step):
        return lax.ppermute(
            block, "frames", [(i, i + step) for i in range(count) if 0 <= i + step < count]
        )

    def view(x):
        return x.reshape(edges, 2, plocal // LANES, LANES).transpose(0, 2, 1, 3).reshape(-1, LANES)

    own, down, up = call(
        scatter_kernel, "scatter",
        [(4 * f_dev * SLOTS, plocal), (8 + 4 * SIDE, plocal), (4 * SIDE, plocal)],
        1, spot, edge_frames, view(flow), view(weight), mask,
    )
    from_after = shift(down, -1)
    from_before = shift(up, 1)
    tab, b, bt = call(
        pose_kernel, "pose",
        [(f_dev * SLOTS, LANES), (f_dev * GROUP, 3 * LANES), (192, f_dev * GROUP)],
        1, spot, rotvec, trans,
    )
    keep, send, g, base, scale = call(
        main_kernel, "main",
        [(96, 384), (96, 384), (f_dev * GROUP, plocal), (f_dev * 8, plocal), (f_dev * 8, plocal)],
        1, spot, own, from_after, from_before, inv_depth, depth_damping, tab, b, bt,
        scratch=[
            pltpu.VMEM((4 * FD * 8, plocal), F32),
            pltpu.VMEM((7 * 16, plocal), F32),
            pltpu.VMEM((GROUP, plocal), F32),
            pltpu.VMEM((256, plocal), F32),
            pltpu.VMEM((GROUP, LANES), F32),
            pltpu.VMEM((f_dev * GROUP, 3 * LANES), F32),
            pltpu.VMEM((192, 3 * LANES), F32),
        ],
    )
    got = lax.ppermute(send, "pix", [(i, i ^ 1) for i in range(pixes)])
    both = keep + got
    own_half, rim = both[:48], both[48:]
    both_axes = ("frames", "pix")

    def to_neighbour(flip):
        route = []
        for i in range(count):
            for k in range(pixes):
                to = i + 1 if k % 2 == 0 else i - 1
                if 0 <= to < count:
                    route.append((i * pixes + k, to * pixes + (k ^ flip)))
        return lax.ppermute(rim, both_axes, route)

    own_far = lax.ppermute(own_half, "pix", [(i, i ^ 2) for i in range(pixes)])
    rim_near = to_neighbour(0)
    rim_far = to_neighbour(2)
    (half,) = call(rows_kernel, "rows", [(48, 384)], 1, spot, own_half, own_far, rim_near, rim_far)
    other = lax.ppermute(half, "pix", [(i, i ^ 1) for i in range(pixes)])
    s, residual = call(full_kernel, "full", [(96, 384), (8, LANES)], 1, spot, half, other)

    def halo(v):
        return shift(v, 1), v, shift(v, -1)

    def total(v):
        for step in (1, 4, 16):
            v = v + sum(
                lax.ppermute(v, "frames", [(i, i ^ (k * step)) for i in range(count)])
                for k in (1, 2, 3)
            )
        return v

    def reduced(v):
        q, dots = call(mv_kernel, "mv", [(8, LANES), (8, LANES)], 0, s, *halo(v))
        dots = total(dots)
        return q, dots[0, 0], dots[1, 0]

    solution = jnp.zeros_like(residual)
    image, norm_now, product = reduced(residual)
    alpha = norm_now / product
    direction, along = residual, image
    for step in range(ITERS):
        solution = solution + alpha * direction
        residual = residual - alpha * along
        if step + 1 < ITERS:
            image, norm_next, product = reduced(residual)
            ratio = norm_next / norm_now
            alpha = norm_next / (product - ratio * norm_next / alpha)
            direction = residual + ratio * direction
            along = image + ratio * along
            norm_now = norm_next
    (depth_step,) = call(
        final_kernel, "final", [(f_dev, plocal)], 0, *halo(solution), b, g, base, scale,
        scratch=[pltpu.VMEM((f_dev * 8, plocal), F32)],
    )
    pose_step = solution[0, : f_dev * 6].reshape(f_dev, 6).T
    return pose_step, depth_step


def solution(mesh):
    return jax.shard_map(
        per_device,
        mesh=mesh,
        in_specs=(
            P(None, "frames"),
            P(),
            P(),
            P("frames", "pix"),
            P("frames", "pix"),
            P("frames", None, "pix"),
            P("frames", None, "pix"),
            P("frames", "pix"),
        ),
        out_specs=(P(None, "frames"), P("frames", "pix")),
        check_vma=False,
    )
```

time: 730 us -> 395 us (0.54); the launches traced: 716 us -> 389 us
  blocking collectives: 183 us -> 0 us
  starting transfers between devices: 326 us -> 172 us
  waiting for transfers between devices: 37.8 us -> 113 us
  Pallas kernels: 0 us -> 56 us
  local copies, waits for them, and re-layouts: 64.6 us -> 16.7 us
  other arithmetic: 57.3 us -> 10 us
  matrix products: 22.6 us -> 0 us
    ppermute x60 -> x75, starting transfers between devices: 326 us -> 172 us  [the longest x54 84.2 us: total(): lax.ppermute(v, 'frames', [(i, i ^ k * step) for i in range(count)])]
    all_to_all x6 -> x0, blocking collectives: 118 us -> none  [from_everyone(): lax.all_to_all(jnp.broadcast_to(shard[None], (count, *shard.shape)), axis...]
    ppermute x60 -> x75, waiting for transfers between devices: 37.8 us -> 113 us  [the longest x16 70.2 us: shift(): lax.ppermute(block, 'frames', [(i, i + step) for i in range(count) if 0 <...]
    all_gather x7 -> x0, blocking collectives: 65.1 us -> none  [total_of_pieces(): tiles = lax.all_gather(shard, axis)]
    pallas_call x0 -> x12, Pallas kernels: none -> 56 us  [call(): pl.pallas_call(kernel, name=name, out_shape=[jax.ShapeDtypeStruct(s, F32)...]
    gather x27 -> x0, local copies, waits for them, and re-layouts: 31.8 us -> none  [the longest x7 12.5 us: fetch_image(): return jnp.take(table, source_ext, axis=0)]
    dot_general x32 -> x0, matrix products: 22.6 us -> none  [the longest x7 9.56 us: fetch_step(): jnp.einsum('jke,ke->je', adjoint, at_source, precision=exact)]
    slice x46 -> x8, local copies, waits for them, and re-layouts: 21.2 us -> 3.23 us  [the longest x6 3.2 us: reduced(): return (q, dots[0, 0], dots[1, 0])]
  transfers between devices with their start and end apart: 60 -> 75, of which waited for: 28 -> 52; matrix products, arithmetic and copies ran while one was open for 5% -> 0% of each run, Pallas kernels for 0% -> 2%
where the time goes in v1:
time: 395 us; the launch traced here: 389 us
  starting transfers between devices  172 us (44%)
  waiting for transfers between devices  113 us (29%)
  Pallas kernels  56 us (14%)
  between operations  21.4 us (5%)
  local copies, waits for them, and re-layouts  16.7 us (4%)
  other arithmetic  10 us (3%)
    ppermute x54, starting transfers between devices, total(): lax.ppermute(v, 'frames', [(i, i ^ k * step) for i in range(count)])  84.2 us
    ppermute x16, starting transfers between devices, shift(): lax.ppermute(block, 'frames', [(i, i + step) for i in range(count) if 0 <...  77.3 us
    ppermute x16, waiting for transfers between devices, shift(): lax.ppermute(block, 'frames', [(i, i + step) for i in range(count) if 0 <...  70.2 us
    pallas_call x12, Pallas kernels, call(): pl.pallas_call(kernel, name=name, out_shape=[jax.ShapeDtypeStruct(s, F32)...  56 us
    ppermute x54, waiting for transfers between devices, total(): lax.ppermute(v, 'frames', [(i, i ^ k * step) for i in range(count)])  31.4 us
    ppermute x2, starting transfers between devices, to_neighbour(): return lax.ppermute(rim, both_axes, route)  9.25 us
    unnamed x61, local copies, waits for them, and re-layouts  9.13 us
  transfers between devices with their start and end apart: 75, of which 52 were waited for; matrix products, arithmetic and copies ran while one was open for 0% of the time, Pallas kernels for 2%

profile of v1, /device:TPU:8, one launch (start us, length us, event | category | flops | bytes accessed | tf_op | source)
XLA Modules:
  0.0 388.5 jit_solution(8254268962866773103)
XLA Ops:
  2.2 1.9 copy.14
  4.4 1.9 copy.16
  7.0 5.7 %scatter.1 = (f32[1024,768]{1,0:T(8,128)}, f32[152,768]{1,0:T(8,128)}, f32[144,768]{1,0:T(8,128)}) custom-call(s32[3]{0:T(128)} %pad_add_fusion.where_ref, s32[2,192]{1,0:T(2,128)} %ef_ref.1, f32[2304,128]{1,0:T(8,128)} %bitcast.26, f32[2304,128]{1,0:T(8,128)} %bitcast.27, s32[192,768]{1,0:T(8,128)} %mask_ref.1), custom_call_target="tpu_custom_call" | custom-call | tf_op jit(solution)/shard_map/scatter/pallas_call | solution.py:421
  12.7 8.6 %collective-permute-start = (f32[152,768]{1,0:T(8,128)}, f32[152,768]{1,0:T(8,128)S(1)}, u32[]{:S(2)}, u32[]{:S(2)}) collective-permute-start(f32[152,768]{1,0:T(8,128)} %get-tuple-element.27), channel_id=1, source_target_pairs={{4,0},{8,4},{12,8},{16,12},{20,16},{24,20},{28,24},{32,28},{36,32}... | collective-permute-start | bytes 1400840 | tf_op jit(solution)/shard_map/ppermute | solution.py:441
  21.3 1.9 collective-permute-start.1
  23.2 6.2 %pose.1 = (f32[256,128]{1,0:T(8,128)}, f32[1536,384]{1,0:T(8,128)}, f32[192,1536]{1,0:T(8,128)}) custom-call(s32[3]{0:T(128)} %pad_add_fusion.where_ref, f32[3,1024]{1,0:T(4,128)} %rotvec_ref.1, f32[3,1024]{1,0:T(4,128)} %trans_ref.1), custom_call_target="tpu_custom_call" | custom-call | tf_op jit(solution)/shard_map/pose/pallas_call | solution.py:421
  29.4 12.2 %collective-permute-done.1.rup_ref = f32[144,768]{1,0:T(8,128)S(1)} collective-permute-done((f32[144,768]{1,0:T(8,128)}, f32[144,768]{1,0:T(8,128)S(1)}, u32[]{:S(2)}, u32[]{:S(2)}) %collective-permute-start.1) | collective-permute-done | bytes 442400 | tf_op jit(solution)/shard_map/ppermute | solution.py:441
  42.6 25.2 %main.1 = (f32[96,384]{1,0:T(8,128)}, f32[96,384]{1,0:T(8,128)}, f32[1536,768]{1,0:T(8,128)}, f32[128,768]{1,0:T(8,128)}, f32[128,768]{1,0:T(8,128)}) custom-call(s32[3]{0:T(128)} %pad_add_fusion.where_ref, f32[1024,768]{1,0:T(8,128)} %get-tuple-element.26.own_ref, f32[152,768]{1,0:T(8,128)} %copy-done.1, f32[144,768]{1,0:T(8,128)} %copy-done.2, ...), custom_call_target="tpu_custom_call" | custom-call | tf_op jit(solution)/shard_map/main/pallas_call | solution.py:421
  67.7 1.6 collective-permute-done.2
  70.3 6.7 %collective-permute-start.5 = (f32[48,384]{1,0:T(8,128)S(1)}, f32[48,384]{1,0:T(8,128)S(1)}, u32[]{:S(2)}, u32[]{:S(2)}) collective-permute-start(f32[48,384]{1,0:T(8,128)S(1)} %get-tuple-element.56), channel_id=1, source_target_pairs={{0,6},{2,4},{4,10},{5,3},{6,8},{7,1},{8,14},{9,7},{10,12},{11,5},{... | collective-permute-start | bytes 221192 | tf_op jit(solution)/shard_map/ppermute | solution.py:486
  77.0 2.5 collective-permute-start.4
  81.4 7.0 %collective-permute-done.4.rim_ref = f32[48,384]{1,0:T(8,128)S(1)} collective-permute-done((f32[48,384]{1,0:T(8,128)S(1)}, f32[48,384]{1,0:T(8,128)S(1)}, u32[]{:S(2)}, u32[]{:S(2)}) %collective-permute-start.4) | collective-permute-done | bytes 73760 | tf_op jit(solution)/shard_map/ppermute | solution.py:486
  89.6 1.6 rows.1.mine_ref
  91.5 1.5 collective-permute-done.6.other_ref
  93.6 1.6 full.1
  95.2 7.2 %collective-permute-start.8 = (f32[8,128]{1,0:T(8,128)}, f32[8,128]{1,0:T(8,128)S(1)}, u32[]{:S(2)}, u32[]{:S(2)}) collective-permute-start(f32[8,128]{1,0:T(8,128)} %get-tuple-element.35.own_ref), channel_id=1, source_target_pairs={{4,0},{8,4},{12,8},{16,12},{20,16},{24,20},{28,24},{32,28},{36,32}... | collective-permute-start | bytes 12296 | tf_op jit(solution)/shard_map/ppermute | solution.py:441
  102.4 1.9 collective-permute-start.7
  104.3 8.6 %collective-permute-done.7.below_ref = f32[8,128]{1,0:T(8,128)S(1)} collective-permute-done((f32[8,128]{1,0:T(8,128)}, f32[8,128]{1,0:T(8,128)S(1)}, u32[]{:S(2)}, u32[]{:S(2)}) %collective-permute-start.7) | collective-permute-done | bytes 4128 | tf_op jit(solution)/shard_map/ppermute | solution.py:441
  113.5 1.7 mv.6
  115.2 4.4 %collective-permute-start.9 = (f32[8,128]{1,0:T(8,128)}, f32[8,128]{1,0:T(8,128)S(1)}, u32[]{:S(2)}, u32[]{:S(2)}) collective-permute-start(f32[8,128]{1,0:T(8,128)} %get-tuple-element.36), channel_id=1, source_target_pairs={{0,4},{4,0},{8,12},{12,8},{16,20},{20,16},{24,28},{28,24},{32,36},... | collective-permute-start | bytes 12296 | tf_op jit(solution)/shard_map/ppermute | solution.py:501
  122.1 4.1 %collective-permute-start.12 = (f32[8,128]{1,0:T(8,128)S(1)}, f32[8,128]{1,0:T(8,128)S(1)}, u32[]{:S(2)}, u32[]{:S(2)}) collective-permute-start(f32[8,128]{1,0:T(8,128)S(1)} %add_add_fusion.17), channel_id=1, source_target_pairs={{0,16},{4,20},{8,24},{12,28},{16,0},{20,4},{24,8},{28,12},{32,48},... | collective-permute-start | bytes 12296 | tf_op jit(solution)/shard_map/ppermute | solution.py:501
  127.8 1.6 collective-permute-start.17
  131.9 2.6 collective-permute-done.16
  137.0 8.0 %collective-permute-start.19 = (f32[8,128]{1,0:T(8,128)S(1)}, f32[8,128]{1,0:T(8,128)S(1)}, u32[]{:S(2)}, u32[]{:S(2)}) collective-permute-start(f32[8,128]{1,0:T(8,128)S(1)} %multiply_subtract_fusion.4.own_ref), channel_id=1, source_target_pairs={{4,0},{8,4},{12,8},{16,12},{20,16},{24,20},{28,24},{32,28},{36,32}... | collective-permute-start | bytes 12296 | tf_op jit(solution)/shard_map/ppermute | solution.py:441
  145.0 1.9 collective-permute-start.18
  147.0 8.4 %collective-permute-done.18.below_ref = f32[8,128]{1,0:T(8,128)S(1)} collective-permute-done((f32[8,128]{1,0:T(8,128)S(1)}, f32[8,128]{1,0:T(8,128)S(1)}, u32[]{:S(2)}, u32[]{:S(2)}) %collective-permute-start.18) | collective-permute-done | bytes 4128 | tf_op jit(solution)/shard_map/ppermute | solution.py:441
  155.9 1.7 mv.7
  157.6 4.4 %collective-permute-start.20 = (f32[8,128]{1,0:T(8,128)}, f32[8,128]{1,0:T(8,128)S(1)}, u32[]{:S(2)}, u32[]{:S(2)}) collective-permute-start(f32[8,128]{1,0:T(8,128)} %get-tuple-element.38), channel_id=1, source_target_pairs={{0,4},{4,0},{8,12},{12,8},{16,20},{20,16},{24,28},{28,24},{32,36},... | collective-permute-start | bytes 12296 | tf_op jit(solution)/shard_map/ppermute | solution.py:501
  164.5 4.1 %collective-permute-start.23 = (f32[8,128]{1,0:T(8,128)S(1)}, f32[8,128]{1,0:T(8,128)S(1)}, u32[]{:S(2)}, u32[]{:S(2)}) collective-permute-start(f32[8,128]{1,0:T(8,128)S(1)} %add_add_fusion.14), channel_id=1, source_target_pairs={{0,16},{4,20},{8,24},{12,28},{16,0},{20,4},{24,8},{28,12},{32,48},... | collective-permute-start | bytes 12296 | tf_op jit(solution)/shard_map/ppermute | solution.py:501
  170.3 1.5 collective-permute-start.27
  171.7 2.6 collective-permute-start.26
  181.6 7.8 %collective-permute-start.30 = (f32[8,128]{1,0:T(8,128)S(1)}, f32[8,128]{1,0:T(8,128)S(1)}, u32[]{:S(2)}, u32[]{:S(2)}) collective-permute-start(f32[8,128]{1,0:T(8,128)S(1)} %multiply_subtract_fusion.3.own_ref), channel_id=1, source_target_pairs={{4,0},{8,4},{12,8},{16,12},{20,16},{24,20},{28,24},{32,28},{36,32}... | collective-permute-start | bytes 12296 | tf_op jit(solution)/shard_map/ppermute | solution.py:441
  189.5 1.9 collective-permute-start.29
  191.4 8.4 %collective-permute-done.29.below_ref = f32[8,128]{1,0:T(8,128)S(1)} collective-permute-done((f32[8,128]{1,0:T(8,128)S(1)}, f32[8,128]{1,0:T(8,128)S(1)}, u32[]{:S(2)}, u32[]{:S(2)}) %collective-permute-start.29) | collective-permute-done | bytes 4128 | tf_op jit(solution)/shard_map/ppermute | solution.py:441
  200.4 1.7 mv.8
  202.1 13.0 %collective-permute-start.31 = (f32[8,128]{1,0:T(8,128)}, f32[8,128]{1,0:T(8,128)S(1)}, u32[]{:S(2)}, u32[]{:S(2)}) collective-permute-start(f32[8,128]{1,0:T(8,128)} %get-tuple-element.40), channel_id=1, source_target_pairs={{0,4},{4,0},{8,12},{12,8},{16,20},{20,16},{24,28},{28,24},{32,36},... | collective-permute-start | bytes 12296 | tf_op jit(solution)/shard_map/ppermute | solution.py:501
  215.1 1.8 collective-permute-done.31
  217.6 4.1 %collective-permute-start.34 = (f32[8,128]{1,0:T(8,128)S(1)}, f32[8,128]{1,0:T(8,128)S(1)}, u32[]{:S(2)}, u32[]{:S(2)}) collective-permute-start(f32[8,128]{1,0:T(8,128)S(1)} %add_add_fusion.11), channel_id=1, source_target_pairs={{0,16},{4,20},{8,24},{12,28},{16,0},{20,4},{24,8},{28,12},{32,48},... | collective-permute-start | bytes 12296 | tf_op jit(solution)/shard_map/ppermute | solution.py:501
  224.8 2.6 collective-permute-start.37
  233.8 6.9 %collective-permute-start.41 = (f32[8,128]{1,0:T(8,128)S(1)}, f32[8,128]{1,0:T(8,128)S(1)}, u32[]{:S(2)}, u32[]{:S(2)}) collective-permute-start(f32[8,128]{1,0:T(8,128)S(1)} %get-tuple-element.54.own_ref), channel_id=1, source_target_pairs={{4,0},{8,4},{12,8},{16,12},{20,16},{24,20},{28,24},{32,28},{36,32}... | collective-permute-start | bytes 12296 | tf_op jit(solution)/shard_map/ppermute | solution.py:441
  240.7 1.9 collective-permute-start.40
  242.7 8.4 %collective-permute-done.40.below_ref = f32[8,128]{1,0:T(8,128)S(1)} collective-permute-done((f32[8,128]{1,0:T(8,128)S(1)}, f32[8,128]{1,0:T(8,128)S(1)}, u32[]{:S(2)}, u32[]{:S(2)}) %collective-permute-start.40) | collective-permute-done | bytes 4128 | tf_op jit(solution)/shard_map/ppermute | solution.py:441
  251.7 1.7 mv.9
  253.3 4.4 %collective-permute-start.42 = (f32[8,128]{1,0:T(8,128)}, f32[8,128]{1,0:T(8,128)S(1)}, u32[]{:S(2)}, u32[]{:S(2)}) collective-permute-start(f32[8,128]{1,0:T(8,128)} %get-tuple-element.42), channel_id=1, source_target_pairs={{0,4},{4,0},{8,12},{12,8},{16,20},{20,16},{24,28},{28,24},{32,36},... | collective-permute-start | bytes 12296 | tf_op jit(solution)/shard_map/ppermute | solution.py:501
  260.2 4.1 %collective-permute-start.45 = (f32[8,128]{1,0:T(8,128)S(1)}, f32[8,128]{1,0:T(8,128)S(1)}, u32[]{:S(2)}, u32[]{:S(2)}) collective-permute-start(f32[8,128]{1,0:T(8,128)S(1)} %add_add_fusion.8), channel_id=1, source_target_pairs={{0,16},{4,20},{8,24},{12,28},{16,0},{20,4},{24,8},{28,12},{32,48},... | collective-permute-start | bytes 12296 | tf_op jit(solution)/shard_map/ppermute | solution.py:501
  267.4 2.6 collective-permute-start.48
  276.6 7.8 %collective-permute-start.52 = (f32[8,128]{1,0:T(8,128)S(1)}, f32[8,128]{1,0:T(8,128)S(1)}, u32[]{:S(2)}, u32[]{:S(2)}) collective-permute-start(f32[8,128]{1,0:T(8,128)S(1)} %multiply_subtract_fusion.1.own_ref), channel_id=1, source_target_pairs={{4,0},{8,4},{12,8},{16,12},{20,16},{24,20},{28,24},{32,28},{36,32}... | collective-permute-start | bytes 12296 | tf_op jit(solution)/shard_map/ppermute | solution.py:441
  284.4 1.9 collective-permute-start.51
  286.4 8.4 %collective-permute-done.51.below_ref = f32[8,128]{1,0:T(8,128)S(1)} collective-permute-done((f32[8,128]{1,0:T(8,128)S(1)}, f32[8,128]{1,0:T(8,128)S(1)}, u32[]{:S(2)}, u32[]{:S(2)}) %collective-permute-start.51) | collective-permute-done | bytes 4128 | tf_op jit(solution)/shard_map/ppermute | solution.py:441
  295.3 1.7 mv.10
  297.0 4.4 %collective-permute-start.53 = (f32[8,128]{1,0:T(8,128)}, f32[8,128]{1,0:T(8,128)S(1)}, u32[]{:S(2)}, u32[]{:S(2)}) collective-permute-start(f32[8,128]{1,0:T(8,128)} %get-tuple-element.44), channel_id=1, source_target_pairs={{0,4},{4,0},{8,12},{12,8},{16,20},{20,16},{24,28},{28,24},{32,36},... | collective-permute-start | bytes 12296 | tf_op jit(solution)/shard_map/ppermute | solution.py:501
  303.9 4.1 %collective-permute-start.56 = (f32[8,128]{1,0:T(8,128)S(1)}, f32[8,128]{1,0:T(8,128)S(1)}, u32[]{:S(2)}, u32[]{:S(2)}) collective-permute-start(f32[8,128]{1,0:T(8,128)S(1)} %add_add_fusion.5), channel_id=1, source_target_pairs={{0,16},{4,20},{8,24},{12,28},{16,0},{20,4},{24,8},{28,12},{32,48},... | collective-permute-start | bytes 12296 | tf_op jit(solution)/shard_map/ppermute | solution.py:501
  311.3 2.6 collective-permute-start.59
  320.4 7.8 %collective-permute-start.63 = (f32[8,128]{1,0:T(8,128)S(1)}, f32[8,128]{1,0:T(8,128)S(1)}, u32[]{:S(2)}, u32[]{:S(2)}) collective-permute-start(f32[8,128]{1,0:T(8,128)S(1)} %multiply_subtract_fusion.own_ref), channel_id=1, source_target_pairs={{4,0},{8,4},{12,8},{16,12},{20,16},{24,20},{28,24},{32,28},{36,32}... | collective-permute-start | bytes 12296 | tf_op jit(solution)/shard_map/ppermute | solution.py:441
  328.2 1.9 collective-permute-start.62
  330.1 8.4 %collective-permute-done.62.below_ref = f32[8,128]{1,0:T(8,128)S(1)} collective-permute-done((f32[8,128]{1,0:T(8,128)S(1)}, f32[8,128]{1,0:T(8,128)S(1)}, u32[]{:S(2)}, u32[]{:S(2)}) %collective-permute-start.62) | collective-permute-done | bytes 4128 | tf_op jit(solution)/shard_map/ppermute | solution.py:441
  339.1 1.7 mv.11
  340.8 4.4 %collective-permute-start.64 = (f32[8,128]{1,0:T(8,128)}, f32[8,128]{1,0:T(8,128)S(1)}, u32[]{:S(2)}, u32[]{:S(2)}) collective-permute-start(f32[8,128]{1,0:T(8,128)} %get-tuple-element.46), channel_id=1, source_target_pairs={{0,4},{4,0},{8,12},{12,8},{16,20},{20,16},{24,28},{28,24},{32,36},... | collective-permute-start | bytes 12296 | tf_op jit(solution)/shard_map/ppermute | solution.py:501
  347.7 4.1 %collective-permute-start.67 = (f32[8,128]{1,0:T(8,128)S(1)}, f32[8,128]{1,0:T(8,128)S(1)}, u32[]{:S(2)}, u32[]{:S(2)}) collective-permute-start(f32[8,128]{1,0:T(8,128)S(1)} %add_add_fusion.2), channel_id=1, source_target_pairs={{0,16},{4,20},{8,24},{12,28},{16,0},{20,4},{24,8},{28,12},{32,48},... | collective-permute-start | bytes 12296 | tf_op jit(solution)/shard_map/ppermute | solution.py:501
  354.9 2.6 collective-permute-start.70
  364.0 7.8 %collective-permute-start.74 = (f32[8,128]{1,0:T(8,128)S(1)}, f32[8,128]{1,0:T(8,128)S(1)}, u32[]{:S(2)}, u32[]{:S(2)}) collective-permute-start(f32[8,128]{1,0:T(8,128)S(1)} %multiply_add_fusion.own_ref), channel_id=1, source_target_pairs={{4,0},{8,4},{12,8},{16,12},{20,16},{24,20},{28,24},{32,28},{36,32}... | collective-permute-start | bytes 12296 | tf_op jit(solution)/shard_map/ppermute | solution.py:441
  371.8 1.9 collective-permute-start.73
  374.5 7.6 %collective-permute-done.73.below_ref = f32[8,128]{1,0:T(8,128)S(1)} collective-permute-done((f32[8,128]{1,0:T(8,128)S(1)}, f32[8,128]{1,0:T(8,128)S(1)}, u32[]{:S(2)}, u32[]{:S(2)}) %collective-permute-start.73) | collective-permute-done | bytes 4128 | tf_op jit(solution)/shard_map/ppermute | solution.py:441
  382.7 5.6 %final.1 = f32[16,768]{1,0:T(8,128)} custom-call(f32[8,128]{1,0:T(8,128)} %copy-done.16, f32[8,128]{1,0:T(8,128)} %copy-done.14, f32[8,128]{1,0:T(8,128)} %copy-done.15, f32[1536,384]{1,0:T(8,128)} %get-tuple-element.30.b_ref, f32[1536,768]{1,0:T(8,128)} %get-tuple-element.47.g_ref, f32[128,768]{1,0:T(8,128)} %get-tuple-element.48.base_ref, ...), custom_call_target="tpu_custom_call" | custom-call | tf_op jit(solution)/shard_map/final/pallas_call | solution.py:421
  (198 shorter events, 60.6 us)
Async XLA Ops:
  12.7 29.0 %collective-permute-start = (f32[152,768]{1,0:T(8,128)}, f32[152,768]{1,0:T(8,128)S(1)}, u32[]{:S(2)}, u32[]{:S(2)}) collective-permute-start(f32[152,768]{1,0:T(8,128)} %get-tuple-element.27), channel_id=1, source_target_pairs={{4,0},{8,4},{12,8},{16,12},{20,16},{24,20},{28,24},{32,28},{36,32}... | collective-permute-start | bytes 1400840 | tf_op jit(solution)/shard_map/ppermute | solution.py:441
  21.3 20.4 %collective-permute-start.1 = (f32[144,768]{1,0:T(8,128)}, f32[144,768]{1,0:T(8,128)S(1)}, u32[]{:S(2)}, u32[]{:S(2)}) collective-permute-start(f32[144,768]{1,0:T(8,128)} %get-tuple-element.28), channel_id=1, source_target_pairs={{0,4},{4,8},{8,12},{12,16},{16,20},{20,24},{24,28},{28,32},{32,36}... | collective-permute-start | bytes 1327112 | tf_op jit(solution)/shard_map/ppermute | solution.py:441
  70.3 11.1 %collective-permute-start.5 = (f32[48,384]{1,0:T(8,128)S(1)}, f32[48,384]{1,0:T(8,128)S(1)}, u32[]{:S(2)}, u32[]{:S(2)}) collective-permute-start(f32[48,384]{1,0:T(8,128)S(1)} %get-tuple-element.56), channel_id=1, source_target_pairs={{0,6},{2,4},{4,10},{5,3},{6,8},{7,1},{8,14},{9,7},{10,12},{11,5},{... | collective-permute-start | bytes 221192 | tf_op jit(solution)/shard_map/ppermute | solution.py:486
  77.0 11.3 %collective-permute-start.4 = (f32[48,384]{1,0:T(8,128)S(1)}, f32[48,384]{1,0:T(8,128)S(1)}, u32[]{:S(2)}, u32[]{:S(2)}) collective-permute-start(f32[48,384]{1,0:T(8,128)S(1)} %get-tuple-element.56), channel_id=1, source_target_pairs={{0,4},{2,6},{4,8},{5,1},{6,10},{7,3},{8,12},{9,5},{10,14},{11,7},{... | collective-permute-start | bytes 221192 | tf_op jit(solution)/shard_map/ppermute | solution.py:486
  79.5 8.8 %collective-permute-start.3 = (f32[48,384]{1,0:T(8,128)S(1)}, f32[48,384]{1,0:T(8,128)S(1)}, u32[]{:S(2)}, u32[]{:S(2)}) collective-permute-start(f32[48,384]{1,0:T(8,128)S(1)} %get-tuple-element.57.own_ref), channel_id=1, source_target_pairs={{0,2},{1,3},{2,0},{3,1},{4,6},{5,7},{6,4},{7,5},{8,10},{9,11},{10,... | collective-permute-start | bytes 221192 | tf_op jit(solution)/shard_map/ppermute | solution.py:488
  95.2 9.1 %collective-permute-start.8 = (f32[8,128]{1,0:T(8,128)}, f32[8,128]{1,0:T(8,128)S(1)}, u32[]{:S(2)}, u32[]{:S(2)}) collective-permute-start(f32[8,128]{1,0:T(8,128)} %get-tuple-element.35.own_ref), channel_id=1, source_target_pairs={{4,0},{8,4},{12,8},{16,12},{20,16},{24,20},{28,24},{32,28},{36,32}... | collective-permute-start | bytes 12296 | tf_op jit(solution)/shard_map/ppermute | solution.py:441
  102.4 10.5 %collective-permute-start.7 = (f32[8,128]{1,0:T(8,128)}, f32[8,128]{1,0:T(8,128)S(1)}, u32[]{:S(2)}, u32[]{:S(2)}) collective-permute-start(f32[8,128]{1,0:T(8,128)} %get-tuple-element.35.own_ref), channel_id=1, source_target_pairs={{0,4},{4,8},{8,12},{12,16},{16,20},{20,24},{24,28},{28,32},{32,36}... | collective-permute-start | bytes 12296 | tf_op jit(solution)/shard_map/ppermute | solution.py:441
  115.2 5.6 %collective-permute-start.11 = (f32[8,128]{1,0:T(8,128)}, f32[8,128]{1,0:T(8,128)S(1)}, u32[]{:S(2)}, u32[]{:S(2)}) collective-permute-start(f32[8,128]{1,0:T(8,128)} %get-tuple-element.36), channel_id=1, source_target_pairs={{0,12},{4,8},{8,4},{12,0},{16,28},{20,24},{24,20},{28,16},{32,44},... | collective-permute-start | bytes 12296 | tf_op jit(solution)/shard_map/ppermute | solution.py:501
  115.2 5.6 %collective-permute-start.10 = (f32[8,128]{1,0:T(8,128)}, f32[8,128]{1,0:T(8,128)S(1)}, u32[]{:S(2)}, u32[]{:S(2)}) collective-permute-start(f32[8,128]{1,0:T(8,128)} %get-tuple-element.36), channel_id=1, source_target_pairs={{0,8},{4,12},{8,0},{12,4},{16,24},{20,28},{24,16},{28,20},{32,40},... | collective-permute-start | bytes 12296 | tf_op jit(solution)/shard_map/ppermute | solution.py:501
  115.2 6.2 %collective-permute-start.9 = (f32[8,128]{1,0:T(8,128)}, f32[8,128]{1,0:T(8,128)S(1)}, u32[]{:S(2)}, u32[]{:S(2)}) collective-permute-start(f32[8,128]{1,0:T(8,128)} %get-tuple-element.36), channel_id=1, source_target_pairs={{0,4},{4,0},{8,12},{12,8},{16,20},{20,16},{24,28},{28,24},{32,36},... | collective-permute-start | bytes 12296 | tf_op jit(solution)/shard_map/ppermute | solution.py:501
  122.1 4.8 %collective-permute-start.14 = (f32[8,128]{1,0:T(8,128)S(1)}, f32[8,128]{1,0:T(8,128)S(1)}, u32[]{:S(2)}, u32[]{:S(2)}) collective-permute-start(f32[8,128]{1,0:T(8,128)S(1)} %add_add_fusion.17), channel_id=1, source_target_pairs={{0,48},{4,52},{8,56},{12,60},{16,32},{20,36},{24,40},{28,44},{32,1... | collective-permute-start | bytes 12296 | tf_op jit(solution)/shard_map/ppermute | solution.py:501
  122.1 5.1 %collective-permute-start.13 = (f32[8,128]{1,0:T(8,128)S(1)}, f32[8,128]{1,0:T(8,128)S(1)}, u32[]{:S(2)}, u32[]{:S(2)}) collective-permute-start(f32[8,128]{1,0:T(8,128)S(1)} %add_add_fusion.17), channel_id=1, source_target_pairs={{0,32},{4,36},{8,40},{12,44},{16,48},{20,52},{24,56},{28,60},{32,0... | collective-permute-start | bytes 12296 | tf_op jit(solution)/shard_map/ppermute | solution.py:501
  122.1 5.7 %collective-permute-start.12 = (f32[8,128]{1,0:T(8,128)S(1)}, f32[8,128]{1,0:T(8,128)S(1)}, u32[]{:S(2)}, u32[]{:S(2)}) collective-permute-start(f32[8,128]{1,0:T(8,128)S(1)} %add_add_fusion.17), channel_id=1, source_target_pairs={{0,16},{4,20},{8,24},{12,28},{16,0},{20,4},{24,8},{28,12},{32,48},... | collective-permute-start | bytes 12296 | tf_op jit(solution)/shard_map/ppermute | solution.py:501
  129.4 5.1 %collective-permute-start.16 = (f32[8,128]{1,0:T(8,128)S(1)}, f32[8,128]{1,0:T(8,128)S(1)}, u32[]{:S(2)}, u32[]{:S(2)}) collective-permute-start(f32[8,128]{1,0:T(8,128)S(1)} %add_add_fusion.16), channel_id=1, source_target_pairs={{0,128},{4,132},{8,136},{12,140},{16,144},{20,148},{24,152},{28,15... | collective-permute-start | bytes 12296 | tf_op jit(solution)/shard_map/ppermute | solution.py:501
  137.0 9.9 %collective-permute-start.19 = (f32[8,128]{1,0:T(8,128)S(1)}, f32[8,128]{1,0:T(8,128)S(1)}, u32[]{:S(2)}, u32[]{:S(2)}) collective-permute-start(f32[8,128]{1,0:T(8,128)S(1)} %multiply_subtract_fusion.4.own_ref), channel_id=1, source_target_pairs={{4,0},{8,4},{12,8},{16,12},{20,16},{24,20},{28,24},{32,28},{36,32}... | collective-permute-start | bytes 12296 | tf_op jit(solution)/shard_map/ppermute | solution.py:441
  145.0 10.3 %collective-permute-start.18 = (f32[8,128]{1,0:T(8,128)S(1)}, f32[8,128]{1,0:T(8,128)S(1)}, u32[]{:S(2)}, u32[]{:S(2)}) collective-permute-start(f32[8,128]{1,0:T(8,128)S(1)} %multiply_subtract_fusion.4.own_ref), channel_id=1, source_target_pairs={{0,4},{4,8},{8,12},{12,16},{16,20},{20,24},{24,28},{28,32},{32,36}... | collective-permute-start | bytes 12296 | tf_op jit(solution)/shard_map/ppermute | solution.py:441
  157.6 5.6 %collective-permute-start.22 = (f32[8,128]{1,0:T(8,128)}, f32[8,128]{1,0:T(8,128)S(1)}, u32[]{:S(2)}, u32[]{:S(2)}) collective-permute-start(f32[8,128]{1,0:T(8,128)} %get-tuple-element.38), channel_id=1, source_target_pairs={{0,12},{4,8},{8,4},{12,0},{16,28},{20,24},{24,20},{28,16},{32,44},... | collective-permute-start | bytes 12296 | tf_op jit(solution)/shard_map/ppermute | solution.py:501
  157.6 5.6 %collective-permute-start.21 = (f32[8,128]{1,0:T(8,128)}, f32[8,128]{1,0:T(8,128)S(1)}, u32[]{:S(2)}, u32[]{:S(2)}) collective-permute-start(f32[8,128]{1,0:T(8,128)} %get-tuple-element.38), channel_id=1, source_target_pairs={{0,8},{4,12},{8,0},{12,4},{16,24},{20,28},{24,16},{28,20},{32,40},... | collective-permute-start | bytes 12296 | tf_op jit(solution)/shard_map/ppermute | solution.py:501
  157.6 6.2 %collective-permute-start.20 = (f32[8,128]{1,0:T(8,128)}, f32[8,128]{1,0:T(8,128)S(1)}, u32[]{:S(2)}, u32[]{:S(2)}) collective-permute-start(f32[8,128]{1,0:T(8,128)} %get-tuple-element.38), channel_id=1, source_target_pairs={{0,4},{4,0},{8,12},{12,8},{16,20},{20,16},{24,28},{28,24},{32,36},... | collective-permute-start | bytes 12296 | tf_op jit(solution)/shard_map/ppermute | solution.py:501
  164.5 4.8 %collective-permute-start.25 = (f32[8,128]{1,0:T(8,128)S(1)}, f32[8,128]{1,0:T(8,128)S(1)}, u32[]{:S(2)}, u32[]{:S(2)}) collective-permute-start(f32[8,128]{1,0:T(8,128)S(1)} %add_add_fusion.14), channel_id=1, source_target_pairs={{0,48},{4,52},{8,56},{12,60},{16,32},{20,36},{24,40},{28,44},{32,1... | collective-permute-start | bytes 12296 | tf_op jit(solution)/shard_map/ppermute | solution.py:501
  164.5 5.1 %collective-permute-start.24 = (f32[8,128]{1,0:T(8,128)S(1)}, f32[8,128]{1,0:T(8,128)S(1)}, u32[]{:S(2)}, u32[]{:S(2)}) collective-permute-start(f32[8,128]{1,0:T(8,128)S(1)} %add_add_fusion.14), channel_id=1, source_target_pairs={{0,32},{4,36},{8,40},{12,44},{16,48},{20,52},{24,56},{28,60},{32,0... | collective-permute-start | bytes 12296 | tf_op jit(solution)/shard_map/ppermute | solution.py:501
  164.5 5.7 %collective-permute-start.23 = (f32[8,128]{1,0:T(8,128)S(1)}, f32[8,128]{1,0:T(8,128)S(1)}, u32[]{:S(2)}, u32[]{:S(2)}) collective-permute-start(f32[8,128]{1,0:T(8,128)S(1)} %add_add_fusion.14), channel_id=1, source_target_pairs={{0,16},{4,20},{8,24},{12,28},{16,0},{20,4},{24,8},{28,12},{32,48},... | collective-permute-start | bytes 12296 | tf_op jit(solution)/shard_map/ppermute | solution.py:501
  170.3 5.2 %collective-permute-start.27 = (f32[8,128]{1,0:T(8,128)S(1)}, f32[8,128]{1,0:T(8,128)S(1)}, u32[]{:S(2)}, u32[]{:S(2)}) collective-permute-start(f32[8,128]{1,0:T(8,128)S(1)} %add_add_fusion.13), channel_id=1, source_target_pairs={{0,128},{4,132},{8,136},{12,140},{16,144},{20,148},{24,152},{28,15... | collective-permute-start | bytes 12296 | tf_op jit(solution)/shard_map/ppermute | solution.py:501
  181.6 9.7 %collective-permute-start.30 = (f32[8,128]{1,0:T(8,128)S(1)}, f32[8,128]{1,0:T(8,128)S(1)}, u32[]{:S(2)}, u32[]{:S(2)}) collective-permute-start(f32[8,128]{1,0:T(8,128)S(1)} %multiply_subtract_fusion.3.own_ref), channel_id=1, source_target_pairs={{4,0},{8,4},{12,8},{16,12},{20,16},{24,20},{28,24},{32,28},{36,32}... | collective-permute-start | bytes 12296 | tf_op jit(solution)/shard_map/ppermute | solution.py:441
  189.5 10.3 %collective-permute-start.29 = (f32[8,128]{1,0:T(8,128)S(1)}, f32[8,128]{1,0:T(8,128)S(1)}, u32[]{:S(2)}, u32[]{:S(2)}) collective-permute-start(f32[8,128]{1,0:T(8,128)S(1)} %multiply_subtract_fusion.3.own_ref), channel_id=1, source_target_pairs={{0,4},{4,8},{8,12},{12,16},{16,20},{20,24},{24,28},{28,32},{32,36}... | collective-permute-start | bytes 12296 | tf_op jit(solution)/shard_map/ppermute | solution.py:441
  202.1 13.0 %collective-permute-start.33 = (f32[8,128]{1,0:T(8,128)}, f32[8,128]{1,0:T(8,128)S(1)}, u32[]{:S(2)}, u32[]{:S(2)}) collective-permute-start(f32[8,128]{1,0:T(8,128)} %get-tuple-element.40), channel_id=1, source_target_pairs={{0,12},{4,8},{8,4},{12,0},{16,28},{20,24},{24,20},{28,16},{32,44},... | collective-permute-start | bytes 12296 | tf_op jit(solution)/shard_map/ppermute | solution.py:501
  202.1 13.0 %collective-permute-start.32 = (f32[8,128]{1,0:T(8,128)}, f32[8,128]{1,0:T(8,128)S(1)}, u32[]{:S(2)}, u32[]{:S(2)}) collective-permute-start(f32[8,128]{1,0:T(8,128)} %get-tuple-element.40), channel_id=1, source_target_pairs={{0,8},{4,12},{8,0},{12,4},{16,24},{20,28},{24,16},{28,20},{32,40},... | collective-permute-start | bytes 12296 | tf_op jit(solution)/shard_map/ppermute | solution.py:501
  202.1 14.8 %collective-permute-start.31 = (f32[8,128]{1,0:T(8,128)}, f32[8,128]{1,0:T(8,128)S(1)}, u32[]{:S(2)}, u32[]{:S(2)}) collective-permute-start(f32[8,128]{1,0:T(8,128)} %get-tuple-element.40), channel_id=1, source_target_pairs={{0,4},{4,0},{8,12},{12,8},{16,20},{20,16},{24,28},{28,24},{32,36},... | collective-permute-start | bytes 12296 | tf_op jit(solution)/shard_map/ppermute | solution.py:501
  217.6 4.8 %collective-permute-start.36 = (f32[8,128]{1,0:T(8,128)S(1)}, f32[8,128]{1,0:T(8,128)S(1)}, u32[]{:S(2)}, u32[]{:S(2)}) collective-permute-start(f32[8,128]{1,0:T(8,128)S(1)} %add_add_fusion.11), channel_id=1, source_target_pairs={{0,48},{4,52},{8,56},{12,60},{16,32},{20,36},{24,40},{28,44},{32,1... | collective-permute-start | bytes 12296 | tf_op jit(solution)/shard_map/ppermute | solution.py:501
  217.6 5.1 %collective-permute-start.35 = (f32[8,128]{1,0:T(8,128)S(1)}, f32[8,128]{1,0:T(8,128)S(1)}, u32[]{:S(2)}, u32[]{:S(2)}) collective-permute-start(f32[8,128]{1,0:T(8,128)S(1)} %add_add_fusion.11), channel_id=1, source_target_pairs={{0,32},{4,36},{8,40},{12,44},{16,48},{20,52},{24,56},{28,60},{32,0... | collective-permute-start | bytes 12296 | tf_op jit(solution)/shard_map/ppermute | solution.py:501
  217.6 5.7 %collective-permute-start.34 = (f32[8,128]{1,0:T(8,128)S(1)}, f32[8,128]{1,0:T(8,128)S(1)}, u32[]{:S(2)}, u32[]{:S(2)}) collective-permute-start(f32[8,128]{1,0:T(8,128)S(1)} %add_add_fusion.11), channel_id=1, source_target_pairs={{0,16},{4,20},{8,24},{12,28},{16,0},{20,4},{24,8},{28,12},{32,48},... | collective-permute-start | bytes 12296 | tf_op jit(solution)/shard_map/ppermute | solution.py:501
  223.3 5.2 %collective-permute-start.38 = (f32[8,128]{1,0:T(8,128)S(1)}, f32[8,128]{1,0:T(8,128)S(1)}, u32[]{:S(2)}, u32[]{:S(2)}) collective-permute-start(f32[8,128]{1,0:T(8,128)S(1)} %add_add_fusion.10), channel_id=1, source_target_pairs={{0,128},{4,132},{8,136},{12,140},{16,144},{20,148},{24,152},{28,15... | collective-permute-start | bytes 12296 | tf_op jit(solution)/shard_map/ppermute | solution.py:501
  233.8 8.9 %collective-permute-start.41 = (f32[8,128]{1,0:T(8,128)S(1)}, f32[8,128]{1,0:T(8,128)S(1)}, u32[]{:S(2)}, u32[]{:S(2)}) collective-permute-start(f32[8,128]{1,0:T(8,128)S(1)} %get-tuple-element.54.own_ref), channel_id=1, source_target_pairs={{4,0},{8,4},{12,8},{16,12},{20,16},{24,20},{28,24},{32,28},{36,32}... | collective-permute-start | bytes 12296 | tf_op jit(solution)/shard_map/ppermute | solution.py:441
  240.7 10.3 %collective-permute-start.40 = (f32[8,128]{1,0:T(8,128)S(1)}, f32[8,128]{1,0:T(8,128)S(1)}, u32[]{:S(2)}, u32[]{:S(2)}) collective-permute-start(f32[8,128]{1,0:T(8,128)S(1)} %get-tuple-element.54.own_ref), channel_id=1, source_target_pairs={{0,4},{4,8},{8,12},{12,16},{16,20},{20,24},{24,28},{28,32},{32,36}... | collective-permute-start | bytes 12296 | tf_op jit(solution)/shard_map/ppermute | solution.py:441
  253.3 5.6 %collective-permute-start.44 = (f32[8,128]{1,0:T(8,128)}, f32[8,128]{1,0:T(8,128)S(1)}, u32[]{:S(2)}, u32[]{:S(2)}) collective-permute-start(f32[8,128]{1,0:T(8,128)} %get-tuple-element.42), channel_id=1, source_target_pairs={{0,12},{4,8},{8,4},{12,0},{16,28},{20,24},{24,20},{28,16},{32,44},... | collective-permute-start | bytes 12296 | tf_op jit(solution)/shard_map/ppermute | solution.py:501
  253.3 5.6 %collective-permute-start.43 = (f32[8,128]{1,0:T(8,128)}, f32[8,128]{1,0:T(8,128)S(1)}, u32[]{:S(2)}, u32[]{:S(2)}) collective-permute-start(f32[8,128]{1,0:T(8,128)} %get-tuple-element.42), channel_id=1, source_target_pairs={{0,8},{4,12},{8,0},{12,4},{16,24},{20,28},{24,16},{28,20},{32,40},... | collective-permute-start | bytes 12296 | tf_op jit(solution)/shard_map/ppermute | solution.py:501
  253.3 6.2 %collective-permute-start.42 = (f32[8,128]{1,0:T(8,128)}, f32[8,128]{1,0:T(8,128)S(1)}, u32[]{:S(2)}, u32[]{:S(2)}) collective-permute-start(f32[8,128]{1,0:T(8,128)} %get-tuple-element.42), channel_id=1, source_target_pairs={{0,4},{4,0},{8,12},{12,8},{16,20},{20,16},{24,28},{28,24},{32,36},... | collective-permute-start | bytes 12296 | tf_op jit(solution)/shard_map/ppermute | solution.py:501
  260.2 4.8 %collective-permute-start.47 = (f32[8,128]{1,0:T(8,128)S(1)}, f32[8,128]{1,0:T(8,128)S(1)}, u32[]{:S(2)}, u32[]{:S(2)}) collective-permute-start(f32[8,128]{1,0:T(8,128)S(1)} %add_add_fusion.8), channel_id=1, source_target_pairs={{0,48},{4,52},{8,56},{12,60},{16,32},{20,36},{24,40},{28,44},{32,1... | collective-permute-start | bytes 12296 | tf_op jit(solution)/shard_map/ppermute | solution.py:501
  260.2 5.1 %collective-permute-start.46 = (f32[8,128]{1,0:T(8,128)S(1)}, f32[8,128]{1,0:T(8,128)S(1)}, u32[]{:S(2)}, u32[]{:S(2)}) collective-permute-start(f32[8,128]{1,0:T(8,128)S(1)} %add_add_fusion.8), channel_id=1, source_target_pairs={{0,32},{4,36},{8,40},{12,44},{16,48},{20,52},{24,56},{28,60},{32,0... | collective-permute-start | bytes 12296 | tf_op jit(solution)/shard_map/ppermute | solution.py:501
  260.2 5.7 %collective-permute-start.45 = (f32[8,128]{1,0:T(8,128)S(1)}, f32[8,128]{1,0:T(8,128)S(1)}, u32[]{:S(2)}, u32[]{:S(2)}) collective-permute-start(f32[8,128]{1,0:T(8,128)S(1)} %add_add_fusion.8), channel_id=1, source_target_pairs={{0,16},{4,20},{8,24},{12,28},{16,0},{20,4},{24,8},{28,12},{32,48},... | collective-permute-start | bytes 12296 | tf_op jit(solution)/shard_map/ppermute | solution.py:501
  266.0 5.2 %collective-permute-start.49 = (f32[8,128]{1,0:T(8,128)S(1)}, f32[8,128]{1,0:T(8,128)S(1)}, u32[]{:S(2)}, u32[]{:S(2)}) collective-permute-start(f32[8,128]{1,0:T(8,128)S(1)} %add_add_fusion.7), channel_id=1, source_target_pairs={{0,128},{4,132},{8,136},{12,140},{16,144},{20,148},{24,152},{28,15... | collective-permute-start | bytes 12296 | tf_op jit(solution)/shard_map/ppermute | solution.py:501
  267.4 4.2 %collective-permute-start.48 = (f32[8,128]{1,0:T(8,128)S(1)}, f32[8,128]{1,0:T(8,128)S(1)}, u32[]{:S(2)}, u32[]{:S(2)}) collective-permute-start(f32[8,128]{1,0:T(8,128)S(1)} %add_add_fusion.7), channel_id=1, source_target_pairs={{0,64},{4,68},{8,72},{12,76},{16,80},{20,84},{24,88},{28,92},{32,9... | collective-permute-start | bytes 12296 | tf_op jit(solution)/shard_map/ppermute | solution.py:501
  276.6 9.7 %collective-permute-start.52 = (f32[8,128]{1,0:T(8,128)S(1)}, f32[8,128]{1,0:T(8,128)S(1)}, u32[]{:S(2)}, u32[]{:S(2)}) collective-permute-start(f32[8,128]{1,0:T(8,128)S(1)} %multiply_subtract_fusion.1.own_ref), channel_id=1, source_target_pairs={{4,0},{8,4},{12,8},{16,12},{20,16},{24,20},{28,24},{32,28},{36,32}... | collective-permute-start | bytes 12296 | tf_op jit(solution)/shard_map/ppermute | solution.py:441
  284.4 10.3 %collective-permute-start.51 = (f32[8,128]{1,0:T(8,128)S(1)}, f32[8,128]{1,0:T(8,128)S(1)}, u32[]{:S(2)}, u32[]{:S(2)}) collective-permute-start(f32[8,128]{1,0:T(8,128)S(1)} %multiply_subtract_fusion.1.own_ref), channel_id=1, source_target_pairs={{0,4},{4,8},{8,12},{12,16},{16,20},{20,24},{24,28},{28,32},{32,36}... | collective-permute-start | bytes 12296 | tf_op jit(solution)/shard_map/ppermute | solution.py:441
  297.0 5.6 %collective-permute-start.55 = (f32[8,128]{1,0:T(8,128)}, f32[8,128]{1,0:T(8,128)S(1)}, u32[]{:S(2)}, u32[]{:S(2)}) collective-permute-start(f32[8,128]{1,0:T(8,128)} %get-tuple-element.44), channel_id=1, source_target_pairs={{0,12},{4,8},{8,4},{12,0},{16,28},{20,24},{24,20},{28,16},{32,44},... | collective-permute-start | bytes 12296 | tf_op jit(solution)/shard_map/ppermute | solution.py:501
  297.0 5.6 %collective-permute-start.54 = (f32[8,128]{1,0:T(8,128)}, f32[8,128]{1,0:T(8,128)S(1)}, u32[]{:S(2)}, u32[]{:S(2)}) collective-permute-start(f32[8,128]{1,0:T(8,128)} %get-tuple-element.44), channel_id=1, source_target_pairs={{0,8},{4,12},{8,0},{12,4},{16,24},{20,28},{24,16},{28,20},{32,40},... | collective-permute-start | bytes 12296 | tf_op jit(solution)/shard_map/ppermute | solution.py:501
  297.0 6.2 %collective-permute-start.53 = (f32[8,128]{1,0:T(8,128)}, f32[8,128]{1,0:T(8,128)S(1)}, u32[]{:S(2)}, u32[]{:S(2)}) collective-permute-start(f32[8,128]{1,0:T(8,128)} %get-tuple-element.44), channel_id=1, source_target_pairs={{0,4},{4,0},{8,12},{12,8},{16,20},{20,16},{24,28},{28,24},{32,36},... | collective-permute-start | bytes 12296 | tf_op jit(solution)/shard_map/ppermute | solution.py:501
  303.9 4.8 %collective-permute-start.58 = (f32[8,128]{1,0:T(8,128)S(1)}, f32[8,128]{1,0:T(8,128)S(1)}, u32[]{:S(2)}, u32[]{:S(2)}) collective-permute-start(f32[8,128]{1,0:T(8,128)S(1)} %add_add_fusion.5), channel_id=1, source_target_pairs={{0,48},{4,52},{8,56},{12,60},{16,32},{20,36},{24,40},{28,44},{32,1... | collective-permute-start | bytes 12296 | tf_op jit(solution)/shard_map/ppermute | solution.py:501
  303.9 5.1 %collective-permute-start.57 = (f32[8,128]{1,0:T(8,128)S(1)}, f32[8,128]{1,0:T(8,128)S(1)}, u32[]{:S(2)}, u32[]{:S(2)}) collective-permute-start(f32[8,128]{1,0:T(8,128)S(1)} %add_add_fusion.5), channel_id=1, source_target_pairs={{0,32},{4,36},{8,40},{12,44},{16,48},{20,52},{24,56},{28,60},{32,0... | collective-permute-start | bytes 12296 | tf_op jit(solution)/shard_map/ppermute | solution.py:501
  303.9 5.7 %collective-permute-start.56 = (f32[8,128]{1,0:T(8,128)S(1)}, f32[8,128]{1,0:T(8,128)S(1)}, u32[]{:S(2)}, u32[]{:S(2)}) collective-permute-start(f32[8,128]{1,0:T(8,128)S(1)} %add_add_fusion.5), channel_id=1, source_target_pairs={{0,16},{4,20},{8,24},{12,28},{16,0},{20,4},{24,8},{28,12},{32,48},... | collective-permute-start | bytes 12296 | tf_op jit(solution)/shard_map/ppermute | solution.py:501
  309.6 4.3 %collective-permute-start.61 = (f32[8,128]{1,0:T(8,128)S(1)}, f32[8,128]{1,0:T(8,128)S(1)}, u32[]{:S(2)}, u32[]{:S(2)}) collective-permute-start(f32[8,128]{1,0:T(8,128)S(1)} %add_add_fusion.4), channel_id=1, source_target_pairs={{0,192},{4,196},{8,200},{12,204},{16,208},{20,212},{24,216},{28,22... | collective-permute-start | bytes 12296 | tf_op jit(solution)/shard_map/ppermute | solution.py:501
  309.9 5.2 %collective-permute-start.60 = (f32[8,128]{1,0:T(8,128)S(1)}, f32[8,128]{1,0:T(8,128)S(1)}, u32[]{:S(2)}, u32[]{:S(2)}) collective-permute-start(f32[8,128]{1,0:T(8,128)S(1)} %add_add_fusion.4), channel_id=1, source_target_pairs={{0,128},{4,132},{8,136},{12,140},{16,144},{20,148},{24,152},{28,15... | collective-permute-start | bytes 12296 | tf_op jit(solution)/shard_map/ppermute | solution.py:501
  320.4 9.8 %collective-permute-start.63 = (f32[8,128]{1,0:T(8,128)S(1)}, f32[8,128]{1,0:T(8,128)S(1)}, u32[]{:S(2)}, u32[]{:S(2)}) collective-permute-start(f32[8,128]{1,0:T(8,128)S(1)} %multiply_subtract_fusion.own_ref), channel_id=1, source_target_pairs={{4,0},{8,4},{12,8},{16,12},{20,16},{24,20},{28,24},{32,28},{36,32}... | collective-permute-start | bytes 12296 | tf_op jit(solution)/shard_map/ppermute | solution.py:441
  328.2 10.3 %collective-permute-start.62 = (f32[8,128]{1,0:T(8,128)S(1)}, f32[8,128]{1,0:T(8,128)S(1)}, u32[]{:S(2)}, u32[]{:S(2)}) collective-permute-start(f32[8,128]{1,0:T(8,128)S(1)} %multiply_subtract_fusion.own_ref), channel_id=1, source_target_pairs={{0,4},{4,8},{8,12},{12,16},{16,20},{20,24},{24,28},{28,32},{32,36}... | collective-permute-start | bytes 12296 | tf_op jit(solution)/shard_map/ppermute | solution.py:441
  340.8 5.6 %collective-permute-start.66 = (f32[8,128]{1,0:T(8,128)}, f32[8,128]{1,0:T(8,128)S(1)}, u32[]{:S(2)}, u32[]{:S(2)}) collective-permute-start(f32[8,128]{1,0:T(8,128)} %get-tuple-element.46), channel_id=1, source_target_pairs={{0,12},{4,8},{8,4},{12,0},{16,28},{20,24},{24,20},{28,16},{32,44},... | collective-permute-start | bytes 12296 | tf_op jit(solution)/shard_map/ppermute | solution.py:501
  340.8 5.6 %collective-permute-start.65 = (f32[8,128]{1,0:T(8,128)}, f32[8,128]{1,0:T(8,128)S(1)}, u32[]{:S(2)}, u32[]{:S(2)}) collective-permute-start(f32[8,128]{1,0:T(8,128)} %get-tuple-element.46), channel_id=1, source_target_pairs={{0,8},{4,12},{8,0},{12,4},{16,24},{20,28},{24,16},{28,20},{32,40},... | collective-permute-start | bytes 12296 | tf_op jit(solution)/shard_map/ppermute | solution.py:501
  340.8 6.2 %collective-permute-start.64 = (f32[8,128]{1,0:T(8,128)}, f32[8,128]{1,0:T(8,128)S(1)}, u32[]{:S(2)}, u32[]{:S(2)}) collective-permute-start(f32[8,128]{1,0:T(8,128)} %get-tuple-element.46), channel_id=1, source_target_pairs={{0,4},{4,0},{8,12},{12,8},{16,20},{20,16},{24,28},{28,24},{32,36},... | collective-permute-start | bytes 12296 | tf_op jit(solution)/shard_map/ppermute | solution.py:501
  347.7 4.8 %collective-permute-start.69 = (f32[8,128]{1,0:T(8,128)S(1)}, f32[8,128]{1,0:T(8,128)S(1)}, u32[]{:S(2)}, u32[]{:S(2)}) collective-permute-start(f32[8,128]{1,0:T(8,128)S(1)} %add_add_fusion.2), channel_id=1, source_target_pairs={{0,48},{4,52},{8,56},{12,60},{16,32},{20,36},{24,40},{28,44},{32,1... | collective-permute-start | bytes 12296 | tf_op jit(solution)/shard_map/ppermute | solution.py:501
  347.7 5.1 %collective-permute-start.68 = (f32[8,128]{1,0:T(8,128)S(1)}, f32[8,128]{1,0:T(8,128)S(1)}, u32[]{:S(2)}, u32[]{:S(2)}) collective-permute-start(f32[8,128]{1,0:T(8,128)S(1)} %add_add_fusion.2), channel_id=1, source_target_pairs={{0,32},{4,36},{8,40},{12,44},{16,48},{20,52},{24,56},{28,60},{32,0... | collective-permute-start | bytes 12296 | tf_op jit(solution)/shard_map/ppermute | solution.py:501
  347.7 5.7 %collective-permute-start.67 = (f32[8,128]{1,0:T(8,128)S(1)}, f32[8,128]{1,0:T(8,128)S(1)}, u32[]{:S(2)}, u32[]{:S(2)}) collective-permute-start(f32[8,128]{1,0:T(8,128)S(1)} %add_add_fusion.2), channel_id=1, source_target_pairs={{0,16},{4,20},{8,24},{12,28},{16,0},{20,4},{24,8},{28,12},{32,48},... | collective-permute-start | bytes 12296 | tf_op jit(solution)/shard_map/ppermute | solution.py:501
  353.4 5.2 %collective-permute-start.71 = (f32[8,128]{1,0:T(8,128)S(1)}, f32[8,128]{1,0:T(8,128)S(1)}, u32[]{:S(2)}, u32[]{:S(2)}) collective-permute-start(f32[8,128]{1,0:T(8,128)S(1)} %add_add_fusion.1), channel_id=1, source_target_pairs={{0,128},{4,132},{8,136},{12,140},{16,144},{20,148},{24,152},{28,15... | collective-permute-start | bytes 12296 | tf_op jit(solution)/shard_map/ppermute | solution.py:501
  354.9 4.2 %collective-permute-start.70 = (f32[8,128]{1,0:T(8,128)S(1)}, f32[8,128]{1,0:T(8,128)S(1)}, u32[]{:S(2)}, u32[]{:S(2)}) collective-permute-start(f32[8,128]{1,0:T(8,128)S(1)} %add_add_fusion.1), channel_id=1, source_target_pairs={{0,64},{4,68},{8,72},{12,76},{16,80},{20,84},{24,88},{28,92},{32,9... | collective-permute-start | bytes 12296 | tf_op jit(solution)/shard_map/ppermute | solution.py:501
  364.0 10.5 %collective-permute-start.74 = (f32[8,128]{1,0:T(8,128)S(1)}, f32[8,128]{1,0:T(8,128)S(1)}, u32[]{:S(2)}, u32[]{:S(2)}) collective-permute-start(f32[8,128]{1,0:T(8,128)S(1)} %multiply_add_fusion.own_ref), channel_id=1, source_target_pairs={{4,0},{8,4},{12,8},{16,12},{20,16},{24,20},{28,24},{32,28},{36,32}... | collective-permute-start | bytes 12296 | tf_op jit(solution)/shard_map/ppermute | solution.py:441
  371.8 10.3 %collective-permute-start.73 = (f32[8,128]{1,0:T(8,128)S(1)}, f32[8,128]{1,0:T(8,128)S(1)}, u32[]{:S(2)}, u32[]{:S(2)}) collective-permute-start(f32[8,128]{1,0:T(8,128)S(1)} %multiply_add_fusion.own_ref), channel_id=1, source_target_pairs={{0,4},{4,8},{8,12},{12,16},{16,20},{20,24},{24,28},{28,32},{32,36}... | collective-permute-start | bytes 12296 | tf_op jit(solution)/shard_map/ppermute | solution.py:441
  (40 other events, 509.5 us)

commit v2 on v1

--- a/solution.py
+++ b/solution.py
@@ -158,7 +158,7 @@
 def main_kernel(
     where_ref, own_ref, rdown_ref, rup_ref, depth_ref, damp_ref, tab_ref, b_ref, bt_ref,
     keep_ref, send_ref, g_ref, base_ref, scale_ref,
-    half_ref, geo_ref, hi_ref, in_ref, q_ref, w_ref, t_ref,
+    half_ref, geo_ref, hi_ref, in_ref, q_ref, w_ref, t_ref, sym_ref,
 ):
     core = where_ref[2]
     plocal = depth_ref.shape[1]
@@ -328,7 +328,24 @@
 
     lax.fori_loop(0, 8, functools.partial(frame, merged=0), 0)
     lax.fori_loop(8, 16, functools.partial(frame, merged=1), 0)
-    t_ref[...] = jnp.dot(bt_ref[...], w_ref[...], precision=HIGHEST, preferred_element_type=F32)
+    t = jnp.dot(bt_ref[...], w_ref[...], precision=HIGHEST, preferred_element_type=F32)
+    spans = ((0, 48, 48), (48, 144, LANES), (144, 192, 2 * LANES))
+    t_ref[...] = jnp.zeros_like(t_ref)
+    for lo, hi, at in spans:
+        t_ref[at : at + hi - lo, :] = t[lo:hi]
+    vector = iota((LANES, LANES), 1) == LANES - 1
+    for a in range(3):
+        for b in range(a, 3):
+            at_a = slice(a * LANES, (a + 1) * LANES)
+            at_b = slice(b * LANES, (b + 1) * LANES)
+            upper = t_ref[at_a, at_b]
+            lower = t_ref[at_b, at_a]
+            mean = 0.5 * (jnp.where(vector, 0.0, upper) + jnp.where(vector, 0.0, lower).T)
+            sym_ref[at_a, at_b] = jnp.where(vector, upper, mean)
+            if a != b:
+                sym_ref[at_b, at_a] = jnp.where(vector, lower, mean.T)
+    for lo, hi, at in spans:
+        t_ref[lo:hi, :] = sym_ref[at : at + hi - lo, :]
     keep_ref[0:48, :] = t_ref[pl.ds(pl.multiple_of(48 + 48 * core, 8), 48), :]
     keep_ref[48:96, :] = t_ref[pl.ds(pl.multiple_of(144 - 144 * core, 8), 48), :]
     send_ref[0:48, :] = t_ref[pl.ds(pl.multiple_of(96 - 48 * core, 8), 48), :]
@@ -366,34 +383,176 @@
     low = core == 0
     s = jnp.concatenate([jnp.where(low, mine, other), jnp.where(low, other, mine)], axis=0)
     r_ref[...] = jnp.zeros((8, LANES), F32)
-    r_ref[0:1, :] = to_row(s[:, LANES - 1 : LANES])
+    r_ref[0:1, :] = to_row(s[:, LANES - 1 : LANES]) * FIRST
     r = iota((GROUP, 3 * LANES), 0)
     l = iota((GROUP, 3 * LANES), 1)
     s = jnp.where(l == LANES - 1, 0.0, s)
     s_ref[...] = s + jnp.where(l == LANES + r, POSE_REG, 0.0)
 
 
-def mv_kernel(s_ref, below_ref, own_ref, above_ref, out_ref, dots_ref):
-    own = own_ref[0:1, :]
-    s = s_ref[...]
-    prod = (
-        s[:, 0:LANES] * below_ref[0:1, :]
-        + s[:, LANES : 2 * LANES] * own
-        + s[:, 2 * LANES :] * above_ref[0:1, :]
-    )
-    y = to_row(jnp.sum(prod, axis=1, keepdims=True))
-    out_ref[...] = jnp.zeros((8, LANES), F32)
-    out_ref[0:1, :] = y
-    rr = jnp.sum(own * own, axis=1, keepdims=True)
-    ry = jnp.sum(own * y, axis=1, keepdims=True)
-    row = iota((8, LANES), 0)
-    dots_ref[...] = jnp.where(row == 0, jnp.broadcast_to(rr, (8, LANES)), jnp.broadcast_to(ry, (8, LANES)))
-
-
-def final_kernel(below_ref, own_ref, above_ref, b_ref, g_ref, base_ref, scale_ref, out_ref, sum_ref):
-    x0 = below_ref[0:1, :]
-    x1 = own_ref[0:1, :]
-    x2 = above_ref[0:1, :]
+SHRINK = 2.0**-15
+FIRST = 2.0**-10
+LARGEST_STEP = 1.001 / (POSE_REG * SHRINK)
+
+
+def halves(x):
+    t = 4097.0 * x
+    top = t - (t - x)
+    return top, x - top
+
+
+def times(a, b):
+    p = a * b
+    ah, al = halves(a)
+    bh, bl = halves(b)
+    return p, ((ah * bh - p) + ah * bl + al * bh) + al * bl
+
+
+def plus(a, b):
+    t = a[0] + b[0]
+    back = t - a[0]
+    return t, (a[1] + b[1]) + ((a[0] - (t - back)) + (b[0] - back))
+
+
+def tidy(a):
+    t = a[0] + a[1]
+    return t, a[1] - (t - a[0])
+
+
+def mul(a, b):
+    p, e = times(a[0], b[0])
+    return tidy((p, e + (a[0] * b[1] + a[1] * b[0])))
+
+
+def add(a, b):
+    return tidy(plus(a, b))
+
+
+def neg(a):
+    return -a[0], -a[1]
+
+
+def div(a, b):
+    q = a[0] / b[0]
+    rest = add(a, neg(mul((q, jnp.zeros_like(q)), b)))
+    return tidy((q, rest[0] / b[0]))
+
+
+def lane_total(a):
+    for step in (64, 32, 16, 8, 4, 2, 1):
+        a = plus(a, (pltpu.roll(a[0], step, 1), pltpu.roll(a[1], step, 1)))
+    return a
+
+
+def next_vector(s_ref, below_ref, own_ref, above_ref):
+    acc = None
+    for g, ref in enumerate((below_ref, own_ref, above_ref)):
+        s = s_ref[:, g * LANES : (g + 1) * LANES]
+        p, e = times(s, jnp.broadcast_to(ref[0:1, :], s.shape))
+        term = p, e + s * ref[1:2, :]
+        acc = term if acc is None else plus(acc, term)
+    acc = lane_total(acc)
+    row = tidy((to_row(acc[0]), to_row(acc[1])))
+    return row[0] * SHRINK, row[1] * SHRINK
+
+
+def put(ref, pair):
+    ref[...] = jnp.zeros((8, LANES), F32)
+    ref[0:1, :] = pair[0]
+    ref[1:2, :] = pair[1]
+
+
+def step_kernel(s_ref, below_ref, own_ref, above_ref, out_ref):
+    put(out_ref, next_vector(s_ref, below_ref, own_ref, above_ref))
+
+
+def moment_kernel(s_ref, below_ref, own_ref, above_ref, *rest):
+    out_ref = rest[-1]
+    rows = [(r[0:1, :], r[1:2, :]) for r in rest[:-1]] + [(own_ref[0:1, :], own_ref[1:2, :])]
+    rows.append(next_vector(s_ref, below_ref, own_ref, above_ref))
+    zero = jnp.zeros((1, LANES), F32)
+
+    def stack(pick, part):
+        lines = [rows[pick(m)][part] for m in range(2 * ITERS)]
+        return jnp.concatenate(lines + [zero] * (16 - len(lines)), axis=0)
+
+    lower, upper = (lambda m: m // 2), (lambda m: m - m // 2)
+    a, b = (stack(lower, 0), stack(lower, 1)), (stack(upper, 0), stack(upper, 1))
+    p, e = times(a[0], b[0])
+    total = tidy(lane_total((p, e + (a[0] * b[1] + a[1] * b[0]))))
+    diagonal = iota((16, LANES), 0) == iota((16, LANES), 1)
+    put(
+        out_ref,
+        [jnp.sum(jnp.where(diagonal, x, 0.0), axis=0, keepdims=True) for x in total],
+    )
+
+
+def gather_sum(refs):
+    acc = refs[0][0:1, :], refs[0][1:2, :]
+    for r in refs[1:]:
+        acc = plus(acc, (r[0:1, :], r[1:2, :]))
+    return tidy(acc)
+
+
+def sum_kernel(a_ref, b_ref, c_ref, d_ref, out_ref):
+    put(out_ref, gather_sum((a_ref, b_ref, c_ref, d_ref)))
+
+
+def solve_kernel(*refs):
+    out_ref = refs[-1]
+    total = gather_sum(refs[:4])
+    vectors = refs[4:-1]
+    m = [(total[0][:, k : k + 1], total[1][:, k : k + 1]) for k in range(2 * ITERS)]
+    one = jnp.ones((1, 1), F32)
+    zero = jnp.zeros((1, 1), F32)
+    none = (zero, zero)
+
+    def where(live, a, b):
+        return jnp.where(live, a[0], b[0]), jnp.where(live, a[1], b[1])
+
+    sigma = list(m)
+    tau = list(m)
+    rc = [(one, zero)] + [none] * ITERS
+    pc = list(rc)
+    xc = [none] * ITERS
+    lead = one
+    live = m[0][0] > 0.0
+    for k in range(ITERS):
+        alpha = div(sigma[k], where(live, tau[k + 1], (one, zero)))
+        live = live & (alpha[0] > 0.0) & (alpha[0] < LARGEST_STEP)
+        alpha = where(live, alpha, none)
+        for i in range(k + 1):
+            xc[i] = add(xc[i], mul(alpha, pc[i]))
+        if k + 1 == ITERS:
+            break
+        back = neg(alpha)
+        fresh = {i: add(sigma[i], mul(back, tau[i + 1])) for i in range(k + 1, 2 * ITERS - k - 1)}
+        for i in range(k + 1, 0, -1):
+            rc[i] = add(rc[i], mul(back, pc[i - 1]))
+        lead = -lead * alpha[0]
+        live = live & (lead * fresh[k + 1][0] > 1e-11 * m[0][0])
+        beta = div(mul(back, fresh[k + 1]), where(live, sigma[k], (one, zero)))
+        beta = where(live, beta, none)
+        for i, x in fresh.items():
+            tau[i] = add(x, mul(beta, tau[i]))
+            sigma[i] = x
+        pc = [add(rc[i], mul(beta, pc[i])) for i in range(k + 2)] + [none] * (ITERS - k - 1)
+    for g in range(3):
+        acc = None
+        for k in range(ITERS):
+            ref = vectors[3 * k + g]
+            wide = tuple(jnp.broadcast_to(x, (1, LANES)) for x in xc[k])
+            term = mul(wide, (ref[0:1, :], ref[1:2, :]))
+            acc = term if acc is None else plus(acc, term)
+        out_ref[g * 8 : g * 8 + 8, :] = jnp.broadcast_to(
+            (acc[0] + acc[1]) * (SHRINK / FIRST), (8, LANES)
+        )
+
+
+def final_kernel(pose_ref, b_ref, g_ref, base_ref, scale_ref, out_ref, sum_ref):
+    x0 = pose_ref[0:1, :]
+    x1 = pose_ref[8:9, :]
+    x2 = pose_ref[16:17, :]
 
     def frame(f, carry):
         rows = pl.ds(pl.multiple_of(f * GROUP, 8), GROUP)
@@ -468,7 +627,8 @@
             pltpu.VMEM((256, plocal), F32),
             pltpu.VMEM((GROUP, LANES), F32),
             pltpu.VMEM((f_dev * GROUP, 3 * LANES), F32),
-            pltpu.VMEM((192, 3 * LANES), F32),
+            pltpu.VMEM((3 * LANES, 3 * LANES), F32),
+            pltpu.VMEM((3 * LANES, 3 * LANES), F32),
         ],
     )
     got = lax.ppermute(send, "pix", [(i, i ^ 1) for i in range(pixes)])
@@ -495,38 +655,29 @@
     def halo(v):
         return shift(v, 1), v, shift(v, -1)
 
-    def total(v):
-        for step in (1, 4, 16):
-            v = v + sum(
-                lax.ppermute(v, "frames", [(i, i ^ (k * step)) for i in range(count)])
-                for k in (1, 2, 3)
-            )
-        return v
-
-    def reduced(v):
-        q, dots = call(mv_kernel, "mv", [(8, LANES), (8, LANES)], 0, s, *halo(v))
-        dots = total(dots)
-        return q, dots[0, 0], dots[1, 0]
-
-    solution = jnp.zeros_like(residual)
-    image, norm_now, product = reduced(residual)
-    alpha = norm_now / product
-    direction, along = residual, image
-    for step in range(ITERS):
-        solution = solution + alpha * direction
-        residual = residual - alpha * along
-        if step + 1 < ITERS:
-            image, norm_next, product = reduced(residual)
-            ratio = norm_next / norm_now
-            alpha = norm_next / (product - ratio * norm_next / alpha)
-            direction = residual + ratio * direction
-            along = image + ratio * along
-            norm_now = norm_next
+    def mates(v, step):
+        return [v] + [
+            lax.ppermute(v, "frames", [(i, i ^ (k * step)) for i in range(count)]) for k in (1, 2, 3)
+        ]
+
+    vectors = []
+    for k in range(ITERS - 1):
+        vectors.append(halo(residual))
+        (residual,) = call(step_kernel, "step", [(8, LANES)], 0, s, *vectors[-1])
+    vectors.append(halo(residual))
+    (part,) = call(
+        moment_kernel, "moments", [(8, LANES)], 0, s, *vectors[-1], *[v[1] for v in vectors[:-1]]
+    )
+    for step in (1, 4):
+        (part,) = call(sum_kernel, "sum", [(8, LANES)], 0, *mates(part, step))
+    (pose,) = call(
+        solve_kernel, "solve", [(24, LANES)], 0, *mates(part, 16), *[x for v in vectors for x in v]
+    )
     (depth_step,) = call(
-        final_kernel, "final", [(f_dev, plocal)], 0, *halo(solution), b, g, base, scale,
+        final_kernel, "final", [(f_dev, plocal)], 0, pose, b, g, base, scale,
         scratch=[pltpu.VMEM((f_dev * 8, plocal), F32)],
     )
-    pose_step = solution[0, : f_dev * 6].reshape(f_dev, 6).T
+    pose_step = pose[8, : f_dev * 6].reshape(f_dev, 6).T
     return pose_step, depth_step
 
 

time: 395 us -> 232 us (0.59)
  starting transfers between devices: 172 us -> 71.4 us
  waiting for transfers between devices: 113 us -> 71.1 us
  between operations: 21.4 us -> 0.99 us
  Pallas kernels: 56 us -> 67.4 us
  other arithmetic: 10 us -> 1.58 us
    ppermute x54 -> x9, starting transfers between devices: 84.2 us -> 12.6 us  [mates(): lax.ppermute(v, 'frames', [(i, i ^ k * step) for i in range(count)])]
    ppermute x16 -> x14, starting transfers between devices: 77.3 us -> 48.6 us  [shift(): lax.ppermute(block, 'frames', [(i, i + step) for i in range(count) if 0 <...]
    ppermute x54 -> x9, waiting for transfers between devices: 31.4 us -> 6.46 us  [mates(): lax.ppermute(v, 'frames', [(i, i ^ k * step) for i in range(count)])]
    ppermute x16 -> x14, waiting for transfers between devices: 70.2 us -> 53.8 us  [shift(): lax.ppermute(block, 'frames', [(i, i + step) for i in range(count) if 0 <...]
    pallas_call x12 -> x15, Pallas kernels: 56 us -> 67.4 us  [call(): pl.pallas_call(kernel, name=name, out_shape=[jax.ShapeDtypeStruct(s, F32)...]
    add x19 -> x0, other arithmetic: 4.91 us -> none  [the longest x18 4.16 us: total(): v + sum((lax.ppermute(v, 'frames', [(i, i ^ k * step) for i in range(coun...]
  transfers between devices with their start and end apart: 75 -> 28, of which waited for: 52 -> 17; matrix products, arithmetic and copies ran while one was open for 0% -> 0% of each run, Pallas kernels for 2% -> 3%
where the time goes in v2:
time: 232 us; the launch traced here: 228 us
  starting transfers between devices  71.4 us (31%)
  waiting for transfers between devices  71.1 us (31%)
  Pallas kernels  67.4 us (29%)
  local copies, waits for them, and re-layouts  15.9 us (7%)
    pallas_call x15, Pallas kernels, call(): pl.pallas_call(kernel, name=name, out_shape=[jax.ShapeDtypeStruct(s, F32)...  67.4 us
    ppermute x14, waiting for transfers between devices, shift(): lax.ppermute(block, 'frames', [(i, i + step) for i in range(count) if 0 <...  53.8 us
    ppermute x14, starting transfers between devices, shift(): lax.ppermute(block, 'frames', [(i, i + step) for i in range(count) if 0 <...  48.6 us
    ppermute x9, starting transfers between devices, mates(): lax.ppermute(v, 'frames', [(i, i ^ k * step) for i in range(count)])  12.6 us
    unnamed x61, local copies, waits for them, and re-layouts  10.9 us
    ppermute x2, starting transfers between devices, to_neighbour(): return lax.ppermute(rim, both_axes, route)  9.25 us
    ppermute x2, waiting for transfers between devices, to_neighbour(): return lax.ppermute(rim, both_axes, route)  7.85 us
    ppermute x9, waiting for transfers between devices, mates(): lax.ppermute(v, 'frames', [(i, i ^ k * step) for i in range(count)])  6.46 us
  transfers between devices with their start and end apart: 28, of which 17 were waited for; matrix products, arithmetic and copies ran while one was open for 0% of the time, Pallas kernels for 3%

profile of v2, /device:TPU:8, one launch (start us, length us, event | category | flops | bytes accessed | tf_op | source)
XLA Modules:
  0.0 228.4 jit_solution(17601860878003024399)
XLA Ops:
  0.6 1.4 copy.13
  2.2 2.0 copy.14
  4.4 1.9 copy.16
  6.4 0.7 pad_add_fusion.where_ref
  7.0 5.5 %scatter.1 = (f32[1024,768]{1,0:T(8,128)}, f32[152,768]{1,0:T(8,128)}, f32[144,768]{1,0:T(8,128)}) custom-call(s32[3]{0:T(128)} %pad_add_fusion.where_ref, s32[2,192]{1,0:T(2,128)} %ef_ref.1, f32[2304,128]{1,0:T(8,128)} %bitcast.14, f32[2304,128]{1,0:T(8,128)} %bitcast.15, s32[192,768]{1,0:T(8,128)} %mask_ref.1), custom_call_target="tpu_custom_call" | custom-call | tf_op jit(solution)/shard_map/scatter/pallas_call | solution.py:580
  12.6 8.6 %collective-permute-start = (f32[152,768]{1,0:T(8,128)}, f32[152,768]{1,0:T(8,128)S(1)}, u32[]{:S(2)}, u32[]{:S(2)}) collective-permute-start(f32[152,768]{1,0:T(8,128)} %get-tuple-element.16), channel_id=1, source_target_pairs={{4,0},{8,4},{12,8},{16,12},{20,16},{24,20},{28,24},{32,28},{36,32}... | collective-permute-start | bytes 1400840 | tf_op jit(solution)/shard_map/ppermute | solution.py:600
  21.2 1.9 collective-permute-start.1
  23.1 6.1 %pose.1 = (f32[256,128]{1,0:T(8,128)}, f32[1536,384]{1,0:T(8,128)}, f32[192,1536]{1,0:T(8,128)}) custom-call(s32[3]{0:T(128)} %pad_add_fusion.where_ref, f32[3,1024]{1,0:T(4,128)} %rotvec_ref.1, f32[3,1024]{1,0:T(4,128)} %trans_ref.1), custom_call_target="tpu_custom_call" | custom-call | tf_op jit(solution)/shard_map/pose/pallas_call | solution.py:580
  29.2 12.3 %collective-permute-done.1.rup_ref = f32[144,768]{1,0:T(8,128)S(1)} collective-permute-done((f32[144,768]{1,0:T(8,128)}, f32[144,768]{1,0:T(8,128)S(1)}, u32[]{:S(2)}, u32[]{:S(2)}) %collective-permute-start.1) | collective-permute-done | bytes 442400 | tf_op jit(solution)/shard_map/ppermute | solution.py:600
  41.6 0.8 copy-done.2
  42.5 25.4 %main.1 = (f32[96,384]{1,0:T(8,128)}, f32[96,384]{1,0:T(8,128)}, f32[1536,768]{1,0:T(8,128)}, f32[128,768]{1,0:T(8,128)}, f32[128,768]{1,0:T(8,128)}) custom-call(s32[3]{0:T(128)} %pad_add_fusion.where_ref, f32[1024,768]{1,0:T(8,128)} %get-tuple-element.15.own_ref, f32[152,768]{1,0:T(8,128)} %copy-done.1, f32[144,768]{1,0:T(8,128)} %copy-done.2, ...), custom_call_target="tpu_custom_call" | custom-call | tf_op jit(solution)/shard_map/main/pallas_call | solution.py:580
  67.9 1.6 collective-permute-done.2
  69.5 0.9 add.8
  70.4 6.7 %collective-permute-start.5 = (f32[48,384]{1,0:T(8,128)S(1)}, f32[48,384]{1,0:T(8,128)S(1)}, u32[]{:S(2)}, u32[]{:S(2)}) collective-permute-start(f32[48,384]{1,0:T(8,128)S(1)} %get-tuple-element.32), channel_id=1, source_target_pairs={{0,6},{2,4},{4,10},{5,3},{6,8},{7,1},{8,14},{9,7},{10,12},{11,5},{... | collective-permute-start | bytes 221192 | tf_op jit(solution)/shard_map/ppermute | solution.py:646
  77.1 2.5 %collective-permute-start.4 = (f32[48,384]{1,0:T(8,128)S(1)}, f32[48,384]{1,0:T(8,128)S(1)}, u32[]{:S(2)}, u32[]{:S(2)}) collective-permute-start(f32[48,384]{1,0:T(8,128)S(1)} %get-tuple-element.32), channel_id=1, source_target_pairs={{0,4},{2,6},{4,8},{5,1},{6,10},{7,3},{8,12},{9,5},{10,14},{11,7},{... | collective-permute-start | bytes 221192 | tf_op jit(solution)/shard_map/ppermute | solution.py:646
  79.7 0.9 collective-permute-start.3
  80.6 0.9 collective-permute-done.5.rim2_ref
  81.5 7.0 %collective-permute-done.4.rim_ref = f32[48,384]{1,0:T(8,128)S(1)} collective-permute-done((f32[48,384]{1,0:T(8,128)S(1)}, f32[48,384]{1,0:T(8,128)S(1)}, u32[]{:S(2)}, u32[]{:S(2)}) %collective-permute-start.4) | collective-permute-done | bytes 73760 | tf_op jit(solution)/shard_map/ppermute | solution.py:646
  88.5 0.6 copy-done.6
  89.1 0.6 copy-done.7
  89.7 1.6 rows.1.mine_ref
  91.3 1.5 collective-permute-done.6.other_ref
  92.8 0.6 copy-done.4
  93.4 1.6 full.1
  95.1 7.1 %collective-permute-start.8 = (f32[8,128]{1,0:T(8,128)}, f32[8,128]{1,0:T(8,128)S(1)}, u32[]{:S(2)}, u32[]{:S(2)}) collective-permute-start(f32[8,128]{1,0:T(8,128)} %get-tuple-element.24.own_ref.rest_0_.refs_5_), channel_id=1, source_target_pairs={{4,0},{8,4},{12,8},{16,12},{20,16},{24,20},{28,24},{32,28},{36,32}... | collective-permute-start | bytes 12296 | tf_op jit(solution)/shard_map/ppermute | solution.py:600
  102.1 1.9 collective-permute-start.7
  104.1 8.6 %collective-permute-done.7.below_ref.refs_4_ = f32[8,128]{1,0:T(8,128)S(1)} collective-permute-done((f32[8,128]{1,0:T(8,128)}, f32[8,128]{1,0:T(8,128)S(1)}, u32[]{:S(2)}, u32[]{:S(2)}) %collective-permute-start.7) | collective-permute-done | bytes 4128 | tf_op jit(solution)/shard_map/ppermute | solution.py:600
  113.2 2.1 step.5.own_ref.rest_1_.refs_8_
  115.4 1.9 collective-permute-start.10
  117.3 3.9 %collective-permute-start.9 = (f32[8,128]{1,0:T(8,128)}, f32[8,128]{1,0:T(8,128)S(1)}, u32[]{:S(2)}, u32[]{:S(2)}) collective-permute-start(f32[8,128]{1,0:T(8,128)} %step.5.own_ref.rest_1_.refs_8_), channel_id=1, source_target_pairs={{0,4},{4,8},{8,12},{12,16},{16,20},{20,24},{24,28},{28,32},{32,36}... | collective-permute-start | bytes 12296 | tf_op jit(solution)/shard_map/ppermute | solution.py:600
  121.2 6.6 %collective-permute-done.9.below_ref.refs_7_ = f32[8,128]{1,0:T(8,128)S(1)} collective-permute-done((f32[8,128]{1,0:T(8,128)}, f32[8,128]{1,0:T(8,128)S(1)}, u32[]{:S(2)}, u32[]{:S(2)}) %collective-permute-start.9) | collective-permute-done | bytes 4128 | tf_op jit(solution)/shard_map/ppermute | solution.py:600
  128.4 2.1 step.6.own_ref.rest_2_.refs_11_
  130.5 1.9 collective-permute-start.12
  132.4 3.9 %collective-permute-start.11 = (f32[8,128]{1,0:T(8,128)}, f32[8,128]{1,0:T(8,128)S(1)}, u32[]{:S(2)}, u32[]{:S(2)}) collective-permute-start(f32[8,128]{1,0:T(8,128)} %step.6.own_ref.rest_2_.refs_11_), channel_id=1, source_target_pairs={{0,4},{4,8},{8,12},{12,16},{16,20},{20,24},{24,28},{28,32},{32,36}... | collective-permute-start | bytes 12296 | tf_op jit(solution)/shard_map/ppermute | solution.py:600
  136.4 6.6 %collective-permute-done.11.below_ref.refs_10_ = f32[8,128]{1,0:T(8,128)S(1)} collective-permute-done((f32[8,128]{1,0:T(8,128)}, f32[8,128]{1,0:T(8,128)S(1)}, u32[]{:S(2)}, u32[]{:S(2)}) %collective-permute-start.11) | collective-permute-done | bytes 4128 | tf_op jit(solution)/shard_map/ppermute | solution.py:600
  142.9 0.6 copy-done.13
  143.5 2.1 step.7.own_ref.rest_3_.refs_14_
  145.6 1.9 collective-permute-start.14
  147.5 3.9 %collective-permute-start.13 = (f32[8,128]{1,0:T(8,128)}, f32[8,128]{1,0:T(8,128)S(1)}, u32[]{:S(2)}, u32[]{:S(2)}) collective-permute-start(f32[8,128]{1,0:T(8,128)} %step.7.own_ref.rest_3_.refs_14_), channel_id=1, source_target_pairs={{0,4},{4,8},{8,12},{12,16},{16,20},{20,24},{24,28},{28,32},{32,36}... | collective-permute-start | bytes 12296 | tf_op jit(solution)/shard_map/ppermute | solution.py:600
  151.5 6.6 %collective-permute-done.13.below_ref.refs_13_ = f32[8,128]{1,0:T(8,128)S(1)} collective-permute-done((f32[8,128]{1,0:T(8,128)}, f32[8,128]{1,0:T(8,128)S(1)}, u32[]{:S(2)}, u32[]{:S(2)}) %collective-permute-start.13) | collective-permute-done | bytes 4128 | tf_op jit(solution)/shard_map/ppermute | solution.py:600
  158.7 2.1 step.8.own_ref.rest_4_.refs_17_
  160.8 1.9 collective-permute-start.16
  162.7 3.9 %collective-permute-start.15 = (f32[8,128]{1,0:T(8,128)}, f32[8,128]{1,0:T(8,128)S(1)}, u32[]{:S(2)}, u32[]{:S(2)}) collective-permute-start(f32[8,128]{1,0:T(8,128)} %step.8.own_ref.rest_4_.refs_17_), channel_id=1, source_target_pairs={{0,4},{4,8},{8,12},{12,16},{16,20},{20,24},{24,28},{28,32},{32,36}... | collective-permute-start | bytes 12296 | tf_op jit(solution)/shard_map/ppermute | solution.py:600
  166.6 6.6 %collective-permute-done.15.below_ref.refs_16_ = f32[8,128]{1,0:T(8,128)S(1)} collective-permute-done((f32[8,128]{1,0:T(8,128)}, f32[8,128]{1,0:T(8,128)S(1)}, u32[]{:S(2)}, u32[]{:S(2)}) %collective-permute-start.15) | collective-permute-done | bytes 4128 | tf_op jit(solution)/shard_map/ppermute | solution.py:600
  173.8 2.1 step.9.own_ref.refs_20_
  175.9 1.9 collective-permute-start.18
  177.8 3.9 %collective-permute-start.17 = (f32[8,128]{1,0:T(8,128)}, f32[8,128]{1,0:T(8,128)S(1)}, u32[]{:S(2)}, u32[]{:S(2)}) collective-permute-start(f32[8,128]{1,0:T(8,128)} %step.9.own_ref.refs_20_), channel_id=1, source_target_pairs={{0,4},{4,8},{8,12},{12,16},{16,20},{20,24},{24,28},{28,32},{32,36}... | collective-permute-start | bytes 12296 | tf_op jit(solution)/shard_map/ppermute | solution.py:600
  181.8 6.6 %collective-permute-done.17.below_ref.refs_19_ = f32[8,128]{1,0:T(8,128)S(1)} collective-permute-done((f32[8,128]{1,0:T(8,128)}, f32[8,128]{1,0:T(8,128)S(1)}, u32[]{:S(2)}, u32[]{:S(2)}) %collective-permute-start.17) | collective-permute-done | bytes 4128 | tf_op jit(solution)/shard_map/ppermute | solution.py:600
  188.9 2.6 %moments.1.a_ref = f32[8,128]{1,0:T(8,128)} custom-call(f32[96,384]{1,0:T(8,128)} %get-tuple-element.23.s_ref, f32[8,128]{1,0:T(8,128)} %copy-done.19, f32[8,128]{1,0:T(8,128)} %step.9.own_ref.refs_20_, f32[8,128]{1,0:T(8,128)} %copy-done.18, f32[8,128]{1,0:T(8,128)} %get-tuple-element.24.own_ref.rest_0_.refs_5_, f32[8,128]{1,0:T(8,128)} %step.5.own_ref.rest_1_.refs_8_, ...), custom_call_target="tpu_custom_call" | custom-call | tf_op jit(solution)/shard_map/moments/pallas_call | solution.py:580
  191.6 4.4 %collective-permute-start.19 = (f32[8,128]{1,0:T(8,128)}, f32[8,128]{1,0:T(8,128)S(1)}, u32[]{:S(2)}, u32[]{:S(2)}) collective-permute-start(f32[8,128]{1,0:T(8,128)} %moments.1.a_ref), channel_id=1, source_target_pairs={{0,4},{4,0},{8,12},{12,8},{16,20},{20,16},{24,28},{28,24},{32,36},... | collective-permute-start | bytes 12296 | tf_op jit(solution)/shard_map/ppermute | solution.py:660
  196.0 1.2 collective-permute-done.21.d_ref
  198.4 1.3 sum.2.a_ref
  199.7 4.1 %collective-permute-start.22 = (f32[8,128]{1,0:T(8,128)}, f32[8,128]{1,0:T(8,128)S(1)}, u32[]{:S(2)}, u32[]{:S(2)}) collective-permute-start(f32[8,128]{1,0:T(8,128)} %sum.2.a_ref), channel_id=1, source_target_pairs={{0,16},{4,20},{8,24},{12,28},{16,0},{20,4},{24,8},{28,12},{32,48},... | collective-permute-start | bytes 12296 | tf_op jit(solution)/shard_map/ppermute | solution.py:660
  203.8 0.9 collective-permute-done.24.d_ref
  205.0 0.6 collective-permute-done.22.b_ref
  206.2 1.3 sum.3.refs_0_
  207.5 1.6 collective-permute-start.27
  209.1 1.0 collective-permute-start.26
  210.1 1.5 collective-permute-start.25
  211.6 2.8 %collective-permute-done.26.refs_2_ = f32[8,128]{1,0:T(8,128)S(1)} collective-permute-done((f32[8,128]{1,0:T(8,128)}, f32[8,128]{1,0:T(8,128)S(1)}, u32[]{:S(2)}, u32[]{:S(2)}) %collective-permute-start.26) | collective-permute-done | bytes 4128 | tf_op jit(solution)/shard_map/ppermute | solution.py:660
  215.6 5.7 %solve.1.pose_ref = f32[24,128]{1,0:T(8,128)} custom-call(f32[8,128]{1,0:T(8,128)} %sum.3.refs_0_, f32[8,128]{1,0:T(8,128)} %copy-done.22, f32[8,128]{1,0:T(8,128)} %copy-done.21, f32[8,128]{1,0:T(8,128)} %copy-done.20, f32[8,128]{1,0:T(8,128)} %copy-done.9, f32[8,128]{1,0:T(8,128)} %get-tuple-element.24.own_ref.rest_0_.refs_5_, f32[8,128]{1,0:T(8,128)} %copy-done.8, ...), custom_call_target="tpu_custom_call" | custom-call | tf_op jit(solution)/shard_map/solve/pallas_call | solution.py:580
  221.4 0.7 slice_reduce_fusion
  222.1 0.7 copy.17
  222.8 5.6 %final.1 = f32[16,768]{1,0:T(8,128)} custom-call(f32[24,128]{1,0:T(8,128)} %solve.1.pose_ref, f32[1536,384]{1,0:T(8,128)} %get-tuple-element.19.b_ref, f32[1536,768]{1,0:T(8,128)} %get-tuple-element.25.g_ref, f32[128,768]{1,0:T(8,128)} %get-tuple-element.26.base_ref, f32[128,768]{1,0:T(8,128)} %get-tuple-element.27.scale_ref), custom_call_target="tpu_custom_call" | custom-call | tf_op jit(solution)/shard_map/final/pallas_call | solution.py:580
  (77 shorter events, 7.0 us)
Async XLA Ops:
  2.2 2.0 copy-start
  12.6 29.0 %collective-permute-start = (f32[152,768]{1,0:T(8,128)}, f32[152,768]{1,0:T(8,128)S(1)}, u32[]{:S(2)}, u32[]{:S(2)}) collective-permute-start(f32[152,768]{1,0:T(8,128)} %get-tuple-element.16), channel_id=1, source_target_pairs={{4,0},{8,4},{12,8},{16,12},{20,16},{24,20},{28,24},{32,28},{36,32}... | collective-permute-start | bytes 1400840 | tf_op jit(solution)/shard_map/ppermute | solution.py:600
  21.2 20.4 %collective-permute-start.1 = (f32[144,768]{1,0:T(8,128)}, f32[144,768]{1,0:T(8,128)S(1)}, u32[]{:S(2)}, u32[]{:S(2)}) collective-permute-start(f32[144,768]{1,0:T(8,128)} %get-tuple-element.17), channel_id=1, source_target_pairs={{0,4},{4,8},{8,12},{12,16},{16,20},{20,24},{24,28},{28,32},{32,36}... | collective-permute-start | bytes 1327112 | tf_op jit(solution)/shard_map/ppermute | solution.py:600
  41.5 0.8 copy-start.2
  41.5 1.0 copy-start.1
  67.9 1.6 collective-permute-start.2
  70.4 18.1 %copy-start.3 = (f32[48,384]{1,0:T(8,128)}, f32[48,384]{1,0:T(8,128)S(1)}, u32[]{:S(2)}) copy-start(f32[48,384]{1,0:T(8,128)S(1)} %get-tuple-element.33.own_ref) | copy-start | bytes 221188
  70.4 11.1 %collective-permute-start.5 = (f32[48,384]{1,0:T(8,128)S(1)}, f32[48,384]{1,0:T(8,128)S(1)}, u32[]{:S(2)}, u32[]{:S(2)}) collective-permute-start(f32[48,384]{1,0:T(8,128)S(1)} %get-tuple-element.32), channel_id=1, source_target_pairs={{0,6},{2,4},{4,10},{5,3},{6,8},{7,1},{8,14},{9,7},{10,12},{11,5},{... | collective-permute-start | bytes 221192 | tf_op jit(solution)/shard_map/ppermute | solution.py:646
  77.1 11.3 %collective-permute-start.4 = (f32[48,384]{1,0:T(8,128)S(1)}, f32[48,384]{1,0:T(8,128)S(1)}, u32[]{:S(2)}, u32[]{:S(2)}) collective-permute-start(f32[48,384]{1,0:T(8,128)S(1)} %get-tuple-element.32), channel_id=1, source_target_pairs={{0,4},{2,6},{4,8},{5,1},{6,10},{7,3},{8,12},{9,5},{10,14},{11,7},{... | collective-permute-start | bytes 221192 | tf_op jit(solution)/shard_map/ppermute | solution.py:646
  79.7 8.8 %collective-permute-start.3 = (f32[48,384]{1,0:T(8,128)S(1)}, f32[48,384]{1,0:T(8,128)S(1)}, u32[]{:S(2)}, u32[]{:S(2)}) collective-permute-start(f32[48,384]{1,0:T(8,128)S(1)} %get-tuple-element.33.own_ref), channel_id=1, source_target_pairs={{0,2},{1,3},{2,0},{3,1},{4,6},{5,7},{6,4},{7,5},{8,10},{9,11},{10,... | collective-permute-start | bytes 221192 | tf_op jit(solution)/shard_map/ppermute | solution.py:648
  81.5 7.0 %copy-start.5 = (f32[48,384]{1,0:T(8,128)}, f32[48,384]{1,0:T(8,128)S(1)}, u32[]{:S(2)}) copy-start(f32[48,384]{1,0:T(8,128)S(1)} %collective-permute-done.5.rim2_ref) | copy-start | bytes 221188
  88.5 0.6 copy-start.6
  89.1 0.6 copy-start.7
  91.3 1.5 collective-permute-start.6
  92.8 0.6 copy-start.4
  95.1 9.0 %collective-permute-start.8 = (f32[8,128]{1,0:T(8,128)}, f32[8,128]{1,0:T(8,128)S(1)}, u32[]{:S(2)}, u32[]{:S(2)}) collective-permute-start(f32[8,128]{1,0:T(8,128)} %get-tuple-element.24.own_ref.rest_0_.refs_5_), channel_id=1, source_target_pairs={{4,0},{8,4},{12,8},{16,12},{20,16},{24,20},{28,24},{32,28},{36,32}... | collective-permute-start | bytes 12296 | tf_op jit(solution)/shard_map/ppermute | solution.py:600
  102.1 10.5 %collective-permute-start.7 = (f32[8,128]{1,0:T(8,128)}, f32[8,128]{1,0:T(8,128)S(1)}, u32[]{:S(2)}, u32[]{:S(2)}) collective-permute-start(f32[8,128]{1,0:T(8,128)} %get-tuple-element.24.own_ref.rest_0_.refs_5_), channel_id=1, source_target_pairs={{0,4},{4,8},{8,12},{12,16},{16,20},{20,24},{24,28},{28,32},{32,36}... | collective-permute-start | bytes 12296 | tf_op jit(solution)/shard_map/ppermute | solution.py:600
  104.1 8.6 %copy-start.8 = (f32[8,128]{1,0:T(8,128)}, f32[8,128]{1,0:T(8,128)S(1)}, u32[]{:S(2)}) copy-start(f32[8,128]{1,0:T(8,128)S(1)} %collective-permute-done.8.above_ref.refs_6_) | copy-start | bytes 12292
  112.6 0.6 copy-start.9
  115.4 5.8 %collective-permute-start.10 = (f32[8,128]{1,0:T(8,128)}, f32[8,128]{1,0:T(8,128)S(1)}, u32[]{:S(2)}, u32[]{:S(2)}) collective-permute-start(f32[8,128]{1,0:T(8,128)} %step.5.own_ref.rest_1_.refs_8_), channel_id=1, source_target_pairs={{4,0},{8,4},{12,8},{16,12},{20,16},{24,20},{28,24},{32,28},{36,32}... | collective-permute-start | bytes 12296 | tf_op jit(solution)/shard_map/ppermute | solution.py:600
  117.3 10.5 %collective-permute-start.9 = (f32[8,128]{1,0:T(8,128)}, f32[8,128]{1,0:T(8,128)S(1)}, u32[]{:S(2)}, u32[]{:S(2)}) collective-permute-start(f32[8,128]{1,0:T(8,128)} %step.5.own_ref.rest_1_.refs_8_), channel_id=1, source_target_pairs={{0,4},{4,8},{8,12},{12,16},{16,20},{20,24},{24,28},{28,32},{32,36}... | collective-permute-start | bytes 12296 | tf_op jit(solution)/shard_map/ppermute | solution.py:600
  121.2 6.6 %copy-start.10 = (f32[8,128]{1,0:T(8,128)}, f32[8,128]{1,0:T(8,128)S(1)}, u32[]{:S(2)}) copy-start(f32[8,128]{1,0:T(8,128)S(1)} %collective-permute-done.10.above_ref.refs_9_) | copy-start | bytes 12292
  127.8 0.6 copy-start.11
  130.5 5.8 %collective-permute-start.12 = (f32[8,128]{1,0:T(8,128)}, f32[8,128]{1,0:T(8,128)S(1)}, u32[]{:S(2)}, u32[]{:S(2)}) collective-permute-start(f32[8,128]{1,0:T(8,128)} %step.6.own_ref.rest_2_.refs_11_), channel_id=1, source_target_pairs={{4,0},{8,4},{12,8},{16,12},{20,16},{24,20},{28,24},{32,28},{36,32}... | collective-permute-start | bytes 12296 | tf_op jit(solution)/shard_map/ppermute | solution.py:600
  132.4 10.5 %collective-permute-start.11 = (f32[8,128]{1,0:T(8,128)}, f32[8,128]{1,0:T(8,128)S(1)}, u32[]{:S(2)}, u32[]{:S(2)}) collective-permute-start(f32[8,128]{1,0:T(8,128)} %step.6.own_ref.rest_2_.refs_11_), channel_id=1, source_target_pairs={{0,4},{4,8},{8,12},{12,16},{16,20},{20,24},{24,28},{28,32},{32,36}... | collective-permute-start | bytes 12296 | tf_op jit(solution)/shard_map/ppermute | solution.py:600
  136.3 6.6 %copy-start.12 = (f32[8,128]{1,0:T(8,128)}, f32[8,128]{1,0:T(8,128)S(1)}, u32[]{:S(2)}) copy-start(f32[8,128]{1,0:T(8,128)S(1)} %collective-permute-done.12.above_ref.refs_12_) | copy-start | bytes 12292
  142.9 0.6 copy-start.13
  145.6 5.8 %collective-permute-start.14 = (f32[8,128]{1,0:T(8,128)}, f32[8,128]{1,0:T(8,128)S(1)}, u32[]{:S(2)}, u32[]{:S(2)}) collective-permute-start(f32[8,128]{1,0:T(8,128)} %step.7.own_ref.rest_3_.refs_14_), channel_id=1, source_target_pairs={{4,0},{8,4},{12,8},{16,12},{20,16},{24,20},{28,24},{32,28},{36,32}... | collective-permute-start | bytes 12296 | tf_op jit(solution)/shard_map/ppermute | solution.py:600
  147.5 10.5 %collective-permute-start.13 = (f32[8,128]{1,0:T(8,128)}, f32[8,128]{1,0:T(8,128)S(1)}, u32[]{:S(2)}, u32[]{:S(2)}) collective-permute-start(f32[8,128]{1,0:T(8,128)} %step.7.own_ref.rest_3_.refs_14_), channel_id=1, source_target_pairs={{0,4},{4,8},{8,12},{12,16},{16,20},{20,24},{24,28},{28,32},{32,36}... | collective-permute-start | bytes 12296 | tf_op jit(solution)/shard_map/ppermute | solution.py:600
  151.5 6.6 %copy-start.14 = (f32[8,128]{1,0:T(8,128)}, f32[8,128]{1,0:T(8,128)S(1)}, u32[]{:S(2)}) copy-start(f32[8,128]{1,0:T(8,128)S(1)} %collective-permute-done.14.above_ref.refs_15_) | copy-start | bytes 12292
  158.1 0.6 copy-start.15
  160.8 5.8 %collective-permute-start.16 = (f32[8,128]{1,0:T(8,128)}, f32[8,128]{1,0:T(8,128)S(1)}, u32[]{:S(2)}, u32[]{:S(2)}) collective-permute-start(f32[8,128]{1,0:T(8,128)} %step.8.own_ref.rest_4_.refs_17_), channel_id=1, source_target_pairs={{4,0},{8,4},{12,8},{16,12},{20,16},{24,20},{28,24},{32,28},{36,32}... | collective-permute-start | bytes 12296 | tf_op jit(solution)/shard_map/ppermute | solution.py:600
  162.7 10.5 %collective-permute-start.15 = (f32[8,128]{1,0:T(8,128)}, f32[8,128]{1,0:T(8,128)S(1)}, u32[]{:S(2)}, u32[]{:S(2)}) collective-permute-start(f32[8,128]{1,0:T(8,128)} %step.8.own_ref.rest_4_.refs_17_), channel_id=1, source_target_pairs={{0,4},{4,8},{8,12},{12,16},{16,20},{20,24},{24,28},{28,32},{32,36}... | collective-permute-start | bytes 12296 | tf_op jit(solution)/shard_map/ppermute | solution.py:600
  166.6 6.6 %copy-start.16 = (f32[8,128]{1,0:T(8,128)}, f32[8,128]{1,0:T(8,128)S(1)}, u32[]{:S(2)}) copy-start(f32[8,128]{1,0:T(8,128)S(1)} %collective-permute-done.16.above_ref.refs_18_) | copy-start | bytes 12292
  173.2 0.6 copy-start.17
  175.9 5.8 %collective-permute-start.18 = (f32[8,128]{1,0:T(8,128)}, f32[8,128]{1,0:T(8,128)S(1)}, u32[]{:S(2)}, u32[]{:S(2)}) collective-permute-start(f32[8,128]{1,0:T(8,128)} %step.9.own_ref.refs_20_), channel_id=1, source_target_pairs={{4,0},{8,4},{12,8},{16,12},{20,16},{24,20},{28,24},{32,28},{36,32}... | collective-permute-start | bytes 12296 | tf_op jit(solution)/shard_map/ppermute | solution.py:600
  177.8 10.5 %collective-permute-start.17 = (f32[8,128]{1,0:T(8,128)}, f32[8,128]{1,0:T(8,128)S(1)}, u32[]{:S(2)}, u32[]{:S(2)}) collective-permute-start(f32[8,128]{1,0:T(8,128)} %step.9.own_ref.refs_20_), channel_id=1, source_target_pairs={{0,4},{4,8},{8,12},{12,16},{16,20},{20,24},{24,28},{28,32},{32,36}... | collective-permute-start | bytes 12296 | tf_op jit(solution)/shard_map/ppermute | solution.py:600
  181.8 6.6 %copy-start.18 = (f32[8,128]{1,0:T(8,128)}, f32[8,128]{1,0:T(8,128)S(1)}, u32[]{:S(2)}) copy-start(f32[8,128]{1,0:T(8,128)S(1)} %collective-permute-done.18.above_ref.refs_21_) | copy-start | bytes 12292
  188.3 0.6 copy-start.19
  191.6 5.6 %collective-permute-start.21 = (f32[8,128]{1,0:T(8,128)}, f32[8,128]{1,0:T(8,128)S(1)}, u32[]{:S(2)}, u32[]{:S(2)}) collective-permute-start(f32[8,128]{1,0:T(8,128)} %moments.1.a_ref), channel_id=1, source_target_pairs={{0,12},{4,8},{8,4},{12,0},{16,28},{20,24},{24,20},{28,16},{32,44},... | collective-permute-start | bytes 12296 | tf_op jit(solution)/shard_map/ppermute | solution.py:660
  191.6 5.6 %collective-permute-start.20 = (f32[8,128]{1,0:T(8,128)}, f32[8,128]{1,0:T(8,128)S(1)}, u32[]{:S(2)}, u32[]{:S(2)}) collective-permute-start(f32[8,128]{1,0:T(8,128)} %moments.1.a_ref), channel_id=1, source_target_pairs={{0,8},{4,12},{8,0},{12,4},{16,24},{20,28},{24,16},{28,20},{32,40},... | collective-permute-start | bytes 12296 | tf_op jit(solution)/shard_map/ppermute | solution.py:660
  191.6 6.2 %collective-permute-start.19 = (f32[8,128]{1,0:T(8,128)}, f32[8,128]{1,0:T(8,128)S(1)}, u32[]{:S(2)}, u32[]{:S(2)}) collective-permute-start(f32[8,128]{1,0:T(8,128)} %moments.1.a_ref), channel_id=1, source_target_pairs={{0,4},{4,0},{8,12},{12,8},{16,20},{20,16},{24,28},{28,24},{32,36},... | collective-permute-start | bytes 12296 | tf_op jit(solution)/shard_map/ppermute | solution.py:660
  197.2 0.6 copy-start.23
  197.2 0.6 copy-start.25
  197.8 0.6 copy-start.27
  199.7 5.0 %collective-permute-start.24 = (f32[8,128]{1,0:T(8,128)}, f32[8,128]{1,0:T(8,128)S(1)}, u32[]{:S(2)}, u32[]{:S(2)}) collective-permute-start(f32[8,128]{1,0:T(8,128)} %sum.2.a_ref), channel_id=1, source_target_pairs={{0,48},{4,52},{8,56},{12,60},{16,32},{20,36},{24,40},{28,44},{32,1... | collective-permute-start | bytes 12296 | tf_op jit(solution)/shard_map/ppermute | solution.py:660
  199.7 5.3 %collective-permute-start.23 = (f32[8,128]{1,0:T(8,128)}, f32[8,128]{1,0:T(8,128)S(1)}, u32[]{:S(2)}, u32[]{:S(2)}) collective-permute-start(f32[8,128]{1,0:T(8,128)} %sum.2.a_ref), channel_id=1, source_target_pairs={{0,32},{4,36},{8,40},{12,44},{16,48},{20,52},{24,56},{28,60},{32,0... | collective-permute-start | bytes 12296 | tf_op jit(solution)/shard_map/ppermute | solution.py:660
  199.7 5.9 %collective-permute-start.22 = (f32[8,128]{1,0:T(8,128)}, f32[8,128]{1,0:T(8,128)S(1)}, u32[]{:S(2)}, u32[]{:S(2)}) collective-permute-start(f32[8,128]{1,0:T(8,128)} %sum.2.a_ref), channel_id=1, source_target_pairs={{0,16},{4,20},{8,24},{12,28},{16,0},{20,4},{24,8},{28,12},{32,48},... | collective-permute-start | bytes 12296 | tf_op jit(solution)/shard_map/ppermute | solution.py:660
  204.7 0.9 copy-start.24
  205.0 0.6 copy-start.26
  205.6 0.6 copy-start.28
  207.5 4.1 %collective-permute-start.27 = (f32[8,128]{1,0:T(8,128)}, f32[8,128]{1,0:T(8,128)S(1)}, u32[]{:S(2)}, u32[]{:S(2)}) collective-permute-start(f32[8,128]{1,0:T(8,128)} %sum.3.refs_0_), channel_id=1, source_target_pairs={{0,192},{4,196},{8,200},{12,204},{16,208},{20,212},{24,216},{28,22... | collective-permute-start | bytes 12296 | tf_op jit(solution)/shard_map/ppermute | solution.py:660
  209.1 5.3 %collective-permute-start.26 = (f32[8,128]{1,0:T(8,128)}, f32[8,128]{1,0:T(8,128)S(1)}, u32[]{:S(2)}, u32[]{:S(2)}) collective-permute-start(f32[8,128]{1,0:T(8,128)} %sum.3.refs_0_), channel_id=1, source_target_pairs={{0,128},{4,132},{8,136},{12,140},{16,144},{20,148},{24,152},{28,15... | collective-permute-start | bytes 12296 | tf_op jit(solution)/shard_map/ppermute | solution.py:660
  210.1 4.3 %collective-permute-start.25 = (f32[8,128]{1,0:T(8,128)}, f32[8,128]{1,0:T(8,128)S(1)}, u32[]{:S(2)}, u32[]{:S(2)}) collective-permute-start(f32[8,128]{1,0:T(8,128)} %sum.3.refs_0_), channel_id=1, source_target_pairs={{0,64},{4,68},{8,72},{12,76},{16,80},{20,84},{24,88},{28,92},{32,9... | collective-permute-start | bytes 12296 | tf_op jit(solution)/shard_map/ppermute | solution.py:660
  211.6 2.8 %copy-start.20 = (f32[8,128]{1,0:T(8,128)}, f32[8,128]{1,0:T(8,128)S(1)}, u32[]{:S(2)}) copy-start(f32[8,128]{1,0:T(8,128)S(1)} %collective-permute-done.27.refs_3_) | copy-start | bytes 12292
  214.4 0.6 copy-start.21
  215.0 0.6 copy-start.22

commit v3 on v2

--- a/solution.py
+++ b/solution.py
@@ -158,7 +158,7 @@
 def main_kernel(
     where_ref, own_ref, rdown_ref, rup_ref, depth_ref, damp_ref, tab_ref, b_ref, bt_ref,
     keep_ref, send_ref, g_ref, base_ref, scale_ref,
-    half_ref, geo_ref, hi_ref, in_ref, q_ref, w_ref, t_ref, sym_ref,
+    half_ref, geo_ref, hi_ref, in_ref, q_ref, w_ref, t_ref,
 ):
     core = where_ref[2]
     plocal = depth_ref.shape[1]
@@ -329,43 +329,41 @@
     lax.fori_loop(0, 8, functools.partial(frame, merged=0), 0)
     lax.fori_loop(8, 16, functools.partial(frame, merged=1), 0)
     t = jnp.dot(bt_ref[...], w_ref[...], precision=HIGHEST, preferred_element_type=F32)
-    spans = ((0, 48, 48), (48, 144, LANES), (144, 192, 2 * LANES))
-    t_ref[...] = jnp.zeros_like(t_ref)
-    for lo, hi, at in spans:
-        t_ref[at : at + hi - lo, :] = t[lo:hi]
-    vector = iota((LANES, LANES), 1) == LANES - 1
-    for a in range(3):
-        for b in range(a, 3):
-            at_a = slice(a * LANES, (a + 1) * LANES)
-            at_b = slice(b * LANES, (b + 1) * LANES)
-            upper = t_ref[at_a, at_b]
-            lower = t_ref[at_b, at_a]
-            mean = 0.5 * (jnp.where(vector, 0.0, upper) + jnp.where(vector, 0.0, lower).T)
-            sym_ref[at_a, at_b] = jnp.where(vector, upper, mean)
-            if a != b:
-                sym_ref[at_b, at_a] = jnp.where(vector, lower, mean.T)
-    for lo, hi, at in spans:
-        t_ref[lo:hi, :] = sym_ref[at : at + hi - lo, :]
-    keep_ref[0:48, :] = t_ref[pl.ds(pl.multiple_of(48 + 48 * core, 8), 48), :]
-    keep_ref[48:96, :] = t_ref[pl.ds(pl.multiple_of(144 - 144 * core, 8), 48), :]
-    send_ref[0:48, :] = t_ref[pl.ds(pl.multiple_of(96 - 48 * core, 8), 48), :]
-    send_ref[48:96, :] = t_ref[pl.ds(pl.multiple_of(144 * core, 8), 48), :]
-
-
-def rows_kernel(where_ref, own_ref, own2_ref, rim_ref, rim2_ref, out_ref):
-    core = where_ref[2]
-    own = own_ref[...] + own2_ref[...]
-    rim = rim_ref[...] + rim2_ref[...]
-    lane = iota((48, LANES), 1)
-    below = rim[:, 0:LANES]
-    mid = rim[:, LANES : 2 * LANES]
-    above = rim[:, 2 * LANES :]
-    vec = jnp.where(lane == LANES - 1, below, 0.0)
-    below = jnp.where(lane == LANES - 1, 0.0, below)
-    low = core == 0
-    out_ref[:, 0:LANES] = own[:, 0:LANES] + vec + jnp.where(low, mid, 0.0)
-    out_ref[:, LANES : 2 * LANES] = own[:, LANES : 2 * LANES] + jnp.where(low, above, below)
-    out_ref[:, 2 * LANES :] = own[:, 2 * LANES :] + jnp.where(low, 0.0, mid)
+    t_ref[...] = t
+    for lo, hi, group, first in ((0, 48, 0, 48), (48, 144, 1, 0), (144, 192, 2, 0)):
+        count = hi - lo
+        lanes = slice(group * LANES, (group + 1) * LANES)
+        square = jnp.concatenate(
+            [jnp.zeros((first, LANES), F32)] * (first > 0)
+            + [t[lo:hi, lanes], jnp.zeros((LANES - first - count, LANES), F32)],
+            axis=0,
+        )
+        mean = 0.5 * (square + square.T)
+        t_ref[lo:hi, lanes] = mean[first : first + count]
+    last = iota((48, LANES), 1) == LANES - 1
+
+    def half(core):
+        own = slice(48 + 48 * core, 96 + 48 * core)
+        rim = slice(0, 48) if core else slice(144, 192)
+        group = 0 if core else 2
+        mine = jnp.where(last, t[own, 0:LANES], t_ref[own, LANES : 2 * LANES])
+        theirs = jnp.where(last, t[rim, 0:LANES], t_ref[rim, group * LANES : (group + 1) * LANES])
+        far = t_ref[rim, LANES : 2 * LANES] if core else jnp.zeros((48, LANES), F32)
+        return mine, t_ref[own, 2 * LANES :], theirs, far
+
+    def put_half(ref, core):
+        for k, x in enumerate(half(core)):
+            ref[(k // 2) * 48 : (k // 2 + 1) * 48, (k % 2) * LANES : (k % 2 + 1) * LANES] = x
+
+    @pl.when(core == 0)
+    def _():
+        put_half(keep_ref, 0)
+        put_half(send_ref, 1)
+
+    @pl.when(core == 1)
+    def _():
+        put_half(keep_ref, 1)
+        put_half(send_ref, 0)
 
 
 def to_row(column):
@@ -376,18 +374,17 @@
     )
 
 
-def full_kernel(where_ref, mine_ref, other_ref, s_ref, r_ref):
-    core = where_ref[2]
-    mine = mine_ref[...]
-    other = other_ref[...]
-    low = core == 0
-    s = jnp.concatenate([jnp.where(low, mine, other), jnp.where(low, other, mine)], axis=0)
-    r_ref[...] = jnp.zeros((8, LANES), F32)
-    r_ref[0:1, :] = to_row(s[:, LANES - 1 : LANES]) * FIRST
-    r = iota((GROUP, 3 * LANES), 0)
-    l = iota((GROUP, 3 * LANES), 1)
-    s = jnp.where(l == LANES - 1, 0.0, s)
-    s_ref[...] = s + jnp.where(l == LANES + r, POSE_REG, 0.0)
+BLOCKS = 12
+
+
+def quad_kernel(where_ref, own_ref, own2_ref, rim_ref, rim2_ref, out_ref):
+    out_ref[...] = (own_ref[...] + own2_ref[...]) + (rim_ref[...] + rim2_ref[...])
+
+
+def place_kernel(where_ref, a_ref, b_ref, c_ref, d_ref, out_ref):
+    at = where_ref[3]
+    for k, ref in enumerate((a_ref, b_ref, c_ref, d_ref)):
+        out_ref[pl.ds(pl.multiple_of(48 * (at ^ k), 8), 48), :] = ref[...]
 
 
 SHRINK = 2.0**-15
@@ -444,47 +441,143 @@
     return a
 
 
-def next_vector(s_ref, below_ref, own_ref, above_ref):
+def to_column(row):
+    eye = iota((GROUP, LANES), 0) == iota((GROUP, LANES), 1)
+    return jnp.broadcast_to(
+        jnp.sum(jnp.where(eye, row, 0.0), axis=1, keepdims=True), (GROUP, LANES)
+    )
+
+
+def block_at(j):
+    return pl.ds(pl.multiple_of(j * GROUP, 8), GROUP)
+
+
+def tile_at(j):
+    return pl.ds(pl.multiple_of(j * 8, 8), 8)
+
+
+def product(s_ref, up_ref, high_ref, low_ref, j):
     acc = None
+    sources = (
+        (s_ref[block_at(j), 0:LANES], j),
+        (s_ref[block_at(j - 1), LANES : 2 * LANES], j - 1),
+        (up_ref[block_at(j), :], j + 1),
+    )
+    for s, at in sources:
+        high = high_ref[block_at(at), :]
+        p, e = times(s, high)
+        e = e + s * low_ref[block_at(at), :]
+        for r in range(0, GROUP, 8):
+            term = p[r : r + 8], e[r : r + 8]
+            acc = term if acc is None else plus(acc, term)
+    for step in (4, 2, 1):
+        acc = plus(acc, (pltpu.roll(acc[0], step, 0), pltpu.roll(acc[1], step, 0)))
+    acc = tidy(acc)
+    return acc[0] * SHRINK, acc[1] * SHRINK
+
+
+def store_tile(ref, at, pair):
+    row = iota((8, LANES), 0)
+    ref[tile_at(at), :] = jnp.where(row == 0, pair[0], jnp.where(row == 1, pair[1], 0.0))
+
+
+def powers(s_ref, up_ref, v_ref, cols, first, count, edge, base):
+    for k in range(count):
+        here, there = cols[k % 2], cols[1 - k % 2]
+
+        def one(j, carry):
+            pair = product(s_ref, up_ref, here[0], here[1], j)
+            store_tile(v_ref, (first + k) * BLOCKS + j, pair)
+            there[0][block_at(j), :] = to_column(pair[0][0:1])
+            there[1][block_at(j), :] = to_column(pair[1][0:1])
+            return carry
+
+        lax.fori_loop(base + k * edge, BLOCKS - base - k * edge, one, 0)
+
+
+def first_kernel(
+    where_ref, p_ref, c_ref, n_ref, p2_ref, c2_ref, n2_ref,
+    s_ref, up_ref, v_ref, v4_ref, h0_ref, l0_ref, h1_ref, l1_ref,
+):
+    core = where_ref[2]
+    mine = pl.multiple_of(48 * core, 8)
+    theirs = pl.multiple_of(48 - 48 * core, 8)
+    diagonal = iota((GROUP, LANES), 0) == iota((GROUP, LANES), 1)
+    lane = iota((GROUP, LANES), 1)
+    for j in range(BLOCKS):
+        rows = slice((j % 4) * 48, (j % 4 + 1) * 48)
+        a = (p_ref, c_ref, n_ref)[j // 4]
+        b = (p2_ref, c2_ref, n2_ref)[j // 4]
+        s_ref[pl.ds(j * GROUP + mine, 48), :] = a[rows, :]
+        s_ref[pl.ds(j * GROUP + theirs, 48), :] = b[rows, :]
+    zero = jnp.zeros((LANES - GROUP, LANES), F32)
+
+    def prepare(j, carry):
+        own = s_ref[block_at(j), 0:LANES]
+        rhs = jnp.broadcast_to(own[:, LANES - 1 : LANES], (GROUP, LANES)) * FIRST
+        h0_ref[block_at(j), :] = rhs
+        l0_ref[block_at(j), :] = jnp.zeros_like(rhs)
+        store_tile(v_ref, j, (to_row(rhs), jnp.zeros((1, LANES), F32)))
+        s_ref[block_at(j), 0:LANES] = jnp.where(lane < GROUP, own, 0.0) + jnp.where(
+            diagonal, POSE_REG, 0.0
+        )
+        up = jnp.concatenate([s_ref[block_at(j), LANES : 2 * LANES], zero], axis=0).T
+        up_ref[block_at(j), :] = up[0:GROUP]
+        return carry
+
+    lax.fori_loop(0, BLOCKS, prepare, 0)
+    cols = ((h0_ref, l0_ref), (h1_ref, l1_ref))
+    powers(s_ref, up_ref, v_ref, cols, 1, 4, 1, 1)
+    for j in range(4):
+        at = (4 * BLOCKS + 4 + j) * 8
+        v4_ref[j : j + 1, :] = v_ref[at : at + 1, :]
+        v4_ref[4 + j : 5 + j, :] = v_ref[at + 1 : at + 2, :]
+
+
+def second_kernel(
+    s_ref, up_ref, v_ref, below_ref, own_ref, above_ref, out_ref, v45_ref,
+    h0_ref, l0_ref, h1_ref, l1_ref,
+):
     for g, ref in enumerate((below_ref, own_ref, above_ref)):
-        s = s_ref[:, g * LANES : (g + 1) * LANES]
-        p, e = times(s, jnp.broadcast_to(ref[0:1, :], s.shape))
-        term = p, e + s * ref[1:2, :]
-        acc = term if acc is None else plus(acc, term)
-    acc = lane_total(acc)
-    row = tidy((to_row(acc[0]), to_row(acc[1])))
-    return row[0] * SHRINK, row[1] * SHRINK
+        for j in range(4):
+            pair = ref[j : j + 1, :], ref[4 + j : 5 + j, :]
+            at = g * 4 + j
+            store_tile(v45_ref, at, pair)
+            if 1 < at < 10:
+                h0_ref[block_at(at), :] = to_column(pair[0])
+                l0_ref[block_at(at), :] = to_column(pair[1])
+    cols = ((h0_ref, l0_ref), (h1_ref, l1_ref))
+    powers(s_ref, up_ref, v45_ref, cols, 1, 2, 1, 3)
+    zero = jnp.zeros((1, LANES), F32)
+    total = None
+    for j in range(4, 8):
+
+        def row(k, part):
+            ref, at = (v_ref, k) if k < 4 else (v45_ref, k - 4)
+            at = (at * BLOCKS + j) * 8 + part
+            return ref[at : at + 1, :]
+
+        def stack(pick, part):
+            lines = [row(pick(m), part) for m in range(2 * ITERS)]
+            return jnp.concatenate(lines + [zero] * (16 - len(lines)), axis=0)
+
+        lower, upper = (lambda m: m // 2), (lambda m: m - m // 2)
+        a, b = (stack(lower, 0), stack(lower, 1)), (stack(upper, 0), stack(upper, 1))
+        p, e = times(a[0], b[0])
+        term = p, e + (a[0] * b[1] + a[1] * b[0])
+        total = term if total is None else plus(total, term)
+    total = tidy(lane_total(total))
+    diagonal = iota((16, LANES), 0) == iota((16, LANES), 1)
+    put(
+        out_ref,
+        [jnp.sum(jnp.where(diagonal, x, 0.0), axis=0, keepdims=True) for x in total],
+    )
 
 
 def put(ref, pair):
     ref[...] = jnp.zeros((8, LANES), F32)
     ref[0:1, :] = pair[0]
     ref[1:2, :] = pair[1]
-
-
-def step_kernel(s_ref, below_ref, own_ref, above_ref, out_ref):
-    put(out_ref, next_vector(s_ref, below_ref, own_ref, above_ref))
-
-
-def moment_kernel(s_ref, below_ref, own_ref, above_ref, *rest):
-    out_ref = rest[-1]
-    rows = [(r[0:1, :], r[1:2, :]) for r in rest[:-1]] + [(own_ref[0:1, :], own_ref[1:2, :])]
-    rows.append(next_vector(s_ref, below_ref, own_ref, above_ref))
-    zero = jnp.zeros((1, LANES), F32)
-
-    def stack(pick, part):
-        lines = [rows[pick(m)][part] for m in range(2 * ITERS)]
-        return jnp.concatenate(lines + [zero] * (16 - len(lines)), axis=0)
-
-    lower, upper = (lambda m: m // 2), (lambda m: m - m // 2)
-    a, b = (stack(lower, 0), stack(lower, 1)), (stack(upper, 0), stack(upper, 1))
-    p, e = times(a[0], b[0])
-    total = tidy(lane_total((p, e + (a[0] * b[1] + a[1] * b[0]))))
-    diagonal = iota((16, LANES), 0) == iota((16, LANES), 1)
-    put(
-        out_ref,
-        [jnp.sum(jnp.where(diagonal, x, 0.0), axis=0, keepdims=True) for x in total],
-    )
 
 
 def gather_sum(refs):
@@ -498,10 +591,9 @@
     put(out_ref, gather_sum((a_ref, b_ref, c_ref, d_ref)))
 
 
-def solve_kernel(*refs):
-    out_ref = refs[-1]
-    total = gather_sum(refs[:4])
-    vectors = refs[4:-1]
+def solve_kernel(where_ref, a_ref, b_ref, c_ref, d_ref, v_ref, v45_ref, out_ref):
+    at_quad = where_ref[3]
+    total = gather_sum((a_ref, b_ref, c_ref, d_ref))
     m = [(total[0][:, k : k + 1], total[1][:, k : k + 1]) for k in range(2 * ITERS)]
     one = jnp.ones((1, 1), F32)
     zero = jnp.zeros((1, 1), F32)
@@ -540,9 +632,10 @@
     for g in range(3):
         acc = None
         for k in range(ITERS):
-            ref = vectors[3 * k + g]
+            ref = v_ref if k < 4 else v45_ref
+            tile = ref[tile_at((k if k < 4 else k - 4) * BLOCKS + 3 + at_quad + g), :]
             wide = tuple(jnp.broadcast_to(x, (1, LANES)) for x in xc[k])
-            term = mul(wide, (ref[0:1, :], ref[1:2, :]))
+            term = mul(wide, (tile[0:1], tile[1:2]))
             acc = term if acc is None else plus(acc, term)
         out_ref[g * 8 : g * 8 + 8, :] = jnp.broadcast_to(
             (acc[0] + acc[1]) * (SHRINK / FIRST), (8, LANES)
@@ -594,7 +687,7 @@
     pixes = lax.axis_size("pix")
     fi = lax.axis_index("frames")
     pi = lax.axis_index("pix")
-    spot = jnp.stack([fi * f_dev, pi * plocal, pi % 2]).astype(jnp.int32)
+    spot = jnp.stack([fi * f_dev, pi * plocal, pi % 2, fi % 4]).astype(jnp.int32)
 
     def shift(block, step):
         return lax.ppermute(
@@ -618,7 +711,7 @@
     )
     keep, send, g, base, scale = call(
         main_kernel, "main",
-        [(96, 384), (96, 384), (f_dev * GROUP, plocal), (f_dev * 8, plocal), (f_dev * 8, plocal)],
+        [(96, 256), (96, 256), (f_dev * GROUP, plocal), (f_dev * 8, plocal), (f_dev * 8, plocal)],
         1, spot, own, from_after, from_before, inv_depth, depth_damping, tab, b, bt,
         scratch=[
             pltpu.VMEM((4 * FD * 8, plocal), F32),
@@ -627,8 +720,7 @@
             pltpu.VMEM((256, plocal), F32),
             pltpu.VMEM((GROUP, LANES), F32),
             pltpu.VMEM((f_dev * GROUP, 3 * LANES), F32),
-            pltpu.VMEM((3 * LANES, 3 * LANES), F32),
-            pltpu.VMEM((3 * LANES, 3 * LANES), F32),
+            pltpu.VMEM((192, 3 * LANES), F32),
         ],
     )
     got = lax.ppermute(send, "pix", [(i, i ^ 1) for i in range(pixes)])
@@ -648,31 +740,34 @@
     own_far = lax.ppermute(own_half, "pix", [(i, i ^ 2) for i in range(pixes)])
     rim_near = to_neighbour(0)
     rim_far = to_neighbour(2)
-    (half,) = call(rows_kernel, "rows", [(48, 384)], 1, spot, own_half, own_far, rim_near, rim_far)
-    other = lax.ppermute(half, "pix", [(i, i ^ 1) for i in range(pixes)])
-    s, residual = call(full_kernel, "full", [(96, 384), (8, LANES)], 1, spot, half, other)
-
-    def halo(v):
-        return shift(v, 1), v, shift(v, -1)
+    (half,) = call(quad_kernel, "half", [(48, 256)], 1, spot, own_half, own_far, rim_near, rim_far)
 
     def mates(v, step):
         return [v] + [
             lax.ppermute(v, "frames", [(i, i ^ (k * step)) for i in range(count)]) for k in (1, 2, 3)
         ]
 
-    vectors = []
-    for k in range(ITERS - 1):
-        vectors.append(halo(residual))
-        (residual,) = call(step_kernel, "step", [(8, LANES)], 0, s, *vectors[-1])
-    vectors.append(halo(residual))
-    (part,) = call(
-        moment_kernel, "moments", [(8, LANES)], 0, s, *vectors[-1], *[v[1] for v in vectors[:-1]]
-    )
-    for step in (1, 4):
-        (part,) = call(sum_kernel, "sum", [(8, LANES)], 0, *mates(part, step))
-    (pose,) = call(
-        solve_kernel, "solve", [(24, LANES)], 0, *mates(part, 16), *[x for v in vectors for x in v]
-    )
+    def twin(v):
+        return lax.ppermute(v, "pix", [(i, i ^ 1) for i in range(pixes)])
+
+    def halo(v):
+        return shift(v, 4), v, shift(v, -4)
+
+    (quad,) = call(place_kernel, "place", [(192, 256)], 1, spot, *mates(half, 1))
+    pieces = halo(quad)
+    wide = BLOCKS * GROUP
+    scratch = [pltpu.VMEM((wide, LANES), F32)] * 4
+    s, up, vs, v4 = call(
+        first_kernel, "first",
+        [(wide, 256), (wide, LANES), (5 * BLOCKS * 8, LANES), (8, LANES)],
+        1, spot, *pieces, *[twin(x) for x in pieces], scratch=scratch,
+    )
+    part, v45 = call(
+        second_kernel, "second", [(8, LANES), (3 * BLOCKS * 8, LANES)], 0, s, up, vs, *halo(v4),
+        scratch=scratch,
+    )
+    (part,) = call(sum_kernel, "sum", [(8, LANES)], 0, *mates(part, 4))
+    (pose,) = call(solve_kernel, "solve", [(24, LANES)], 1, spot, *mates(part, 16), vs, v45)
     (depth_step,) = call(
         final_kernel, "final", [(f_dev, plocal)], 0, pose, b, g, base, scale,
         scratch=[pltpu.VMEM((f_dev * 8, plocal), F32)],

time: 232 us -> 177 us (0.76)
  waiting for transfers between devices: 71.1 us -> 42.1 us
  starting transfers between devices: 71.4 us -> 46.7 us
  local copies, waits for them, and re-layouts: 15.9 us -> 13 us
    ppermute x14 -> x6, waiting for transfers between devices: 53.8 us -> 24 us  [shift(): lax.ppermute(block, 'frames', [(i, i + step) for i in range(count) if 0 <...]
    ppermute x14 -> x6, starting transfers between devices: 48.6 us -> 23.9 us  [shift(): lax.ppermute(block, 'frames', [(i, i + step) for i in range(count) if 0 <...]
    unnamed x61 -> x49, local copies, waits for them, and re-layouts: 10.9 us -> 7.96 us
    pallas_call x15 -> x10, Pallas kernels: 67.4 us -> 69.4 us  [call(): pl.pallas_call(kernel, name=name, out_shape=[jax.ShapeDtypeStruct(s, F32)...]
  transfers between devices with their start and end apart: 28 -> 22, of which waited for: 17 -> 13; matrix products, arithmetic and copies ran while one was open for 0% -> 0% of each run, Pallas kernels for 3% -> 4%
where the time goes in v3:
time: 177 us; the launch traced here: 174 us
  Pallas kernels  69.4 us (39%)
  starting transfers between devices  46.7 us (26%)
  waiting for transfers between devices  42.1 us (24%)
  local copies, waits for them, and re-layouts  13 us (7%)
    pallas_call x10, Pallas kernels, call(): pl.pallas_call(kernel, name=name, out_shape=[jax.ShapeDtypeStruct(s, F32)...  69.4 us
    ppermute x6, waiting for transfers between devices, shift(): lax.ppermute(block, 'frames', [(i, i + step) for i in range(count) if 0 <...  24 us
    ppermute x6, starting transfers between devices, shift(): lax.ppermute(block, 'frames', [(i, i + step) for i in range(count) if 0 <...  23.9 us
    ppermute x9, starting transfers between devices, mates(): lax.ppermute(v, 'frames', [(i, i ^ k * step) for i in range(count)])  12.6 us
    ppermute x2, starting transfers between devices, to_neighbour(): return lax.ppermute(rim, both_axes, route)  9.25 us
    unnamed x49, local copies, waits for them, and re-layouts  7.96 us
    ppermute x9, waiting for transfers between devices, mates(): lax.ppermute(v, 'frames', [(i, i ^ k * step) for i in range(count)])  7.77 us
    ppermute x2, waiting for transfers between devices, to_neighbour(): return lax.ppermute(rim, both_axes, route)  7.33 us
  transfers between devices with their start and end apart: 22, of which 13 were waited for; matrix products, arithmetic and copies ran while one was open for 0% of the time, Pallas kernels for 4%

profile of v3, /device:TPU:8, one launch (start us, length us, event | category | flops | bytes accessed | tf_op | source)
XLA Modules:
  0.0 173.6 jit_solution(5476155378077228411)
XLA Ops:
  0.6 1.4 copy.13
  2.0 0.2 reshape.16
  2.2 0.0 copy-start
  2.2 2.0 %copy.14 = f32[192,6,2,128]{3,2,1,0:T(2,128)} copy(f32[192,6,2,128]{3,1,0,2:T(8,128)S(1)} %bitcast.13) | data formatting | bytes 2359296 | tf_op jit(solution)/shard_map/transpose | solution.py:698
  4.2 0.1 copy.15
  4.2 0.2 reshape.18
  4.4 1.9 %copy.16 = f32[192,6,2,128]{3,2,1,0:T(2,128)} copy(f32[192,6,2,128]{3,1,0,2:T(8,128)S(1)} %bitcast.14) | data formatting | bytes 2359296 | tf_op jit(solution)/shard_map/transpose | solution.py:698
  6.4 0.6 pad_add_fusion.where_ref
  7.0 5.5 %scatter.1 = (f32[1024,768]{1,0:T(8,128)}, f32[152,768]{1,0:T(8,128)}, f32[144,768]{1,0:T(8,128)}) custom-call(s32[4]{0:T(128)} %pad_add_fusion.where_ref, s32[2,192]{1,0:T(2,128)} %ef_ref.1, f32[2304,128]{1,0:T(8,128)} %bitcast.15, f32[2304,128]{1,0:T(8,128)} %bitcast.16, s32[192,768]{1,0:T(8,128)} %mask_ref.1), custom_call_target="tpu_custom_call" | custom-call | tf_op jit(solution)/shard_map/scatter/pallas_call | solution.py:673
  12.5 8.6 %collective-permute-start = (f32[152,768]{1,0:T(8,128)}, f32[152,768]{1,0:T(8,128)S(1)}, u32[]{:S(2)}, u32[]{:S(2)}) collective-permute-start(f32[152,768]{1,0:T(8,128)} %get-tuple-element.20), channel_id=1, source_target_pairs={{4,0},{8,4},{12,8},{16,12},{20,16},{24,20},{28,24},{32,28},{36,32}... | collective-permute-start | bytes 1400840 | tf_op jit(solution)/shard_map/ppermute | solution.py:693
  21.1 1.9 %collective-permute-start.1 = (f32[144,768]{1,0:T(8,128)}, f32[144,768]{1,0:T(8,128)S(1)}, u32[]{:S(2)}, u32[]{:S(2)}) collective-permute-start(f32[144,768]{1,0:T(8,128)} %get-tuple-element.21), channel_id=1, source_target_pairs={{0,4},{4,8},{8,12},{12,16},{16,20},{20,24},{24,28},{28,32},{32,36}... | collective-permute-start | bytes 1327112 | tf_op jit(solution)/shard_map/ppermute | solution.py:693
  23.0 6.1 %pose.1 = (f32[256,128]{1,0:T(8,128)}, f32[1536,384]{1,0:T(8,128)}, f32[192,1536]{1,0:T(8,128)}) custom-call(s32[4]{0:T(128)} %pad_add_fusion.where_ref, f32[3,1024]{1,0:T(4,128)} %rotvec_ref.1, f32[3,1024]{1,0:T(4,128)} %trans_ref.1), custom_call_target="tpu_custom_call" | custom-call | tf_op jit(solution)/shard_map/pose/pallas_call | solution.py:673
  29.2 12.3 %collective-permute-done.1.rup_ref = f32[144,768]{1,0:T(8,128)S(1)} collective-permute-done((f32[144,768]{1,0:T(8,128)}, f32[144,768]{1,0:T(8,128)S(1)}, u32[]{:S(2)}, u32[]{:S(2)}) %collective-permute-start.1) | collective-permute-done | bytes 442400 | tf_op jit(solution)/shard_map/ppermute | solution.py:693
  41.5 0.8 copy-done.2
  42.3 0.1 copy-done.1
  42.4 25.4 %main.1 = (f32[96,256]{1,0:T(8,128)}, f32[96,256]{1,0:T(8,128)}, f32[1536,768]{1,0:T(8,128)}, f32[128,768]{1,0:T(8,128)}, f32[128,768]{1,0:T(8,128)}) custom-call(s32[4]{0:T(128)} %pad_add_fusion.where_ref, f32[1024,768]{1,0:T(8,128)} %get-tuple-element.19.own_ref, f32[152,768]{1,0:T(8,128)} %copy-done.1, f32[144,768]{1,0:T(8,128)} %copy-done.2, ...), custom_call_target="tpu_custom_call" | custom-call | tf_op jit(solution)/shard_map/main/pallas_call | solution.py:673
  67.8 1.5 collective-permute-done.2
  69.3 0.9 add.12
  70.3 6.7 %collective-permute-start.5 = (f32[48,256]{1,0:T(8,128)S(1)}, f32[48,256]{1,0:T(8,128)S(1)}, u32[]{:S(2)}, u32[]{:S(2)}) collective-permute-start(f32[48,256]{1,0:T(8,128)S(1)} %get-tuple-element.40), channel_id=1, source_target_pairs={{0,6},{2,4},{4,10},{5,3},{6,8},{7,1},{8,14},{9,7},{10,12},{11,5},{... | collective-permute-start | bytes 147464 | tf_op jit(solution)/shard_map/ppermute | solution.py:738
  77.0 2.5 %collective-permute-start.4 = (f32[48,256]{1,0:T(8,128)S(1)}, f32[48,256]{1,0:T(8,128)S(1)}, u32[]{:S(2)}, u32[]{:S(2)}) collective-permute-start(f32[48,256]{1,0:T(8,128)S(1)} %get-tuple-element.40), channel_id=1, source_target_pairs={{0,4},{2,6},{4,8},{5,1},{6,10},{7,3},{8,12},{9,5},{10,14},{11,7},{... | collective-permute-start | bytes 147464 | tf_op jit(solution)/shard_map/ppermute | solution.py:738
  79.5 0.9 collective-permute-start.3
  80.5 7.3 %collective-permute-done.4.rim_ref = f32[48,256]{1,0:T(8,128)S(1)} collective-permute-done((f32[48,256]{1,0:T(8,128)S(1)}, f32[48,256]{1,0:T(8,128)S(1)}, u32[]{:S(2)}, u32[]{:S(2)}) %collective-permute-start.4) | collective-permute-done | bytes 49184 | tf_op jit(solution)/shard_map/ppermute | solution.py:738
  87.8 0.6 copy-done.13
  88.4 0.6 copy-done.14
  89.0 1.5 half.1.a_ref
  90.5 1.2 collective-permute-start.8
  91.8 0.9 collective-permute-start.7
  92.7 2.2 %collective-permute-start.6 = (f32[48,256]{1,0:T(8,128)}, f32[48,256]{1,0:T(8,128)S(1)}, u32[]{:S(2)}, u32[]{:S(2)}) collective-permute-start(f32[48,256]{1,0:T(8,128)} %half.1.a_ref), channel_id=1, source_target_pairs={{0,4},{4,0},{8,12},{12,8},{16,20},{20,16},{24,28},{28,24},{32,36},... | collective-permute-start | bytes 147464 | tf_op jit(solution)/shard_map/ppermute | solution.py:747
  94.9 2.0 %collective-permute-done.8.d_ref = f32[48,256]{1,0:T(8,128)S(1)} collective-permute-done((f32[48,256]{1,0:T(8,128)}, f32[48,256]{1,0:T(8,128)S(1)}, u32[]{:S(2)}, u32[]{:S(2)}) %collective-permute-start.8) | collective-permute-done | bytes 49184 | tf_op jit(solution)/shard_map/ppermute | solution.py:747
  96.9 1.1 collective-permute-done.7.c_ref
  98.0 0.6 copy-done.10
  98.7 0.6 copy-done.11
  99.3 1.6 place.1.c_ref
  100.8 5.6 %collective-permute-start.10 = (f32[192,256]{1,0:T(8,128)}, f32[192,256]{1,0:T(8,128)S(1)}, u32[]{:S(2)}, u32[]{:S(2)}) collective-permute-start(f32[192,256]{1,0:T(8,128)} %place.1.c_ref), channel_id=1, source_target_pairs={{16,0},{20,4},{24,8},{28,12},{32,16},{36,20},{40,24},{44,28},{48,3... | collective-permute-start | bytes 589832 | tf_op jit(solution)/shard_map/ppermute | solution.py:693
  106.4 1.9 %collective-permute-start.9 = (f32[192,256]{1,0:T(8,128)}, f32[192,256]{1,0:T(8,128)S(1)}, u32[]{:S(2)}, u32[]{:S(2)}) collective-permute-start(f32[192,256]{1,0:T(8,128)} %place.1.c_ref), channel_id=1, source_target_pairs={{0,16},{4,20},{8,24},{12,28},{16,32},{20,36},{24,40},{28,44},{32,4... | collective-permute-start | bytes 589832 | tf_op jit(solution)/shard_map/ppermute | solution.py:693
  108.3 0.1 collective-permute-start.12
  108.4 1.5 collective-permute-done.10.n_ref
  109.9 6.4 %collective-permute-done.9.p_ref = f32[192,256]{1,0:T(8,128)S(1)} collective-permute-done((f32[192,256]{1,0:T(8,128)}, f32[192,256]{1,0:T(8,128)S(1)}, u32[]{:S(2)}, u32[]{:S(2)}) %collective-permute-start.9) | collective-permute-done | bytes 196640 | tf_op jit(solution)/shard_map/ppermute | solution.py:693
  116.3 1.4 collective-permute-done.11.p2_ref
  117.8 0.7 copy-done.8
  118.4 10.9 %first.1 = (f32[1152,256]{1,0:T(8,128)}, f32[1152,128]{1,0:T(8,128)}, f32[480,128]{1,0:T(8,128)}, f32[8,128]{1,0:T(8,128)}) custom-call(s32[4]{0:T(128)} %pad_add_fusion.where_ref, f32[192,256]{1,0:T(8,128)} %copy-done.5, f32[192,256]{1,0:T(8,128)} %place.1.c_ref, f32[192,256]{1,0:T(8,128)} %copy-done.4, f32[192,256]{1,0:T(8,128)} %copy-done.8, ...), custom_call_target="tpu_custom_call" | custom-call | tf_op jit(solution)/shard_map/first/pallas_call | solution.py:673
  129.4 1.9 %collective-permute-start.15 = (f32[8,128]{1,0:T(8,128)}, f32[8,128]{1,0:T(8,128)S(1)}, u32[]{:S(2)}, u32[]{:S(2)}) collective-permute-start(f32[8,128]{1,0:T(8,128)} %get-tuple-element.30.own_ref), channel_id=1, source_target_pairs={{16,0},{20,4},{24,8},{28,12},{32,16},{36,20},{40,24},{44,28},{48,3... | collective-permute-start | bytes 12296 | tf_op jit(solution)/shard_map/ppermute | solution.py:693
  131.3 3.9 %collective-permute-start.14 = (f32[8,128]{1,0:T(8,128)}, f32[8,128]{1,0:T(8,128)S(1)}, u32[]{:S(2)}, u32[]{:S(2)}) collective-permute-start(f32[8,128]{1,0:T(8,128)} %get-tuple-element.30.own_ref), channel_id=1, source_target_pairs={{0,16},{4,20},{8,24},{12,28},{16,32},{20,36},{24,40},{28,44},{32,4... | collective-permute-start | bytes 12296 | tf_op jit(solution)/shard_map/ppermute | solution.py:693
  135.3 3.9 %collective-permute-done.14.below_ref = f32[8,128]{1,0:T(8,128)S(1)} collective-permute-done((f32[8,128]{1,0:T(8,128)}, f32[8,128]{1,0:T(8,128)S(1)}, u32[]{:S(2)}, u32[]{:S(2)}) %collective-permute-start.14) | collective-permute-done | bytes 4128 | tf_op jit(solution)/shard_map/ppermute | solution.py:693
  139.1 0.6 copy-done.19
  139.7 5.4 %second.1 = (f32[8,128]{1,0:T(8,128)}, f32[288,128]{1,0:T(8,128)}) custom-call(f32[1152,256]{1,0:T(8,128)} %get-tuple-element.27.s_ref, f32[1152,128]{1,0:T(8,128)} %get-tuple-element.28.up_ref, f32[480,128]{1,0:T(8,128)} %get-tuple-element.29.v_ref, f32[8,128]{1,0:T(8,128)} %copy-done.19, f32[8,128]{1,0:T(8,128)} %get-tuple-element.30.own_ref, ...), custom_call_target="tpu_custom_call" | custom-call | tf_op jit(solution)/shard_map/second/pallas_call | solution.py:673
  145.2 2.0 %collective-permute-start.17 = (f32[8,128]{1,0:T(8,128)}, f32[8,128]{1,0:T(8,128)S(1)}, u32[]{:S(2)}, u32[]{:S(2)}) collective-permute-start(f32[8,128]{1,0:T(8,128)} %get-tuple-element.31.a_ref), channel_id=1, source_target_pairs={{0,32},{4,36},{8,40},{12,44},{16,48},{20,52},{24,56},{28,60},{32,0... | collective-permute-start | bytes 12296 | tf_op jit(solution)/shard_map/ppermute | solution.py:747
  147.1 2.1 %collective-permute-start.16 = (f32[8,128]{1,0:T(8,128)}, f32[8,128]{1,0:T(8,128)S(1)}, u32[]{:S(2)}, u32[]{:S(2)}) collective-permute-start(f32[8,128]{1,0:T(8,128)} %get-tuple-element.31.a_ref), channel_id=1, source_target_pairs={{0,16},{4,20},{8,24},{12,28},{16,0},{20,4},{24,8},{28,12},{32,48},... | collective-permute-start | bytes 12296 | tf_op jit(solution)/shard_map/ppermute | solution.py:747
  149.3 0.9 collective-permute-done.18.d_ref
  150.2 0.3 collective-permute-done.17.c_ref
  150.5 0.6 collective-permute-done.16.b_ref
  151.1 0.6 copy-done.22
  151.7 1.4 sum.1.a_ref
  153.0 1.6 collective-permute-start.21
  154.6 1.0 collective-permute-start.20
  155.6 1.5 collective-permute-start.19
  157.1 2.8 %collective-permute-done.20.c_ref = f32[8,128]{1,0:T(8,128)S(1)} collective-permute-done((f32[8,128]{1,0:T(8,128)}, f32[8,128]{1,0:T(8,128)S(1)}, u32[]{:S(2)}, u32[]{:S(2)}) %collective-permute-start.20) | collective-permute-done | bytes 4128 | tf_op jit(solution)/shard_map/ppermute | solution.py:747
  160.0 0.6 copy-done.16
  160.5 0.0 copy-done.18
  160.6 6.0 %solve.1.pose_ref = f32[24,128]{1,0:T(8,128)} custom-call(s32[4]{0:T(128)} %pad_add_fusion.where_ref, f32[8,128]{1,0:T(8,128)} %sum.1.a_ref, f32[8,128]{1,0:T(8,128)} %copy-done.18, f32[8,128]{1,0:T(8,128)} %copy-done.16, f32[8,128]{1,0:T(8,128)} %copy-done.15, f32[480,128]{1,0:T(8,128)} %get-tuple-element.29.v_ref, f32[288,128]{1,0:T(8,128)} %get-tuple-element.32.v45_ref), custom_call_target="tpu_custom_call" | custom-call | tf_op jit(solution)/shard_map/solve/pallas_call | solution.py:673
  166.6 0.7 slice_reduce_fusion
  167.3 0.1 reshape_squeeze.3
  167.4 0.7 copy.17
  168.0 5.6 %final.1 = f32[16,768]{1,0:T(8,128)} custom-call(f32[24,128]{1,0:T(8,128)} %solve.1.pose_ref, f32[1536,384]{1,0:T(8,128)} %get-tuple-element.23.b_ref, f32[1536,768]{1,0:T(8,128)} %get-tuple-element.33.g_ref, f32[128,768]{1,0:T(8,128)} %get-tuple-element.34.base_ref, f32[128,768]{1,0:T(8,128)} %get-tuple-element.35.scale_ref), custom_call_target="tpu_custom_call" | custom-call | tf_op jit(solution)/shard_map/final/pallas_call | solution.py:673
  (48 shorter events, 0.1 us)
Async XLA Ops:
  2.2 2.0 %copy-start = (f32[192,2,768]{2,1,0:T(2,128)S(1)}, f32[192,2,768]{2,1,0:T(2,128)}, u32[]{:S(2)}) copy-start(f32[192,2,768]{2,1,0:T(2,128)} %param.14) | copy-start | bytes 3538948
  12.5 29.0 %collective-permute-start = (f32[152,768]{1,0:T(8,128)}, f32[152,768]{1,0:T(8,128)S(1)}, u32[]{:S(2)}, u32[]{:S(2)}) collective-permute-start(f32[152,768]{1,0:T(8,128)} %get-tuple-element.20), channel_id=1, source_target_pairs={{4,0},{8,4},{12,8},{16,12},{20,16},{24,20},{28,24},{32,28},{36,32}... | collective-permute-start | bytes 1400840 | tf_op jit(solution)/shard_map/ppermute | solution.py:693
  21.1 20.4 %collective-permute-start.1 = (f32[144,768]{1,0:T(8,128)}, f32[144,768]{1,0:T(8,128)S(1)}, u32[]{:S(2)}, u32[]{:S(2)}) collective-permute-start(f32[144,768]{1,0:T(8,128)} %get-tuple-element.21), channel_id=1, source_target_pairs={{0,4},{4,8},{8,12},{12,16},{16,20},{20,24},{24,28},{28,32},{32,36}... | collective-permute-start | bytes 1327112 | tf_op jit(solution)/shard_map/ppermute | solution.py:693
  41.5 0.8 copy-start.2
  41.5 0.9 copy-start.1
  67.8 1.5 collective-permute-start.2
  70.3 17.5 %copy-start.3 = (f32[48,256]{1,0:T(8,128)}, f32[48,256]{1,0:T(8,128)S(1)}, u32[]{:S(2)}) copy-start(f32[48,256]{1,0:T(8,128)S(1)} %get-tuple-element.41.own_ref) | copy-start | bytes 147460
  70.3 10.2 %collective-permute-start.5 = (f32[48,256]{1,0:T(8,128)S(1)}, f32[48,256]{1,0:T(8,128)S(1)}, u32[]{:S(2)}, u32[]{:S(2)}) collective-permute-start(f32[48,256]{1,0:T(8,128)S(1)} %get-tuple-element.40), channel_id=1, source_target_pairs={{0,6},{2,4},{4,10},{5,3},{6,8},{7,1},{8,14},{9,7},{10,12},{11,5},{... | collective-permute-start | bytes 147464 | tf_op jit(solution)/shard_map/ppermute | solution.py:738
  77.0 10.8 %collective-permute-start.4 = (f32[48,256]{1,0:T(8,128)S(1)}, f32[48,256]{1,0:T(8,128)S(1)}, u32[]{:S(2)}, u32[]{:S(2)}) collective-permute-start(f32[48,256]{1,0:T(8,128)S(1)} %get-tuple-element.40), channel_id=1, source_target_pairs={{0,4},{2,6},{4,8},{5,1},{6,10},{7,3},{8,12},{9,5},{10,14},{11,7},{... | collective-permute-start | bytes 147464 | tf_op jit(solution)/shard_map/ppermute | solution.py:738
  79.5 8.3 %collective-permute-start.3 = (f32[48,256]{1,0:T(8,128)S(1)}, f32[48,256]{1,0:T(8,128)S(1)}, u32[]{:S(2)}, u32[]{:S(2)}) collective-permute-start(f32[48,256]{1,0:T(8,128)S(1)} %get-tuple-element.41.own_ref), channel_id=1, source_target_pairs={{0,2},{1,3},{2,0},{3,1},{4,6},{5,7},{6,4},{7,5},{8,10},{9,11},{10,... | collective-permute-start | bytes 147464 | tf_op jit(solution)/shard_map/ppermute | solution.py:740
  80.5 7.3 %copy-start.12 = (f32[48,256]{1,0:T(8,128)}, f32[48,256]{1,0:T(8,128)S(1)}, u32[]{:S(2)}) copy-start(f32[48,256]{1,0:T(8,128)S(1)} %collective-permute-done.5.rim2_ref) | copy-start | bytes 147460
  87.8 0.6 copy-start.13
  88.4 0.6 copy-start.14
  90.5 6.4 %collective-permute-start.8 = (f32[48,256]{1,0:T(8,128)}, f32[48,256]{1,0:T(8,128)S(1)}, u32[]{:S(2)}, u32[]{:S(2)}) collective-permute-start(f32[48,256]{1,0:T(8,128)} %half.1.a_ref), channel_id=1, source_target_pairs={{0,12},{4,8},{8,4},{12,0},{16,28},{20,24},{24,20},{28,16},{32,44},... | collective-permute-start | bytes 147464 | tf_op jit(solution)/shard_map/ppermute | solution.py:747
  91.8 6.3 %collective-permute-start.7 = (f32[48,256]{1,0:T(8,128)}, f32[48,256]{1,0:T(8,128)S(1)}, u32[]{:S(2)}, u32[]{:S(2)}) collective-permute-start(f32[48,256]{1,0:T(8,128)} %half.1.a_ref), channel_id=1, source_target_pairs={{0,8},{4,12},{8,0},{12,4},{16,24},{20,28},{24,16},{28,20},{32,40},... | collective-permute-start | bytes 147464 | tf_op jit(solution)/shard_map/ppermute | solution.py:747
  92.7 5.4 %collective-permute-start.6 = (f32[48,256]{1,0:T(8,128)}, f32[48,256]{1,0:T(8,128)S(1)}, u32[]{:S(2)}, u32[]{:S(2)}) collective-permute-start(f32[48,256]{1,0:T(8,128)} %half.1.a_ref), channel_id=1, source_target_pairs={{0,4},{4,0},{8,12},{12,8},{16,20},{20,16},{24,28},{28,24},{32,36},... | collective-permute-start | bytes 147464 | tf_op jit(solution)/shard_map/ppermute | solution.py:747
  96.9 1.1 copy-start.9
  98.0 0.6 copy-start.10
  98.6 0.6 copy-start.11
  100.8 9.1 %collective-permute-start.10 = (f32[192,256]{1,0:T(8,128)}, f32[192,256]{1,0:T(8,128)S(1)}, u32[]{:S(2)}, u32[]{:S(2)}) collective-permute-start(f32[192,256]{1,0:T(8,128)} %place.1.c_ref), channel_id=1, source_target_pairs={{16,0},{20,4},{24,8},{28,12},{32,16},{36,20},{40,24},{44,28},{48,3... | collective-permute-start | bytes 589832 | tf_op jit(solution)/shard_map/ppermute | solution.py:693
  106.4 9.9 %collective-permute-start.9 = (f32[192,256]{1,0:T(8,128)}, f32[192,256]{1,0:T(8,128)S(1)}, u32[]{:S(2)}, u32[]{:S(2)}) collective-permute-start(f32[192,256]{1,0:T(8,128)} %place.1.c_ref), channel_id=1, source_target_pairs={{0,16},{4,20},{8,24},{12,28},{16,32},{20,36},{24,40},{28,44},{32,4... | collective-permute-start | bytes 589832 | tf_op jit(solution)/shard_map/ppermute | solution.py:693
  108.3 8.0 %collective-permute-start.12 = (f32[192,256]{1,0:T(8,128)}, f32[192,256]{1,0:T(8,128)S(1)}, u32[]{:S(2)}, u32[]{:S(2)}) collective-permute-start(f32[192,256]{1,0:T(8,128)} %place.1.c_ref), channel_id=1, source_target_pairs={{0,1},{1,0},{2,3},{3,2},{4,5},{5,4},{6,7},{7,6},{8,9},{9,8},{10,11... | collective-permute-start | bytes 589832 | tf_op jit(solution)/shard_map/ppermute | solution.py:751
  109.9 7.8 %copy-start.4 = (f32[192,256]{1,0:T(8,128)}, f32[192,256]{1,0:T(8,128)S(1)}, u32[]{:S(2)}) copy-start(f32[192,256]{1,0:T(8,128)S(1)} %collective-permute-done.10.n_ref) | copy-start | bytes 589828
  109.9 6.4 %collective-permute-start.13 = (f32[192,256]{1,0:T(8,128)S(1)}, f32[192,256]{1,0:T(8,128)S(1)}, u32[]{:S(2)}, u32[]{:S(2)}) collective-permute-start(f32[192,256]{1,0:T(8,128)S(1)} %collective-permute-done.10.n_ref), channel_id=1, source_target_pairs={{0,1},{1,0},{2,3},{3,2},{4,5},{5,4},{6,7},{7,6},{8,9},{9,8},{10,11... | collective-permute-start | bytes 589832 | tf_op jit(solution)/shard_map/ppermute | solution.py:751
  116.3 1.4 copy-start.5
  116.3 1.4 collective-permute-start.11
  116.3 1.4 copy-start.6
  116.3 1.4 copy-start.7
  117.8 0.7 copy-start.8
  129.4 5.8 %collective-permute-start.15 = (f32[8,128]{1,0:T(8,128)}, f32[8,128]{1,0:T(8,128)S(1)}, u32[]{:S(2)}, u32[]{:S(2)}) collective-permute-start(f32[8,128]{1,0:T(8,128)} %get-tuple-element.30.own_ref), channel_id=1, source_target_pairs={{16,0},{20,4},{24,8},{28,12},{32,16},{36,20},{40,24},{44,28},{48,3... | collective-permute-start | bytes 12296 | tf_op jit(solution)/shard_map/ppermute | solution.py:693
  131.3 7.8 %collective-permute-start.14 = (f32[8,128]{1,0:T(8,128)}, f32[8,128]{1,0:T(8,128)S(1)}, u32[]{:S(2)}, u32[]{:S(2)}) collective-permute-start(f32[8,128]{1,0:T(8,128)} %get-tuple-element.30.own_ref), channel_id=1, source_target_pairs={{0,16},{4,20},{8,24},{12,28},{16,32},{20,36},{24,40},{28,44},{32,4... | collective-permute-start | bytes 12296 | tf_op jit(solution)/shard_map/ppermute | solution.py:693
  135.3 3.9 %copy-start.17 = (f32[8,128]{1,0:T(8,128)}, f32[8,128]{1,0:T(8,128)S(1)}, u32[]{:S(2)}) copy-start(f32[8,128]{1,0:T(8,128)S(1)} %collective-permute-done.15.above_ref) | copy-start | bytes 12292
  139.1 0.6 copy-start.19
  145.2 5.0 %collective-permute-start.18 = (f32[8,128]{1,0:T(8,128)}, f32[8,128]{1,0:T(8,128)S(1)}, u32[]{:S(2)}, u32[]{:S(2)}) collective-permute-start(f32[8,128]{1,0:T(8,128)} %get-tuple-element.31.a_ref), channel_id=1, source_target_pairs={{0,48},{4,52},{8,56},{12,60},{16,32},{20,36},{24,40},{28,44},{32,1... | collective-permute-start | bytes 12296 | tf_op jit(solution)/shard_map/ppermute | solution.py:747
  145.2 5.3 %collective-permute-start.17 = (f32[8,128]{1,0:T(8,128)}, f32[8,128]{1,0:T(8,128)S(1)}, u32[]{:S(2)}, u32[]{:S(2)}) collective-permute-start(f32[8,128]{1,0:T(8,128)} %get-tuple-element.31.a_ref), channel_id=1, source_target_pairs={{0,32},{4,36},{8,40},{12,44},{16,48},{20,52},{24,56},{28,60},{32,0... | collective-permute-start | bytes 12296 | tf_op jit(solution)/shard_map/ppermute | solution.py:747
  147.1 4.0 %collective-permute-start.16 = (f32[8,128]{1,0:T(8,128)}, f32[8,128]{1,0:T(8,128)S(1)}, u32[]{:S(2)}, u32[]{:S(2)}) collective-permute-start(f32[8,128]{1,0:T(8,128)} %get-tuple-element.31.a_ref), channel_id=1, source_target_pairs={{0,16},{4,20},{8,24},{12,28},{16,0},{20,4},{24,8},{28,12},{32,48},... | collective-permute-start | bytes 12296 | tf_op jit(solution)/shard_map/ppermute | solution.py:747
  150.2 0.9 copy-start.20
  150.5 0.6 copy-start.21
  151.1 0.6 copy-start.22
  153.0 4.1 %collective-permute-start.21 = (f32[8,128]{1,0:T(8,128)}, f32[8,128]{1,0:T(8,128)S(1)}, u32[]{:S(2)}, u32[]{:S(2)}) collective-permute-start(f32[8,128]{1,0:T(8,128)} %sum.1.a_ref), channel_id=1, source_target_pairs={{0,192},{4,196},{8,200},{12,204},{16,208},{20,212},{24,216},{28,22... | collective-permute-start | bytes 12296 | tf_op jit(solution)/shard_map/ppermute | solution.py:747
  154.6 5.3 %collective-permute-start.20 = (f32[8,128]{1,0:T(8,128)}, f32[8,128]{1,0:T(8,128)S(1)}, u32[]{:S(2)}, u32[]{:S(2)}) collective-permute-start(f32[8,128]{1,0:T(8,128)} %sum.1.a_ref), channel_id=1, source_target_pairs={{0,128},{4,132},{8,136},{12,140},{16,144},{20,148},{24,152},{28,15... | collective-permute-start | bytes 12296 | tf_op jit(solution)/shard_map/ppermute | solution.py:747
  155.6 4.3 %collective-permute-start.19 = (f32[8,128]{1,0:T(8,128)}, f32[8,128]{1,0:T(8,128)S(1)}, u32[]{:S(2)}, u32[]{:S(2)}) collective-permute-start(f32[8,128]{1,0:T(8,128)} %sum.1.a_ref), channel_id=1, source_target_pairs={{0,64},{4,68},{8,72},{12,76},{16,80},{20,84},{24,88},{28,92},{32,9... | collective-permute-start | bytes 12296 | tf_op jit(solution)/shard_map/ppermute | solution.py:747
  157.1 2.8 %copy-start.15 = (f32[8,128]{1,0:T(8,128)}, f32[8,128]{1,0:T(8,128)S(1)}, u32[]{:S(2)}) copy-start(f32[8,128]{1,0:T(8,128)S(1)} %collective-permute-done.21.d_ref) | copy-start | bytes 12292
  160.0 0.6 copy-start.16
  160.0 0.6 copy-start.18

commit v4 on v3

--- a/solution.py
+++ b/solution.py
@@ -30,6 +30,15 @@
     rest = x - first.astype(F32)
     second = rest.astype(BF16)
     return first, second, (rest - second.astype(F32)).astype(BF16)
+
+
+def pair_of(x):
+    first = x.astype(BF16)
+    return first, (x - first.astype(F32)).astype(BF16)
+
+
+def dot(a, b):
+    return jnp.dot(a, b, preferred_element_type=F32)
 
 
 def scatter_kernel(where_ref, ef_ref, flow_ref, weight_ref, mask_ref, own_ref, down_ref, up_ref):
@@ -52,15 +61,13 @@
         axis=0,
     ).astype(BF16)
     down_ref[0:8, :] = jnp.zeros((8, down_ref.shape[1]), F32)
-    per_edge = 2 * (mask_ref.shape[1] // LANES)
     for chunk in range(mask_ref.shape[1] // LANES):
         lanes = pl.ds(chunk * LANES, LANES)
         live = mask_ref[:, lanes].astype(F32)
         parts = []
         for comp in range(2):
-            rows = pl.ds(chunk * 2 + comp, edges, stride=per_edge)
-            conf = weight_ref[rows, :] * live
-            parts.append((conf, conf * flow_ref[rows, :]))
+            conf = weight_ref[comp, :, lanes] * live
+            parts.append((conf, conf * flow_ref[comp, :, lanes]))
         values = jnp.concatenate([parts[0][0], parts[1][0], parts[0][1], parts[1][1]], axis=1)
         got = sum(
             jnp.dot(hot, piece, preferred_element_type=F32) for piece in reversed(thirds(values))
@@ -310,14 +317,20 @@
                 q_ref[c * SLOTS + 8 * h : c * SLOTS + 8 * h + 8, :] = block
                 cols[(c, h)] = sums[c]
         g = hi_ref[...]
-        top = g.astype(BF16)
-        low = (g - top.astype(F32)).astype(BF16)
-        left = jnp.concatenate([top, low, top], axis=1)
-        right = jnp.concatenate([top, top, low], axis=1)
-        m = lax.dot_general(left, right, (((1,), (1,)), ((), ())), preferred_element_type=F32)
+        top, low = pair_of(g)
+        both = lax.dot_general(
+            jnp.concatenate([top, low], axis=0), top, (((1,), (1,)), ((), ())),
+            preferred_element_type=F32,
+        )
+        m = both[0:GROUP] + both[GROUP:] + both[GROUP:].T
         q = q_ref[:, 0:GROUP] - m
         rows = pl.ds(pl.multiple_of(f * GROUP, 8), GROUP)
-        w_ref[rows, :] = jnp.dot(q, b_ref[rows, :], precision=HIGHEST, preferred_element_type=F32)
+        q_top, q_low = pair_of(q)
+        b_top, b_low = pair_of(b_ref[rows, :])
+        both = dot(jnp.concatenate([q_top, q_low], axis=0), b_top)
+        w_ref[rows, :] = both[0:GROUP] + both[GROUP:]
+        own_group = slice(LANES, 2 * LANES)
+        w_ref[rows, own_group] = w_ref[rows, own_group] + dot(q_top, b_low[:, own_group])
         for c in range(6):
             for h in range(2):
                 at = pl.ds(pl.multiple_of(f * GROUP + c * SLOTS + 8 * h, 8), 8)
@@ -328,7 +341,10 @@
 
     lax.fori_loop(0, 8, functools.partial(frame, merged=0), 0)
     lax.fori_loop(8, 16, functools.partial(frame, merged=1), 0)
-    t = jnp.dot(bt_ref[...], w_ref[...], precision=HIGHEST, preferred_element_type=F32)
+    bt_top, bt_low = pair_of(bt_ref[...])
+    w_top, w_low = pair_of(w_ref[...])
+    both = dot(jnp.concatenate([bt_top, bt_low], axis=0), w_top)
+    t = both[0:192] + both[192:] + dot(bt_top, w_low)
     t_ref[...] = t
     for lo, hi, group, first in ((0, 48, 0, 48), (48, 144, 1, 0), (144, 192, 2, 0)):
         count = hi - lo
@@ -594,41 +610,44 @@
 def solve_kernel(where_ref, a_ref, b_ref, c_ref, d_ref, v_ref, v45_ref, out_ref):
     at_quad = where_ref[3]
     total = gather_sum((a_ref, b_ref, c_ref, d_ref))
-    m = [(total[0][:, k : k + 1], total[1][:, k : k + 1]) for k in range(2 * ITERS)]
-    one = jnp.ones((1, 1), F32)
-    zero = jnp.zeros((1, 1), F32)
-    none = (zero, zero)
+    shape = (8, LANES)
+    row = iota(shape, 0)
+    lane = iota(shape, 1)
+    zero = jnp.zeros(shape, F32)
+    unit = jnp.where((row == 1) & (lane == LANES - 1), 1.0, 0.0)
 
     def where(live, a, b):
         return jnp.where(live, a[0], b[0]), jnp.where(live, a[1], b[1])
 
-    sigma = list(m)
-    tau = list(m)
-    rc = [(one, zero)] + [none] * ITERS
-    pc = list(rc)
-    xc = [none] * ITERS
-    lead = one
-    live = m[0][0] > 0.0
+    def at(a, r, k):
+        return tuple(jnp.broadcast_to(x[r : r + 1, k : k + 1], shape) for x in a)
+
+    x = jnp.where(row == 0, total[0], unit), jnp.where(row == 0, total[1], 0.0)
+    y = x
+    found = (zero, zero)
+    one = (zero + 1.0, zero)
+    start = at(x, 0, 0)
+    now = start
+    lead = one[0]
+    live = start[0] > 0.0
     for k in range(ITERS):
-        alpha = div(sigma[k], where(live, tau[k + 1], (one, zero)))
+        alpha = div(now, where(live, at(y, 0, k + 1), one))
         live = live & (alpha[0] > 0.0) & (alpha[0] < LARGEST_STEP)
-        alpha = where(live, alpha, none)
-        for i in range(k + 1):
-            xc[i] = add(xc[i], mul(alpha, pc[i]))
+        alpha = where(live, alpha, (zero, zero))
+        found = add(found, mul(alpha, y))
         if k + 1 == ITERS:
             break
         back = neg(alpha)
-        fresh = {i: add(sigma[i], mul(back, tau[i + 1])) for i in range(k + 1, 2 * ITERS - k - 1)}
-        for i in range(k + 1, 0, -1):
-            rc[i] = add(rc[i], mul(back, pc[i - 1]))
+        moved = tuple(pltpu.roll(p, LANES - 1, 1) for p in y)
+        x = add(x, mul(back, moved))
+        fresh = at(x, 0, k + 1)
         lead = -lead * alpha[0]
-        live = live & (lead * fresh[k + 1][0] > 1e-11 * m[0][0])
-        beta = div(mul(back, fresh[k + 1]), where(live, sigma[k], (one, zero)))
-        beta = where(live, beta, none)
-        for i, x in fresh.items():
-            tau[i] = add(x, mul(beta, tau[i]))
-            sigma[i] = x
-        pc = [add(rc[i], mul(beta, pc[i])) for i in range(k + 2)] + [none] * (ITERS - k - 1)
+        live = live & (lead * fresh[0] > 1e-11 * start[0])
+        beta = div(mul(back, fresh), where(live, now, one))
+        beta = where(live, beta, (zero, zero))
+        y = add(x, mul(beta, y))
+        now = fresh
+    xc = [tuple(p[1:2, LANES - 1 - k : LANES - k] for p in found) for k in range(ITERS)]
     for g in range(3):
         acc = None
         for k in range(ITERS):
@@ -682,7 +701,6 @@
 
 def per_device(edge_frames, rotvec, trans, inv_depth, depth_damping, flow, weight, mask):
     f_dev, plocal = inv_depth.shape
-    edges = mask.shape[0]
     count = lax.axis_size("frames")
     pixes = lax.axis_size("pix")
     fi = lax.axis_index("frames")
@@ -694,13 +712,10 @@
             block, "frames", [(i, i + step) for i in range(count) if 0 <= i + step < count]
         )
 
-    def view(x):
-        return x.reshape(edges, 2, plocal // LANES, LANES).transpose(0, 2, 1, 3).reshape(-1, LANES)
-
     own, down, up = call(
         scatter_kernel, "scatter",
         [(4 * f_dev * SLOTS, plocal), (8 + 4 * SIDE, plocal), (4 * SIDE, plocal)],
-        1, spot, edge_frames, view(flow), view(weight), mask,
+        1, spot, edge_frames, flow.transpose(1, 0, 2), weight.transpose(1, 0, 2), mask,
     )
     from_after = shift(down, -1)
     from_before = shift(up, 1)

time: 177 us -> 167 us (0.944)
  Pallas kernels: 69.4 us -> 62.8 us
  local copies, waits for them, and re-layouts: 13 us -> 10.6 us
    pallas_call x10, Pallas kernels: 69.4 us -> 62.8 us  [call(): pl.pallas_call(kernel, name=name, out_shape=[jax.ShapeDtypeStruct(s, F32)...]
    unnamed x49 -> x45, local copies, waits for them, and re-layouts: 7.96 us -> 6.53 us
    transpose x2 -> x1, local copies, waits for them, and re-layouts: 3.9 us -> 3.27 us  [per_device(): weight.transpose(1, 0, 2)]
where the time goes in v4:
time: 167 us; the launch traced here: 164 us
  Pallas kernels  62.8 us (38%)
  starting transfers between devices  46.7 us (28%)
  waiting for transfers between devices  42 us (25%)
  local copies, waits for them, and re-layouts  10.6 us (6%)
    pallas_call x10, Pallas kernels, call(): pl.pallas_call(kernel, name=name, out_shape=[jax.ShapeDtypeStruct(s, F32)...  62.8 us
    ppermute x6, waiting for transfers between devices, shift(): lax.ppermute(block, 'frames', [(i, i + step) for i in range(count) if 0 <...  24 us
    ppermute x6, starting transfers between devices, shift(): lax.ppermute(block, 'frames', [(i, i + step) for i in range(count) if 0 <...  23.8 us
    ppermute x9, starting transfers between devices, mates(): lax.ppermute(v, 'frames', [(i, i ^ k * step) for i in range(count)])  12.6 us
    ppermute x2, starting transfers between devices, to_neighbour(): return lax.ppermute(rim, both_axes, route)  9.25 us
    ppermute x9, waiting for transfers between devices, mates(): lax.ppermute(v, 'frames', [(i, i ^ k * step) for i in range(count)])  7.78 us
    ppermute x2, waiting for transfers between devices, to_neighbour(): return lax.ppermute(rim, both_axes, route)  7.32 us
    unnamed x45, local copies, waits for them, and re-layouts  6.53 us
  transfers between devices with their start and end apart: 22, of which 13 were waited for; matrix products, arithmetic and copies ran while one was open for 0% of the time, Pallas kernels for 4%

profile of v4, /device:TPU:8, one launch (start us, length us, event | category | flops | bytes accessed | tf_op | source)
XLA Modules:
  0.0 164.5 jit_solution(15790821299613021374)
XLA Ops:
  0.7 3.3 %copy_bitcast_fusion = (f32[2,192,768]{2,1,0:T(8,128)}, f32[2,192,768]{2,1,0:T(8,128)}) fusion(f32[192,2,768]{2,1,0:T(2,128)} %param.14, f32[192,2,768]{2,1,0:T(2,128)} %param.13), kind=kLoop, calls=%fused_computation | loop fusion | bytes 4718592 | tf_op jit(solution)/shard_map/transpose | solution.py:718
  3.9 0.6 pad_add_fusion.where_ref
  4.5 5.5 %scatter.1 = (f32[1024,768]{1,0:T(8,128)}, f32[152,768]{1,0:T(8,128)}, f32[144,768]{1,0:T(8,128)}) custom-call(s32[4]{0:T(128)} %pad_add_fusion.where_ref, s32[2,192]{1,0:T(2,128)} %ef_ref.1, f32[2,192,768]{2,1,0:T(8,128)} %get-tuple-element.43.flow_ref, f32[2,192,768]{2,1,0:T(8,128)} %get-tuple-element.42.weight_ref, s32[192,768]{1,0:T(8,128)} %mask_ref.1), custom_call_target="tpu_custom_call" | custom-call | tf_op jit(solution)/shard_map/scatter/pallas_call | solution.py:692
  10.0 8.6 %collective-permute-start = (f32[152,768]{1,0:T(8,128)}, f32[152,768]{1,0:T(8,128)S(1)}, u32[]{:S(2)}, u32[]{:S(2)}) collective-permute-start(f32[152,768]{1,0:T(8,128)} %get-tuple-element.20), channel_id=1, source_target_pairs={{4,0},{8,4},{12,8},{16,12},{20,16},{24,20},{28,24},{32,28},{36,32}... | collective-permute-start | bytes 1400840 | tf_op jit(solution)/shard_map/ppermute | solution.py:711
  18.6 1.9 %collective-permute-start.1 = (f32[144,768]{1,0:T(8,128)}, f32[144,768]{1,0:T(8,128)S(1)}, u32[]{:S(2)}, u32[]{:S(2)}) collective-permute-start(f32[144,768]{1,0:T(8,128)} %get-tuple-element.21), channel_id=1, source_target_pairs={{0,4},{4,8},{8,12},{12,16},{16,20},{20,24},{24,28},{28,32},{32,36}... | collective-permute-start | bytes 1327112 | tf_op jit(solution)/shard_map/ppermute | solution.py:711
  20.6 6.1 %pose.1 = (f32[256,128]{1,0:T(8,128)}, f32[1536,384]{1,0:T(8,128)}, f32[192,1536]{1,0:T(8,128)}) custom-call(s32[4]{0:T(128)} %pad_add_fusion.where_ref, f32[3,1024]{1,0:T(4,128)} %rotvec_ref.1, f32[3,1024]{1,0:T(4,128)} %trans_ref.1), custom_call_target="tpu_custom_call" | custom-call | tf_op jit(solution)/shard_map/pose/pallas_call | solution.py:692
  26.7 12.3 %collective-permute-done.1.rup_ref = f32[144,768]{1,0:T(8,128)S(1)} collective-permute-done((f32[144,768]{1,0:T(8,128)}, f32[144,768]{1,0:T(8,128)S(1)}, u32[]{:S(2)}, u32[]{:S(2)}) %collective-permute-start.1) | collective-permute-done | bytes 442400 | tf_op jit(solution)/shard_map/ppermute | solution.py:711
  39.0 0.0 collective-permute-done.rdown_ref
  39.0 0.8 copy-done.1
  39.8 0.1 copy-done
  40.0 21.3 %main.1 = (f32[96,256]{1,0:T(8,128)}, f32[96,256]{1,0:T(8,128)}, f32[1536,768]{1,0:T(8,128)}, f32[128,768]{1,0:T(8,128)}, f32[128,768]{1,0:T(8,128)}) custom-call(s32[4]{0:T(128)} %pad_add_fusion.where_ref, f32[1024,768]{1,0:T(8,128)} %get-tuple-element.19.own_ref, f32[152,768]{1,0:T(8,128)} %copy-done, f32[144,768]{1,0:T(8,128)} %copy-done.1, ...), custom_call_target="tpu_custom_call" | custom-call | tf_op jit(solution)/shard_map/main/pallas_call | solution.py:692
  61.3 1.5 collective-permute-done.2
  62.8 0.9 add.12
  63.7 0.0 copy-start.2
  63.7 6.7 %collective-permute-start.5 = (f32[48,256]{1,0:T(8,128)S(1)}, f32[48,256]{1,0:T(8,128)S(1)}, u32[]{:S(2)}, u32[]{:S(2)}) collective-permute-start(f32[48,256]{1,0:T(8,128)S(1)} %get-tuple-element.40), channel_id=1, source_target_pairs={{0,6},{2,4},{4,10},{5,3},{6,8},{7,1},{8,14},{9,7},{10,12},{11,5},{... | collective-permute-start | bytes 147464 | tf_op jit(solution)/shard_map/ppermute | solution.py:753
  70.4 2.5 %collective-permute-start.4 = (f32[48,256]{1,0:T(8,128)S(1)}, f32[48,256]{1,0:T(8,128)S(1)}, u32[]{:S(2)}, u32[]{:S(2)}) collective-permute-start(f32[48,256]{1,0:T(8,128)S(1)} %get-tuple-element.40), channel_id=1, source_target_pairs={{0,4},{2,6},{4,8},{5,1},{6,10},{7,3},{8,12},{9,5},{10,14},{11,7},{... | collective-permute-start | bytes 147464 | tf_op jit(solution)/shard_map/ppermute | solution.py:753
  73.0 0.9 collective-permute-start.3
  73.9 7.3 %collective-permute-done.4.rim_ref = f32[48,256]{1,0:T(8,128)S(1)} collective-permute-done((f32[48,256]{1,0:T(8,128)S(1)}, f32[48,256]{1,0:T(8,128)S(1)}, u32[]{:S(2)}, u32[]{:S(2)}) %collective-permute-start.4) | collective-permute-done | bytes 49184 | tf_op jit(solution)/shard_map/ppermute | solution.py:753
  81.2 0.0 collective-permute-done.3.own2_ref
  81.3 0.6 copy-done.12
  81.8 0.6 copy-done.13
  82.5 1.5 half.1.a_ref
  84.0 1.3 collective-permute-start.8
  85.2 0.9 collective-permute-start.7
  86.1 2.2 %collective-permute-start.6 = (f32[48,256]{1,0:T(8,128)}, f32[48,256]{1,0:T(8,128)S(1)}, u32[]{:S(2)}, u32[]{:S(2)}) collective-permute-start(f32[48,256]{1,0:T(8,128)} %half.1.a_ref), channel_id=1, source_target_pairs={{0,4},{4,0},{8,12},{12,8},{16,20},{20,16},{24,28},{28,24},{32,36},... | collective-permute-start | bytes 147464 | tf_op jit(solution)/shard_map/ppermute | solution.py:762
  88.3 2.0 %collective-permute-done.8.d_ref = f32[48,256]{1,0:T(8,128)S(1)} collective-permute-done((f32[48,256]{1,0:T(8,128)}, f32[48,256]{1,0:T(8,128)S(1)}, u32[]{:S(2)}, u32[]{:S(2)}) %collective-permute-start.8) | collective-permute-done | bytes 49184 | tf_op jit(solution)/shard_map/ppermute | solution.py:762
  90.4 1.1 collective-permute-done.7.c_ref
  91.5 0.6 copy-done.9
  92.1 0.6 copy-done.10
  92.7 1.6 place.1.c_ref
  94.3 5.6 %collective-permute-start.10 = (f32[192,256]{1,0:T(8,128)}, f32[192,256]{1,0:T(8,128)S(1)}, u32[]{:S(2)}, u32[]{:S(2)}) collective-permute-start(f32[192,256]{1,0:T(8,128)} %place.1.c_ref), channel_id=1, source_target_pairs={{16,0},{20,4},{24,8},{28,12},{32,16},{36,20},{40,24},{44,28},{48,3... | collective-permute-start | bytes 589832 | tf_op jit(solution)/shard_map/ppermute | solution.py:711
  99.9 1.9 %collective-permute-start.9 = (f32[192,256]{1,0:T(8,128)}, f32[192,256]{1,0:T(8,128)S(1)}, u32[]{:S(2)}, u32[]{:S(2)}) collective-permute-start(f32[192,256]{1,0:T(8,128)} %place.1.c_ref), channel_id=1, source_target_pairs={{0,16},{4,20},{8,24},{12,28},{16,32},{20,36},{24,40},{28,44},{32,4... | collective-permute-start | bytes 589832 | tf_op jit(solution)/shard_map/ppermute | solution.py:711
  101.8 0.1 collective-permute-start.12
  101.9 1.5 collective-permute-done.10.n_ref
  103.3 0.0 collective-permute-start.13
  103.4 6.4 %collective-permute-done.9.p_ref = f32[192,256]{1,0:T(8,128)S(1)} collective-permute-done((f32[192,256]{1,0:T(8,128)}, f32[192,256]{1,0:T(8,128)S(1)}, u32[]{:S(2)}, u32[]{:S(2)}) %collective-permute-start.9) | collective-permute-done | bytes 196640 | tf_op jit(solution)/shard_map/ppermute | solution.py:711
  109.8 0.0 collective-permute-start.11
  109.8 1.4 collective-permute-done.11.p2_ref
  111.2 0.7 copy-done.7
  111.9 10.9 %first.1 = (f32[1152,256]{1,0:T(8,128)}, f32[1152,128]{1,0:T(8,128)}, f32[480,128]{1,0:T(8,128)}, f32[8,128]{1,0:T(8,128)}) custom-call(s32[4]{0:T(128)} %pad_add_fusion.where_ref, f32[192,256]{1,0:T(8,128)} %copy-done.4, f32[192,256]{1,0:T(8,128)} %place.1.c_ref, f32[192,256]{1,0:T(8,128)} %copy-done.3, f32[192,256]{1,0:T(8,128)} %copy-done.7, ...), custom_call_target="tpu_custom_call" | custom-call | tf_op jit(solution)/shard_map/first/pallas_call | solution.py:692
  122.8 1.9 %collective-permute-start.15 = (f32[8,128]{1,0:T(8,128)}, f32[8,128]{1,0:T(8,128)S(1)}, u32[]{:S(2)}, u32[]{:S(2)}) collective-permute-start(f32[8,128]{1,0:T(8,128)} %get-tuple-element.30.own_ref), channel_id=1, source_target_pairs={{16,0},{20,4},{24,8},{28,12},{32,16},{36,20},{40,24},{44,28},{48,3... | collective-permute-start | bytes 12296 | tf_op jit(solution)/shard_map/ppermute | solution.py:711
  124.8 3.9 %collective-permute-start.14 = (f32[8,128]{1,0:T(8,128)}, f32[8,128]{1,0:T(8,128)S(1)}, u32[]{:S(2)}, u32[]{:S(2)}) collective-permute-start(f32[8,128]{1,0:T(8,128)} %get-tuple-element.30.own_ref), channel_id=1, source_target_pairs={{0,16},{4,20},{8,24},{12,28},{16,32},{20,36},{24,40},{28,44},{32,4... | collective-permute-start | bytes 12296 | tf_op jit(solution)/shard_map/ppermute | solution.py:711
  128.7 0.0 collective-permute-done.15.above_ref
  128.7 3.9 %collective-permute-done.14.below_ref = f32[8,128]{1,0:T(8,128)S(1)} collective-permute-done((f32[8,128]{1,0:T(8,128)}, f32[8,128]{1,0:T(8,128)S(1)}, u32[]{:S(2)}, u32[]{:S(2)}) %collective-permute-start.14) | collective-permute-done | bytes 4128 | tf_op jit(solution)/shard_map/ppermute | solution.py:711
  132.6 0.6 copy-done.18
  133.2 5.4 %second.1 = (f32[8,128]{1,0:T(8,128)}, f32[288,128]{1,0:T(8,128)}) custom-call(f32[1152,256]{1,0:T(8,128)} %get-tuple-element.27.s_ref, f32[1152,128]{1,0:T(8,128)} %get-tuple-element.28.up_ref, f32[480,128]{1,0:T(8,128)} %get-tuple-element.29.v_ref, f32[8,128]{1,0:T(8,128)} %copy-done.18, f32[8,128]{1,0:T(8,128)} %get-tuple-element.30.own_ref, ...), custom_call_target="tpu_custom_call" | custom-call | tf_op jit(solution)/shard_map/second/pallas_call | solution.py:692
  138.6 2.0 %collective-permute-start.17 = (f32[8,128]{1,0:T(8,128)}, f32[8,128]{1,0:T(8,128)S(1)}, u32[]{:S(2)}, u32[]{:S(2)}) collective-permute-start(f32[8,128]{1,0:T(8,128)} %get-tuple-element.31.a_ref), channel_id=1, source_target_pairs={{0,32},{4,36},{8,40},{12,44},{16,48},{20,52},{24,56},{28,60},{32,0... | collective-permute-start | bytes 12296 | tf_op jit(solution)/shard_map/ppermute | solution.py:762
  140.6 2.1 %collective-permute-start.16 = (f32[8,128]{1,0:T(8,128)}, f32[8,128]{1,0:T(8,128)S(1)}, u32[]{:S(2)}, u32[]{:S(2)}) collective-permute-start(f32[8,128]{1,0:T(8,128)} %get-tuple-element.31.a_ref), channel_id=1, source_target_pairs={{0,16},{4,20},{8,24},{12,28},{16,0},{20,4},{24,8},{28,12},{32,48},... | collective-permute-start | bytes 12296 | tf_op jit(solution)/shard_map/ppermute | solution.py:762
  142.7 0.9 collective-permute-done.18.d_ref
  143.6 0.3 collective-permute-done.17.c_ref
  143.9 0.6 collective-permute-done.16.b_ref
  144.5 0.6 copy-done.21
  145.1 1.3 sum.1.a_ref
  146.5 1.6 collective-permute-start.21
  148.0 1.0 collective-permute-start.20
  149.0 1.5 collective-permute-start.19
  150.6 2.8 %collective-permute-done.20.c_ref = f32[8,128]{1,0:T(8,128)S(1)} collective-permute-done((f32[8,128]{1,0:T(8,128)}, f32[8,128]{1,0:T(8,128)S(1)}, u32[]{:S(2)}, u32[]{:S(2)}) %collective-permute-start.20) | collective-permute-done | bytes 4128 | tf_op jit(solution)/shard_map/ppermute | solution.py:762
  153.4 0.6 copy-done.15
  153.9 0.0 copy-done.17
  154.0 3.5 %solve.1.pose_ref = f32[24,128]{1,0:T(8,128)} custom-call(s32[4]{0:T(128)} %pad_add_fusion.where_ref, f32[8,128]{1,0:T(8,128)} %sum.1.a_ref, f32[8,128]{1,0:T(8,128)} %copy-done.17, f32[8,128]{1,0:T(8,128)} %copy-done.15, f32[8,128]{1,0:T(8,128)} %copy-done.14, f32[480,128]{1,0:T(8,128)} %get-tuple-element.29.v_ref, f32[288,128]{1,0:T(8,128)} %get-tuple-element.32.v45_ref), custom_call_target="tpu_custom_call" | custom-call | tf_op jit(solution)/shard_map/solve/pallas_call | solution.py:692
  157.4 0.7 slice_reduce_fusion
  158.1 0.1 reshape_squeeze.3
  158.2 0.7 copy.15
  158.9 5.6 %final.1 = f32[16,768]{1,0:T(8,128)} custom-call(f32[24,128]{1,0:T(8,128)} %solve.1.pose_ref, f32[1536,384]{1,0:T(8,128)} %get-tuple-element.23.b_ref, f32[1536,768]{1,0:T(8,128)} %get-tuple-element.33.g_ref, f32[128,768]{1,0:T(8,128)} %get-tuple-element.34.base_ref, f32[128,768]{1,0:T(8,128)} %get-tuple-element.35.scale_ref), custom_call_target="tpu_custom_call" | custom-call | tf_op jit(solution)/shard_map/final/pallas_call | solution.py:692
  (41 shorter events, 0.1 us)
Async XLA Ops:
  10.0 29.0 %collective-permute-start = (f32[152,768]{1,0:T(8,128)}, f32[152,768]{1,0:T(8,128)S(1)}, u32[]{:S(2)}, u32[]{:S(2)}) collective-permute-start(f32[152,768]{1,0:T(8,128)} %get-tuple-element.20), channel_id=1, source_target_pairs={{4,0},{8,4},{12,8},{16,12},{20,16},{24,20},{28,24},{32,28},{36,32}... | collective-permute-start | bytes 1400840 | tf_op jit(solution)/shard_map/ppermute | solution.py:711
  18.6 20.4 %collective-permute-start.1 = (f32[144,768]{1,0:T(8,128)}, f32[144,768]{1,0:T(8,128)S(1)}, u32[]{:S(2)}, u32[]{:S(2)}) collective-permute-start(f32[144,768]{1,0:T(8,128)} %get-tuple-element.21), channel_id=1, source_target_pairs={{0,4},{4,8},{8,12},{12,16},{16,20},{20,24},{24,28},{28,32},{32,36}... | collective-permute-start | bytes 1327112 | tf_op jit(solution)/shard_map/ppermute | solution.py:711
  39.0 0.8 copy-start.1
  39.0 0.9 copy-start
  61.3 1.5 collective-permute-start.2
  63.7 17.5 %copy-start.2 = (f32[48,256]{1,0:T(8,128)}, f32[48,256]{1,0:T(8,128)S(1)}, u32[]{:S(2)}) copy-start(f32[48,256]{1,0:T(8,128)S(1)} %get-tuple-element.41.own_ref) | copy-start | bytes 147460
  63.7 10.2 %collective-permute-start.5 = (f32[48,256]{1,0:T(8,128)S(1)}, f32[48,256]{1,0:T(8,128)S(1)}, u32[]{:S(2)}, u32[]{:S(2)}) collective-permute-start(f32[48,256]{1,0:T(8,128)S(1)} %get-tuple-element.40), channel_id=1, source_target_pairs={{0,6},{2,4},{4,10},{5,3},{6,8},{7,1},{8,14},{9,7},{10,12},{11,5},{... | collective-permute-start | bytes 147464 | tf_op jit(solution)/shard_map/ppermute | solution.py:753
  70.4 10.8 %collective-permute-start.4 = (f32[48,256]{1,0:T(8,128)S(1)}, f32[48,256]{1,0:T(8,128)S(1)}, u32[]{:S(2)}, u32[]{:S(2)}) collective-permute-start(f32[48,256]{1,0:T(8,128)S(1)} %get-tuple-element.40), channel_id=1, source_target_pairs={{0,4},{2,6},{4,8},{5,1},{6,10},{7,3},{8,12},{9,5},{10,14},{11,7},{... | collective-permute-start | bytes 147464 | tf_op jit(solution)/shard_map/ppermute | solution.py:753
  73.0 8.3 %collective-permute-start.3 = (f32[48,256]{1,0:T(8,128)S(1)}, f32[48,256]{1,0:T(8,128)S(1)}, u32[]{:S(2)}, u32[]{:S(2)}) collective-permute-start(f32[48,256]{1,0:T(8,128)S(1)} %get-tuple-element.41.own_ref), channel_id=1, source_target_pairs={{0,2},{1,3},{2,0},{3,1},{4,6},{5,7},{6,4},{7,5},{8,10},{9,11},{10,... | collective-permute-start | bytes 147464 | tf_op jit(solution)/shard_map/ppermute | solution.py:755
  73.9 7.3 %copy-start.11 = (f32[48,256]{1,0:T(8,128)}, f32[48,256]{1,0:T(8,128)S(1)}, u32[]{:S(2)}) copy-start(f32[48,256]{1,0:T(8,128)S(1)} %collective-permute-done.5.rim2_ref) | copy-start | bytes 147460
  81.2 0.6 copy-start.12
  81.8 0.6 copy-start.13
  84.0 6.4 %collective-permute-start.8 = (f32[48,256]{1,0:T(8,128)}, f32[48,256]{1,0:T(8,128)S(1)}, u32[]{:S(2)}, u32[]{:S(2)}) collective-permute-start(f32[48,256]{1,0:T(8,128)} %half.1.a_ref), channel_id=1, source_target_pairs={{0,12},{4,8},{8,4},{12,0},{16,28},{20,24},{24,20},{28,16},{32,44},... | collective-permute-start | bytes 147464 | tf_op jit(solution)/shard_map/ppermute | solution.py:762
  85.2 6.3 %collective-permute-start.7 = (f32[48,256]{1,0:T(8,128)}, f32[48,256]{1,0:T(8,128)S(1)}, u32[]{:S(2)}, u32[]{:S(2)}) collective-permute-start(f32[48,256]{1,0:T(8,128)} %half.1.a_ref), channel_id=1, source_target_pairs={{0,8},{4,12},{8,0},{12,4},{16,24},{20,28},{24,16},{28,20},{32,40},... | collective-permute-start | bytes 147464 | tf_op jit(solution)/shard_map/ppermute | solution.py:762
  86.1 5.4 %collective-permute-start.6 = (f32[48,256]{1,0:T(8,128)}, f32[48,256]{1,0:T(8,128)S(1)}, u32[]{:S(2)}, u32[]{:S(2)}) collective-permute-start(f32[48,256]{1,0:T(8,128)} %half.1.a_ref), channel_id=1, source_target_pairs={{0,4},{4,0},{8,12},{12,8},{16,20},{20,16},{24,28},{28,24},{32,36},... | collective-permute-start | bytes 147464 | tf_op jit(solution)/shard_map/ppermute | solution.py:762
  90.4 1.1 copy-start.8
  91.5 0.6 copy-start.9
  92.1 0.6 copy-start.10
  94.3 9.1 %collective-permute-start.10 = (f32[192,256]{1,0:T(8,128)}, f32[192,256]{1,0:T(8,128)S(1)}, u32[]{:S(2)}, u32[]{:S(2)}) collective-permute-start(f32[192,256]{1,0:T(8,128)} %place.1.c_ref), channel_id=1, source_target_pairs={{16,0},{20,4},{24,8},{28,12},{32,16},{36,20},{40,24},{44,28},{48,3... | collective-permute-start | bytes 589832 | tf_op jit(solution)/shard_map/ppermute | solution.py:711
  99.9 9.9 %collective-permute-start.9 = (f32[192,256]{1,0:T(8,128)}, f32[192,256]{1,0:T(8,128)S(1)}, u32[]{:S(2)}, u32[]{:S(2)}) collective-permute-start(f32[192,256]{1,0:T(8,128)} %place.1.c_ref), channel_id=1, source_target_pairs={{0,16},{4,20},{8,24},{12,28},{16,32},{20,36},{24,40},{28,44},{32,4... | collective-permute-start | bytes 589832 | tf_op jit(solution)/shard_map/ppermute | solution.py:711
  101.8 8.0 %collective-permute-start.12 = (f32[192,256]{1,0:T(8,128)}, f32[192,256]{1,0:T(8,128)S(1)}, u32[]{:S(2)}, u32[]{:S(2)}) collective-permute-start(f32[192,256]{1,0:T(8,128)} %place.1.c_ref), channel_id=1, source_target_pairs={{0,1},{1,0},{2,3},{3,2},{4,5},{5,4},{6,7},{7,6},{8,9},{9,8},{10,11... | collective-permute-start | bytes 589832 | tf_op jit(solution)/shard_map/ppermute | solution.py:766
  103.3 7.8 %copy-start.3 = (f32[192,256]{1,0:T(8,128)}, f32[192,256]{1,0:T(8,128)S(1)}, u32[]{:S(2)}) copy-start(f32[192,256]{1,0:T(8,128)S(1)} %collective-permute-done.10.n_ref) | copy-start | bytes 589828
  103.3 6.4 %collective-permute-start.13 = (f32[192,256]{1,0:T(8,128)S(1)}, f32[192,256]{1,0:T(8,128)S(1)}, u32[]{:S(2)}, u32[]{:S(2)}) collective-permute-start(f32[192,256]{1,0:T(8,128)S(1)} %collective-permute-done.10.n_ref), channel_id=1, source_target_pairs={{0,1},{1,0},{2,3},{3,2},{4,5},{5,4},{6,7},{7,6},{8,9},{9,8},{10,11... | collective-permute-start | bytes 589832 | tf_op jit(solution)/shard_map/ppermute | solution.py:766
  109.7 1.4 copy-start.4
  109.8 1.4 collective-permute-start.11
  109.8 1.4 copy-start.5
  109.8 1.4 copy-start.6
  111.2 0.7 copy-start.7
  122.8 5.8 %collective-permute-start.15 = (f32[8,128]{1,0:T(8,128)}, f32[8,128]{1,0:T(8,128)S(1)}, u32[]{:S(2)}, u32[]{:S(2)}) collective-permute-start(f32[8,128]{1,0:T(8,128)} %get-tuple-element.30.own_ref), channel_id=1, source_target_pairs={{16,0},{20,4},{24,8},{28,12},{32,16},{36,20},{40,24},{44,28},{48,3... | collective-permute-start | bytes 12296 | tf_op jit(solution)/shard_map/ppermute | solution.py:711
  124.8 7.8 %collective-permute-start.14 = (f32[8,128]{1,0:T(8,128)}, f32[8,128]{1,0:T(8,128)S(1)}, u32[]{:S(2)}, u32[]{:S(2)}) collective-permute-start(f32[8,128]{1,0:T(8,128)} %get-tuple-element.30.own_ref), channel_id=1, source_target_pairs={{0,16},{4,20},{8,24},{12,28},{16,32},{20,36},{24,40},{28,44},{32,4... | collective-permute-start | bytes 12296 | tf_op jit(solution)/shard_map/ppermute | solution.py:711
  128.7 3.9 %copy-start.16 = (f32[8,128]{1,0:T(8,128)}, f32[8,128]{1,0:T(8,128)S(1)}, u32[]{:S(2)}) copy-start(f32[8,128]{1,0:T(8,128)S(1)} %collective-permute-done.15.above_ref) | copy-start | bytes 12292
  132.6 0.6 copy-start.18
  138.6 5.0 %collective-permute-start.18 = (f32[8,128]{1,0:T(8,128)}, f32[8,128]{1,0:T(8,128)S(1)}, u32[]{:S(2)}, u32[]{:S(2)}) collective-permute-start(f32[8,128]{1,0:T(8,128)} %get-tuple-element.31.a_ref), channel_id=1, source_target_pairs={{0,48},{4,52},{8,56},{12,60},{16,32},{20,36},{24,40},{28,44},{32,1... | collective-permute-start | bytes 12296 | tf_op jit(solution)/shard_map/ppermute | solution.py:762
  138.6 5.3 %collective-permute-start.17 = (f32[8,128]{1,0:T(8,128)}, f32[8,128]{1,0:T(8,128)S(1)}, u32[]{:S(2)}, u32[]{:S(2)}) collective-permute-start(f32[8,128]{1,0:T(8,128)} %get-tuple-element.31.a_ref), channel_id=1, source_target_pairs={{0,32},{4,36},{8,40},{12,44},{16,48},{20,52},{24,56},{28,60},{32,0... | collective-permute-start | bytes 12296 | tf_op jit(solution)/shard_map/ppermute | solution.py:762
  140.6 4.0 %collective-permute-start.16 = (f32[8,128]{1,0:T(8,128)}, f32[8,128]{1,0:T(8,128)S(1)}, u32[]{:S(2)}, u32[]{:S(2)}) collective-permute-start(f32[8,128]{1,0:T(8,128)} %get-tuple-element.31.a_ref), channel_id=1, source_target_pairs={{0,16},{4,20},{8,24},{12,28},{16,0},{20,4},{24,8},{28,12},{32,48},... | collective-permute-start | bytes 12296 | tf_op jit(solution)/shard_map/ppermute | solution.py:762
  143.6 0.9 copy-start.19
  143.9 0.6 copy-start.20
  144.5 0.6 copy-start.21
  146.5 4.1 %collective-permute-start.21 = (f32[8,128]{1,0:T(8,128)}, f32[8,128]{1,0:T(8,128)S(1)}, u32[]{:S(2)}, u32[]{:S(2)}) collective-permute-start(f32[8,128]{1,0:T(8,128)} %sum.1.a_ref), channel_id=1, source_target_pairs={{0,192},{4,196},{8,200},{12,204},{16,208},{20,212},{24,216},{28,22... | collective-permute-start | bytes 12296 | tf_op jit(solution)/shard_map/ppermute | solution.py:762
  148.0 5.3 %collective-permute-start.20 = (f32[8,128]{1,0:T(8,128)}, f32[8,128]{1,0:T(8,128)S(1)}, u32[]{:S(2)}, u32[]{:S(2)}) collective-permute-start(f32[8,128]{1,0:T(8,128)} %sum.1.a_ref), channel_id=1, source_target_pairs={{0,128},{4,132},{8,136},{12,140},{16,144},{20,148},{24,152},{28,15... | collective-permute-start | bytes 12296 | tf_op jit(solution)/shard_map/ppermute | solution.py:762
  149.0 4.3 %collective-permute-start.19 = (f32[8,128]{1,0:T(8,128)}, f32[8,128]{1,0:T(8,128)S(1)}, u32[]{:S(2)}, u32[]{:S(2)}) collective-permute-start(f32[8,128]{1,0:T(8,128)} %sum.1.a_ref), channel_id=1, source_target_pairs={{0,64},{4,68},{8,72},{12,76},{16,80},{20,84},{24,88},{28,92},{32,9... | collective-permute-start | bytes 12296 | tf_op jit(solution)/shard_map/ppermute | solution.py:762
  150.6 2.8 %copy-start.14 = (f32[8,128]{1,0:T(8,128)}, f32[8,128]{1,0:T(8,128)S(1)}, u32[]{:S(2)}) copy-start(f32[8,128]{1,0:T(8,128)S(1)} %collective-permute-done.21.d_ref) | copy-start | bytes 12292
  153.4 0.6 copy-start.15
  153.4 0.6 copy-start.17

commit v5 on v4

--- a/solution.py
+++ b/solution.py
@@ -162,10 +162,131 @@
         bt_ref[144:192, cols] = above[0:48]
 
 
+def coords(first, chunk):
+    pixel = first + chunk * LANES + iota((8, LANES), 1)
+    col = ((pixel & (COLS - 1)).astype(F32) - 0.5 * (COLS - 1)) / COLS
+    line = ((pixel >> 6).astype(F32) - 0.5 * (ROWS - 1)) / COLS
+    return col, line
+
+
+def pull(u, v, s, uv, u1, v1, pu, pv):
+    spu = s * pu
+    spv = s * pv
+    return (
+        spu,
+        spv,
+        -(u * spu + v * spv),
+        -(uv * pu) - v1 * pv,
+        u1 * pu + uv * pv,
+        u * pv - v * pu,
+    )
+
+
+def pose_sums(u, v, s, cu, cv, eu, ev):
+    uv = u * v
+    u1 = 1.0 + u * u
+    v1 = 1.0 + v * v
+    terms = list(pull(u, v, s, uv, u1, v1, -eu, -ev))
+    su_ = cu * s
+    sv_ = cv * s
+    ju = (-uv, u1, -v)
+    jv = (-v1, uv, u)
+    a00 = su_ * s
+    a11 = sv_ * s
+    a02 = -(a00 * u)
+    a12 = -(a11 * v)
+    terms += [a00, a11, a02, a12, -(a02 * u + a12 * v)]
+    tu = [su_ * x for x in ju]
+    tv = [sv_ * x for x in jv]
+    terms += tu + tv
+    terms += [-(u * x + v * y) for x, y in zip(tu, tv)]
+    wu = [cu * x for x in ju]
+    wv = [cv * x for x in jv]
+    for a in range(3):
+        for b in range(a, 3):
+            terms.append(wu[a] * ju[b] + wv[a] * jv[b])
+    return terms
+
+
+def diagonal_rows(acc, h):
+    lane = iota((8, LANES), 1)
+    row = iota((8, LANES), 0)
+    sums = [jnp.broadcast_to(jnp.sum(x, axis=1, keepdims=True), (8, LANES)) for x in acc]
+    a = {(0, 0): 6, (1, 1): 7, (0, 2): 8, (1, 2): 9, (2, 2): 10}
+    for k in range(3):
+        a[(0, 3 + k)] = 11 + k
+        a[(1, 3 + k)] = 14 + k
+        a[(2, 3 + k)] = 17 + k
+    at = 20
+    for x in range(3):
+        for y in range(x, 3):
+            a[(3 + x, 3 + y)] = at
+            at += 1
+    tiles = []
+    for c in range(6):
+        tile = jnp.where(lane == LANES - 1, sums[c], 0.0)
+        for d in range(6):
+            key = (min(c, d), max(c, d))
+            if key != (0, 1):
+                tile = jnp.where(lane == d * SLOTS + 8 * h + row, sums[a[key]], tile)
+        tiles.append(tile)
+    return tiles
+
+
+def early_kernel(
+    where_ref, own_ref, depth_ref, tab_ref, geo_ref, curv_ref, grad_ref, block_ref, in_ref
+):
+    plocal = depth_ref.shape[1]
+    chunks = plocal // LANES
+    for f in range(FD):
+        in_ref[f * 8 : f * 8 + 8, :] = jnp.broadcast_to(depth_ref[f : f + 1, :], (8, plocal))
+
+    def frame(f, carry):
+        eight = pl.ds(pl.multiple_of(f * 8, 8), 8)
+        for h in range(2):
+            tab = tab_ref[pl.ds(pl.multiple_of(f * SLOTS + 8 * h, 8), 8), :]
+            r = [jnp.broadcast_to(tab[:, k : k + 1], (8, LANES)) for k in range(12)]
+            acc = [0.0] * 26
+            for c in range(chunks):
+                lanes = pl.ds(c * LANES, LANES)
+                col, line = coords(where_ref[1], c)
+                depth = in_ref[eight, lanes]
+
+                def at(q):
+                    return pl.ds(pl.multiple_of(q * 256 + f * SLOTS + 8 * h, 8), 8)
+
+                cu, cv, fu, fv = [own_ref[at(q), lanes] for q in range(4)]
+                inv = 1.0 / (r[6] * col + r[7] * line + r[8] + depth * r[11])
+                u = (r[0] * col + r[1] * line + r[2] + depth * r[9]) * inv
+                v = (r[3] * col + r[4] * line + r[5] + depth * r[10]) * inv
+                su = inv * (r[9] - u * r[11])
+                sv = inv * (r[10] - v * r[11])
+                eu = cu * (col - u) + fu
+                ev = cv * (line - v) + fv
+                au = cu * su
+                av = cv * sv
+                curv = au * su + av * sv
+                grad = -(su * eu + sv * ev)
+                if h:
+                    curv = curv + curv_ref[eight, lanes]
+                    grad = grad + grad_ref[eight, lanes]
+                curv_ref[eight, lanes] = curv
+                grad_ref[eight, lanes] = grad
+                for q, x in enumerate((u, v, inv, au, av)):
+                    geo_ref[at(q), lanes] = x
+                acc = [x + y for x, y in zip(acc, pose_sums(u, v, depth * inv, cu, cv, eu, ev))]
+            for c, tile in enumerate(diagonal_rows(acc, h)):
+                block_ref[pl.ds(pl.multiple_of(f * GROUP + c * SLOTS + 8 * h, 8), 8), :] = tile
+        return carry
+
+    lax.fori_loop(0, FD, frame, 0)
+
+
 def main_kernel(
-    where_ref, own_ref, rdown_ref, rup_ref, depth_ref, damp_ref, tab_ref, b_ref, bt_ref,
+    where_ref, rdown_ref, rup_ref, geo_ref, curv_ref, grad_ref, block_ref, depth_ref, damp_ref, tab_ref,
+    b_ref, bt_ref,
     keep_ref, send_ref, g_ref, base_ref, scale_ref,
-    half_ref, geo_ref, hi_ref, in_ref, q_ref, w_ref, t_ref,
+    half_ref, hi_ref, in_ref, q_ref, w_ref, t_ref,
 ):
     core = where_ref[2]
     plocal = depth_ref.shape[1]
@@ -176,167 +297,93 @@
         base = j * (j + 1) // 2
         for q in range(4):
             if f < 8:
-                extra = jnp.where(row8 <= j, rup_ref[q * SIDE + base : q * SIDE + base + 8, :], 0.0)
-                at = q * 256 + f * SLOTS
+                first = q * SIDE + base
+                extra = jnp.where(row8 <= j, rup_ref[first : first + 8, :], 0.0)
             else:
                 first = 8 + q * SIDE + base - 7 + j
                 extra = jnp.where(row8 >= 7 - j, rdown_ref[first : first + 8, :], 0.0)
-                at = q * 256 + f * SLOTS + 8
-            half_ref[(q * FD + f) * 8 : (q * FD + f + 1) * 8, :] = own_ref[at : at + 8, :] + extra
+            half_ref[(q * FD + f) * 8 : (q * FD + f + 1) * 8, :] = extra
         in_ref[f * 8 : f * 8 + 8, :] = jnp.broadcast_to(depth_ref[f : f + 1, :], (8, plocal))
         in_ref[128 + f * 8 : 136 + f * 8, :] = jnp.broadcast_to(damp_ref[f : f + 1, :], (8, plocal))
     lane = iota((8, LANES), 1)
-    row = iota((8, LANES), 0)
 
     def frame(f, carry, merged):
         eight = pl.ds(pl.multiple_of(f * 8, 8), 8)
-        def conf(q, h, lanes):
-            if h == merged:
-                at = (q * FD + f) * 8
-                return half_ref[pl.ds(pl.multiple_of(at, 8), 8), lanes]
-            at = q * 256 + f * SLOTS + 8 * h
-            return own_ref[pl.ds(pl.multiple_of(at, 8), 8), lanes]
-
-        params = []
-        for h in range(2):
-            tab = tab_ref[pl.ds(pl.multiple_of(f * SLOTS + 8 * h, 8), 8), :]
-            params.append([jnp.broadcast_to(tab[:, k : k + 1], (8, LANES)) for k in range(12)])
-        base_all = []
-        scale_all = []
+        tab = tab_ref[pl.ds(pl.multiple_of(f * SLOTS + 8 * merged, 8), 8), :]
+        t0, t1, t2 = [jnp.broadcast_to(tab[:, k : k + 1], (8, LANES)) for k in (9, 10, 11)]
+        acc = [0.0] * 26
         for c in range(chunks):
             lanes = pl.ds(c * LANES, LANES)
-            pixel = where_ref[1] + c * LANES + lane
-            col = ((pixel & (COLS - 1)).astype(F32) - 0.5 * (COLS - 1)) / COLS
-            line = ((pixel >> 6).astype(F32) - 0.5 * (ROWS - 1)) / COLS
+            col, line = coords(where_ref[1], c)
             depth = in_ref[eight, lanes]
-            curv = 0.0
-            grad = 0.0
-            for h in range(2):
-                r = params[h]
-                z = r[6] * col + r[7] * line + r[8] + depth * r[11]
-                inv = 1.0 / z
-                u = (r[0] * col + r[1] * line + r[2] + depth * r[9]) * inv
-                v = (r[3] * col + r[4] * line + r[5] + depth * r[10]) * inv
-                s = depth * inv
-                su = inv * (r[9] - u * r[11])
-                sv = inv * (r[10] - v * r[11])
-                cu = conf(0, h, lanes)
-                cv = conf(1, h, lanes)
-                eu = cu * (col - u) + conf(2, h, lanes)
-                ev = cv * (line - v) + conf(3, h, lanes)
-                au = cu * su
-                av = cv * sv
-                curv = curv + au * su + av * sv
-                grad = grad - (su * eu + sv * ev)
-                for k, x in enumerate((u, v, s, au, av, eu, ev)):
-                    geo_ref[k * 16 + 8 * h : k * 16 + 8 * h + 8, lanes] = x
-            damp = in_ref[pl.ds(pl.multiple_of(128 + f * 8, 8), 8), lanes]
-            total = damp + jnp.sum(curv, axis=0, keepdims=True)
+
+            def geo(q, h):
+                return geo_ref[pl.ds(pl.multiple_of(q * 256 + f * SLOTS + 8 * h, 8), 8), lanes]
+
+            cu, cv, fu, fv = [
+                half_ref[pl.ds(pl.multiple_of((q * FD + f) * 8, 8), 8), lanes] for q in range(4)
+            ]
+            u, v, inv = [geo(q, merged) for q in range(3)]
+            su = inv * (t0 - u * t2)
+            sv = inv * (t1 - v * t2)
+            eu = cu * (col - u) + fu
+            ev = cv * (line - v) + fv
+            au = cu * su
+            av = cv * sv
+            acc = [x + y for x, y in zip(acc, pose_sums(u, v, depth * inv, cu, cv, eu, ev))]
+            curv = curv_ref[eight, lanes] + (au * su + av * sv)
+            grad = grad_ref[eight, lanes] - (su * eu + sv * ev)
+            total = in_ref[pl.ds(pl.multiple_of(128 + f * 8, 8), 8), lanes] + jnp.sum(
+                curv, axis=0, keepdims=True
+            )
             base = jnp.sum(grad, axis=0, keepdims=True) / total
-            scale = 1.0 / jnp.sqrt(total)
+            root = jnp.sqrt(total)
+            scale = 1.0 / root
             base_ref[eight, lanes] = base
             scale_ref[eight, lanes] = scale
-            base_all.append(base)
-            scale_all.append(scale)
-        cols = {}
-        for h in range(2):
-            acc = [0.0] * 27
-            for c in range(chunks):
-                lanes = pl.ds(c * LANES, LANES)
-                u, v, s, au, av, eu, ev = [
-                    geo_ref[k * 16 + 8 * h : k * 16 + 8 * h + 8, lanes] for k in range(7)
-                ]
-                cu = conf(0, h, lanes)
-                cv = conf(1, h, lanes)
-                base = base_all[c]
-                scale = scale_all[c]
-                hu = -eu - au * base
-                hv = -ev - av * base
-                uv = u * v
-                u1 = 1.0 + u * u
-                v1 = 1.0 + v * v
-
-                def pull(pu, pv):
-                    spu = s * pu
-                    spv = s * pv
-                    return (
-                        spu,
-                        spv,
-                        -(u * spu + v * spv),
-                        -(uv * pu) - v1 * pv,
-                        u1 * pu + uv * pv,
-                        u * pv - v * pu,
-                    )
-
-                for k, x in enumerate(pull(au * scale, av * scale)):
-                    at = pl.ds(pl.multiple_of(f * GROUP + k * SLOTS + 8 * h, 8), 8)
-                    g_ref[at, lanes] = x
+            lifted = base * root
+            hi_ref[GROUP : GROUP + 8, lanes] = lifted
+            hi_ref[GROUP + 8 : GROUP + 16, lanes] = lifted - lifted.astype(BF16).astype(F32)
+            for h in range(2):
+                if h != merged:
+                    u, v, inv = [geo(q, h) for q in range(3)]
+                    gu, gv = geo(3, h), geo(4, h)
+                else:
+                    u, v, inv = [geo(q, h) for q in range(3)]
+                    gu, gv = geo(3, h) + au, geo(4, h) + av
+                rows = pull(
+                    u, v, depth * inv, u * v, 1.0 + u * u, 1.0 + v * v, gu * scale, gv * scale
+                )
+                for k, x in enumerate(rows):
+                    g_ref[pl.ds(pl.multiple_of(f * GROUP + k * SLOTS + 8 * h, 8), 8), lanes] = x
                     hi_ref[k * SLOTS + 8 * h : k * SLOTS + 8 * h + 8, lanes] = x
-                su_ = cu * s
-                sv_ = cv * s
-                ju = (None, None, None, -uv, u1, -v)
-                jv = (None, None, None, -v1, uv, u)
-                terms = list(pull(hu, hv))
-                a00 = su_ * s
-                a11 = sv_ * s
-                a02 = -(a00 * u)
-                a12 = -(a11 * v)
-                a22 = -(a02 * u + a12 * v)
-                terms += [a00, a11, a02, a12, a22]
-                tu = [su_ * ju[k] for k in (3, 4, 5)]
-                tv = [sv_ * jv[k] for k in (3, 4, 5)]
-                terms += tu + tv
-                terms += [-(u * tu[k] + v * tv[k]) for k in range(3)]
-                wu = [cu * ju[k] for k in (3, 4, 5)]
-                wv = [cv * jv[k] for k in (3, 4, 5)]
-                for a in range(3):
-                    for b in range(a, 3):
-                        terms.append(wu[a] * ju[3 + b] + wv[a] * jv[3 + b])
-                acc = [x + y for x, y in zip(acc, terms)]
-            assert len(acc) == len(terms)
-            sums = [jnp.sum(x, axis=1, keepdims=True) for x in acc]
-            a = {(0, 0): sums[6], (1, 1): sums[7], (0, 2): sums[8], (1, 2): sums[9], (2, 2): sums[10]}
-            for k in range(3):
-                a[(0, 3 + k)] = sums[11 + k]
-                a[(1, 3 + k)] = sums[14 + k]
-                a[(2, 3 + k)] = sums[17 + k]
-            at = 20
-            for x in range(3):
-                for y in range(x, 3):
-                    a[(3 + x, 3 + y)] = sums[at]
-                    at += 1
-            for c in range(6):
-                block = jnp.zeros((8, LANES), F32)
-                for d in range(6):
-                    key = (min(c, d), max(c, d))
-                    if key == (0, 1):
-                        continue
-                    block = jnp.where(
-                        lane == d * SLOTS + 8 * h + row, jnp.broadcast_to(a[key], (8, LANES)), block
-                    )
-                q_ref[c * SLOTS + 8 * h : c * SLOTS + 8 * h + 8, :] = block
-                cols[(c, h)] = sums[c]
+        rows = pl.ds(pl.multiple_of(f * GROUP, 8), GROUP)
+        q_ref[...] = block_ref[rows, :]
+        for c, tile in enumerate(diagonal_rows(acc, merged)):
+            at = slice(c * SLOTS + 8 * merged, c * SLOTS + 8 * merged + 8)
+            q_ref[at, :] = q_ref[at, :] + tile
         g = hi_ref[...]
         top, low = pair_of(g)
         both = lax.dot_general(
-            jnp.concatenate([top, low], axis=0), top, (((1,), (1,)), ((), ())),
+            jnp.concatenate([top[0:GROUP], low[0:GROUP]], axis=0), top, (((1,), (1,)), ((), ())),
             preferred_element_type=F32,
         )
-        m = both[0:GROUP] + both[GROUP:] + both[GROUP:].T
+        m = both[0:GROUP, 0:GROUP] + both[GROUP:, 0:GROUP] + both[GROUP:, 0:GROUP].T
+        vec = q_ref[:, LANES - 1 : LANES] - (
+            both[0:GROUP, GROUP : GROUP + 1]
+            + both[GROUP:, GROUP : GROUP + 1]
+            + both[0:GROUP, GROUP + 8 : GROUP + 9]
+        )
         q = q_ref[:, 0:GROUP] - m
-        rows = pl.ds(pl.multiple_of(f * GROUP, 8), GROUP)
         q_top, q_low = pair_of(q)
         b_top, b_low = pair_of(b_ref[rows, :])
         both = dot(jnp.concatenate([q_top, q_low], axis=0), b_top)
-        w_ref[rows, :] = both[0:GROUP] + both[GROUP:]
-        own_group = slice(LANES, 2 * LANES)
-        w_ref[rows, own_group] = w_ref[rows, own_group] + dot(q_top, b_low[:, own_group])
-        for c in range(6):
-            for h in range(2):
-                at = pl.ds(pl.multiple_of(f * GROUP + c * SLOTS + 8 * h, 8), 8)
-                w_ref[at, 0:LANES] = jnp.where(
-                    lane == LANES - 1, jnp.broadcast_to(cols[(c, h)], (8, LANES)), w_ref[at, 0:LANES]
-                )
+        w = both[0:GROUP] + both[GROUP:]
+        w_ref[rows, 0:LANES] = jnp.where(
+            iota((GROUP, LANES), 1) == LANES - 1, jnp.broadcast_to(vec, (GROUP, LANES)), w[:, 0:LANES]
+        )
+        w_ref[rows, LANES : 2 * LANES] = w[:, LANES : 2 * LANES] + dot(q_top, b_low[:, LANES : 2 * LANES])
+        w_ref[rows, 2 * LANES :] = w[:, 2 * LANES :]
         return carry
 
     lax.fori_loop(0, 8, functools.partial(frame, merged=0), 0)
@@ -607,7 +654,16 @@
     put(out_ref, gather_sum((a_ref, b_ref, c_ref, d_ref)))
 
 
-def solve_kernel(where_ref, a_ref, b_ref, c_ref, d_ref, v_ref, v45_ref, out_ref):
+def solve_kernel(
+    where_ref, a_ref, b_ref, c_ref, d_ref, v_ref, v45_ref, base_ref, scale_ref, move_hbm, g_hbm,
+    pose_ref, out_ref, sum_ref, move_ref, g_ref, sems,
+):
+    copies = [
+        pltpu.make_async_copy(move_hbm, move_ref, sems.at[0]),
+        pltpu.make_async_copy(g_hbm, g_ref, sems.at[1]),
+    ]
+    for copy in copies:
+        copy.start()
     at_quad = where_ref[3]
     total = gather_sum((a_ref, b_ref, c_ref, d_ref))
     shape = (8, LANES)
@@ -648,6 +704,7 @@
         y = add(x, mul(beta, y))
         now = fresh
     xc = [tuple(p[1:2, LANES - 1 - k : LANES - k] for p in found) for k in range(ITERS)]
+    poses = []
     for g in range(3):
         acc = None
         for k in range(ITERS):
@@ -656,26 +713,26 @@
             wide = tuple(jnp.broadcast_to(x, (1, LANES)) for x in xc[k])
             term = mul(wide, (tile[0:1], tile[1:2]))
             acc = term if acc is None else plus(acc, term)
-        out_ref[g * 8 : g * 8 + 8, :] = jnp.broadcast_to(
-            (acc[0] + acc[1]) * (SHRINK / FIRST), (8, LANES)
-        )
-
-
-def final_kernel(pose_ref, b_ref, g_ref, base_ref, scale_ref, out_ref, sum_ref):
-    x0 = pose_ref[0:1, :]
-    x1 = pose_ref[8:9, :]
-    x2 = pose_ref[16:17, :]
+        poses.append((acc[0] + acc[1]) * (SHRINK / FIRST))
+    column = to_column(poses[1])
+    r = iota((GROUP, LANES), 0)
+    l = iota((GROUP, LANES), 1)
+    for c in range(6):
+        line = jnp.sum(jnp.where(r == l * 6 + c, column, 0.0), axis=0, keepdims=True)
+        pose_ref[c : c + 1, :] = line[:, 0:FD]
+    for copy in copies:
+        copy.wait()
 
     def frame(f, carry):
         rows = pl.ds(pl.multiple_of(f * GROUP, 8), GROUP)
         prod = (
-            b_ref[rows, 0:LANES] * x0
-            + b_ref[rows, LANES : 2 * LANES] * x1
-            + b_ref[rows, 2 * LANES : 3 * LANES] * x2
+            move_ref[rows, 0:LANES] * poses[0]
+            + move_ref[rows, LANES : 2 * LANES] * poses[1]
+            + move_ref[rows, 2 * LANES : 3 * LANES] * poses[2]
         )
         x = jnp.sum(prod, axis=1, keepdims=True)
         image = jnp.sum(g_ref[rows, :] * x, axis=0, keepdims=True)
-        at = pl.ds(pl.multiple_of(f * 8, 8), 8)
+        at = tile_at(f)
         sum_ref[at, :] = base_ref[at, :] - scale_ref[at, :] * image
         return carry
 
@@ -686,14 +743,15 @@
 
 SMEM = pl.BlockSpec(memory_space=pltpu.SMEM)
 VMEM = pl.BlockSpec(memory_space=pltpu.VMEM)
-
-
-def call(kernel, name, outs, smem, *args, scratch=()):
+ANY = pl.BlockSpec(memory_space=pl.ANY)
+
+
+def call(kernel, name, outs, smem, *args, scratch=(), hbm=0):
     return pl.pallas_call(
         kernel,
         name=name,
         out_shape=[jax.ShapeDtypeStruct(s, F32) for s in outs],
-        in_specs=[SMEM] * smem + [VMEM] * (len(args) - smem),
+        in_specs=[SMEM] * smem + [VMEM] * (len(args) - smem - hbm) + [ANY] * hbm,
         out_specs=[VMEM] * len(outs),
         scratch_shapes=list(scratch),
     )(*args)
@@ -724,14 +782,19 @@
         [(f_dev * SLOTS, LANES), (f_dev * GROUP, 3 * LANES), (192, f_dev * GROUP)],
         1, spot, rotvec, trans,
     )
+    pairs = f_dev * SLOTS
+    geo, curv, grad, block = call(
+        early_kernel, "early",
+        [(5 * pairs, plocal), (f_dev * 8, plocal), (f_dev * 8, plocal), (f_dev * GROUP, LANES)],
+        1, spot, own, inv_depth, tab, scratch=[pltpu.VMEM((f_dev * 8, plocal), F32)],
+    )
     keep, send, g, base, scale = call(
         main_kernel, "main",
         [(96, 256), (96, 256), (f_dev * GROUP, plocal), (f_dev * 8, plocal), (f_dev * 8, plocal)],
-        1, spot, own, from_after, from_before, inv_depth, depth_damping, tab, b, bt,
+        1, spot, from_after, from_before, geo, curv, grad, block, inv_depth, depth_damping, tab, b, bt,
         scratch=[
             pltpu.VMEM((4 * FD * 8, plocal), F32),
-            pltpu.VMEM((7 * 16, plocal), F32),
-            pltpu.VMEM((GROUP, plocal), F32),
+            pltpu.VMEM((GROUP + 16, plocal), F32),
             pltpu.VMEM((256, plocal), F32),
             pltpu.VMEM((GROUP, LANES), F32),
             pltpu.VMEM((f_dev * GROUP, 3 * LANES), F32),
@@ -782,12 +845,17 @@
         scratch=scratch,
     )
     (part,) = call(sum_kernel, "sum", [(8, LANES)], 0, *mates(part, 4))
-    (pose,) = call(solve_kernel, "solve", [(24, LANES)], 1, spot, *mates(part, 16), vs, v45)
-    (depth_step,) = call(
-        final_kernel, "final", [(f_dev, plocal)], 0, pose, b, g, base, scale,
-        scratch=[pltpu.VMEM((f_dev * 8, plocal), F32)],
-    )
-    pose_step = pose[8, : f_dev * 6].reshape(f_dev, 6).T
+    pose_step, depth_step = call(
+        solve_kernel, "solve", [(6, f_dev), (f_dev, plocal)], 1, spot, *mates(part, 16), vs, v45,
+        base, scale, b, g,
+        scratch=[
+            pltpu.VMEM((f_dev * 8, plocal), F32),
+            pltpu.VMEM((f_dev * GROUP, 3 * LANES), F32),
+            pltpu.VMEM((f_dev * GROUP, plocal), F32),
+            pltpu.SemaphoreType.DMA((2,)),
+        ],
+        hbm=2,
+    )
     return pose_step, depth_step
 
 

time: 167 us -> 161 us (0.964)
  waiting for transfers between devices: 42 us -> 31.7 us
  Pallas kernels: 62.8 us -> 68.7 us
    ppermute x6, waiting for transfers between devices: 24 us -> 13.2 us  [shift(): lax.ppermute(block, 'frames', [(i, i + step) for i in range(count) if 0 <...]
    pallas_call x10, Pallas kernels: 62.8 us -> 68.7 us  [call(): pl.pallas_call(kernel, name=name, out_shape=[jax.ShapeDtypeStruct(s, F32)...]
    unnamed x45 -> x44, local copies, waits for them, and re-layouts: 6.53 us -> 5.85 us
  transfers between devices with their start and end apart: 22 -> 22, of which waited for: 13 -> 14; matrix products, arithmetic and copies ran while one was open for 0% -> 0% of each run, Pallas kernels for 4% -> 11%
where the time goes in v5:
time: 161 us; the launch traced here: 158 us
  Pallas kernels  68.7 us (43%)
  starting transfers between devices  46.2 us (29%)
  waiting for transfers between devices  31.7 us (20%)
  local copies, waits for them, and re-layouts  9.1 us (6%)
    pallas_call x10, Pallas kernels, call(): pl.pallas_call(kernel, name=name, out_shape=[jax.ShapeDtypeStruct(s, F32)...  68.7 us
    ppermute x6, starting transfers between devices, shift(): lax.ppermute(block, 'frames', [(i, i + step) for i in range(count) if 0 <...  23.4 us
    ppermute x6, waiting for transfers between devices, shift(): lax.ppermute(block, 'frames', [(i, i + step) for i in range(count) if 0 <...  13.2 us
    ppermute x9, starting transfers between devices, mates(): lax.ppermute(v, 'frames', [(i, i ^ k * step) for i in range(count)])  12.6 us
    ppermute x2, starting transfers between devices, to_neighbour(): return lax.ppermute(rim, both_axes, route)  9.25 us
    ppermute x9, waiting for transfers between devices, mates(): lax.ppermute(v, 'frames', [(i, i ^ k * step) for i in range(count)])  8.23 us
    ppermute x2, waiting for transfers between devices, to_neighbour(): return lax.ppermute(rim, both_axes, route)  7.33 us
    unnamed x44, local copies, waits for them, and re-layouts  5.85 us
  transfers between devices with their start and end apart: 22, of which 14 were waited for; matrix products, arithmetic and copies ran while one was open for 0% of the time, Pallas kernels for 11%

profile of v5, /device:TPU:8, one launch (start us, length us, event | category | flops | bytes accessed | tf_op | source)
XLA Modules:
  0.0 158.3 jit_solution(11800331206893065261)
XLA Ops:
  0.7 3.2 %copy_bitcast_fusion = (f32[2,192,768]{2,1,0:T(8,128)}, f32[2,192,768]{2,1,0:T(8,128)}) fusion(f32[192,2,768]{2,1,0:T(2,128)} %param.14, f32[192,2,768]{2,1,0:T(2,128)} %param.13), kind=kLoop, calls=%fused_computation | loop fusion | bytes 4718592 | tf_op jit(solution)/shard_map/transpose | solution.py:776
  3.9 0.7 pad_add_fusion.where_ref
  4.5 5.5 %scatter.1 = (f32[1024,768]{1,0:T(8,128)}, f32[152,768]{1,0:T(8,128)}, f32[144,768]{1,0:T(8,128)}) custom-call(s32[4]{0:T(128)} %pad_add_fusion.where_ref, s32[2,192]{1,0:T(2,128)} %ef_ref.1, f32[2,192,768]{2,1,0:T(8,128)} %get-tuple-element.47.flow_ref, f32[2,192,768]{2,1,0:T(8,128)} %get-tuple-element.46.weight_ref, s32[192,768]{1,0:T(8,128)} %mask_ref.1), custom_call_target="tpu_custom_call" | custom-call | tf_op jit(solution)/shard_map/scatter/pallas_call | solution.py:750
  10.1 8.6 %collective-permute-start = (f32[152,768]{1,0:T(8,128)}, f32[152,768]{1,0:T(8,128)S(1)}, u32[]{:S(2)}, u32[]{:S(2)}) collective-permute-start(f32[152,768]{1,0:T(8,128)} %get-tuple-element.23), channel_id=1, source_target_pairs={{4,0},{8,4},{12,8},{16,12},{20,16},{24,20},{28,24},{32,28},{36,32}... | collective-permute-start | bytes 1400840 | tf_op jit(solution)/shard_map/ppermute | solution.py:769
  18.7 1.9 %collective-permute-start.1 = (f32[144,768]{1,0:T(8,128)}, f32[144,768]{1,0:T(8,128)S(1)}, u32[]{:S(2)}, u32[]{:S(2)}) collective-permute-start(f32[144,768]{1,0:T(8,128)} %get-tuple-element.24), channel_id=1, source_target_pairs={{0,4},{4,8},{8,12},{12,16},{16,20},{20,24},{24,28},{28,32},{32,36}... | collective-permute-start | bytes 1327112 | tf_op jit(solution)/shard_map/ppermute | solution.py:769
  20.6 6.1 %pose.1 = (f32[256,128]{1,0:T(8,128)}, f32[1536,384]{1,0:T(8,128)}, f32[192,1536]{1,0:T(8,128)}) custom-call(s32[4]{0:T(128)} %pad_add_fusion.where_ref, f32[3,1024]{1,0:T(4,128)} %rotvec_ref.1, f32[3,1024]{1,0:T(4,128)} %trans_ref.1), custom_call_target="tpu_custom_call" | custom-call | tf_op jit(solution)/shard_map/pose/pallas_call | solution.py:750
  26.7 10.8 %early.1 = (f32[1280,768]{1,0:T(8,128)}, f32[128,768]{1,0:T(8,128)}, f32[128,768]{1,0:T(8,128)}, f32[1536,128]{1,0:T(8,128)}) custom-call(s32[4]{0:T(128)} %pad_add_fusion.where_ref, f32[1024,768]{1,0:T(8,128)} %get-tuple-element.25.own_ref, f32[16,768]{1,0:T(8,128)} %depth_ref.3, f32[256,128]{1,0:T(8,128)} %get-tuple-element.26.tab_ref), custom_call_target="tpu_custom_call" | custom-call | tf_op jit(solution)/shard_map/early/pallas_call | solution.py:750
  37.6 1.5 collective-permute-done.1.rup_ref
  39.0 0.0 collective-permute-done.rdown_ref
  39.0 0.7 copy-done.1
  39.8 0.2 copy-done
  40.0 18.0 %main.1 = (f32[96,256]{1,0:T(8,128)}, f32[96,256]{1,0:T(8,128)}, f32[1536,768]{1,0:T(8,128)}, f32[128,768]{1,0:T(8,128)}, f32[128,768]{1,0:T(8,128)}) custom-call(s32[4]{0:T(128)} %pad_add_fusion.where_ref, f32[152,768]{1,0:T(8,128)} %copy-done, f32[144,768]{1,0:T(8,128)} %copy-done.1, f32[1280,768]{1,0:T(8,128)} %get-tuple-element.27.geo_ref, ...), custom_call_target="tpu_custom_call" | custom-call | tf_op jit(solution)/shard_map/main/pallas_call | solution.py:750
  58.0 0.0 collective-permute-start.2
  58.0 1.5 collective-permute-done.2
  59.5 0.9 add.12
  60.4 0.0 copy-start.2
  60.4 6.7 %collective-permute-start.5 = (f32[48,256]{1,0:T(8,128)S(1)}, f32[48,256]{1,0:T(8,128)S(1)}, u32[]{:S(2)}, u32[]{:S(2)}) collective-permute-start(f32[48,256]{1,0:T(8,128)S(1)} %get-tuple-element.44), channel_id=1, source_target_pairs={{0,6},{2,4},{4,10},{5,3},{6,8},{7,1},{8,14},{9,7},{10,12},{11,5},{... | collective-permute-start | bytes 147464 | tf_op jit(solution)/shard_map/ppermute | solution.py:816
  67.2 2.5 %collective-permute-start.4 = (f32[48,256]{1,0:T(8,128)S(1)}, f32[48,256]{1,0:T(8,128)S(1)}, u32[]{:S(2)}, u32[]{:S(2)}) collective-permute-start(f32[48,256]{1,0:T(8,128)S(1)} %get-tuple-element.44), channel_id=1, source_target_pairs={{0,4},{2,6},{4,8},{5,1},{6,10},{7,3},{8,12},{9,5},{10,14},{11,7},{... | collective-permute-start | bytes 147464 | tf_op jit(solution)/shard_map/ppermute | solution.py:816
  69.7 0.9 collective-permute-start.3
  70.6 0.4 collective-permute-done.5.rim2_ref
  71.0 7.0 %collective-permute-done.4.rim_ref = f32[48,256]{1,0:T(8,128)S(1)} collective-permute-done((f32[48,256]{1,0:T(8,128)S(1)}, f32[48,256]{1,0:T(8,128)S(1)}, u32[]{:S(2)}, u32[]{:S(2)}) %collective-permute-start.4) | collective-permute-done | bytes 49184 | tf_op jit(solution)/shard_map/ppermute | solution.py:816
  78.0 0.0 collective-permute-done.3.own2_ref
  78.0 0.6 copy-done.12
  78.6 0.6 copy-done.13
  79.2 1.5 half.1.a_ref
  80.7 1.3 collective-permute-start.8
  82.0 1.6 collective-permute-start.7
  83.5 1.6 collective-permute-start.6
  85.1 2.0 %collective-permute-done.8.d_ref = f32[48,256]{1,0:T(8,128)S(1)} collective-permute-done((f32[48,256]{1,0:T(8,128)}, f32[48,256]{1,0:T(8,128)S(1)}, u32[]{:S(2)}, u32[]{:S(2)}) %collective-permute-start.8) | collective-permute-done | bytes 49184 | tf_op jit(solution)/shard_map/ppermute | solution.py:825
  87.1 1.6 %collective-permute-done.7.c_ref = f32[48,256]{1,0:T(8,128)S(1)} collective-permute-done((f32[48,256]{1,0:T(8,128)}, f32[48,256]{1,0:T(8,128)S(1)}, u32[]{:S(2)}, u32[]{:S(2)}) %collective-permute-start.7) | collective-permute-done | bytes 49184 | tf_op jit(solution)/shard_map/ppermute | solution.py:825
  88.7 0.0 collective-permute-done.6.b_ref
  88.7 0.6 copy-done.9
  89.3 0.6 copy-done.10
  89.9 1.6 place.1.c_ref
  91.5 5.1 %collective-permute-start.10 = (f32[192,256]{1,0:T(8,128)}, f32[192,256]{1,0:T(8,128)S(1)}, u32[]{:S(2)}, u32[]{:S(2)}) collective-permute-start(f32[192,256]{1,0:T(8,128)} %place.1.c_ref), channel_id=1, source_target_pairs={{16,0},{20,4},{24,8},{28,12},{32,16},{36,20},{40,24},{44,28},{48,3... | collective-permute-start | bytes 589832 | tf_op jit(solution)/shard_map/ppermute | solution.py:769
  96.6 1.9 %collective-permute-start.9 = (f32[192,256]{1,0:T(8,128)}, f32[192,256]{1,0:T(8,128)S(1)}, u32[]{:S(2)}, u32[]{:S(2)}) collective-permute-start(f32[192,256]{1,0:T(8,128)} %place.1.c_ref), channel_id=1, source_target_pairs={{0,16},{4,20},{8,24},{12,28},{16,32},{20,36},{24,40},{28,44},{32,4... | collective-permute-start | bytes 589832 | tf_op jit(solution)/shard_map/ppermute | solution.py:769
  98.5 0.1 collective-permute-start.12
  98.6 1.5 collective-permute-done.10.n_ref
  100.1 6.4 %collective-permute-done.9.p_ref = f32[192,256]{1,0:T(8,128)S(1)} collective-permute-done((f32[192,256]{1,0:T(8,128)}, f32[192,256]{1,0:T(8,128)S(1)}, u32[]{:S(2)}, u32[]{:S(2)}) %collective-permute-start.9) | collective-permute-done | bytes 196640 | tf_op jit(solution)/shard_map/ppermute | solution.py:769
  106.5 0.0 collective-permute-start.11
  106.5 0.0 collective-permute-done.13.n2_ref
  106.5 1.4 collective-permute-done.11.p2_ref
  107.9 0.7 copy-done.7
  108.6 11.0 %first.1 = (f32[1152,256]{1,0:T(8,128)}, f32[1152,128]{1,0:T(8,128)}, f32[480,128]{1,0:T(8,128)}, f32[8,128]{1,0:T(8,128)}) custom-call(s32[4]{0:T(128)} %pad_add_fusion.where_ref, f32[192,256]{1,0:T(8,128)} %copy-done.4, f32[192,256]{1,0:T(8,128)} %place.1.c_ref, f32[192,256]{1,0:T(8,128)} %copy-done.3, f32[192,256]{1,0:T(8,128)} %copy-done.7, ...), custom_call_target="tpu_custom_call" | custom-call | tf_op jit(solution)/shard_map/first/pallas_call | solution.py:750
  119.6 1.9 %collective-permute-start.15 = (f32[8,128]{1,0:T(8,128)}, f32[8,128]{1,0:T(8,128)S(1)}, u32[]{:S(2)}, u32[]{:S(2)}) collective-permute-start(f32[8,128]{1,0:T(8,128)} %get-tuple-element.38.own_ref), channel_id=1, source_target_pairs={{16,0},{20,4},{24,8},{28,12},{32,16},{36,20},{40,24},{44,28},{48,3... | collective-permute-start | bytes 12296 | tf_op jit(solution)/shard_map/ppermute | solution.py:769
  121.5 3.9 %collective-permute-start.14 = (f32[8,128]{1,0:T(8,128)}, f32[8,128]{1,0:T(8,128)S(1)}, u32[]{:S(2)}, u32[]{:S(2)}) collective-permute-start(f32[8,128]{1,0:T(8,128)} %get-tuple-element.38.own_ref), channel_id=1, source_target_pairs={{0,16},{4,20},{8,24},{12,28},{16,32},{20,36},{24,40},{28,44},{32,4... | collective-permute-start | bytes 12296 | tf_op jit(solution)/shard_map/ppermute | solution.py:769
  125.4 0.0 collective-permute-done.15.above_ref
  125.5 3.9 %collective-permute-done.14.below_ref = f32[8,128]{1,0:T(8,128)S(1)} collective-permute-done((f32[8,128]{1,0:T(8,128)}, f32[8,128]{1,0:T(8,128)S(1)}, u32[]{:S(2)}, u32[]{:S(2)}) %collective-permute-start.14) | collective-permute-done | bytes 4128 | tf_op jit(solution)/shard_map/ppermute | solution.py:769
  129.3 0.6 copy-done.18
  129.9 5.4 %second.1 = (f32[8,128]{1,0:T(8,128)}, f32[288,128]{1,0:T(8,128)}) custom-call(f32[1152,256]{1,0:T(8,128)} %get-tuple-element.35.s_ref, f32[1152,128]{1,0:T(8,128)} %get-tuple-element.36.up_ref, f32[480,128]{1,0:T(8,128)} %get-tuple-element.37.v_ref, f32[8,128]{1,0:T(8,128)} %copy-done.18, f32[8,128]{1,0:T(8,128)} %get-tuple-element.38.own_ref, ...), custom_call_target="tpu_custom_call" | custom-call | tf_op jit(solution)/shard_map/second/pallas_call | solution.py:750
  135.4 2.0 %collective-permute-start.17 = (f32[8,128]{1,0:T(8,128)}, f32[8,128]{1,0:T(8,128)S(1)}, u32[]{:S(2)}, u32[]{:S(2)}) collective-permute-start(f32[8,128]{1,0:T(8,128)} %get-tuple-element.39.a_ref), channel_id=1, source_target_pairs={{0,32},{4,36},{8,40},{12,44},{16,48},{20,52},{24,56},{28,60},{32,0... | collective-permute-start | bytes 12296 | tf_op jit(solution)/shard_map/ppermute | solution.py:825
  137.3 2.1 %collective-permute-start.16 = (f32[8,128]{1,0:T(8,128)}, f32[8,128]{1,0:T(8,128)S(1)}, u32[]{:S(2)}, u32[]{:S(2)}) collective-permute-start(f32[8,128]{1,0:T(8,128)} %get-tuple-element.39.a_ref), channel_id=1, source_target_pairs={{0,16},{4,20},{8,24},{12,28},{16,0},{20,4},{24,8},{28,12},{32,48},... | collective-permute-start | bytes 12296 | tf_op jit(solution)/shard_map/ppermute | solution.py:825
  139.4 0.9 collective-permute-done.18.d_ref
  140.4 0.3 collective-permute-done.17.c_ref
  140.7 0.6 collective-permute-done.16.b_ref
  141.3 0.6 copy-done.21
  141.9 1.4 sum.1.a_ref
  143.2 1.6 collective-permute-start.21
  144.8 1.0 collective-permute-start.20
  145.8 1.5 collective-permute-start.19
  147.3 0.0 collective-permute-done.21.d_ref
  147.3 2.8 %collective-permute-done.20.c_ref = f32[8,128]{1,0:T(8,128)S(1)} collective-permute-done((f32[8,128]{1,0:T(8,128)}, f32[8,128]{1,0:T(8,128)S(1)}, u32[]{:S(2)}, u32[]{:S(2)}) %collective-permute-start.20) | collective-permute-done | bytes 4128 | tf_op jit(solution)/shard_map/ppermute | solution.py:825
  150.2 0.6 copy-done.15
  150.7 7.4 %solve.1 = (f32[6,16]{1,0:T(8,128)}, f32[16,768]{1,0:T(8,128)}) custom-call(s32[4]{0:T(128)} %pad_add_fusion.where_ref, f32[8,128]{1,0:T(8,128)} %sum.1.a_ref, f32[8,128]{1,0:T(8,128)} %copy-done.16, f32[8,128]{1,0:T(8,128)} %copy-done.15, f32[8,128]{1,0:T(8,128)} %copy-done.14, f32[480,128]{1,0:T(8,128)} %get-tuple-element.37.v_ref, ...), custom_call_target="tpu_custom_call" | custom-call | tf_op jit(solution)/shard_map/solve/pallas_call | solution.py:750
  (38 shorter events, 0.1 us)
Async XLA Ops:
  10.1 29.0 %collective-permute-start = (f32[152,768]{1,0:T(8,128)}, f32[152,768]{1,0:T(8,128)S(1)}, u32[]{:S(2)}, u32[]{:S(2)}) collective-permute-start(f32[152,768]{1,0:T(8,128)} %get-tuple-element.23), channel_id=1, source_target_pairs={{4,0},{8,4},{12,8},{16,12},{20,16},{24,20},{28,24},{32,28},{36,32}... | collective-permute-start | bytes 1400840 | tf_op jit(solution)/shard_map/ppermute | solution.py:769
  18.7 20.4 %collective-permute-start.1 = (f32[144,768]{1,0:T(8,128)}, f32[144,768]{1,0:T(8,128)S(1)}, u32[]{:S(2)}, u32[]{:S(2)}) collective-permute-start(f32[144,768]{1,0:T(8,128)} %get-tuple-element.24), channel_id=1, source_target_pairs={{0,4},{4,8},{8,12},{12,16},{16,20},{20,24},{24,28},{28,32},{32,36}... | collective-permute-start | bytes 1327112 | tf_op jit(solution)/shard_map/ppermute | solution.py:769
  39.0 0.8 copy-start.1
  39.0 0.9 copy-start
  58.0 1.5 collective-permute-start.2
  60.4 17.6 %copy-start.2 = (f32[48,256]{1,0:T(8,128)}, f32[48,256]{1,0:T(8,128)S(1)}, u32[]{:S(2)}) copy-start(f32[48,256]{1,0:T(8,128)S(1)} %get-tuple-element.45.own_ref) | copy-start | bytes 147460
  60.4 10.6 %collective-permute-start.5 = (f32[48,256]{1,0:T(8,128)S(1)}, f32[48,256]{1,0:T(8,128)S(1)}, u32[]{:S(2)}, u32[]{:S(2)}) collective-permute-start(f32[48,256]{1,0:T(8,128)S(1)} %get-tuple-element.44), channel_id=1, source_target_pairs={{0,6},{2,4},{4,10},{5,3},{6,8},{7,1},{8,14},{9,7},{10,12},{11,5},{... | collective-permute-start | bytes 147464 | tf_op jit(solution)/shard_map/ppermute | solution.py:816
  67.2 10.8 %collective-permute-start.4 = (f32[48,256]{1,0:T(8,128)S(1)}, f32[48,256]{1,0:T(8,128)S(1)}, u32[]{:S(2)}, u32[]{:S(2)}) collective-permute-start(f32[48,256]{1,0:T(8,128)S(1)} %get-tuple-element.44), channel_id=1, source_target_pairs={{0,4},{2,6},{4,8},{5,1},{6,10},{7,3},{8,12},{9,5},{10,14},{11,7},{... | collective-permute-start | bytes 147464 | tf_op jit(solution)/shard_map/ppermute | solution.py:816
  69.7 8.3 %collective-permute-start.3 = (f32[48,256]{1,0:T(8,128)S(1)}, f32[48,256]{1,0:T(8,128)S(1)}, u32[]{:S(2)}, u32[]{:S(2)}) collective-permute-start(f32[48,256]{1,0:T(8,128)S(1)} %get-tuple-element.45.own_ref), channel_id=1, source_target_pairs={{0,2},{1,3},{2,0},{3,1},{4,6},{5,7},{6,4},{7,5},{8,10},{9,11},{10,... | collective-permute-start | bytes 147464 | tf_op jit(solution)/shard_map/ppermute | solution.py:818
  71.0 7.0 %copy-start.11 = (f32[48,256]{1,0:T(8,128)}, f32[48,256]{1,0:T(8,128)S(1)}, u32[]{:S(2)}) copy-start(f32[48,256]{1,0:T(8,128)S(1)} %collective-permute-done.5.rim2_ref) | copy-start | bytes 147460
  78.0 0.6 copy-start.12
  78.6 0.6 copy-start.13
  80.7 6.4 %collective-permute-start.8 = (f32[48,256]{1,0:T(8,128)}, f32[48,256]{1,0:T(8,128)S(1)}, u32[]{:S(2)}, u32[]{:S(2)}) collective-permute-start(f32[48,256]{1,0:T(8,128)} %half.1.a_ref), channel_id=1, source_target_pairs={{0,12},{4,8},{8,4},{12,0},{16,28},{20,24},{24,20},{28,16},{32,44},... | collective-permute-start | bytes 147464 | tf_op jit(solution)/shard_map/ppermute | solution.py:825
  82.0 6.7 %collective-permute-start.7 = (f32[48,256]{1,0:T(8,128)}, f32[48,256]{1,0:T(8,128)S(1)}, u32[]{:S(2)}, u32[]{:S(2)}) collective-permute-start(f32[48,256]{1,0:T(8,128)} %half.1.a_ref), channel_id=1, source_target_pairs={{0,8},{4,12},{8,0},{12,4},{16,24},{20,28},{24,16},{28,20},{32,40},... | collective-permute-start | bytes 147464 | tf_op jit(solution)/shard_map/ppermute | solution.py:825
  83.5 5.2 %collective-permute-start.6 = (f32[48,256]{1,0:T(8,128)}, f32[48,256]{1,0:T(8,128)S(1)}, u32[]{:S(2)}, u32[]{:S(2)}) collective-permute-start(f32[48,256]{1,0:T(8,128)} %half.1.a_ref), channel_id=1, source_target_pairs={{0,4},{4,0},{8,12},{12,8},{16,20},{20,16},{24,28},{28,24},{32,36},... | collective-permute-start | bytes 147464 | tf_op jit(solution)/shard_map/ppermute | solution.py:825
  87.0 1.6 %copy-start.8 = (f32[48,256]{1,0:T(8,128)}, f32[48,256]{1,0:T(8,128)S(1)}, u32[]{:S(2)}) copy-start(f32[48,256]{1,0:T(8,128)S(1)} %collective-permute-done.8.d_ref) | copy-start | bytes 147460
  88.7 0.6 copy-start.9
  89.3 0.6 copy-start.10
  91.5 8.6 %collective-permute-start.10 = (f32[192,256]{1,0:T(8,128)}, f32[192,256]{1,0:T(8,128)S(1)}, u32[]{:S(2)}, u32[]{:S(2)}) collective-permute-start(f32[192,256]{1,0:T(8,128)} %place.1.c_ref), channel_id=1, source_target_pairs={{16,0},{20,4},{24,8},{28,12},{32,16},{36,20},{40,24},{44,28},{48,3... | collective-permute-start | bytes 589832 | tf_op jit(solution)/shard_map/ppermute | solution.py:769
  96.6 9.9 %collective-permute-start.9 = (f32[192,256]{1,0:T(8,128)}, f32[192,256]{1,0:T(8,128)S(1)}, u32[]{:S(2)}, u32[]{:S(2)}) collective-permute-start(f32[192,256]{1,0:T(8,128)} %place.1.c_ref), channel_id=1, source_target_pairs={{0,16},{4,20},{8,24},{12,28},{16,32},{20,36},{24,40},{28,44},{32,4... | collective-permute-start | bytes 589832 | tf_op jit(solution)/shard_map/ppermute | solution.py:769
  98.5 8.0 %collective-permute-start.12 = (f32[192,256]{1,0:T(8,128)}, f32[192,256]{1,0:T(8,128)S(1)}, u32[]{:S(2)}, u32[]{:S(2)}) collective-permute-start(f32[192,256]{1,0:T(8,128)} %place.1.c_ref), channel_id=1, source_target_pairs={{0,1},{1,0},{2,3},{3,2},{4,5},{5,4},{6,7},{7,6},{8,9},{9,8},{10,11... | collective-permute-start | bytes 589832 | tf_op jit(solution)/shard_map/ppermute | solution.py:829
  100.1 7.8 %copy-start.3 = (f32[192,256]{1,0:T(8,128)}, f32[192,256]{1,0:T(8,128)S(1)}, u32[]{:S(2)}) copy-start(f32[192,256]{1,0:T(8,128)S(1)} %collective-permute-done.10.n_ref) | copy-start | bytes 589828
  100.1 6.4 %collective-permute-start.13 = (f32[192,256]{1,0:T(8,128)S(1)}, f32[192,256]{1,0:T(8,128)S(1)}, u32[]{:S(2)}, u32[]{:S(2)}) collective-permute-start(f32[192,256]{1,0:T(8,128)S(1)} %collective-permute-done.10.n_ref), channel_id=1, source_target_pairs={{0,1},{1,0},{2,3},{3,2},{4,5},{5,4},{6,7},{7,6},{8,9},{9,8},{10,11... | collective-permute-start | bytes 589832 | tf_op jit(solution)/shard_map/ppermute | solution.py:829
  106.5 1.4 copy-start.4
  106.5 1.4 collective-permute-start.11
  106.5 1.4 copy-start.5
  106.5 1.4 copy-start.6
  107.9 0.7 copy-start.7
  119.6 5.8 %collective-permute-start.15 = (f32[8,128]{1,0:T(8,128)}, f32[8,128]{1,0:T(8,128)S(1)}, u32[]{:S(2)}, u32[]{:S(2)}) collective-permute-start(f32[8,128]{1,0:T(8,128)} %get-tuple-element.38.own_ref), channel_id=1, source_target_pairs={{16,0},{20,4},{24,8},{28,12},{32,16},{36,20},{40,24},{44,28},{48,3... | collective-permute-start | bytes 12296 | tf_op jit(solution)/shard_map/ppermute | solution.py:769
  121.5 7.8 %collective-permute-start.14 = (f32[8,128]{1,0:T(8,128)}, f32[8,128]{1,0:T(8,128)S(1)}, u32[]{:S(2)}, u32[]{:S(2)}) collective-permute-start(f32[8,128]{1,0:T(8,128)} %get-tuple-element.38.own_ref), channel_id=1, source_target_pairs={{0,16},{4,20},{8,24},{12,28},{16,32},{20,36},{24,40},{28,44},{32,4... | collective-permute-start | bytes 12296 | tf_op jit(solution)/shard_map/ppermute | solution.py:769
  125.4 3.9 %copy-start.17 = (f32[8,128]{1,0:T(8,128)}, f32[8,128]{1,0:T(8,128)S(1)}, u32[]{:S(2)}) copy-start(f32[8,128]{1,0:T(8,128)S(1)} %collective-permute-done.15.above_ref) | copy-start | bytes 12292
  129.3 0.6 copy-start.18
  135.4 5.0 %collective-permute-start.18 = (f32[8,128]{1,0:T(8,128)}, f32[8,128]{1,0:T(8,128)S(1)}, u32[]{:S(2)}, u32[]{:S(2)}) collective-permute-start(f32[8,128]{1,0:T(8,128)} %get-tuple-element.39.a_ref), channel_id=1, source_target_pairs={{0,48},{4,52},{8,56},{12,60},{16,32},{20,36},{24,40},{28,44},{32,1... | collective-permute-start | bytes 12296 | tf_op jit(solution)/shard_map/ppermute | solution.py:825
  135.4 5.3 %collective-permute-start.17 = (f32[8,128]{1,0:T(8,128)}, f32[8,128]{1,0:T(8,128)S(1)}, u32[]{:S(2)}, u32[]{:S(2)}) collective-permute-start(f32[8,128]{1,0:T(8,128)} %get-tuple-element.39.a_ref), channel_id=1, source_target_pairs={{0,32},{4,36},{8,40},{12,44},{16,48},{20,52},{24,56},{28,60},{32,0... | collective-permute-start | bytes 12296 | tf_op jit(solution)/shard_map/ppermute | solution.py:825
  137.3 4.0 %collective-permute-start.16 = (f32[8,128]{1,0:T(8,128)}, f32[8,128]{1,0:T(8,128)S(1)}, u32[]{:S(2)}, u32[]{:S(2)}) collective-permute-start(f32[8,128]{1,0:T(8,128)} %get-tuple-element.39.a_ref), channel_id=1, source_target_pairs={{0,16},{4,20},{8,24},{12,28},{16,0},{20,4},{24,8},{28,12},{32,48},... | collective-permute-start | bytes 12296 | tf_op jit(solution)/shard_map/ppermute | solution.py:825
  140.4 0.9 copy-start.19
  140.7 0.6 copy-start.20
  141.3 0.6 copy-start.21
  143.2 4.1 %collective-permute-start.21 = (f32[8,128]{1,0:T(8,128)}, f32[8,128]{1,0:T(8,128)S(1)}, u32[]{:S(2)}, u32[]{:S(2)}) collective-permute-start(f32[8,128]{1,0:T(8,128)} %sum.1.a_ref), channel_id=1, source_target_pairs={{0,192},{4,196},{8,200},{12,204},{16,208},{20,212},{24,216},{28,22... | collective-permute-start | bytes 12296 | tf_op jit(solution)/shard_map/ppermute | solution.py:825
  144.8 5.3 %collective-permute-start.20 = (f32[8,128]{1,0:T(8,128)}, f32[8,128]{1,0:T(8,128)S(1)}, u32[]{:S(2)}, u32[]{:S(2)}) collective-permute-start(f32[8,128]{1,0:T(8,128)} %sum.1.a_ref), channel_id=1, source_target_pairs={{0,128},{4,132},{8,136},{12,140},{16,144},{20,148},{24,152},{28,15... | collective-permute-start | bytes 12296 | tf_op jit(solution)/shard_map/ppermute | solution.py:825
  145.8 4.3 %collective-permute-start.19 = (f32[8,128]{1,0:T(8,128)}, f32[8,128]{1,0:T(8,128)S(1)}, u32[]{:S(2)}, u32[]{:S(2)}) collective-permute-start(f32[8,128]{1,0:T(8,128)} %sum.1.a_ref), channel_id=1, source_target_pairs={{0,64},{4,68},{8,72},{12,76},{16,80},{20,84},{24,88},{28,92},{32,9... | collective-permute-start | bytes 12296 | tf_op jit(solution)/shard_map/ppermute | solution.py:825
  147.3 2.8 %copy-start.14 = (f32[8,128]{1,0:T(8,128)}, f32[8,128]{1,0:T(8,128)S(1)}, u32[]{:S(2)}) copy-start(f32[8,128]{1,0:T(8,128)S(1)} %collective-permute-done.21.d_ref) | copy-start | bytes 12292
  150.1 0.6 copy-start.15
  150.1 0.6 copy-start.16

commit v6 on v5

--- a/solution.py
+++ b/solution.py
@@ -41,26 +41,23 @@
     return jnp.dot(a, b, preferred_element_type=F32)
 
 
-def scatter_kernel(where_ref, ef_ref, flow_ref, weight_ref, mask_ref, own_ref, down_ref, up_ref):
+def spread(where_ref, ef_ref, flow_ref, weight_ref, mask_ref, rims, write):
     edges = ef_ref.shape[1]
     start = where_ref[0]
     source = ef_ref[0:1, :] - start
     delta = ef_ref[1:2, :] - start - source
     slot = jnp.where(delta < 0, delta + 8, delta + 7)
-    own_at = jnp.where((source >= 0) & (source < FD), source * SLOTS + slot, -1)
-    j = source + 8
-    down_at = jnp.where(source < 0, ((j * (j + 1)) >> 1) + delta - 8 + j, -1)
-    j = 23 - source
-    up_at = jnp.where(source >= FD, ((j * (j + 1)) >> 1) + slot, -1)
-    hot = jnp.concatenate(
-        [
-            (iota((FD * SLOTS, edges), 0) == own_at).astype(F32),
-            (iota((40, edges), 0) == down_at).astype(F32),
-            (iota((40, edges), 0) == up_at).astype(F32),
-        ],
-        axis=0,
-    ).astype(BF16)
-    down_ref[0:8, :] = jnp.zeros((8, down_ref.shape[1]), F32)
+    if rims:
+        j = source + 8
+        down_at = jnp.where(source < 0, ((j * (j + 1)) >> 1) + delta - 8 + j, -1)
+        j = 23 - source
+        up_at = jnp.where(source >= FD, ((j * (j + 1)) >> 1) + slot, -1)
+        row = iota((40, edges), 0)
+        hot = jnp.concatenate([(row == down_at).astype(F32), (row == up_at).astype(F32)], axis=0)
+    else:
+        own_at = jnp.where((source >= 0) & (source < FD), source * SLOTS + slot, -1)
+        hot = (iota((FD * SLOTS, edges), 0) == own_at).astype(F32)
+    hot = hot.astype(BF16)
     for chunk in range(mask_ref.shape[1] // LANES):
         lanes = pl.ds(chunk * LANES, LANES)
         live = mask_ref[:, lanes].astype(F32)
@@ -69,14 +66,26 @@
             conf = weight_ref[comp, :, lanes] * live
             parts.append((conf, conf * flow_ref[comp, :, lanes]))
         values = jnp.concatenate([parts[0][0], parts[1][0], parts[0][1], parts[1][1]], axis=1)
-        got = sum(
-            jnp.dot(hot, piece, preferred_element_type=F32) for piece in reversed(thirds(values))
-        )
+        got = sum(dot(hot, piece) for piece in reversed(thirds(values)))
         for q in range(4):
-            cut = got[:, q * LANES : (q + 1) * LANES]
-            own_ref[q * 256 : (q + 1) * 256, lanes] = cut[0:256]
-            down_ref[8 + q * SIDE : 8 + (q + 1) * SIDE, lanes] = cut[256 : 256 + SIDE]
-            up_ref[q * SIDE : (q + 1) * SIDE, lanes] = cut[296 : 296 + SIDE]
+            write(q, lanes, got[:, q * LANES : (q + 1) * LANES])
+
+
+def rim_kernel(where_ref, ef_ref, flow_ref, weight_ref, mask_ref, down_ref, up_ref):
+    down_ref[0:8, :] = jnp.zeros((8, down_ref.shape[1]), F32)
+
+    def write(q, lanes, cut):
+        down_ref[8 + q * SIDE : 8 + (q + 1) * SIDE, lanes] = cut[0:SIDE]
+        up_ref[q * SIDE : (q + 1) * SIDE, lanes] = cut[40 : 40 + SIDE]
+
+    spread(where_ref, ef_ref, flow_ref, weight_ref, mask_ref, True, write)
+
+
+def own_kernel(where_ref, ef_ref, flow_ref, weight_ref, mask_ref, own_ref):
+    def write(q, lanes, cut):
+        own_ref[q * 256 : (q + 1) * 256, lanes] = cut
+
+    spread(where_ref, ef_ref, flow_ref, weight_ref, mask_ref, False, write)
 
 
 def rotation_rows(w):
@@ -273,7 +282,8 @@
                 curv_ref[eight, lanes] = curv
                 grad_ref[eight, lanes] = grad
                 for q, x in enumerate((u, v, inv, au, av)):
-                    geo_ref[at(q), lanes] = x
+                    row = pl.multiple_of((f * 5 + q) * SLOTS + 8 * h, 8)
+                    geo_ref[pl.ds(row, 8), lanes] = x
                 acc = [x + y for x, y in zip(acc, pose_sums(u, v, depth * inv, cu, cv, eu, ev))]
             for c, tile in enumerate(diagonal_rows(acc, h)):
                 block_ref[pl.ds(pl.multiple_of(f * GROUP + c * SLOTS + 8 * h, 8), 8), :] = tile
@@ -283,11 +293,21 @@
 
 
 def main_kernel(
-    where_ref, rdown_ref, rup_ref, geo_ref, curv_ref, grad_ref, block_ref, depth_ref, damp_ref, tab_ref,
-    b_ref, bt_ref,
-    keep_ref, send_ref, g_ref, base_ref, scale_ref,
-    half_ref, hi_ref, in_ref, q_ref, w_ref, t_ref,
+    where_ref, rdown_ref, rup_ref, curv_ref, grad_ref, block_ref, depth_ref, damp_ref, tab_ref,
+    geo_hbm, b_hbm, bt_hbm,
+    keep_ref, send_ref, base_ref, scale_ref, g_hbm,
+    half_ref, hi_ref, in_ref, q_ref, w_ref, t_ref, geo_ref, b_ref, bt_ref, g_ref,
+    geo_sems, b_sems, g_sems, bt_sem,
 ):
+    def piece(src, dst, sems, f, rows):
+        at = pl.ds(pl.multiple_of(f * rows, 8), rows)
+        return pltpu.make_async_copy(src.at[at, :], dst.at[at, :], sems.at[f])
+
+    for f in range(FD):
+        piece(geo_hbm, geo_ref, geo_sems, f, 5 * SLOTS).start()
+        piece(b_hbm, b_ref, b_sems, f, GROUP).start()
+    bt_copy = pltpu.make_async_copy(bt_hbm, bt_ref, bt_sem.at[0])
+    bt_copy.start()
     core = where_ref[2]
     plocal = depth_ref.shape[1]
     chunks = plocal // LANES
@@ -309,6 +329,8 @@
 
     def frame(f, carry, merged):
         eight = pl.ds(pl.multiple_of(f * 8, 8), 8)
+        piece(geo_hbm, geo_ref, geo_sems, f, 5 * SLOTS).wait()
+        piece(b_hbm, b_ref, b_sems, f, GROUP).wait()
         tab = tab_ref[pl.ds(pl.multiple_of(f * SLOTS + 8 * merged, 8), 8), :]
         t0, t1, t2 = [jnp.broadcast_to(tab[:, k : k + 1], (8, LANES)) for k in (9, 10, 11)]
         acc = [0.0] * 26
@@ -318,7 +340,7 @@
             depth = in_ref[eight, lanes]
 
             def geo(q, h):
-                return geo_ref[pl.ds(pl.multiple_of(q * 256 + f * SLOTS + 8 * h, 8), 8), lanes]
+                return geo_ref[pl.ds(pl.multiple_of((f * 5 + q) * SLOTS + 8 * h, 8), 8), lanes]
 
             cu, cv, fu, fv = [
                 half_ref[pl.ds(pl.multiple_of((q * FD + f) * 8, 8), 8), lanes] for q in range(4)
@@ -357,6 +379,7 @@
                 for k, x in enumerate(rows):
                     g_ref[pl.ds(pl.multiple_of(f * GROUP + k * SLOTS + 8 * h, 8), 8), lanes] = x
                     hi_ref[k * SLOTS + 8 * h : k * SLOTS + 8 * h + 8, lanes] = x
+        piece(g_ref, g_hbm, g_sems, f, GROUP).start()
         rows = pl.ds(pl.multiple_of(f * GROUP, 8), GROUP)
         q_ref[...] = block_ref[rows, :]
         for c, tile in enumerate(diagonal_rows(acc, merged)):
@@ -388,6 +411,7 @@
 
     lax.fori_loop(0, 8, functools.partial(frame, merged=0), 0)
     lax.fori_loop(8, 16, functools.partial(frame, merged=1), 0)
+    bt_copy.wait()
     bt_top, bt_low = pair_of(bt_ref[...])
     w_top, w_low = pair_of(w_ref[...])
     both = dot(jnp.concatenate([bt_top, bt_low], axis=0), w_top)
@@ -428,6 +452,9 @@
         put_half(keep_ref, 1)
         put_half(send_ref, 0)
 
+    for f in range(FD):
+        piece(g_ref, g_hbm, g_sems, f, GROUP).wait()
+
 
 def to_row(column):
     return jnp.sum(
@@ -438,10 +465,6 @@
 
 
 BLOCKS = 12
-
-
-def quad_kernel(where_ref, own_ref, own2_ref, rim_ref, rim2_ref, out_ref):
-    out_ref[...] = (own_ref[...] + own2_ref[...]) + (rim_ref[...] + rim2_ref[...])
 
 
 def place_kernel(where_ref, a_ref, b_ref, c_ref, d_ref, out_ref):
@@ -746,13 +769,13 @@
 ANY = pl.BlockSpec(memory_space=pl.ANY)
 
 
-def call(kernel, name, outs, smem, *args, scratch=(), hbm=0):
+def call(kernel, name, outs, smem, *args, scratch=(), hbm=0, hbm_out=0):
     return pl.pallas_call(
         kernel,
         name=name,
         out_shape=[jax.ShapeDtypeStruct(s, F32) for s in outs],
         in_specs=[SMEM] * smem + [VMEM] * (len(args) - smem - hbm) + [ANY] * hbm,
-        out_specs=[VMEM] * len(outs),
+        out_specs=[VMEM] * (len(outs) - hbm_out) + [ANY] * hbm_out,
         scratch_shapes=list(scratch),
     )(*args)
 
@@ -770,13 +793,13 @@
             block, "frames", [(i, i + step) for i in range(count) if 0 <= i + step < count]
         )
 
-    own, down, up = call(
-        scatter_kernel, "scatter",
-        [(4 * f_dev * SLOTS, plocal), (8 + 4 * SIDE, plocal), (4 * SIDE, plocal)],
-        1, spot, edge_frames, flow.transpose(1, 0, 2), weight.transpose(1, 0, 2), mask,
+    edges = (edge_frames, flow.transpose(1, 0, 2), weight.transpose(1, 0, 2), mask)
+    down, up = call(
+        rim_kernel, "rim", [(8 + 4 * SIDE, plocal), (4 * SIDE, plocal)], 1, spot, *edges
     )
     from_after = shift(down, -1)
     from_before = shift(up, 1)
+    (own,) = call(own_kernel, "own", [(4 * f_dev * SLOTS, plocal)], 1, spot, *edges)
     tab, b, bt = call(
         pose_kernel, "pose",
         [(f_dev * SLOTS, LANES), (f_dev * GROUP, 3 * LANES), (192, f_dev * GROUP)],
@@ -788,10 +811,11 @@
         [(5 * pairs, plocal), (f_dev * 8, plocal), (f_dev * 8, plocal), (f_dev * GROUP, LANES)],
         1, spot, own, inv_depth, tab, scratch=[pltpu.VMEM((f_dev * 8, plocal), F32)],
     )
-    keep, send, g, base, scale = call(
+    keep, send, base, scale, g = call(
         main_kernel, "main",
-        [(96, 256), (96, 256), (f_dev * GROUP, plocal), (f_dev * 8, plocal), (f_dev * 8, plocal)],
-        1, spot, from_after, from_before, geo, curv, grad, block, inv_depth, depth_damping, tab, b, bt,
+        [(96, 256), (96, 256), (f_dev * 8, plocal), (f_dev * 8, plocal), (f_dev * GROUP, plocal)],
+        1, spot, from_after, from_before, curv, grad, block, inv_depth, depth_damping, tab, geo, b, bt,
+        hbm=3, hbm_out=1,
         scratch=[
             pltpu.VMEM((4 * FD * 8, plocal), F32),
             pltpu.VMEM((GROUP + 16, plocal), F32),
@@ -799,6 +823,14 @@
             pltpu.VMEM((GROUP, LANES), F32),
             pltpu.VMEM((f_dev * GROUP, 3 * LANES), F32),
             pltpu.VMEM((192, 3 * LANES), F32),
+            pltpu.VMEM((5 * pairs, plocal), F32),
+            pltpu.VMEM((f_dev * GROUP, 3 * LANES), F32),
+            pltpu.VMEM((192, f_dev * GROUP), F32),
+            pltpu.VMEM((f_dev * GROUP, plocal), F32),
+            pltpu.SemaphoreType.DMA((f_dev,)),
+            pltpu.SemaphoreType.DMA((f_dev,)),
+            pltpu.SemaphoreType.DMA((f_dev,)),
+            pltpu.SemaphoreType.DMA((1,)),
         ],
     )
     got = lax.ppermute(send, "pix", [(i, i ^ 1) for i in range(pixes)])
@@ -818,7 +850,7 @@
     own_far = lax.ppermute(own_half, "pix", [(i, i ^ 2) for i in range(pixes)])
     rim_near = to_neighbour(0)
     rim_far = to_neighbour(2)
-    (half,) = call(quad_kernel, "half", [(48, 256)], 1, spot, own_half, own_far, rim_near, rim_far)
+    half = (own_half + own_far) + (rim_near + rim_far)
 
     def mates(v, step):
         return [v] + [

time: 161 us -> 157 us (0.975)
  local copies, waits for them, and re-layouts: 9.1 us -> 7.33 us
    ppermute x2, starting transfers between devices: 9.25 us -> 3.83 us  [to_neighbour(): return lax.ppermute(rim, both_axes, route)]
    ppermute x1, starting transfers between devices: 0.94 us -> 4.58 us  [per_device(): own_far = lax.ppermute(own_half, 'pix', [(i, i ^ 2) for i in range(pixes)])]
    unnamed x44 -> x38, local copies, waits for them, and re-layouts: 5.85 us -> 4.07 us
  transfers between devices with their start and end apart: 22 -> 22, of which waited for: 14 -> 14; matrix products, arithmetic and copies ran while one was open for 0% -> 0% of each run, Pallas kernels for 11% -> 14%
where the time goes in v6:
time: 157 us; the launch traced here: 154 us
  Pallas kernels  67.8 us (43%)
  starting transfers between devices  45 us (29%)
  waiting for transfers between devices  31.3 us (20%)
  local copies, waits for them, and re-layouts  7.33 us (5%)
    pallas_call x10, Pallas kernels, call(): pl.pallas_call(kernel, name=name, out_shape=[jax.ShapeDtypeStruct(s, F32)...  67.8 us
    ppermute x6, starting transfers between devices, shift(): lax.ppermute(block, 'frames', [(i, i + step) for i in range(count) if 0 <...  23.6 us
    ppermute x6, waiting for transfers between devices, shift(): lax.ppermute(block, 'frames', [(i, i + step) for i in range(count) if 0 <...  12.9 us
    ppermute x9, starting transfers between devices, mates(): lax.ppermute(v, 'frames', [(i, i ^ k * step) for i in range(count)])  12.6 us
    ppermute x2, waiting for transfers between devices, to_neighbour(): return lax.ppermute(rim, both_axes, route)  8.14 us
    ppermute x9, waiting for transfers between devices, mates(): lax.ppermute(v, 'frames', [(i, i ^ k * step) for i in range(count)])  6.7 us
    ppermute x1, starting transfers between devices, per_device(): own_far = lax.ppermute(own_half, 'pix', [(i, i ^ 2) for i in range(pixes)])  4.58 us
    unnamed x38, local copies, waits for them, and re-layouts  4.07 us
  transfers between devices with their start and end apart: 22, of which 14 were waited for; matrix products, arithmetic and copies ran while one was open for 0% of the time, Pallas kernels for 14%

profile of v6, /device:TPU:8, one launch (start us, length us, event | category | flops | bytes accessed | tf_op | source)
XLA Modules:
  0.0 154.1 jit_solution(8979254214963222781)
XLA Ops:
  0.7 3.3 %copy_bitcast_fusion = (f32[2,192,768]{2,1,0:T(8,128)}, f32[2,192,768]{2,1,0:T(8,128)}) fusion(f32[192,2,768]{2,1,0:T(2,128)} %param.14, f32[192,2,768]{2,1,0:T(2,128)} %param.13), kind=kLoop, calls=%fused_computation | loop fusion | bytes 4718592 | tf_op jit(solution)/shard_map/transpose | solution.py:796
  3.9 0.6 pad_add_fusion.where_ref
  4.5 3.6 %rim.1 = (f32[152,768]{1,0:T(8,128)}, f32[144,768]{1,0:T(8,128)}) custom-call(s32[4]{0:T(128)} %pad_add_fusion.where_ref, s32[2,192]{1,0:T(2,128)} %ef_ref.3, f32[2,192,768]{2,1,0:T(8,128)} %get-tuple-element.45.flow_ref, f32[2,192,768]{2,1,0:T(8,128)} %get-tuple-element.44.weight_ref, s32[192,768]{1,0:T(8,128)} %mask_ref.3), custom_call_target="tpu_custom_call" | custom-call | tf_op jit(solution)/shard_map/rim/pallas_call | solution.py:773
  8.1 8.6 %collective-permute-start = (f32[152,768]{1,0:T(8,128)}, f32[152,768]{1,0:T(8,128)S(1)}, u32[]{:S(2)}, u32[]{:S(2)}) collective-permute-start(f32[152,768]{1,0:T(8,128)} %get-tuple-element.22), channel_id=1, source_target_pairs={{4,0},{8,4},{12,8},{16,12},{20,16},{24,20},{28,24},{32,28},{36,32}... | collective-permute-start | bytes 1400840 | tf_op jit(solution)/shard_map/ppermute | solution.py:792
  16.8 1.9 %collective-permute-start.1 = (f32[144,768]{1,0:T(8,128)}, f32[144,768]{1,0:T(8,128)S(1)}, u32[]{:S(2)}, u32[]{:S(2)}) collective-permute-start(f32[144,768]{1,0:T(8,128)} %get-tuple-element.23), channel_id=1, source_target_pairs={{0,4},{4,8},{8,12},{12,16},{16,20},{20,24},{24,28},{28,32},{32,36}... | collective-permute-start | bytes 1327112 | tf_op jit(solution)/shard_map/ppermute | solution.py:792
  18.7 4.9 %own.1.own_ref = f32[1024,768]{1,0:T(8,128)} custom-call(s32[4]{0:T(128)} %pad_add_fusion.where_ref, s32[2,192]{1,0:T(2,128)} %ef_ref.3, f32[2,192,768]{2,1,0:T(8,128)} %get-tuple-element.45.flow_ref, f32[2,192,768]{2,1,0:T(8,128)} %get-tuple-element.44.weight_ref, s32[192,768]{1,0:T(8,128)} %mask_ref.3), custom_call_target="tpu_custom_call" | custom-call | tf_op jit(solution)/shard_map/own/pallas_call | solution.py:773
  23.6 6.1 %pose.1 = (f32[256,128]{1,0:T(8,128)}, f32[1536,384]{1,0:T(8,128)}, f32[192,1536]{1,0:T(8,128)}) custom-call(s32[4]{0:T(128)} %pad_add_fusion.where_ref, f32[3,1024]{1,0:T(4,128)} %rotvec_ref.1, f32[3,1024]{1,0:T(4,128)} %trans_ref.1), custom_call_target="tpu_custom_call" | custom-call | tf_op jit(solution)/shard_map/pose/pallas_call | solution.py:773
  29.7 10.9 %early.1 = (f32[1280,768]{1,0:T(8,128)}, f32[128,768]{1,0:T(8,128)}, f32[128,768]{1,0:T(8,128)}, f32[1536,128]{1,0:T(8,128)}) custom-call(s32[4]{0:T(128)} %pad_add_fusion.where_ref, f32[1024,768]{1,0:T(8,128)} %own.1.own_ref, f32[16,768]{1,0:T(8,128)} %depth_ref.3, f32[256,128]{1,0:T(8,128)} %get-tuple-element.24.tab_ref), custom_call_target="tpu_custom_call" | custom-call | tf_op jit(solution)/shard_map/early/pallas_call | solution.py:773
  40.6 0.0 collective-permute-done.1.rup_ref
  40.6 0.0 collective-permute-done.rdown_ref
  40.6 0.7 copy-done.1
  41.4 0.2 copy-done
  41.5 15.6 %main.1 = (f32[96,256]{1,0:T(8,128)}, f32[96,256]{1,0:T(8,128)}, f32[128,768]{1,0:T(8,128)}, f32[128,768]{1,0:T(8,128)}, f32[1536,768]{1,0:T(8,128)}) custom-call(s32[4]{0:T(128)} %pad_add_fusion.where_ref, f32[152,768]{1,0:T(8,128)} %copy-done, f32[144,768]{1,0:T(8,128)} %copy-done.1, f32[128,768]{1,0:T(8,128)} %get-tuple-element.25.curv_ref, ...), custom_call_target="tpu_custom_call" | custom-call | tf_op jit(solution)/shard_map/main/pallas_call | solution.py:773
  57.1 0.1 collective-permute-start.2
  57.2 1.5 collective-permute-done.2
  58.7 0.9 add.21
  59.7 4.6 %collective-permute-start.3 = (f32[48,256]{1,0:T(8,128)S(1)}, f32[48,256]{1,0:T(8,128)S(1)}, u32[]{:S(2)}, u32[]{:S(2)}) collective-permute-start(f32[48,256]{1,0:T(8,128)S(1)} %get-tuple-element.42), channel_id=1, source_target_pairs={{0,2},{1,3},{2,0},{3,1},{4,6},{5,7},{6,4},{7,5},{8,10},{9,11},{10,... | collective-permute-start | bytes 147464 | tf_op jit(solution)/shard_map/ppermute | solution.py:850
  64.3 1.9 %collective-permute-start.5 = (f32[48,256]{1,0:T(8,128)S(1)}, f32[48,256]{1,0:T(8,128)S(1)}, u32[]{:S(2)}, u32[]{:S(2)}) collective-permute-start(f32[48,256]{1,0:T(8,128)S(1)} %get-tuple-element.43), channel_id=1, source_target_pairs={{0,6},{2,4},{4,10},{5,3},{6,8},{7,1},{8,14},{9,7},{10,12},{11,5},{... | collective-permute-start | bytes 147464 | tf_op jit(solution)/shard_map/ppermute | solution.py:848
  66.2 1.9 %collective-permute-start.4 = (f32[48,256]{1,0:T(8,128)S(1)}, f32[48,256]{1,0:T(8,128)S(1)}, u32[]{:S(2)}, u32[]{:S(2)}) collective-permute-start(f32[48,256]{1,0:T(8,128)S(1)} %get-tuple-element.43), channel_id=1, source_target_pairs={{0,4},{2,6},{4,8},{5,1},{6,10},{7,3},{8,12},{9,5},{10,14},{11,7},{... | collective-permute-start | bytes 147464 | tf_op jit(solution)/shard_map/ppermute | solution.py:848
  68.1 0.7 collective-permute-done.3
  68.8 5.6 %collective-permute-done.5 = f32[48,256]{1,0:T(8,128)S(1)} collective-permute-done((f32[48,256]{1,0:T(8,128)S(1)}, f32[48,256]{1,0:T(8,128)S(1)}, u32[]{:S(2)}, u32[]{:S(2)}) %collective-permute-start.5) | collective-permute-done | bytes 49184 | tf_op jit(solution)/shard_map/ppermute | solution.py:848
  74.4 2.5 %collective-permute-done.4 = f32[48,256]{1,0:T(8,128)S(1)} collective-permute-done((f32[48,256]{1,0:T(8,128)S(1)}, f32[48,256]{1,0:T(8,128)S(1)}, u32[]{:S(2)}, u32[]{:S(2)}) %collective-permute-start.4) | collective-permute-done | bytes 49184 | tf_op jit(solution)/shard_map/ppermute | solution.py:848
  77.0 0.0 copy-start.2
  77.0 0.1 collective-permute-start.8
  77.1 0.1 collective-permute-start.7
  77.2 4.3 %collective-permute-start.6 = (f32[48,256]{1,0:T(8,128)S(1)}, f32[48,256]{1,0:T(8,128)S(1)}, u32[]{:S(2)}, u32[]{:S(2)}) collective-permute-start(f32[48,256]{1,0:T(8,128)S(1)} %add_add_fusion.a_ref), channel_id=1, source_target_pairs={{0,4},{4,0},{8,12},{12,8},{16,20},{20,16},{24,28},{28,24},{32,36},... | collective-permute-start | bytes 147464 | tf_op jit(solution)/shard_map/ppermute | solution.py:857
  81.5 1.5 collective-permute-done.8.d_ref
  83.0 0.0 collective-permute-done.7.c_ref
  83.0 0.6 collective-permute-done.6.b_ref
  83.5 0.0 copy-done.8
  83.6 0.0 copy-done.9
  83.6 0.6 copy-done.10
  84.2 1.6 %place.1.c_ref = f32[192,256]{1,0:T(8,128)} custom-call(s32[4]{0:T(128)} %pad_add_fusion.where_ref, f32[48,256]{1,0:T(8,128)} %copy-done.2, f32[48,256]{1,0:T(8,128)} %copy-done.10, f32[48,256]{1,0:T(8,128)} %copy-done.9, f32[48,256]{1,0:T(8,128)} %copy-done.8), custom_call_target="tpu_custom_call" | custom-call | tf_op jit(solution)/shard_map/place/pallas_call | solution.py:773
  85.8 5.3 %collective-permute-start.10 = (f32[192,256]{1,0:T(8,128)}, f32[192,256]{1,0:T(8,128)S(1)}, u32[]{:S(2)}, u32[]{:S(2)}) collective-permute-start(f32[192,256]{1,0:T(8,128)} %place.1.c_ref), channel_id=1, source_target_pairs={{16,0},{20,4},{24,8},{28,12},{32,16},{36,20},{40,24},{44,28},{48,3... | collective-permute-start | bytes 589832 | tf_op jit(solution)/shard_map/ppermute | solution.py:792
  91.1 1.9 %collective-permute-start.9 = (f32[192,256]{1,0:T(8,128)}, f32[192,256]{1,0:T(8,128)S(1)}, u32[]{:S(2)}, u32[]{:S(2)}) collective-permute-start(f32[192,256]{1,0:T(8,128)} %place.1.c_ref), channel_id=1, source_target_pairs={{0,16},{4,20},{8,24},{12,28},{16,32},{20,36},{24,40},{28,44},{32,4... | collective-permute-start | bytes 589832 | tf_op jit(solution)/shard_map/ppermute | solution.py:792
  93.0 0.3 collective-permute-start.12
  93.2 2.9 %collective-permute-done.10.n_ref = f32[192,256]{1,0:T(8,128)S(1)} collective-permute-done((f32[192,256]{1,0:T(8,128)}, f32[192,256]{1,0:T(8,128)S(1)}, u32[]{:S(2)}, u32[]{:S(2)}) %collective-permute-start.10) | collective-permute-done | bytes 196640 | tf_op jit(solution)/shard_map/ppermute | solution.py:792
  96.1 0.0 collective-permute-start.13
  96.1 6.1 %collective-permute-done.9.p_ref = f32[192,256]{1,0:T(8,128)S(1)} collective-permute-done((f32[192,256]{1,0:T(8,128)}, f32[192,256]{1,0:T(8,128)S(1)}, u32[]{:S(2)}, u32[]{:S(2)}) %collective-permute-start.9) | collective-permute-done | bytes 196640 | tf_op jit(solution)/shard_map/ppermute | solution.py:792
  102.3 0.0 collective-permute-start.11
  102.3 0.0 collective-permute-done.13.n2_ref
  102.3 1.4 collective-permute-done.11.p2_ref
  103.7 0.7 copy-done.7
  104.4 10.9 %first.1 = (f32[1152,256]{1,0:T(8,128)}, f32[1152,128]{1,0:T(8,128)}, f32[480,128]{1,0:T(8,128)}, f32[8,128]{1,0:T(8,128)}) custom-call(s32[4]{0:T(128)} %pad_add_fusion.where_ref, f32[192,256]{1,0:T(8,128)} %copy-done.4, f32[192,256]{1,0:T(8,128)} %place.1.c_ref, f32[192,256]{1,0:T(8,128)} %copy-done.3, f32[192,256]{1,0:T(8,128)} %copy-done.7, ...), custom_call_target="tpu_custom_call" | custom-call | tf_op jit(solution)/shard_map/first/pallas_call | solution.py:773
  115.3 1.9 %collective-permute-start.15 = (f32[8,128]{1,0:T(8,128)}, f32[8,128]{1,0:T(8,128)S(1)}, u32[]{:S(2)}, u32[]{:S(2)}) collective-permute-start(f32[8,128]{1,0:T(8,128)} %get-tuple-element.36.own_ref), channel_id=1, source_target_pairs={{16,0},{20,4},{24,8},{28,12},{32,16},{36,20},{40,24},{44,28},{48,3... | collective-permute-start | bytes 12296 | tf_op jit(solution)/shard_map/ppermute | solution.py:792
  117.3 3.9 %collective-permute-start.14 = (f32[8,128]{1,0:T(8,128)}, f32[8,128]{1,0:T(8,128)S(1)}, u32[]{:S(2)}, u32[]{:S(2)}) collective-permute-start(f32[8,128]{1,0:T(8,128)} %get-tuple-element.36.own_ref), channel_id=1, source_target_pairs={{0,16},{4,20},{8,24},{12,28},{16,32},{20,36},{24,40},{28,44},{32,4... | collective-permute-start | bytes 12296 | tf_op jit(solution)/shard_map/ppermute | solution.py:792
  121.2 3.9 %collective-permute-done.14.below_ref = f32[8,128]{1,0:T(8,128)S(1)} collective-permute-done((f32[8,128]{1,0:T(8,128)}, f32[8,128]{1,0:T(8,128)S(1)}, u32[]{:S(2)}, u32[]{:S(2)}) %collective-permute-start.14) | collective-permute-done | bytes 4128 | tf_op jit(solution)/shard_map/ppermute | solution.py:792
  125.1 0.6 copy-done.15
  125.7 5.4 %second.1 = (f32[8,128]{1,0:T(8,128)}, f32[288,128]{1,0:T(8,128)}) custom-call(f32[1152,256]{1,0:T(8,128)} %get-tuple-element.33.s_ref, f32[1152,128]{1,0:T(8,128)} %get-tuple-element.34.up_ref, f32[480,128]{1,0:T(8,128)} %get-tuple-element.35.v_ref, f32[8,128]{1,0:T(8,128)} %copy-done.15, f32[8,128]{1,0:T(8,128)} %get-tuple-element.36.own_ref, ...), custom_call_target="tpu_custom_call" | custom-call | tf_op jit(solution)/shard_map/second/pallas_call | solution.py:773
  131.1 2.0 %collective-permute-start.17 = (f32[8,128]{1,0:T(8,128)}, f32[8,128]{1,0:T(8,128)S(1)}, u32[]{:S(2)}, u32[]{:S(2)}) collective-permute-start(f32[8,128]{1,0:T(8,128)} %get-tuple-element.37.a_ref), channel_id=1, source_target_pairs={{0,32},{4,36},{8,40},{12,44},{16,48},{20,52},{24,56},{28,60},{32,0... | collective-permute-start | bytes 12296 | tf_op jit(solution)/shard_map/ppermute | solution.py:857
  133.1 2.1 %collective-permute-start.16 = (f32[8,128]{1,0:T(8,128)}, f32[8,128]{1,0:T(8,128)S(1)}, u32[]{:S(2)}, u32[]{:S(2)}) collective-permute-start(f32[8,128]{1,0:T(8,128)} %get-tuple-element.37.a_ref), channel_id=1, source_target_pairs={{0,16},{4,20},{8,24},{12,28},{16,0},{20,4},{24,8},{28,12},{32,48},... | collective-permute-start | bytes 12296 | tf_op jit(solution)/shard_map/ppermute | solution.py:857
  135.2 0.9 collective-permute-done.18.d_ref
  136.1 0.3 collective-permute-done.17.c_ref
  136.4 0.6 collective-permute-done.16.b_ref
  137.0 0.6 copy-done.18
  137.6 1.4 sum.1.a_ref
  139.0 1.6 %collective-permute-start.21 = (f32[8,128]{1,0:T(8,128)}, f32[8,128]{1,0:T(8,128)S(1)}, u32[]{:S(2)}, u32[]{:S(2)}) collective-permute-start(f32[8,128]{1,0:T(8,128)} %sum.1.a_ref), channel_id=1, source_target_pairs={{0,192},{4,196},{8,200},{12,204},{16,208},{20,212},{24,216},{28,22... | collective-permute-start | bytes 12296 | tf_op jit(solution)/shard_map/ppermute | solution.py:857
  140.6 1.1 collective-permute-start.20
  141.6 1.4 collective-permute-start.19
  143.1 0.0 collective-permute-done.21.d_ref
  143.1 2.8 %collective-permute-done.20.c_ref = f32[8,128]{1,0:T(8,128)S(1)} collective-permute-done((f32[8,128]{1,0:T(8,128)}, f32[8,128]{1,0:T(8,128)S(1)}, u32[]{:S(2)}, u32[]{:S(2)}) %collective-permute-start.20) | collective-permute-done | bytes 4128 | tf_op jit(solution)/shard_map/ppermute | solution.py:857
  145.9 0.0 collective-permute-done.19.b_ref
  145.9 0.6 copy-done.12
  146.5 7.4 %solve.1 = (f32[6,16]{1,0:T(8,128)}, f32[16,768]{1,0:T(8,128)}) custom-call(s32[4]{0:T(128)} %pad_add_fusion.where_ref, f32[8,128]{1,0:T(8,128)} %sum.1.a_ref, f32[8,128]{1,0:T(8,128)} %copy-done.13, f32[8,128]{1,0:T(8,128)} %copy-done.12, f32[8,128]{1,0:T(8,128)} %copy-done.11, f32[480,128]{1,0:T(8,128)} %get-tuple-element.35.v_ref, ...), custom_call_target="tpu_custom_call" | custom-call | tf_op jit(solution)/shard_map/solve/pallas_call | solution.py:773
  (33 shorter events, 0.1 us)
Async XLA Ops:
  8.1 32.5 %collective-permute-start = (f32[152,768]{1,0:T(8,128)}, f32[152,768]{1,0:T(8,128)S(1)}, u32[]{:S(2)}, u32[]{:S(2)}) collective-permute-start(f32[152,768]{1,0:T(8,128)} %get-tuple-element.22), channel_id=1, source_target_pairs={{4,0},{8,4},{12,8},{16,12},{20,16},{24,20},{28,24},{32,28},{36,32}... | collective-permute-start | bytes 1400840 | tf_op jit(solution)/shard_map/ppermute | solution.py:792
  16.8 23.8 %collective-permute-start.1 = (f32[144,768]{1,0:T(8,128)}, f32[144,768]{1,0:T(8,128)S(1)}, u32[]{:S(2)}, u32[]{:S(2)}) collective-permute-start(f32[144,768]{1,0:T(8,128)} %get-tuple-element.23), channel_id=1, source_target_pairs={{0,4},{4,8},{8,12},{12,16},{16,20},{20,24},{24,28},{28,32},{32,36}... | collective-permute-start | bytes 1327112 | tf_op jit(solution)/shard_map/ppermute | solution.py:792
  40.6 0.8 copy-start.1
  40.6 0.9 copy-start
  57.1 1.6 %collective-permute-start.2 = (f32[96,256]{1,0:T(8,128)}, f32[96,256]{1,0:T(8,128)S(1)}, u32[]{:S(2)}, u32[]{:S(2)}) collective-permute-start(f32[96,256]{1,0:T(8,128)} %get-tuple-element.32), channel_id=1, source_target_pairs={{0,1},{1,0},{2,3},{3,2},{4,5},{5,4},{6,7},{7,6},{8,9},{9,8},{10,11... | collective-permute-start | bytes 294920 | tf_op jit(solution)/shard_map/ppermute | solution.py:836
  59.7 9.1 %collective-permute-start.3 = (f32[48,256]{1,0:T(8,128)S(1)}, f32[48,256]{1,0:T(8,128)S(1)}, u32[]{:S(2)}, u32[]{:S(2)}) collective-permute-start(f32[48,256]{1,0:T(8,128)S(1)} %get-tuple-element.42), channel_id=1, source_target_pairs={{0,2},{1,3},{2,0},{3,1},{4,6},{5,7},{6,4},{7,5},{8,10},{9,11},{10,... | collective-permute-start | bytes 147464 | tf_op jit(solution)/shard_map/ppermute | solution.py:850
  64.3 10.2 %collective-permute-start.5 = (f32[48,256]{1,0:T(8,128)S(1)}, f32[48,256]{1,0:T(8,128)S(1)}, u32[]{:S(2)}, u32[]{:S(2)}) collective-permute-start(f32[48,256]{1,0:T(8,128)S(1)} %get-tuple-element.43), channel_id=1, source_target_pairs={{0,6},{2,4},{4,10},{5,3},{6,8},{7,1},{8,14},{9,7},{10,12},{11,5},{... | collective-permute-start | bytes 147464 | tf_op jit(solution)/shard_map/ppermute | solution.py:848
  66.2 10.8 %collective-permute-start.4 = (f32[48,256]{1,0:T(8,128)S(1)}, f32[48,256]{1,0:T(8,128)S(1)}, u32[]{:S(2)}, u32[]{:S(2)}) collective-permute-start(f32[48,256]{1,0:T(8,128)S(1)} %get-tuple-element.43), channel_id=1, source_target_pairs={{0,4},{2,6},{4,8},{5,1},{6,10},{7,3},{8,12},{9,5},{10,14},{11,7},{... | collective-permute-start | bytes 147464 | tf_op jit(solution)/shard_map/ppermute | solution.py:848
  77.0 6.6 %copy-start.2 = (f32[48,256]{1,0:T(8,128)}, f32[48,256]{1,0:T(8,128)S(1)}, u32[]{:S(2)}) copy-start(f32[48,256]{1,0:T(8,128)S(1)} %add_add_fusion.a_ref) | copy-start | bytes 147460
  77.0 6.0 %collective-permute-start.8 = (f32[48,256]{1,0:T(8,128)S(1)}, f32[48,256]{1,0:T(8,128)S(1)}, u32[]{:S(2)}, u32[]{:S(2)}) collective-permute-start(f32[48,256]{1,0:T(8,128)S(1)} %add_add_fusion.a_ref), channel_id=1, source_target_pairs={{0,12},{4,8},{8,4},{12,0},{16,28},{20,24},{24,20},{28,16},{32,44},... | collective-permute-start | bytes 147464 | tf_op jit(solution)/shard_map/ppermute | solution.py:857
  77.1 5.9 %collective-permute-start.7 = (f32[48,256]{1,0:T(8,128)S(1)}, f32[48,256]{1,0:T(8,128)S(1)}, u32[]{:S(2)}, u32[]{:S(2)}) collective-permute-start(f32[48,256]{1,0:T(8,128)S(1)} %add_add_fusion.a_ref), channel_id=1, source_target_pairs={{0,8},{4,12},{8,0},{12,4},{16,24},{20,28},{24,16},{28,20},{32,40},... | collective-permute-start | bytes 147464 | tf_op jit(solution)/shard_map/ppermute | solution.py:857
  77.2 6.3 %collective-permute-start.6 = (f32[48,256]{1,0:T(8,128)S(1)}, f32[48,256]{1,0:T(8,128)S(1)}, u32[]{:S(2)}, u32[]{:S(2)}) collective-permute-start(f32[48,256]{1,0:T(8,128)S(1)} %add_add_fusion.a_ref), channel_id=1, source_target_pairs={{0,4},{4,0},{8,12},{12,8},{16,20},{20,16},{24,28},{28,24},{32,36},... | collective-permute-start | bytes 147464 | tf_op jit(solution)/shard_map/ppermute | solution.py:857
  83.0 0.6 copy-start.8
  83.0 0.6 copy-start.9
  83.6 0.6 copy-start.10
  85.8 10.4 %collective-permute-start.10 = (f32[192,256]{1,0:T(8,128)}, f32[192,256]{1,0:T(8,128)S(1)}, u32[]{:S(2)}, u32[]{:S(2)}) collective-permute-start(f32[192,256]{1,0:T(8,128)} %place.1.c_ref), channel_id=1, source_target_pairs={{16,0},{20,4},{24,8},{28,12},{32,16},{36,20},{40,24},{44,28},{48,3... | collective-permute-start | bytes 589832 | tf_op jit(solution)/shard_map/ppermute | solution.py:792
  91.1 11.2 %collective-permute-start.9 = (f32[192,256]{1,0:T(8,128)}, f32[192,256]{1,0:T(8,128)S(1)}, u32[]{:S(2)}, u32[]{:S(2)}) collective-permute-start(f32[192,256]{1,0:T(8,128)} %place.1.c_ref), channel_id=1, source_target_pairs={{0,16},{4,20},{8,24},{12,28},{16,32},{20,36},{24,40},{28,44},{32,4... | collective-permute-start | bytes 589832 | tf_op jit(solution)/shard_map/ppermute | solution.py:792
  93.0 9.3 %collective-permute-start.12 = (f32[192,256]{1,0:T(8,128)}, f32[192,256]{1,0:T(8,128)S(1)}, u32[]{:S(2)}, u32[]{:S(2)}) collective-permute-start(f32[192,256]{1,0:T(8,128)} %place.1.c_ref), channel_id=1, source_target_pairs={{0,1},{1,0},{2,3},{3,2},{4,5},{5,4},{6,7},{7,6},{8,9},{9,8},{10,11... | collective-permute-start | bytes 589832 | tf_op jit(solution)/shard_map/ppermute | solution.py:861
  96.1 7.6 %copy-start.3 = (f32[192,256]{1,0:T(8,128)}, f32[192,256]{1,0:T(8,128)S(1)}, u32[]{:S(2)}) copy-start(f32[192,256]{1,0:T(8,128)S(1)} %collective-permute-done.10.n_ref) | copy-start | bytes 589828
  96.1 6.1 %collective-permute-start.13 = (f32[192,256]{1,0:T(8,128)S(1)}, f32[192,256]{1,0:T(8,128)S(1)}, u32[]{:S(2)}, u32[]{:S(2)}) collective-permute-start(f32[192,256]{1,0:T(8,128)S(1)} %collective-permute-done.10.n_ref), channel_id=1, source_target_pairs={{0,1},{1,0},{2,3},{3,2},{4,5},{5,4},{6,7},{7,6},{8,9},{9,8},{10,11... | collective-permute-start | bytes 589832 | tf_op jit(solution)/shard_map/ppermute | solution.py:861
  102.3 1.4 copy-start.4
  102.3 1.4 collective-permute-start.11
  102.3 1.4 copy-start.5
  102.3 1.4 copy-start.6
  103.7 0.7 copy-start.7
  115.3 5.8 %collective-permute-start.15 = (f32[8,128]{1,0:T(8,128)}, f32[8,128]{1,0:T(8,128)S(1)}, u32[]{:S(2)}, u32[]{:S(2)}) collective-permute-start(f32[8,128]{1,0:T(8,128)} %get-tuple-element.36.own_ref), channel_id=1, source_target_pairs={{16,0},{20,4},{24,8},{28,12},{32,16},{36,20},{40,24},{44,28},{48,3... | collective-permute-start | bytes 12296 | tf_op jit(solution)/shard_map/ppermute | solution.py:792
  117.3 7.8 %collective-permute-start.14 = (f32[8,128]{1,0:T(8,128)}, f32[8,128]{1,0:T(8,128)S(1)}, u32[]{:S(2)}, u32[]{:S(2)}) collective-permute-start(f32[8,128]{1,0:T(8,128)} %get-tuple-element.36.own_ref), channel_id=1, source_target_pairs={{0,16},{4,20},{8,24},{12,28},{16,32},{20,36},{24,40},{28,44},{32,4... | collective-permute-start | bytes 12296 | tf_op jit(solution)/shard_map/ppermute | solution.py:792
  121.2 3.9 %copy-start.14 = (f32[8,128]{1,0:T(8,128)}, f32[8,128]{1,0:T(8,128)S(1)}, u32[]{:S(2)}) copy-start(f32[8,128]{1,0:T(8,128)S(1)} %collective-permute-done.15.above_ref) | copy-start | bytes 12292
  125.1 0.6 copy-start.15
  131.1 5.0 %collective-permute-start.18 = (f32[8,128]{1,0:T(8,128)}, f32[8,128]{1,0:T(8,128)S(1)}, u32[]{:S(2)}, u32[]{:S(2)}) collective-permute-start(f32[8,128]{1,0:T(8,128)} %get-tuple-element.37.a_ref), channel_id=1, source_target_pairs={{0,48},{4,52},{8,56},{12,60},{16,32},{20,36},{24,40},{28,44},{32,1... | collective-permute-start | bytes 12296 | tf_op jit(solution)/shard_map/ppermute | solution.py:857
  131.1 5.3 %collective-permute-start.17 = (f32[8,128]{1,0:T(8,128)}, f32[8,128]{1,0:T(8,128)S(1)}, u32[]{:S(2)}, u32[]{:S(2)}) collective-permute-start(f32[8,128]{1,0:T(8,128)} %get-tuple-element.37.a_ref), channel_id=1, source_target_pairs={{0,32},{4,36},{8,40},{12,44},{16,48},{20,52},{24,56},{28,60},{32,0... | collective-permute-start | bytes 12296 | tf_op jit(solution)/shard_map/ppermute | solution.py:857
  133.1 4.0 %collective-permute-start.16 = (f32[8,128]{1,0:T(8,128)}, f32[8,128]{1,0:T(8,128)S(1)}, u32[]{:S(2)}, u32[]{:S(2)}) collective-permute-start(f32[8,128]{1,0:T(8,128)} %get-tuple-element.37.a_ref), channel_id=1, source_target_pairs={{0,16},{4,20},{8,24},{12,28},{16,0},{20,4},{24,8},{28,12},{32,48},... | collective-permute-start | bytes 12296 | tf_op jit(solution)/shard_map/ppermute | solution.py:857
  136.1 0.9 copy-start.16
  136.4 0.6 copy-start.17
  137.0 0.6 copy-start.18
  139.0 4.1 %collective-permute-start.21 = (f32[8,128]{1,0:T(8,128)}, f32[8,128]{1,0:T(8,128)S(1)}, u32[]{:S(2)}, u32[]{:S(2)}) collective-permute-start(f32[8,128]{1,0:T(8,128)} %sum.1.a_ref), channel_id=1, source_target_pairs={{0,192},{4,196},{8,200},{12,204},{16,208},{20,212},{24,216},{28,22... | collective-permute-start | bytes 12296 | tf_op jit(solution)/shard_map/ppermute | solution.py:857
  140.6 5.3 %collective-permute-start.20 = (f32[8,128]{1,0:T(8,128)}, f32[8,128]{1,0:T(8,128)S(1)}, u32[]{:S(2)}, u32[]{:S(2)}) collective-permute-start(f32[8,128]{1,0:T(8,128)} %sum.1.a_ref), channel_id=1, source_target_pairs={{0,128},{4,132},{8,136},{12,140},{16,144},{20,148},{24,152},{28,15... | collective-permute-start | bytes 12296 | tf_op jit(solution)/shard_map/ppermute | solution.py:857
  141.6 4.3 %collective-permute-start.19 = (f32[8,128]{1,0:T(8,128)}, f32[8,128]{1,0:T(8,128)S(1)}, u32[]{:S(2)}, u32[]{:S(2)}) collective-permute-start(f32[8,128]{1,0:T(8,128)} %sum.1.a_ref), channel_id=1, source_target_pairs={{0,64},{4,68},{8,72},{12,76},{16,80},{20,84},{24,88},{28,92},{32,9... | collective-permute-start | bytes 12296 | tf_op jit(solution)/shard_map/ppermute | solution.py:857
  143.1 2.8 %copy-start.11 = (f32[8,128]{1,0:T(8,128)}, f32[8,128]{1,0:T(8,128)S(1)}, u32[]{:S(2)}) copy-start(f32[8,128]{1,0:T(8,128)S(1)} %collective-permute-done.21.d_ref) | copy-start | bytes 12292
  145.9 0.6 copy-start.12
  145.9 0.6 copy-start.13

commit v7 on v6

--- a/solution.py
+++ b/solution.py
@@ -296,7 +296,7 @@
     where_ref, rdown_ref, rup_ref, curv_ref, grad_ref, block_ref, depth_ref, damp_ref, tab_ref,
     geo_hbm, b_hbm, bt_hbm,
     keep_ref, send_ref, base_ref, scale_ref, g_hbm,
-    half_ref, hi_ref, in_ref, q_ref, w_ref, t_ref, geo_ref, b_ref, bt_ref, g_ref,
+    half_ref, hi0_ref, hi1_ref, in_ref, q0_ref, q1_ref, w_ref, t_ref, geo_ref, b_ref, bt_ref, g_ref,
     geo_sems, b_sems, g_sems, bt_sem,
 ):
     def piece(src, dst, sems, f, rows):
@@ -327,10 +327,8 @@
         in_ref[128 + f * 8 : 136 + f * 8, :] = jnp.broadcast_to(damp_ref[f : f + 1, :], (8, plocal))
     lane = iota((8, LANES), 1)
 
-    def frame(f, carry, merged):
+    def tiles(f, merged, hi_ref, q_ref):
         eight = pl.ds(pl.multiple_of(f * 8, 8), 8)
-        piece(geo_hbm, geo_ref, geo_sems, f, 5 * SLOTS).wait()
-        piece(b_hbm, b_ref, b_sems, f, GROUP).wait()
         tab = tab_ref[pl.ds(pl.multiple_of(f * SLOTS + 8 * merged, 8), 8), :]
         t0, t1, t2 = [jnp.broadcast_to(tab[:, k : k + 1], (8, LANES)) for k in (9, 10, 11)]
         acc = [0.0] * 26
@@ -379,12 +377,13 @@
                 for k, x in enumerate(rows):
                     g_ref[pl.ds(pl.multiple_of(f * GROUP + k * SLOTS + 8 * h, 8), 8), lanes] = x
                     hi_ref[k * SLOTS + 8 * h : k * SLOTS + 8 * h + 8, lanes] = x
-        piece(g_ref, g_hbm, g_sems, f, GROUP).start()
-        rows = pl.ds(pl.multiple_of(f * GROUP, 8), GROUP)
-        q_ref[...] = block_ref[rows, :]
+        q_ref[...] = block_ref[pl.ds(pl.multiple_of(f * GROUP, 8), GROUP), :]
         for c, tile in enumerate(diagonal_rows(acc, merged)):
             at = slice(c * SLOTS + 8 * merged, c * SLOTS + 8 * merged + 8)
             q_ref[at, :] = q_ref[at, :] + tile
+
+    def matmuls(f, hi_ref, q_ref):
+        rows = pl.ds(pl.multiple_of(f * GROUP, 8), GROUP)
         g = hi_ref[...]
         top, low = pair_of(g)
         both = lax.dot_general(
@@ -407,10 +406,22 @@
         )
         w_ref[rows, LANES : 2 * LANES] = w[:, LANES : 2 * LANES] + dot(q_top, b_low[:, LANES : 2 * LANES])
         w_ref[rows, 2 * LANES :] = w[:, 2 * LANES :]
+
+    def frames(i, carry, merged):
+        work = ((2 * i, hi0_ref, q0_ref), (2 * i + 1, hi1_ref, q1_ref))
+        for f, _, _ in work:
+            piece(geo_hbm, geo_ref, geo_sems, f, 5 * SLOTS).wait()
+            piece(b_hbm, b_ref, b_sems, f, GROUP).wait()
+        for f, hi_ref, q_ref in work:
+            tiles(f, merged, hi_ref, q_ref)
+        for f, hi_ref, q_ref in work:
+            matmuls(f, hi_ref, q_ref)
+        for f, _, _ in work:
+            piece(g_ref, g_hbm, g_sems, f, GROUP).start()
         return carry
 
-    lax.fori_loop(0, 8, functools.partial(frame, merged=0), 0)
-    lax.fori_loop(8, 16, functools.partial(frame, merged=1), 0)
+    lax.fori_loop(0, 4, functools.partial(frames, merged=0), 0)
+    lax.fori_loop(4, 8, functools.partial(frames, merged=1), 0)
     bt_copy.wait()
     bt_top, bt_low = pair_of(bt_ref[...])
     w_top, w_low = pair_of(w_ref[...])
@@ -542,17 +553,19 @@
     return pl.ds(pl.multiple_of(j * 8, 8), 8)
 
 
-def product(s_ref, up_ref, high_ref, low_ref, j):
+def product(s_ref, up_ref, col, split, j):
     acc = None
-    sources = (
-        (s_ref[block_at(j), 0:LANES], j),
-        (s_ref[block_at(j - 1), LANES : 2 * LANES], j - 1),
-        (up_ref[block_at(j), :], j + 1),
-    )
-    for s, at in sources:
-        high = high_ref[block_at(at), :]
-        p, e = times(s, high)
-        e = e + s * low_ref[block_at(at), :]
+    lower, upper = slice(0, LANES), slice(LANES, 2 * LANES)
+    sources = ((s_ref, lower, j, j), (s_ref, upper, j - 1, j - 1), (up_ref, slice(0, LANES), j, j + 1))
+    for n, (ref, lanes, row, at) in enumerate(sources):
+        s = ref[block_at(row), lanes]
+        if split is None:
+            sh, sl = halves(s)
+        else:
+            sh, sl = [x[block_at(row), lanes] for x in (split[2:] if n == 2 else split[:2])]
+        high, low, hh, hl = [x[block_at(at), :] for x in col]
+        p = s * high
+        e = (((sh * hh - p) + sh * hl + sl * hh) + sl * hl) + s * low
         for r in range(0, GROUP, 8):
             term = p[r : r + 8], e[r : r + 8]
             acc = term if acc is None else plus(acc, term)
@@ -562,20 +575,25 @@
     return acc[0] * SHRINK, acc[1] * SHRINK
 
 
+def put_column(col, j, high, low):
+    col[0][block_at(j), :] = high
+    col[1][block_at(j), :] = low
+    col[2][block_at(j), :], col[3][block_at(j), :] = halves(high)
+
+
 def store_tile(ref, at, pair):
     row = iota((8, LANES), 0)
     ref[tile_at(at), :] = jnp.where(row == 0, pair[0], jnp.where(row == 1, pair[1], 0.0))
 
 
-def powers(s_ref, up_ref, v_ref, cols, first, count, edge, base):
+def powers(s_ref, up_ref, v_ref, cols, split, first, count, edge, base):
     for k in range(count):
         here, there = cols[k % 2], cols[1 - k % 2]
 
         def one(j, carry):
-            pair = product(s_ref, up_ref, here[0], here[1], j)
+            pair = product(s_ref, up_ref, here, split, j)
             store_tile(v_ref, (first + k) * BLOCKS + j, pair)
-            there[0][block_at(j), :] = to_column(pair[0][0:1])
-            there[1][block_at(j), :] = to_column(pair[1][0:1])
+            put_column(there, j, to_column(pair[0][0:1]), to_column(pair[1][0:1]))
             return carry
 
         lax.fori_loop(base + k * edge, BLOCKS - base - k * edge, one, 0)
@@ -583,8 +601,10 @@
 
 def first_kernel(
     where_ref, p_ref, c_ref, n_ref, p2_ref, c2_ref, n2_ref,
-    s_ref, up_ref, v_ref, v4_ref, h0_ref, l0_ref, h1_ref, l1_ref,
+    s_ref, up_ref, v_ref, v4_ref, *scratch,
 ):
+    cols = scratch[0:4], scratch[4:8]
+    split = scratch[8:12]
     core = where_ref[2]
     mine = pl.multiple_of(48 * core, 8)
     theirs = pl.multiple_of(48 - 48 * core, 8)
@@ -601,19 +621,19 @@
     def prepare(j, carry):
         own = s_ref[block_at(j), 0:LANES]
         rhs = jnp.broadcast_to(own[:, LANES - 1 : LANES], (GROUP, LANES)) * FIRST
-        h0_ref[block_at(j), :] = rhs
-        l0_ref[block_at(j), :] = jnp.zeros_like(rhs)
+        put_column(cols[0], j, rhs, jnp.zeros_like(rhs))
         store_tile(v_ref, j, (to_row(rhs), jnp.zeros((1, LANES), F32)))
         s_ref[block_at(j), 0:LANES] = jnp.where(lane < GROUP, own, 0.0) + jnp.where(
             diagonal, POSE_REG, 0.0
         )
         up = jnp.concatenate([s_ref[block_at(j), LANES : 2 * LANES], zero], axis=0).T
         up_ref[block_at(j), :] = up[0:GROUP]
+        split[0][block_at(j), :], split[1][block_at(j), :] = halves(s_ref[block_at(j), :])
+        split[2][block_at(j), :], split[3][block_at(j), :] = halves(up[0:GROUP])
         return carry
 
     lax.fori_loop(0, BLOCKS, prepare, 0)
-    cols = ((h0_ref, l0_ref), (h1_ref, l1_ref))
-    powers(s_ref, up_ref, v_ref, cols, 1, 4, 1, 1)
+    powers(s_ref, up_ref, v_ref, cols, split, 1, 4, 1, 1)
     for j in range(4):
         at = (4 * BLOCKS + 4 + j) * 8
         v4_ref[j : j + 1, :] = v_ref[at : at + 1, :]
@@ -621,19 +641,17 @@
 
 
 def second_kernel(
-    s_ref, up_ref, v_ref, below_ref, own_ref, above_ref, out_ref, v45_ref,
-    h0_ref, l0_ref, h1_ref, l1_ref,
+    s_ref, up_ref, v_ref, below_ref, own_ref, above_ref, out_ref, v45_ref, *scratch,
 ):
+    cols = scratch[0:4], scratch[4:8]
     for g, ref in enumerate((below_ref, own_ref, above_ref)):
         for j in range(4):
             pair = ref[j : j + 1, :], ref[4 + j : 5 + j, :]
             at = g * 4 + j
             store_tile(v45_ref, at, pair)
             if 1 < at < 10:
-                h0_ref[block_at(at), :] = to_column(pair[0])
-                l0_ref[block_at(at), :] = to_column(pair[1])
-    cols = ((h0_ref, l0_ref), (h1_ref, l1_ref))
-    powers(s_ref, up_ref, v45_ref, cols, 1, 2, 1, 3)
+                put_column(cols[0], at, to_column(pair[0]), to_column(pair[1]))
+    powers(s_ref, up_ref, v45_ref, cols, None, 1, 2, 1, 3)
     zero = jnp.zeros((1, LANES), F32)
     total = None
     for j in range(4, 8):
@@ -819,7 +837,9 @@
         scratch=[
             pltpu.VMEM((4 * FD * 8, plocal), F32),
             pltpu.VMEM((GROUP + 16, plocal), F32),
+            pltpu.VMEM((GROUP + 16, plocal), F32),
             pltpu.VMEM((256, plocal), F32),
+            pltpu.VMEM((GROUP, LANES), F32),
             pltpu.VMEM((GROUP, LANES), F32),
             pltpu.VMEM((f_dev * GROUP, 3 * LANES), F32),
             pltpu.VMEM((192, 3 * LANES), F32),
@@ -866,15 +886,16 @@
     (quad,) = call(place_kernel, "place", [(192, 256)], 1, spot, *mates(half, 1))
     pieces = halo(quad)
     wide = BLOCKS * GROUP
-    scratch = [pltpu.VMEM((wide, LANES), F32)] * 4
+    columns = [pltpu.VMEM((wide, LANES), F32)] * 8
+    split = [pltpu.VMEM((wide, 2 * LANES), F32)] * 2 + [pltpu.VMEM((wide, LANES), F32)] * 2
     s, up, vs, v4 = call(
         first_kernel, "first",
         [(wide, 256), (wide, LANES), (5 * BLOCKS * 8, LANES), (8, LANES)],
-        1, spot, *pieces, *[twin(x) for x in pieces], scratch=scratch,
+        1, spot, *pieces, *[twin(x) for x in pieces], scratch=columns + split,
     )
     part, v45 = call(
         second_kernel, "second", [(8, LANES), (3 * BLOCKS * 8, LANES)], 0, s, up, vs, *halo(v4),
-        scratch=scratch,
+        scratch=columns,
     )
     (part,) = call(sum_kernel, "sum", [(8, LANES)], 0, *mates(part, 4))
     pose_step, depth_step = call(

time: 157 us -> 156 us (level)
  no operation moved by 1% of the time
where the time goes in v7:
time: 156 us; the launch traced here: 153 us
  Pallas kernels  66.7 us (43%)
  starting transfers between devices  45 us (29%)
  waiting for transfers between devices  31.3 us (20%)
  local copies, waits for them, and re-layouts  7.33 us (5%)
    pallas_call x10, Pallas kernels, call(): pl.pallas_call(kernel, name=name, out_shape=[jax.ShapeDtypeStruct(s, F32)...  66.7 us
    ppermute x6, starting transfers between devices, shift(): lax.ppermute(block, 'frames', [(i, i + step) for i in range(count) if 0 <...  23.6 us
    ppermute x6, waiting for transfers between devices, shift(): lax.ppermute(block, 'frames', [(i, i + step) for i in range(count) if 0 <...  12.9 us
    ppermute x9, starting transfers between devices, mates(): lax.ppermute(v, 'frames', [(i, i ^ k * step) for i in range(count)])  12.6 us
    ppermute x2, waiting for transfers between devices, to_neighbour(): return lax.ppermute(rim, both_axes, route)  8.67 us
    ppermute x9, waiting for transfers between devices, mates(): lax.ppermute(v, 'frames', [(i, i ^ k * step) for i in range(count)])  6.7 us
    ppermute x1, starting transfers between devices, per_device(): own_far = lax.ppermute(own_half, 'pix', [(i, i ^ 2) for i in range(pixes)])  4.57 us
    unnamed x38, local copies, waits for them, and re-layouts  4.07 us
  transfers between devices with their start and end apart: 22, of which 14 were waited for; matrix products, arithmetic and copies ran while one was open for 0% of the time, Pallas kernels for 14%

profile of v7, /device:TPU:8, one launch (start us, length us, event | category | flops | bytes accessed | tf_op | source)
XLA Modules:
  0.0 152.9 jit_solution(9340920475633300815)
XLA Ops:
  0.7 3.3 %copy_bitcast_fusion = (f32[2,192,768]{2,1,0:T(8,128)}, f32[2,192,768]{2,1,0:T(8,128)}) fusion(f32[192,2,768]{2,1,0:T(2,128)} %param.14, f32[192,2,768]{2,1,0:T(2,128)} %param.13), kind=kLoop, calls=%fused_computation | loop fusion | bytes 4718592 | tf_op jit(solution)/shard_map/transpose | solution.py:814
  3.9 0.6 pad_add_fusion.where_ref
  4.5 3.6 %rim.1 = (f32[152,768]{1,0:T(8,128)}, f32[144,768]{1,0:T(8,128)}) custom-call(s32[4]{0:T(128)} %pad_add_fusion.where_ref, s32[2,192]{1,0:T(2,128)} %ef_ref.3, f32[2,192,768]{2,1,0:T(8,128)} %get-tuple-element.45.flow_ref, f32[2,192,768]{2,1,0:T(8,128)} %get-tuple-element.44.weight_ref, s32[192,768]{1,0:T(8,128)} %mask_ref.3), custom_call_target="tpu_custom_call" | custom-call | tf_op jit(solution)/shard_map/rim/pallas_call | solution.py:791
  8.1 8.6 %collective-permute-start = (f32[152,768]{1,0:T(8,128)}, f32[152,768]{1,0:T(8,128)S(1)}, u32[]{:S(2)}, u32[]{:S(2)}) collective-permute-start(f32[152,768]{1,0:T(8,128)} %get-tuple-element.22), channel_id=1, source_target_pairs={{4,0},{8,4},{12,8},{16,12},{20,16},{24,20},{28,24},{32,28},{36,32}... | collective-permute-start | bytes 1400840 | tf_op jit(solution)/shard_map/ppermute | solution.py:810
  16.8 1.9 %collective-permute-start.1 = (f32[144,768]{1,0:T(8,128)}, f32[144,768]{1,0:T(8,128)S(1)}, u32[]{:S(2)}, u32[]{:S(2)}) collective-permute-start(f32[144,768]{1,0:T(8,128)} %get-tuple-element.23), channel_id=1, source_target_pairs={{0,4},{4,8},{8,12},{12,16},{16,20},{20,24},{24,28},{28,32},{32,36}... | collective-permute-start | bytes 1327112 | tf_op jit(solution)/shard_map/ppermute | solution.py:810
  18.7 4.9 %own.1.own_ref = f32[1024,768]{1,0:T(8,128)} custom-call(s32[4]{0:T(128)} %pad_add_fusion.where_ref, s32[2,192]{1,0:T(2,128)} %ef_ref.3, f32[2,192,768]{2,1,0:T(8,128)} %get-tuple-element.45.flow_ref, f32[2,192,768]{2,1,0:T(8,128)} %get-tuple-element.44.weight_ref, s32[192,768]{1,0:T(8,128)} %mask_ref.3), custom_call_target="tpu_custom_call" | custom-call | tf_op jit(solution)/shard_map/own/pallas_call | solution.py:791
  23.6 6.1 %pose.1 = (f32[256,128]{1,0:T(8,128)}, f32[1536,384]{1,0:T(8,128)}, f32[192,1536]{1,0:T(8,128)}) custom-call(s32[4]{0:T(128)} %pad_add_fusion.where_ref, f32[3,1024]{1,0:T(4,128)} %rotvec_ref.1, f32[3,1024]{1,0:T(4,128)} %trans_ref.1), custom_call_target="tpu_custom_call" | custom-call | tf_op jit(solution)/shard_map/pose/pallas_call | solution.py:791
  29.7 10.9 %early.1 = (f32[1280,768]{1,0:T(8,128)}, f32[128,768]{1,0:T(8,128)}, f32[128,768]{1,0:T(8,128)}, f32[1536,128]{1,0:T(8,128)}) custom-call(s32[4]{0:T(128)} %pad_add_fusion.where_ref, f32[1024,768]{1,0:T(8,128)} %own.1.own_ref, f32[16,768]{1,0:T(8,128)} %depth_ref.3, f32[256,128]{1,0:T(8,128)} %get-tuple-element.24.tab_ref), custom_call_target="tpu_custom_call" | custom-call | tf_op jit(solution)/shard_map/early/pallas_call | solution.py:791
  40.6 0.0 collective-permute-done.1.rup_ref
  40.6 0.0 collective-permute-done.rdown_ref
  40.6 0.7 copy-done.1
  41.4 0.2 copy-done
  41.5 15.0 %main.1 = (f32[96,256]{1,0:T(8,128)}, f32[96,256]{1,0:T(8,128)}, f32[128,768]{1,0:T(8,128)}, f32[128,768]{1,0:T(8,128)}, f32[1536,768]{1,0:T(8,128)}) custom-call(s32[4]{0:T(128)} %pad_add_fusion.where_ref, f32[152,768]{1,0:T(8,128)} %copy-done, f32[144,768]{1,0:T(8,128)} %copy-done.1, f32[128,768]{1,0:T(8,128)} %get-tuple-element.25.curv_ref, ...), custom_call_target="tpu_custom_call" | custom-call | tf_op jit(solution)/shard_map/main/pallas_call | solution.py:791
  56.6 0.1 collective-permute-start.2
  56.7 1.5 collective-permute-done.2
  58.2 0.9 add.21
  59.1 4.6 %collective-permute-start.3 = (f32[48,256]{1,0:T(8,128)S(1)}, f32[48,256]{1,0:T(8,128)S(1)}, u32[]{:S(2)}, u32[]{:S(2)}) collective-permute-start(f32[48,256]{1,0:T(8,128)S(1)} %get-tuple-element.42), channel_id=1, source_target_pairs={{0,2},{1,3},{2,0},{3,1},{4,6},{5,7},{6,4},{7,5},{8,10},{9,11},{10,... | collective-permute-start | bytes 147464 | tf_op jit(solution)/shard_map/ppermute | solution.py:870
  63.7 1.9 %collective-permute-start.5 = (f32[48,256]{1,0:T(8,128)S(1)}, f32[48,256]{1,0:T(8,128)S(1)}, u32[]{:S(2)}, u32[]{:S(2)}) collective-permute-start(f32[48,256]{1,0:T(8,128)S(1)} %get-tuple-element.43), channel_id=1, source_target_pairs={{0,6},{2,4},{4,10},{5,3},{6,8},{7,1},{8,14},{9,7},{10,12},{11,5},{... | collective-permute-start | bytes 147464 | tf_op jit(solution)/shard_map/ppermute | solution.py:868
  65.6 1.9 %collective-permute-start.4 = (f32[48,256]{1,0:T(8,128)S(1)}, f32[48,256]{1,0:T(8,128)S(1)}, u32[]{:S(2)}, u32[]{:S(2)}) collective-permute-start(f32[48,256]{1,0:T(8,128)S(1)} %get-tuple-element.43), channel_id=1, source_target_pairs={{0,4},{2,6},{4,8},{5,1},{6,10},{7,3},{8,12},{9,5},{10,14},{11,7},{... | collective-permute-start | bytes 147464 | tf_op jit(solution)/shard_map/ppermute | solution.py:868
  67.5 0.2 collective-permute-done.3
  67.7 6.1 %collective-permute-done.5 = f32[48,256]{1,0:T(8,128)S(1)} collective-permute-done((f32[48,256]{1,0:T(8,128)S(1)}, f32[48,256]{1,0:T(8,128)S(1)}, u32[]{:S(2)}, u32[]{:S(2)}) %collective-permute-start.5) | collective-permute-done | bytes 49184 | tf_op jit(solution)/shard_map/ppermute | solution.py:868
  73.9 2.5 %collective-permute-done.4 = f32[48,256]{1,0:T(8,128)S(1)} collective-permute-done((f32[48,256]{1,0:T(8,128)S(1)}, f32[48,256]{1,0:T(8,128)S(1)}, u32[]{:S(2)}, u32[]{:S(2)}) %collective-permute-start.4) | collective-permute-done | bytes 49184 | tf_op jit(solution)/shard_map/ppermute | solution.py:868
  76.4 0.0 copy-start.2
  76.4 0.1 collective-permute-start.8
  76.5 0.1 collective-permute-start.7
  76.6 4.3 %collective-permute-start.6 = (f32[48,256]{1,0:T(8,128)S(1)}, f32[48,256]{1,0:T(8,128)S(1)}, u32[]{:S(2)}, u32[]{:S(2)}) collective-permute-start(f32[48,256]{1,0:T(8,128)S(1)} %add_add_fusion.a_ref), channel_id=1, source_target_pairs={{0,4},{4,0},{8,12},{12,8},{16,20},{20,16},{24,28},{28,24},{32,36},... | collective-permute-start | bytes 147464 | tf_op jit(solution)/shard_map/ppermute | solution.py:877
  80.9 1.5 collective-permute-done.8.d_ref
  82.4 0.0 collective-permute-done.7.c_ref
  82.4 0.6 collective-permute-done.6.b_ref
  82.9 0.0 copy-done.8
  83.0 0.0 copy-done.9
  83.0 0.6 copy-done.10
  83.6 1.6 %place.1.c_ref = f32[192,256]{1,0:T(8,128)} custom-call(s32[4]{0:T(128)} %pad_add_fusion.where_ref, f32[48,256]{1,0:T(8,128)} %copy-done.2, f32[48,256]{1,0:T(8,128)} %copy-done.10, f32[48,256]{1,0:T(8,128)} %copy-done.9, f32[48,256]{1,0:T(8,128)} %copy-done.8), custom_call_target="tpu_custom_call" | custom-call | tf_op jit(solution)/shard_map/place/pallas_call | solution.py:791
  85.2 5.3 %collective-permute-start.10 = (f32[192,256]{1,0:T(8,128)}, f32[192,256]{1,0:T(8,128)S(1)}, u32[]{:S(2)}, u32[]{:S(2)}) collective-permute-start(f32[192,256]{1,0:T(8,128)} %place.1.c_ref), channel_id=1, source_target_pairs={{16,0},{20,4},{24,8},{28,12},{32,16},{36,20},{40,24},{44,28},{48,3... | collective-permute-start | bytes 589832 | tf_op jit(solution)/shard_map/ppermute | solution.py:810
  90.5 1.9 %collective-permute-start.9 = (f32[192,256]{1,0:T(8,128)}, f32[192,256]{1,0:T(8,128)S(1)}, u32[]{:S(2)}, u32[]{:S(2)}) collective-permute-start(f32[192,256]{1,0:T(8,128)} %place.1.c_ref), channel_id=1, source_target_pairs={{0,16},{4,20},{8,24},{12,28},{16,32},{20,36},{24,40},{28,44},{32,4... | collective-permute-start | bytes 589832 | tf_op jit(solution)/shard_map/ppermute | solution.py:810
  92.4 0.3 collective-permute-start.12
  92.7 2.9 %collective-permute-done.10.n_ref = f32[192,256]{1,0:T(8,128)S(1)} collective-permute-done((f32[192,256]{1,0:T(8,128)}, f32[192,256]{1,0:T(8,128)S(1)}, u32[]{:S(2)}, u32[]{:S(2)}) %collective-permute-start.10) | collective-permute-done | bytes 196640 | tf_op jit(solution)/shard_map/ppermute | solution.py:810
  95.6 0.0 collective-permute-start.13
  95.6 6.1 %collective-permute-done.9.p_ref = f32[192,256]{1,0:T(8,128)S(1)} collective-permute-done((f32[192,256]{1,0:T(8,128)}, f32[192,256]{1,0:T(8,128)S(1)}, u32[]{:S(2)}, u32[]{:S(2)}) %collective-permute-start.9) | collective-permute-done | bytes 196640 | tf_op jit(solution)/shard_map/ppermute | solution.py:810
  101.7 0.0 collective-permute-done.13.n2_ref
  101.7 1.4 collective-permute-done.11.p2_ref
  103.2 0.7 copy-done.7
  103.8 10.5 %first.1 = (f32[1152,256]{1,0:T(8,128)}, f32[1152,128]{1,0:T(8,128)}, f32[480,128]{1,0:T(8,128)}, f32[8,128]{1,0:T(8,128)}) custom-call(s32[4]{0:T(128)} %pad_add_fusion.where_ref, f32[192,256]{1,0:T(8,128)} %copy-done.4, f32[192,256]{1,0:T(8,128)} %place.1.c_ref, f32[192,256]{1,0:T(8,128)} %copy-done.3, f32[192,256]{1,0:T(8,128)} %copy-done.7, ...), custom_call_target="tpu_custom_call" | custom-call | tf_op jit(solution)/shard_map/first/pallas_call | solution.py:791
  114.3 1.9 %collective-permute-start.15 = (f32[8,128]{1,0:T(8,128)}, f32[8,128]{1,0:T(8,128)S(1)}, u32[]{:S(2)}, u32[]{:S(2)}) collective-permute-start(f32[8,128]{1,0:T(8,128)} %get-tuple-element.36.own_ref), channel_id=1, source_target_pairs={{16,0},{20,4},{24,8},{28,12},{32,16},{36,20},{40,24},{44,28},{48,3... | collective-permute-start | bytes 12296 | tf_op jit(solution)/shard_map/ppermute | solution.py:810
  116.2 3.9 %collective-permute-start.14 = (f32[8,128]{1,0:T(8,128)}, f32[8,128]{1,0:T(8,128)S(1)}, u32[]{:S(2)}, u32[]{:S(2)}) collective-permute-start(f32[8,128]{1,0:T(8,128)} %get-tuple-element.36.own_ref), channel_id=1, source_target_pairs={{0,16},{4,20},{8,24},{12,28},{16,32},{20,36},{24,40},{28,44},{32,4... | collective-permute-start | bytes 12296 | tf_op jit(solution)/shard_map/ppermute | solution.py:810
  120.2 3.9 %collective-permute-done.14.below_ref = f32[8,128]{1,0:T(8,128)S(1)} collective-permute-done((f32[8,128]{1,0:T(8,128)}, f32[8,128]{1,0:T(8,128)S(1)}, u32[]{:S(2)}, u32[]{:S(2)}) %collective-permute-start.14) | collective-permute-done | bytes 4128 | tf_op jit(solution)/shard_map/ppermute | solution.py:810
  124.0 0.6 copy-done.15
  124.6 5.4 %second.1 = (f32[8,128]{1,0:T(8,128)}, f32[288,128]{1,0:T(8,128)}) custom-call(f32[1152,256]{1,0:T(8,128)} %get-tuple-element.33.s_ref, f32[1152,128]{1,0:T(8,128)} %get-tuple-element.34.up_ref, f32[480,128]{1,0:T(8,128)} %get-tuple-element.35.v_ref, f32[8,128]{1,0:T(8,128)} %copy-done.15, f32[8,128]{1,0:T(8,128)} %get-tuple-element.36.own_ref, ...), custom_call_target="tpu_custom_call" | custom-call | tf_op jit(solution)/shard_map/second/pallas_call | solution.py:791
  130.0 0.0 collective-permute-start.18
  130.0 2.0 %collective-permute-start.17 = (f32[8,128]{1,0:T(8,128)}, f32[8,128]{1,0:T(8,128)S(1)}, u32[]{:S(2)}, u32[]{:S(2)}) collective-permute-start(f32[8,128]{1,0:T(8,128)} %get-tuple-element.37.a_ref), channel_id=1, source_target_pairs={{0,32},{4,36},{8,40},{12,44},{16,48},{20,52},{24,56},{28,60},{32,0... | collective-permute-start | bytes 12296 | tf_op jit(solution)/shard_map/ppermute | solution.py:877
  131.9 2.1 %collective-permute-start.16 = (f32[8,128]{1,0:T(8,128)}, f32[8,128]{1,0:T(8,128)S(1)}, u32[]{:S(2)}, u32[]{:S(2)}) collective-permute-start(f32[8,128]{1,0:T(8,128)} %get-tuple-element.37.a_ref), channel_id=1, source_target_pairs={{0,16},{4,20},{8,24},{12,28},{16,0},{20,4},{24,8},{28,12},{32,48},... | collective-permute-start | bytes 12296 | tf_op jit(solution)/shard_map/ppermute | solution.py:877
  134.1 0.9 collective-permute-done.18.d_ref
  135.0 0.3 collective-permute-done.17.c_ref
  135.3 0.6 collective-permute-done.16.b_ref
  135.9 0.6 copy-done.18
  136.5 1.3 sum.1.a_ref
  137.8 1.6 %collective-permute-start.21 = (f32[8,128]{1,0:T(8,128)}, f32[8,128]{1,0:T(8,128)S(1)}, u32[]{:S(2)}, u32[]{:S(2)}) collective-permute-start(f32[8,128]{1,0:T(8,128)} %sum.1.a_ref), channel_id=1, source_target_pairs={{0,192},{4,196},{8,200},{12,204},{16,208},{20,212},{24,216},{28,22... | collective-permute-start | bytes 12296 | tf_op jit(solution)/shard_map/ppermute | solution.py:877
  139.4 1.1 collective-permute-start.20
  140.5 1.4 collective-permute-start.19
  141.9 0.0 collective-permute-done.21.d_ref
  141.9 2.8 %collective-permute-done.20.c_ref = f32[8,128]{1,0:T(8,128)S(1)} collective-permute-done((f32[8,128]{1,0:T(8,128)}, f32[8,128]{1,0:T(8,128)S(1)}, u32[]{:S(2)}, u32[]{:S(2)}) %collective-permute-start.20) | collective-permute-done | bytes 4128 | tf_op jit(solution)/shard_map/ppermute | solution.py:877
  144.7 0.0 collective-permute-done.19.b_ref
  144.8 0.6 copy-done.12
  145.3 7.4 %solve.1 = (f32[6,16]{1,0:T(8,128)}, f32[16,768]{1,0:T(8,128)}) custom-call(s32[4]{0:T(128)} %pad_add_fusion.where_ref, f32[8,128]{1,0:T(8,128)} %sum.1.a_ref, f32[8,128]{1,0:T(8,128)} %copy-done.13, f32[8,128]{1,0:T(8,128)} %copy-done.12, f32[8,128]{1,0:T(8,128)} %copy-done.11, f32[480,128]{1,0:T(8,128)} %get-tuple-element.35.v_ref, ...), custom_call_target="tpu_custom_call" | custom-call | tf_op jit(solution)/shard_map/solve/pallas_call | solution.py:791
  (33 shorter events, 0.1 us)
Async XLA Ops:
  8.1 32.5 %collective-permute-start = (f32[152,768]{1,0:T(8,128)}, f32[152,768]{1,0:T(8,128)S(1)}, u32[]{:S(2)}, u32[]{:S(2)}) collective-permute-start(f32[152,768]{1,0:T(8,128)} %get-tuple-element.22), channel_id=1, source_target_pairs={{4,0},{8,4},{12,8},{16,12},{20,16},{24,20},{28,24},{32,28},{36,32}... | collective-permute-start | bytes 1400840 | tf_op jit(solution)/shard_map/ppermute | solution.py:810
  16.8 23.8 %collective-permute-start.1 = (f32[144,768]{1,0:T(8,128)}, f32[144,768]{1,0:T(8,128)S(1)}, u32[]{:S(2)}, u32[]{:S(2)}) collective-permute-start(f32[144,768]{1,0:T(8,128)} %get-tuple-element.23), channel_id=1, source_target_pairs={{0,4},{4,8},{8,12},{12,16},{16,20},{20,24},{24,28},{28,32},{32,36}... | collective-permute-start | bytes 1327112 | tf_op jit(solution)/shard_map/ppermute | solution.py:810
  40.6 0.8 copy-start.1
  40.6 0.9 copy-start
  56.6 1.6 %collective-permute-start.2 = (f32[96,256]{1,0:T(8,128)}, f32[96,256]{1,0:T(8,128)S(1)}, u32[]{:S(2)}, u32[]{:S(2)}) collective-permute-start(f32[96,256]{1,0:T(8,128)} %get-tuple-element.32), channel_id=1, source_target_pairs={{0,1},{1,0},{2,3},{3,2},{4,5},{5,4},{6,7},{7,6},{8,9},{9,8},{10,11... | collective-permute-start | bytes 294920 | tf_op jit(solution)/shard_map/ppermute | solution.py:856
  59.1 8.6 %collective-permute-start.3 = (f32[48,256]{1,0:T(8,128)S(1)}, f32[48,256]{1,0:T(8,128)S(1)}, u32[]{:S(2)}, u32[]{:S(2)}) collective-permute-start(f32[48,256]{1,0:T(8,128)S(1)} %get-tuple-element.42), channel_id=1, source_target_pairs={{0,2},{1,3},{2,0},{3,1},{4,6},{5,7},{6,4},{7,5},{8,10},{9,11},{10,... | collective-permute-start | bytes 147464 | tf_op jit(solution)/shard_map/ppermute | solution.py:870
  63.7 10.2 %collective-permute-start.5 = (f32[48,256]{1,0:T(8,128)S(1)}, f32[48,256]{1,0:T(8,128)S(1)}, u32[]{:S(2)}, u32[]{:S(2)}) collective-permute-start(f32[48,256]{1,0:T(8,128)S(1)} %get-tuple-element.43), channel_id=1, source_target_pairs={{0,6},{2,4},{4,10},{5,3},{6,8},{7,1},{8,14},{9,7},{10,12},{11,5},{... | collective-permute-start | bytes 147464 | tf_op jit(solution)/shard_map/ppermute | solution.py:868
  65.6 10.8 %collective-permute-start.4 = (f32[48,256]{1,0:T(8,128)S(1)}, f32[48,256]{1,0:T(8,128)S(1)}, u32[]{:S(2)}, u32[]{:S(2)}) collective-permute-start(f32[48,256]{1,0:T(8,128)S(1)} %get-tuple-element.43), channel_id=1, source_target_pairs={{0,4},{2,6},{4,8},{5,1},{6,10},{7,3},{8,12},{9,5},{10,14},{11,7},{... | collective-permute-start | bytes 147464 | tf_op jit(solution)/shard_map/ppermute | solution.py:868
  76.4 6.6 %copy-start.2 = (f32[48,256]{1,0:T(8,128)}, f32[48,256]{1,0:T(8,128)S(1)}, u32[]{:S(2)}) copy-start(f32[48,256]{1,0:T(8,128)S(1)} %add_add_fusion.a_ref) | copy-start | bytes 147460
  76.4 6.0 %collective-permute-start.8 = (f32[48,256]{1,0:T(8,128)S(1)}, f32[48,256]{1,0:T(8,128)S(1)}, u32[]{:S(2)}, u32[]{:S(2)}) collective-permute-start(f32[48,256]{1,0:T(8,128)S(1)} %add_add_fusion.a_ref), channel_id=1, source_target_pairs={{0,12},{4,8},{8,4},{12,0},{16,28},{20,24},{24,20},{28,16},{32,44},... | collective-permute-start | bytes 147464 | tf_op jit(solution)/shard_map/ppermute | solution.py:877
  76.5 5.9 %collective-permute-start.7 = (f32[48,256]{1,0:T(8,128)S(1)}, f32[48,256]{1,0:T(8,128)S(1)}, u32[]{:S(2)}, u32[]{:S(2)}) collective-permute-start(f32[48,256]{1,0:T(8,128)S(1)} %add_add_fusion.a_ref), channel_id=1, source_target_pairs={{0,8},{4,12},{8,0},{12,4},{16,24},{20,28},{24,16},{28,20},{32,40},... | collective-permute-start | bytes 147464 | tf_op jit(solution)/shard_map/ppermute | solution.py:877
  76.6 6.3 %collective-permute-start.6 = (f32[48,256]{1,0:T(8,128)S(1)}, f32[48,256]{1,0:T(8,128)S(1)}, u32[]{:S(2)}, u32[]{:S(2)}) collective-permute-start(f32[48,256]{1,0:T(8,128)S(1)} %add_add_fusion.a_ref), channel_id=1, source_target_pairs={{0,4},{4,0},{8,12},{12,8},{16,20},{20,16},{24,28},{28,24},{32,36},... | collective-permute-start | bytes 147464 | tf_op jit(solution)/shard_map/ppermute | solution.py:877
  82.4 0.6 copy-start.8
  82.4 0.6 copy-start.9
  83.0 0.6 copy-start.10
  85.2 10.4 %collective-permute-start.10 = (f32[192,256]{1,0:T(8,128)}, f32[192,256]{1,0:T(8,128)S(1)}, u32[]{:S(2)}, u32[]{:S(2)}) collective-permute-start(f32[192,256]{1,0:T(8,128)} %place.1.c_ref), channel_id=1, source_target_pairs={{16,0},{20,4},{24,8},{28,12},{32,16},{36,20},{40,24},{44,28},{48,3... | collective-permute-start | bytes 589832 | tf_op jit(solution)/shard_map/ppermute | solution.py:810
  90.5 11.2 %collective-permute-start.9 = (f32[192,256]{1,0:T(8,128)}, f32[192,256]{1,0:T(8,128)S(1)}, u32[]{:S(2)}, u32[]{:S(2)}) collective-permute-start(f32[192,256]{1,0:T(8,128)} %place.1.c_ref), channel_id=1, source_target_pairs={{0,16},{4,20},{8,24},{12,28},{16,32},{20,36},{24,40},{28,44},{32,4... | collective-permute-start | bytes 589832 | tf_op jit(solution)/shard_map/ppermute | solution.py:810
  92.4 9.3 %collective-permute-start.12 = (f32[192,256]{1,0:T(8,128)}, f32[192,256]{1,0:T(8,128)S(1)}, u32[]{:S(2)}, u32[]{:S(2)}) collective-permute-start(f32[192,256]{1,0:T(8,128)} %place.1.c_ref), channel_id=1, source_target_pairs={{0,1},{1,0},{2,3},{3,2},{4,5},{5,4},{6,7},{7,6},{8,9},{9,8},{10,11... | collective-permute-start | bytes 589832 | tf_op jit(solution)/shard_map/ppermute | solution.py:881
  95.6 7.6 %copy-start.3 = (f32[192,256]{1,0:T(8,128)}, f32[192,256]{1,0:T(8,128)S(1)}, u32[]{:S(2)}) copy-start(f32[192,256]{1,0:T(8,128)S(1)} %collective-permute-done.10.n_ref) | copy-start | bytes 589828
  95.6 6.1 %collective-permute-start.13 = (f32[192,256]{1,0:T(8,128)S(1)}, f32[192,256]{1,0:T(8,128)S(1)}, u32[]{:S(2)}, u32[]{:S(2)}) collective-permute-start(f32[192,256]{1,0:T(8,128)S(1)} %collective-permute-done.10.n_ref), channel_id=1, source_target_pairs={{0,1},{1,0},{2,3},{3,2},{4,5},{5,4},{6,7},{7,6},{8,9},{9,8},{10,11... | collective-permute-start | bytes 589832 | tf_op jit(solution)/shard_map/ppermute | solution.py:881
  101.7 1.4 copy-start.4
  101.7 1.4 collective-permute-start.11
  101.7 1.4 copy-start.5
  101.7 1.4 copy-start.6
  103.1 0.7 copy-start.7
  114.3 5.8 %collective-permute-start.15 = (f32[8,128]{1,0:T(8,128)}, f32[8,128]{1,0:T(8,128)S(1)}, u32[]{:S(2)}, u32[]{:S(2)}) collective-permute-start(f32[8,128]{1,0:T(8,128)} %get-tuple-element.36.own_ref), channel_id=1, source_target_pairs={{16,0},{20,4},{24,8},{28,12},{32,16},{36,20},{40,24},{44,28},{48,3... | collective-permute-start | bytes 12296 | tf_op jit(solution)/shard_map/ppermute | solution.py:810
  116.2 7.8 %collective-permute-start.14 = (f32[8,128]{1,0:T(8,128)}, f32[8,128]{1,0:T(8,128)S(1)}, u32[]{:S(2)}, u32[]{:S(2)}) collective-permute-start(f32[8,128]{1,0:T(8,128)} %get-tuple-element.36.own_ref), channel_id=1, source_target_pairs={{0,16},{4,20},{8,24},{12,28},{16,32},{20,36},{24,40},{28,44},{32,4... | collective-permute-start | bytes 12296 | tf_op jit(solution)/shard_map/ppermute | solution.py:810
  120.1 3.9 %copy-start.14 = (f32[8,128]{1,0:T(8,128)}, f32[8,128]{1,0:T(8,128)S(1)}, u32[]{:S(2)}) copy-start(f32[8,128]{1,0:T(8,128)S(1)} %collective-permute-done.15.above_ref) | copy-start | bytes 12292
  124.0 0.6 copy-start.15
  130.0 5.0 %collective-permute-start.18 = (f32[8,128]{1,0:T(8,128)}, f32[8,128]{1,0:T(8,128)S(1)}, u32[]{:S(2)}, u32[]{:S(2)}) collective-permute-start(f32[8,128]{1,0:T(8,128)} %get-tuple-element.37.a_ref), channel_id=1, source_target_pairs={{0,48},{4,52},{8,56},{12,60},{16,32},{20,36},{24,40},{28,44},{32,1... | collective-permute-start | bytes 12296 | tf_op jit(solution)/shard_map/ppermute | solution.py:877
  130.0 5.3 %collective-permute-start.17 = (f32[8,128]{1,0:T(8,128)}, f32[8,128]{1,0:T(8,128)S(1)}, u32[]{:S(2)}, u32[]{:S(2)}) collective-permute-start(f32[8,128]{1,0:T(8,128)} %get-tuple-element.37.a_ref), channel_id=1, source_target_pairs={{0,32},{4,36},{8,40},{12,44},{16,48},{20,52},{24,56},{28,60},{32,0... | collective-permute-start | bytes 12296 | tf_op jit(solution)/shard_map/ppermute | solution.py:877
  131.9 4.0 %collective-permute-start.16 = (f32[8,128]{1,0:T(8,128)}, f32[8,128]{1,0:T(8,128)S(1)}, u32[]{:S(2)}, u32[]{:S(2)}) collective-permute-start(f32[8,128]{1,0:T(8,128)} %get-tuple-element.37.a_ref), channel_id=1, source_target_pairs={{0,16},{4,20},{8,24},{12,28},{16,0},{20,4},{24,8},{28,12},{32,48},... | collective-permute-start | bytes 12296 | tf_op jit(solution)/shard_map/ppermute | solution.py:877
  135.0 0.9 copy-start.16
  135.3 0.6 copy-start.17
  135.9 0.6 copy-start.18
  137.8 4.1 %collective-permute-start.21 = (f32[8,128]{1,0:T(8,128)}, f32[8,128]{1,0:T(8,128)S(1)}, u32[]{:S(2)}, u32[]{:S(2)}) collective-permute-start(f32[8,128]{1,0:T(8,128)} %sum.1.a_ref), channel_id=1, source_target_pairs={{0,192},{4,196},{8,200},{12,204},{16,208},{20,212},{24,216},{28,22... | collective-permute-start | bytes 12296 | tf_op jit(solution)/shard_map/ppermute | solution.py:877
  139.4 5.3 %collective-permute-start.20 = (f32[8,128]{1,0:T(8,128)}, f32[8,128]{1,0:T(8,128)S(1)}, u32[]{:S(2)}, u32[]{:S(2)}) collective-permute-start(f32[8,128]{1,0:T(8,128)} %sum.1.a_ref), channel_id=1, source_target_pairs={{0,128},{4,132},{8,136},{12,140},{16,144},{20,148},{24,152},{28,15... | collective-permute-start | bytes 12296 | tf_op jit(solution)/shard_map/ppermute | solution.py:877
  140.5 4.3 %collective-permute-start.19 = (f32[8,128]{1,0:T(8,128)}, f32[8,128]{1,0:T(8,128)S(1)}, u32[]{:S(2)}, u32[]{:S(2)}) collective-permute-start(f32[8,128]{1,0:T(8,128)} %sum.1.a_ref), channel_id=1, source_target_pairs={{0,64},{4,68},{8,72},{12,76},{16,80},{20,84},{24,88},{28,92},{32,9... | collective-permute-start | bytes 12296 | tf_op jit(solution)/shard_map/ppermute | solution.py:877
  141.9 2.8 %copy-start.11 = (f32[8,128]{1,0:T(8,128)}, f32[8,128]{1,0:T(8,128)S(1)}, u32[]{:S(2)}) copy-start(f32[8,128]{1,0:T(8,128)S(1)} %collective-permute-done.21.d_ref) | copy-start | bytes 12292
  144.7 0.6 copy-start.12
  144.7 0.6 copy-start.13

commit v8 on v7

--- a/solution.py
+++ b/solution.py
@@ -81,13 +81,6 @@
     spread(where_ref, ef_ref, flow_ref, weight_ref, mask_ref, True, write)
 
 
-def own_kernel(where_ref, ef_ref, flow_ref, weight_ref, mask_ref, own_ref):
-    def write(q, lanes, cut):
-        own_ref[q * 256 : (q + 1) * 256, lanes] = cut
-
-    spread(where_ref, ef_ref, flow_ref, weight_ref, mask_ref, False, write)
-
-
 def rotation_rows(w):
     x, y, z = w
     zero = jnp.zeros_like(x)
@@ -115,9 +108,11 @@
     at_source = start + (pair >> 4)
     at_target = jnp.clip(at_source + delta, 0, frames - 1)
     poses = jnp.concatenate([rotvec_ref[...], trans_ref[...], jnp.zeros((2, frames), F32)], axis=0)
+    first = start - RADIUS
+    poses = pltpu.roll(poses, (2 * frames - first) % frames, 1)[:, 0:LANES]
 
     def pick(at):
-        hot = (iota((frames, FD * SLOTS), 0) == at).astype(F32)
+        hot = (iota((LANES, FD * SLOTS), 0) == at - first).astype(F32)
         return jnp.dot(poses, hot, precision=HIGHEST, preferred_element_type=F32)
 
     src = pick(at_source)
@@ -243,8 +238,13 @@
 
 
 def early_kernel(
-    where_ref, own_ref, depth_ref, tab_ref, geo_ref, curv_ref, grad_ref, block_ref, in_ref
+    where_ref, ef_ref, flow_ref, weight_ref, mask_ref, depth_ref, tab_ref,
+    geo_ref, curv_ref, grad_ref, block_ref, in_ref, own_ref,
 ):
+    def write(q, lanes, cut):
+        own_ref[q * 256 : (q + 1) * 256, lanes] = cut
+
+    spread(where_ref, ef_ref, flow_ref, weight_ref, mask_ref, False, write)
     plocal = depth_ref.shape[1]
     chunks = plocal // LANES
     for f in range(FD):
@@ -817,7 +817,6 @@
     )
     from_after = shift(down, -1)
     from_before = shift(up, 1)
-    (own,) = call(own_kernel, "own", [(4 * f_dev * SLOTS, plocal)], 1, spot, *edges)
     tab, b, bt = call(
         pose_kernel, "pose",
         [(f_dev * SLOTS, LANES), (f_dev * GROUP, 3 * LANES), (192, f_dev * GROUP)],
@@ -827,7 +826,8 @@
     geo, curv, grad, block = call(
         early_kernel, "early",
         [(5 * pairs, plocal), (f_dev * 8, plocal), (f_dev * 8, plocal), (f_dev * GROUP, LANES)],
-        1, spot, own, inv_depth, tab, scratch=[pltpu.VMEM((f_dev * 8, plocal), F32)],
+        1, spot, *edges, inv_depth, tab,
+        scratch=[pltpu.VMEM((f_dev * 8, plocal), F32), pltpu.VMEM((4 * pairs, plocal), F32)],
     )
     keep, send, base, scale, g = call(
         main_kernel, "main",

time: 156 us -> 151 us (0.968)
  Pallas kernels: 66.7 us -> 62.2 us
    pallas_call x10 -> x9, Pallas kernels: 66.7 us -> 62.2 us  [call(): pl.pallas_call(kernel, name=name, out_shape=[jax.ShapeDtypeStruct(s, F32)...]
  transfers between devices with their start and end apart: 22 -> 22, of which waited for: 14 -> 14; matrix products, arithmetic and copies ran while one was open for 0% -> 0% of each run, Pallas kernels for 14% -> 12%
where the time goes in v8:
time: 151 us; the launch traced here: 149 us
  Pallas kernels  62.2 us (41%)
  starting transfers between devices  45.2 us (30%)
  waiting for transfers between devices  31.2 us (21%)
  local copies, waits for them, and re-layouts  7.35 us (5%)
  other arithmetic  1.54 us (1%)
    pallas_call x9, Pallas kernels, call(): pl.pallas_call(kernel, name=name, out_shape=[jax.ShapeDtypeStruct(s, F32)...  62.2 us
    ppermute x6, starting transfers between devices, shift(): lax.ppermute(block, 'frames', [(i, i + step) for i in range(count) if 0 <...  22.2 us
    ppermute x6, waiting for transfers between devices, shift(): lax.ppermute(block, 'frames', [(i, i + step) for i in range(count) if 0 <...  12.7 us
    ppermute x9, starting transfers between devices, mates(): lax.ppermute(v, 'frames', [(i, i ^ k * step) for i in range(count)])  12.6 us
    ppermute x2, waiting for transfers between devices, to_neighbour(): return lax.ppermute(rim, both_axes, route)  8.83 us
    ppermute x9, waiting for transfers between devices, mates(): lax.ppermute(v, 'frames', [(i, i ^ k * step) for i in range(count)])  6.7 us
    ppermute x1, starting transfers between devices, per_device(): own_far = lax.ppermute(own_half, 'pix', [(i, i ^ 2) for i in range(pixes)])  5.31 us
    ppermute x2, starting transfers between devices, to_neighbour(): return lax.ppermute(rim, both_axes, route)  4.87 us
  transfers between devices with their start and end apart: 22, of which 14 were waited for; matrix products, arithmetic and copies ran while one was open for 0% of the time, Pallas kernels for 12%

profile of v8, /device:TPU:8, one launch (start us, length us, event | category | flops | bytes accessed | tf_op | source)
XLA Modules:
  0.0 148.5 jit_solution(2631107644893128929)
XLA Ops:
  0.7 3.3 %copy_bitcast_fusion = (f32[2,192,768]{2,1,0:T(8,128)}, f32[2,192,768]{2,1,0:T(8,128)}) fusion(f32[192,2,768]{2,1,0:T(2,128)} %param.14, f32[192,2,768]{2,1,0:T(2,128)} %param.13), kind=kLoop, calls=%fused_computation | loop fusion | bytes 4718592 | tf_op jit(solution)/shard_map/transpose | solution.py:814
  3.9 0.6 pad_add_fusion.where_ref
  4.5 3.6 %rim.1 = (f32[152,768]{1,0:T(8,128)}, f32[144,768]{1,0:T(8,128)}) custom-call(s32[4]{0:T(128)} %pad_add_fusion.where_ref, s32[2,192]{1,0:T(2,128)} %ef_ref.3, f32[2,192,768]{2,1,0:T(8,128)} %get-tuple-element.45.flow_ref, f32[2,192,768]{2,1,0:T(8,128)} %get-tuple-element.44.weight_ref, s32[192,768]{1,0:T(8,128)} %mask_ref.3), custom_call_target="tpu_custom_call" | custom-call | tf_op jit(solution)/shard_map/rim/pallas_call | solution.py:791
  8.2 8.6 %collective-permute-start = (f32[152,768]{1,0:T(8,128)}, f32[152,768]{1,0:T(8,128)S(1)}, u32[]{:S(2)}, u32[]{:S(2)}) collective-permute-start(f32[152,768]{1,0:T(8,128)} %get-tuple-element.22), channel_id=1, source_target_pairs={{4,0},{8,4},{12,8},{16,12},{20,16},{24,20},{28,24},{32,28},{36,32}... | collective-permute-start | bytes 1400840 | tf_op jit(solution)/shard_map/ppermute | solution.py:810
  16.8 1.9 %collective-permute-start.1 = (f32[144,768]{1,0:T(8,128)}, f32[144,768]{1,0:T(8,128)S(1)}, u32[]{:S(2)}, u32[]{:S(2)}) collective-permute-start(f32[144,768]{1,0:T(8,128)} %get-tuple-element.23), channel_id=1, source_target_pairs={{0,4},{4,8},{8,12},{12,16},{16,20},{20,24},{24,28},{28,32},{32,36}... | collective-permute-start | bytes 1327112 | tf_op jit(solution)/shard_map/ppermute | solution.py:810
  18.7 5.1 %pose.1 = (f32[256,128]{1,0:T(8,128)}, f32[1536,384]{1,0:T(8,128)}, f32[192,1536]{1,0:T(8,128)}) custom-call(s32[4]{0:T(128)} %pad_add_fusion.where_ref, f32[3,1024]{1,0:T(4,128)} %rotvec_ref.1, f32[3,1024]{1,0:T(4,128)} %trans_ref.1), custom_call_target="tpu_custom_call" | custom-call | tf_op jit(solution)/shard_map/pose/pallas_call | solution.py:791
  23.9 12.3 %early.1 = (f32[1280,768]{1,0:T(8,128)}, f32[128,768]{1,0:T(8,128)}, f32[128,768]{1,0:T(8,128)}, f32[1536,128]{1,0:T(8,128)}) custom-call(s32[4]{0:T(128)} %pad_add_fusion.where_ref, s32[2,192]{1,0:T(2,128)} %ef_ref.3, f32[2,192,768]{2,1,0:T(8,128)} %get-tuple-element.45.flow_ref, f32[2,192,768]{2,1,0:T(8,128)} %get-tuple-element.44.weight_ref, ...), custom_call_target="tpu_custom_call" | custom-call | tf_op jit(solution)/shard_map/early/pallas_call | solution.py:791
  36.2 1.0 collective-permute-done.1.rup_ref
  37.2 0.0 collective-permute-done.rdown_ref
  37.2 0.8 copy-done.1
  37.9 0.2 copy-done
  38.1 15.0 %main.1 = (f32[96,256]{1,0:T(8,128)}, f32[96,256]{1,0:T(8,128)}, f32[128,768]{1,0:T(8,128)}, f32[128,768]{1,0:T(8,128)}, f32[1536,768]{1,0:T(8,128)}) custom-call(s32[4]{0:T(128)} %pad_add_fusion.where_ref, f32[152,768]{1,0:T(8,128)} %copy-done, f32[144,768]{1,0:T(8,128)} %copy-done.1, f32[128,768]{1,0:T(8,128)} %get-tuple-element.25.curv_ref, ...), custom_call_target="tpu_custom_call" | custom-call | tf_op jit(solution)/shard_map/main/pallas_call | solution.py:791
  53.1 0.1 collective-permute-start.2
  53.2 1.5 %collective-permute-done.2 = f32[96,256]{1,0:T(8,128)S(1)} collective-permute-done((f32[96,256]{1,0:T(8,128)}, f32[96,256]{1,0:T(8,128)S(1)}, u32[]{:S(2)}, u32[]{:S(2)}) %collective-permute-start.2) | collective-permute-done | bytes 98336 | tf_op jit(solution)/shard_map/ppermute | solution.py:856
  54.7 0.9 add.21
  55.6 5.3 %collective-permute-start.3 = (f32[48,256]{1,0:T(8,128)S(1)}, f32[48,256]{1,0:T(8,128)S(1)}, u32[]{:S(2)}, u32[]{:S(2)}) collective-permute-start(f32[48,256]{1,0:T(8,128)S(1)} %get-tuple-element.42), channel_id=1, source_target_pairs={{0,2},{1,3},{2,0},{3,1},{4,6},{5,7},{6,4},{7,5},{8,10},{9,11},{10,... | collective-permute-start | bytes 147464 | tf_op jit(solution)/shard_map/ppermute | solution.py:870
  60.9 2.9 %collective-permute-start.5 = (f32[48,256]{1,0:T(8,128)S(1)}, f32[48,256]{1,0:T(8,128)S(1)}, u32[]{:S(2)}, u32[]{:S(2)}) collective-permute-start(f32[48,256]{1,0:T(8,128)S(1)} %get-tuple-element.43), channel_id=1, source_target_pairs={{0,6},{2,4},{4,10},{5,3},{6,8},{7,1},{8,14},{9,7},{10,12},{11,5},{... | collective-permute-start | bytes 147464 | tf_op jit(solution)/shard_map/ppermute | solution.py:868
  63.9 1.9 %collective-permute-start.4 = (f32[48,256]{1,0:T(8,128)S(1)}, f32[48,256]{1,0:T(8,128)S(1)}, u32[]{:S(2)}, u32[]{:S(2)}) collective-permute-start(f32[48,256]{1,0:T(8,128)S(1)} %get-tuple-element.43), channel_id=1, source_target_pairs={{0,4},{2,6},{4,8},{5,1},{6,10},{7,3},{8,12},{9,5},{10,14},{11,7},{... | collective-permute-start | bytes 147464 | tf_op jit(solution)/shard_map/ppermute | solution.py:868
  65.8 0.0 collective-permute-done.3
  65.8 5.3 %collective-permute-done.5 = f32[48,256]{1,0:T(8,128)S(1)} collective-permute-done((f32[48,256]{1,0:T(8,128)S(1)}, f32[48,256]{1,0:T(8,128)S(1)}, u32[]{:S(2)}, u32[]{:S(2)}) %collective-permute-start.5) | collective-permute-done | bytes 49184 | tf_op jit(solution)/shard_map/ppermute | solution.py:868
  71.1 3.5 %collective-permute-done.4 = f32[48,256]{1,0:T(8,128)S(1)} collective-permute-done((f32[48,256]{1,0:T(8,128)S(1)}, f32[48,256]{1,0:T(8,128)S(1)}, u32[]{:S(2)}, u32[]{:S(2)}) %collective-permute-start.4) | collective-permute-done | bytes 49184 | tf_op jit(solution)/shard_map/ppermute | solution.py:868
  74.7 0.0 copy-start.2
  74.7 0.1 collective-permute-start.8
  74.8 0.1 collective-permute-start.7
  74.9 4.3 %collective-permute-start.6 = (f32[48,256]{1,0:T(8,128)S(1)}, f32[48,256]{1,0:T(8,128)S(1)}, u32[]{:S(2)}, u32[]{:S(2)}) collective-permute-start(f32[48,256]{1,0:T(8,128)S(1)} %add_add_fusion.a_ref), channel_id=1, source_target_pairs={{0,4},{4,0},{8,12},{12,8},{16,20},{20,16},{24,28},{28,24},{32,36},... | collective-permute-start | bytes 147464 | tf_op jit(solution)/shard_map/ppermute | solution.py:877
  79.2 1.5 %collective-permute-done.8.d_ref = f32[48,256]{1,0:T(8,128)S(1)} collective-permute-done((f32[48,256]{1,0:T(8,128)S(1)}, f32[48,256]{1,0:T(8,128)S(1)}, u32[]{:S(2)}, u32[]{:S(2)}) %collective-permute-start.8) | collective-permute-done | bytes 49184 | tf_op jit(solution)/shard_map/ppermute | solution.py:877
  80.7 0.0 collective-permute-done.7.c_ref
  80.7 0.6 collective-permute-done.6.b_ref
  81.2 0.0 copy-done.8
  81.3 0.0 copy-done.9
  81.3 0.6 copy-done.10
  81.9 1.6 %place.1.c_ref = f32[192,256]{1,0:T(8,128)} custom-call(s32[4]{0:T(128)} %pad_add_fusion.where_ref, f32[48,256]{1,0:T(8,128)} %copy-done.2, f32[48,256]{1,0:T(8,128)} %copy-done.10, f32[48,256]{1,0:T(8,128)} %copy-done.9, f32[48,256]{1,0:T(8,128)} %copy-done.8), custom_call_target="tpu_custom_call" | custom-call | tf_op jit(solution)/shard_map/place/pallas_call | solution.py:791
  83.5 2.8 %collective-permute-start.10 = (f32[192,256]{1,0:T(8,128)}, f32[192,256]{1,0:T(8,128)S(1)}, u32[]{:S(2)}, u32[]{:S(2)}) collective-permute-start(f32[192,256]{1,0:T(8,128)} %place.1.c_ref), channel_id=1, source_target_pairs={{16,0},{20,4},{24,8},{28,12},{32,16},{36,20},{40,24},{44,28},{48,3... | collective-permute-start | bytes 589832 | tf_op jit(solution)/shard_map/ppermute | solution.py:810
  86.2 3.1 %collective-permute-start.9 = (f32[192,256]{1,0:T(8,128)}, f32[192,256]{1,0:T(8,128)S(1)}, u32[]{:S(2)}, u32[]{:S(2)}) collective-permute-start(f32[192,256]{1,0:T(8,128)} %place.1.c_ref), channel_id=1, source_target_pairs={{0,16},{4,20},{8,24},{12,28},{16,32},{20,36},{24,40},{28,44},{32,4... | collective-permute-start | bytes 589832 | tf_op jit(solution)/shard_map/ppermute | solution.py:810
  89.3 0.1 collective-permute-start.12
  89.4 1.8 %collective-permute-done.10.n_ref = f32[192,256]{1,0:T(8,128)S(1)} collective-permute-done((f32[192,256]{1,0:T(8,128)}, f32[192,256]{1,0:T(8,128)S(1)}, u32[]{:S(2)}, u32[]{:S(2)}) %collective-permute-start.10) | collective-permute-done | bytes 196640 | tf_op jit(solution)/shard_map/ppermute | solution.py:810
  91.2 0.0 collective-permute-start.13
  91.2 6.0 %collective-permute-done.9.p_ref = f32[192,256]{1,0:T(8,128)S(1)} collective-permute-done((f32[192,256]{1,0:T(8,128)}, f32[192,256]{1,0:T(8,128)S(1)}, u32[]{:S(2)}, u32[]{:S(2)}) %collective-permute-start.9) | collective-permute-done | bytes 196640 | tf_op jit(solution)/shard_map/ppermute | solution.py:810
  97.3 0.0 collective-permute-start.11
  97.3 0.0 collective-permute-done.12.c2_ref
  97.3 0.0 collective-permute-done.13.n2_ref
  97.3 1.4 collective-permute-done.11.p2_ref
  98.8 0.7 copy-done.7
  99.4 10.5 %first.1 = (f32[1152,256]{1,0:T(8,128)}, f32[1152,128]{1,0:T(8,128)}, f32[480,128]{1,0:T(8,128)}, f32[8,128]{1,0:T(8,128)}) custom-call(s32[4]{0:T(128)} %pad_add_fusion.where_ref, f32[192,256]{1,0:T(8,128)} %copy-done.4, f32[192,256]{1,0:T(8,128)} %place.1.c_ref, f32[192,256]{1,0:T(8,128)} %copy-done.3, f32[192,256]{1,0:T(8,128)} %copy-done.7, ...), custom_call_target="tpu_custom_call" | custom-call | tf_op jit(solution)/shard_map/first/pallas_call | solution.py:791
  109.9 1.9 %collective-permute-start.15 = (f32[8,128]{1,0:T(8,128)}, f32[8,128]{1,0:T(8,128)S(1)}, u32[]{:S(2)}, u32[]{:S(2)}) collective-permute-start(f32[8,128]{1,0:T(8,128)} %get-tuple-element.36.own_ref), channel_id=1, source_target_pairs={{16,0},{20,4},{24,8},{28,12},{32,16},{36,20},{40,24},{44,28},{48,3... | collective-permute-start | bytes 12296 | tf_op jit(solution)/shard_map/ppermute | solution.py:810
  111.8 3.9 %collective-permute-start.14 = (f32[8,128]{1,0:T(8,128)}, f32[8,128]{1,0:T(8,128)S(1)}, u32[]{:S(2)}, u32[]{:S(2)}) collective-permute-start(f32[8,128]{1,0:T(8,128)} %get-tuple-element.36.own_ref), channel_id=1, source_target_pairs={{0,16},{4,20},{8,24},{12,28},{16,32},{20,36},{24,40},{28,44},{32,4... | collective-permute-start | bytes 12296 | tf_op jit(solution)/shard_map/ppermute | solution.py:810
  115.8 3.9 %collective-permute-done.14.below_ref = f32[8,128]{1,0:T(8,128)S(1)} collective-permute-done((f32[8,128]{1,0:T(8,128)}, f32[8,128]{1,0:T(8,128)S(1)}, u32[]{:S(2)}, u32[]{:S(2)}) %collective-permute-start.14) | collective-permute-done | bytes 4128 | tf_op jit(solution)/shard_map/ppermute | solution.py:810
  119.6 0.6 copy-done.15
  120.2 5.4 %second.1 = (f32[8,128]{1,0:T(8,128)}, f32[288,128]{1,0:T(8,128)}) custom-call(f32[1152,256]{1,0:T(8,128)} %get-tuple-element.33.s_ref, f32[1152,128]{1,0:T(8,128)} %get-tuple-element.34.up_ref, f32[480,128]{1,0:T(8,128)} %get-tuple-element.35.v_ref, f32[8,128]{1,0:T(8,128)} %copy-done.15, f32[8,128]{1,0:T(8,128)} %get-tuple-element.36.own_ref, ...), custom_call_target="tpu_custom_call" | custom-call | tf_op jit(solution)/shard_map/second/pallas_call | solution.py:791
  125.6 0.0 collective-permute-start.18
  125.6 2.0 %collective-permute-start.17 = (f32[8,128]{1,0:T(8,128)}, f32[8,128]{1,0:T(8,128)S(1)}, u32[]{:S(2)}, u32[]{:S(2)}) collective-permute-start(f32[8,128]{1,0:T(8,128)} %get-tuple-element.37.a_ref), channel_id=1, source_target_pairs={{0,32},{4,36},{8,40},{12,44},{16,48},{20,52},{24,56},{28,60},{32,0... | collective-permute-start | bytes 12296 | tf_op jit(solution)/shard_map/ppermute | solution.py:877
  127.5 2.1 %collective-permute-start.16 = (f32[8,128]{1,0:T(8,128)}, f32[8,128]{1,0:T(8,128)S(1)}, u32[]{:S(2)}, u32[]{:S(2)}) collective-permute-start(f32[8,128]{1,0:T(8,128)} %get-tuple-element.37.a_ref), channel_id=1, source_target_pairs={{0,16},{4,20},{8,24},{12,28},{16,0},{20,4},{24,8},{28,12},{32,48},... | collective-permute-start | bytes 12296 | tf_op jit(solution)/shard_map/ppermute | solution.py:877
  129.7 0.9 collective-permute-done.18.d_ref
  130.6 0.3 collective-permute-done.17.c_ref
  130.9 0.6 collective-permute-done.16.b_ref
  131.5 0.6 copy-done.18
  132.1 1.4 sum.1.a_ref
  133.5 1.6 %collective-permute-start.21 = (f32[8,128]{1,0:T(8,128)}, f32[8,128]{1,0:T(8,128)S(1)}, u32[]{:S(2)}, u32[]{:S(2)}) collective-permute-start(f32[8,128]{1,0:T(8,128)} %sum.1.a_ref), channel_id=1, source_target_pairs={{0,192},{4,196},{8,200},{12,204},{16,208},{20,212},{24,216},{28,22... | collective-permute-start | bytes 12296 | tf_op jit(solution)/shard_map/ppermute | solution.py:877
  135.0 1.0 collective-permute-start.20
  136.0 1.5 %collective-permute-start.19 = (f32[8,128]{1,0:T(8,128)}, f32[8,128]{1,0:T(8,128)S(1)}, u32[]{:S(2)}, u32[]{:S(2)}) collective-permute-start(f32[8,128]{1,0:T(8,128)} %sum.1.a_ref), channel_id=1, source_target_pairs={{0,64},{4,68},{8,72},{12,76},{16,80},{20,84},{24,88},{28,92},{32,9... | collective-permute-start | bytes 12296 | tf_op jit(solution)/shard_map/ppermute | solution.py:877
  137.6 0.0 collective-permute-done.21.d_ref
  137.6 2.8 %collective-permute-done.20.c_ref = f32[8,128]{1,0:T(8,128)S(1)} collective-permute-done((f32[8,128]{1,0:T(8,128)}, f32[8,128]{1,0:T(8,128)S(1)}, u32[]{:S(2)}, u32[]{:S(2)}) %collective-permute-start.20) | collective-permute-done | bytes 4128 | tf_op jit(solution)/shard_map/ppermute | solution.py:877
  140.4 0.6 copy-done.12
  141.0 7.4 %solve.1 = (f32[6,16]{1,0:T(8,128)}, f32[16,768]{1,0:T(8,128)}) custom-call(s32[4]{0:T(128)} %pad_add_fusion.where_ref, f32[8,128]{1,0:T(8,128)} %sum.1.a_ref, f32[8,128]{1,0:T(8,128)} %copy-done.13, f32[8,128]{1,0:T(8,128)} %copy-done.12, f32[8,128]{1,0:T(8,128)} %copy-done.11, f32[480,128]{1,0:T(8,128)} %get-tuple-element.35.v_ref, ...), custom_call_target="tpu_custom_call" | custom-call | tf_op jit(solution)/shard_map/solve/pallas_call | solution.py:791
  (32 shorter events, 0.1 us)
Async XLA Ops:
  8.2 29.0 %collective-permute-start = (f32[152,768]{1,0:T(8,128)}, f32[152,768]{1,0:T(8,128)S(1)}, u32[]{:S(2)}, u32[]{:S(2)}) collective-permute-start(f32[152,768]{1,0:T(8,128)} %get-tuple-element.22), channel_id=1, source_target_pairs={{4,0},{8,4},{12,8},{16,12},{20,16},{24,20},{28,24},{32,28},{36,32}... | collective-permute-start | bytes 1400840 | tf_op jit(solution)/shard_map/ppermute | solution.py:810
  16.8 20.4 %collective-permute-start.1 = (f32[144,768]{1,0:T(8,128)}, f32[144,768]{1,0:T(8,128)S(1)}, u32[]{:S(2)}, u32[]{:S(2)}) collective-permute-start(f32[144,768]{1,0:T(8,128)} %get-tuple-element.23), channel_id=1, source_target_pairs={{0,4},{4,8},{8,12},{12,16},{16,20},{20,24},{24,28},{28,32},{32,36}... | collective-permute-start | bytes 1327112 | tf_op jit(solution)/shard_map/ppermute | solution.py:810
  37.2 0.8 copy-start.1
  37.2 0.9 copy-start
  53.1 1.6 %collective-permute-start.2 = (f32[96,256]{1,0:T(8,128)}, f32[96,256]{1,0:T(8,128)S(1)}, u32[]{:S(2)}, u32[]{:S(2)}) collective-permute-start(f32[96,256]{1,0:T(8,128)} %get-tuple-element.32), channel_id=1, source_target_pairs={{0,1},{1,0},{2,3},{3,2},{4,5},{5,4},{6,7},{7,6},{8,9},{9,8},{10,11... | collective-permute-start | bytes 294920 | tf_op jit(solution)/shard_map/ppermute | solution.py:856
  55.6 10.2 %collective-permute-start.3 = (f32[48,256]{1,0:T(8,128)S(1)}, f32[48,256]{1,0:T(8,128)S(1)}, u32[]{:S(2)}, u32[]{:S(2)}) collective-permute-start(f32[48,256]{1,0:T(8,128)S(1)} %get-tuple-element.42), channel_id=1, source_target_pairs={{0,2},{1,3},{2,0},{3,1},{4,6},{5,7},{6,4},{7,5},{8,10},{9,11},{10,... | collective-permute-start | bytes 147464 | tf_op jit(solution)/shard_map/ppermute | solution.py:870
  60.9 10.2 %collective-permute-start.5 = (f32[48,256]{1,0:T(8,128)S(1)}, f32[48,256]{1,0:T(8,128)S(1)}, u32[]{:S(2)}, u32[]{:S(2)}) collective-permute-start(f32[48,256]{1,0:T(8,128)S(1)} %get-tuple-element.43), channel_id=1, source_target_pairs={{0,6},{2,4},{4,10},{5,3},{6,8},{7,1},{8,14},{9,7},{10,12},{11,5},{... | collective-permute-start | bytes 147464 | tf_op jit(solution)/shard_map/ppermute | solution.py:868
  63.9 10.8 %collective-permute-start.4 = (f32[48,256]{1,0:T(8,128)S(1)}, f32[48,256]{1,0:T(8,128)S(1)}, u32[]{:S(2)}, u32[]{:S(2)}) collective-permute-start(f32[48,256]{1,0:T(8,128)S(1)} %get-tuple-element.43), channel_id=1, source_target_pairs={{0,4},{2,6},{4,8},{5,1},{6,10},{7,3},{8,12},{9,5},{10,14},{11,7},{... | collective-permute-start | bytes 147464 | tf_op jit(solution)/shard_map/ppermute | solution.py:868
  74.7 6.6 %copy-start.2 = (f32[48,256]{1,0:T(8,128)}, f32[48,256]{1,0:T(8,128)S(1)}, u32[]{:S(2)}) copy-start(f32[48,256]{1,0:T(8,128)S(1)} %add_add_fusion.a_ref) | copy-start | bytes 147460
  74.7 6.0 %collective-permute-start.8 = (f32[48,256]{1,0:T(8,128)S(1)}, f32[48,256]{1,0:T(8,128)S(1)}, u32[]{:S(2)}, u32[]{:S(2)}) collective-permute-start(f32[48,256]{1,0:T(8,128)S(1)} %add_add_fusion.a_ref), channel_id=1, source_target_pairs={{0,12},{4,8},{8,4},{12,0},{16,28},{20,24},{24,20},{28,16},{32,44},... | collective-permute-start | bytes 147464 | tf_op jit(solution)/shard_map/ppermute | solution.py:877
  74.8 5.9 %collective-permute-start.7 = (f32[48,256]{1,0:T(8,128)S(1)}, f32[48,256]{1,0:T(8,128)S(1)}, u32[]{:S(2)}, u32[]{:S(2)}) collective-permute-start(f32[48,256]{1,0:T(8,128)S(1)} %add_add_fusion.a_ref), channel_id=1, source_target_pairs={{0,8},{4,12},{8,0},{12,4},{16,24},{20,28},{24,16},{28,20},{32,40},... | collective-permute-start | bytes 147464 | tf_op jit(solution)/shard_map/ppermute | solution.py:877
  74.9 6.3 %collective-permute-start.6 = (f32[48,256]{1,0:T(8,128)S(1)}, f32[48,256]{1,0:T(8,128)S(1)}, u32[]{:S(2)}, u32[]{:S(2)}) collective-permute-start(f32[48,256]{1,0:T(8,128)S(1)} %add_add_fusion.a_ref), channel_id=1, source_target_pairs={{0,4},{4,0},{8,12},{12,8},{16,20},{20,16},{24,28},{28,24},{32,36},... | collective-permute-start | bytes 147464 | tf_op jit(solution)/shard_map/ppermute | solution.py:877
  80.7 0.6 copy-start.8
  80.7 0.6 copy-start.9
  81.3 0.6 copy-start.10
  83.5 7.8 %collective-permute-start.10 = (f32[192,256]{1,0:T(8,128)}, f32[192,256]{1,0:T(8,128)S(1)}, u32[]{:S(2)}, u32[]{:S(2)}) collective-permute-start(f32[192,256]{1,0:T(8,128)} %place.1.c_ref), channel_id=1, source_target_pairs={{16,0},{20,4},{24,8},{28,12},{32,16},{36,20},{40,24},{44,28},{48,3... | collective-permute-start | bytes 589832 | tf_op jit(solution)/shard_map/ppermute | solution.py:810
  86.2 11.0 %collective-permute-start.9 = (f32[192,256]{1,0:T(8,128)}, f32[192,256]{1,0:T(8,128)S(1)}, u32[]{:S(2)}, u32[]{:S(2)}) collective-permute-start(f32[192,256]{1,0:T(8,128)} %place.1.c_ref), channel_id=1, source_target_pairs={{0,16},{4,20},{8,24},{12,28},{16,32},{20,36},{24,40},{28,44},{32,4... | collective-permute-start | bytes 589832 | tf_op jit(solution)/shard_map/ppermute | solution.py:810
  89.3 8.0 %collective-permute-start.12 = (f32[192,256]{1,0:T(8,128)}, f32[192,256]{1,0:T(8,128)S(1)}, u32[]{:S(2)}, u32[]{:S(2)}) collective-permute-start(f32[192,256]{1,0:T(8,128)} %place.1.c_ref), channel_id=1, source_target_pairs={{0,1},{1,0},{2,3},{3,2},{4,5},{5,4},{6,7},{7,6},{8,9},{9,8},{10,11... | collective-permute-start | bytes 589832 | tf_op jit(solution)/shard_map/ppermute | solution.py:881
  91.2 7.5 %copy-start.3 = (f32[192,256]{1,0:T(8,128)}, f32[192,256]{1,0:T(8,128)S(1)}, u32[]{:S(2)}) copy-start(f32[192,256]{1,0:T(8,128)S(1)} %collective-permute-done.10.n_ref) | copy-start | bytes 589828
  91.2 6.1 %collective-permute-start.13 = (f32[192,256]{1,0:T(8,128)S(1)}, f32[192,256]{1,0:T(8,128)S(1)}, u32[]{:S(2)}, u32[]{:S(2)}) collective-permute-start(f32[192,256]{1,0:T(8,128)S(1)} %collective-permute-done.10.n_ref), channel_id=1, source_target_pairs={{0,1},{1,0},{2,3},{3,2},{4,5},{5,4},{6,7},{7,6},{8,9},{9,8},{10,11... | collective-permute-start | bytes 589832 | tf_op jit(solution)/shard_map/ppermute | solution.py:881
  97.3 1.4 copy-start.4
  97.3 1.4 collective-permute-start.11
  97.3 1.4 copy-start.5
  97.3 1.4 copy-start.6
  98.7 0.7 copy-start.7
  109.9 5.8 %collective-permute-start.15 = (f32[8,128]{1,0:T(8,128)}, f32[8,128]{1,0:T(8,128)S(1)}, u32[]{:S(2)}, u32[]{:S(2)}) collective-permute-start(f32[8,128]{1,0:T(8,128)} %get-tuple-element.36.own_ref), channel_id=1, source_target_pairs={{16,0},{20,4},{24,8},{28,12},{32,16},{36,20},{40,24},{44,28},{48,3... | collective-permute-start | bytes 12296 | tf_op jit(solution)/shard_map/ppermute | solution.py:810
  111.8 7.8 %collective-permute-start.14 = (f32[8,128]{1,0:T(8,128)}, f32[8,128]{1,0:T(8,128)S(1)}, u32[]{:S(2)}, u32[]{:S(2)}) collective-permute-start(f32[8,128]{1,0:T(8,128)} %get-tuple-element.36.own_ref), channel_id=1, source_target_pairs={{0,16},{4,20},{8,24},{12,28},{16,32},{20,36},{24,40},{28,44},{32,4... | collective-permute-start | bytes 12296 | tf_op jit(solution)/shard_map/ppermute | solution.py:810
  115.7 3.9 %copy-start.14 = (f32[8,128]{1,0:T(8,128)}, f32[8,128]{1,0:T(8,128)S(1)}, u32[]{:S(2)}) copy-start(f32[8,128]{1,0:T(8,128)S(1)} %collective-permute-done.15.above_ref) | copy-start | bytes 12292
  119.6 0.6 copy-start.15
  125.6 5.0 %collective-permute-start.18 = (f32[8,128]{1,0:T(8,128)}, f32[8,128]{1,0:T(8,128)S(1)}, u32[]{:S(2)}, u32[]{:S(2)}) collective-permute-start(f32[8,128]{1,0:T(8,128)} %get-tuple-element.37.a_ref), channel_id=1, source_target_pairs={{0,48},{4,52},{8,56},{12,60},{16,32},{20,36},{24,40},{28,44},{32,1... | collective-permute-start | bytes 12296 | tf_op jit(solution)/shard_map/ppermute | solution.py:877
  125.6 5.3 %collective-permute-start.17 = (f32[8,128]{1,0:T(8,128)}, f32[8,128]{1,0:T(8,128)S(1)}, u32[]{:S(2)}, u32[]{:S(2)}) collective-permute-start(f32[8,128]{1,0:T(8,128)} %get-tuple-element.37.a_ref), channel_id=1, source_target_pairs={{0,32},{4,36},{8,40},{12,44},{16,48},{20,52},{24,56},{28,60},{32,0... | collective-permute-start | bytes 12296 | tf_op jit(solution)/shard_map/ppermute | solution.py:877
  127.5 4.0 %collective-permute-start.16 = (f32[8,128]{1,0:T(8,128)}, f32[8,128]{1,0:T(8,128)S(1)}, u32[]{:S(2)}, u32[]{:S(2)}) collective-permute-start(f32[8,128]{1,0:T(8,128)} %get-tuple-element.37.a_ref), channel_id=1, source_target_pairs={{0,16},{4,20},{8,24},{12,28},{16,0},{20,4},{24,8},{28,12},{32,48},... | collective-permute-start | bytes 12296 | tf_op jit(solution)/shard_map/ppermute | solution.py:877
  130.6 0.9 copy-start.16
  130.9 0.6 copy-start.17
  131.5 0.6 copy-start.18
  133.5 4.1 %collective-permute-start.21 = (f32[8,128]{1,0:T(8,128)}, f32[8,128]{1,0:T(8,128)S(1)}, u32[]{:S(2)}, u32[]{:S(2)}) collective-permute-start(f32[8,128]{1,0:T(8,128)} %sum.1.a_ref), channel_id=1, source_target_pairs={{0,192},{4,196},{8,200},{12,204},{16,208},{20,212},{24,216},{28,22... | collective-permute-start | bytes 12296 | tf_op jit(solution)/shard_map/ppermute | solution.py:877
  135.0 5.3 %collective-permute-start.20 = (f32[8,128]{1,0:T(8,128)}, f32[8,128]{1,0:T(8,128)S(1)}, u32[]{:S(2)}, u32[]{:S(2)}) collective-permute-start(f32[8,128]{1,0:T(8,128)} %sum.1.a_ref), channel_id=1, source_target_pairs={{0,128},{4,132},{8,136},{12,140},{16,144},{20,148},{24,152},{28,15... | collective-permute-start | bytes 12296 | tf_op jit(solution)/shard_map/ppermute | solution.py:877
  136.0 4.3 %collective-permute-start.19 = (f32[8,128]{1,0:T(8,128)}, f32[8,128]{1,0:T(8,128)S(1)}, u32[]{:S(2)}, u32[]{:S(2)}) collective-permute-start(f32[8,128]{1,0:T(8,128)} %sum.1.a_ref), channel_id=1, source_target_pairs={{0,64},{4,68},{8,72},{12,76},{16,80},{20,84},{24,88},{28,92},{32,9... | collective-permute-start | bytes 12296 | tf_op jit(solution)/shard_map/ppermute | solution.py:877
  137.6 2.8 %copy-start.11 = (f32[8,128]{1,0:T(8,128)}, f32[8,128]{1,0:T(8,128)S(1)}, u32[]{:S(2)}) copy-start(f32[8,128]{1,0:T(8,128)S(1)} %collective-permute-done.21.d_ref) | copy-start | bytes 12292
  140.4 0.6 copy-start.12
  140.4 0.6 copy-start.13

commit v9 on v8

--- a/solution.py
+++ b/solution.py
@@ -66,7 +66,8 @@
             conf = weight_ref[comp, :, lanes] * live
             parts.append((conf, conf * flow_ref[comp, :, lanes]))
         values = jnp.concatenate([parts[0][0], parts[1][0], parts[0][1], parts[1][1]], axis=1)
-        got = sum(dot(hot, piece) for piece in reversed(thirds(values)))
+        split = pair_of if rims else thirds
+        got = sum(dot(hot, piece) for piece in reversed(split(values)))
         for q in range(4):
             write(q, lanes, got[:, q * LANES : (q + 1) * LANES])
 

time: 151 us -> 151 us (level)
  no operation moved by 1% of the time
where the time goes in v9:
time: 151 us; the launch traced here: 148 us
  Pallas kernels  62 us (41%)
  starting transfers between devices  45.2 us (30%)
  waiting for transfers between devices  31.1 us (21%)
  local copies, waits for them, and re-layouts  7.35 us (5%)
  other arithmetic  1.54 us (1%)
    pallas_call x9, Pallas kernels, call(): pl.pallas_call(kernel, name=name, out_shape=[jax.ShapeDtypeStruct(s, F32)...  62 us
    ppermute x6, starting transfers between devices, shift(): lax.ppermute(block, 'frames', [(i, i + step) for i in range(count) if 0 <...  22.2 us
    ppermute x6, waiting for transfers between devices, shift(): lax.ppermute(block, 'frames', [(i, i + step) for i in range(count) if 0 <...  12.7 us
    ppermute x9, starting transfers between devices, mates(): lax.ppermute(v, 'frames', [(i, i ^ k * step) for i in range(count)])  12.6 us
    ppermute x2, waiting for transfers between devices, to_neighbour(): return lax.ppermute(rim, both_axes, route)  8.84 us
    ppermute x9, waiting for transfers between devices, mates(): lax.ppermute(v, 'frames', [(i, i ^ k * step) for i in range(count)])  6.69 us
    ppermute x1, starting transfers between devices, per_device(): own_far = lax.ppermute(own_half, 'pix', [(i, i ^ 2) for i in range(pixes)])  5.29 us
    ppermute x2, starting transfers between devices, to_neighbour(): return lax.ppermute(rim, both_axes, route)  4.88 us
  transfers between devices with their start and end apart: 22, of which 14 were waited for; matrix products, arithmetic and copies ran while one was open for 0% of the time, Pallas kernels for 12%

profile of v9, /device:TPU:8, one launch (start us, length us, event | category | flops | bytes accessed | tf_op | source)
XLA Modules:
  0.0 148.3 jit_solution(15626734101200096790)
XLA Ops:
  0.7 3.3 %copy_bitcast_fusion = (f32[2,192,768]{2,1,0:T(8,128)}, f32[2,192,768]{2,1,0:T(8,128)}) fusion(f32[192,2,768]{2,1,0:T(2,128)} %param.14, f32[192,2,768]{2,1,0:T(2,128)} %param.13), kind=kLoop, calls=%fused_computation | loop fusion | bytes 4718592 | tf_op jit(solution)/shard_map/transpose | solution.py:815
  3.9 0.6 pad_add_fusion.where_ref
  4.5 3.4 %rim.1 = (f32[152,768]{1,0:T(8,128)}, f32[144,768]{1,0:T(8,128)}) custom-call(s32[4]{0:T(128)} %pad_add_fusion.where_ref, s32[2,192]{1,0:T(2,128)} %ef_ref.3, f32[2,192,768]{2,1,0:T(8,128)} %get-tuple-element.45.flow_ref, f32[2,192,768]{2,1,0:T(8,128)} %get-tuple-element.44.weight_ref, s32[192,768]{1,0:T(8,128)} %mask_ref.3), custom_call_target="tpu_custom_call" | custom-call | tf_op jit(solution)/shard_map/rim/pallas_call | solution.py:792
  7.9 8.6 %collective-permute-start = (f32[152,768]{1,0:T(8,128)}, f32[152,768]{1,0:T(8,128)S(1)}, u32[]{:S(2)}, u32[]{:S(2)}) collective-permute-start(f32[152,768]{1,0:T(8,128)} %get-tuple-element.22), channel_id=1, source_target_pairs={{4,0},{8,4},{12,8},{16,12},{20,16},{24,20},{28,24},{32,28},{36,32}... | collective-permute-start | bytes 1400840 | tf_op jit(solution)/shard_map/ppermute | solution.py:811
  16.5 1.9 %collective-permute-start.1 = (f32[144,768]{1,0:T(8,128)}, f32[144,768]{1,0:T(8,128)S(1)}, u32[]{:S(2)}, u32[]{:S(2)}) collective-permute-start(f32[144,768]{1,0:T(8,128)} %get-tuple-element.23), channel_id=1, source_target_pairs={{0,4},{4,8},{8,12},{12,16},{16,20},{20,24},{24,28},{28,32},{32,36}... | collective-permute-start | bytes 1327112 | tf_op jit(solution)/shard_map/ppermute | solution.py:811
  18.5 5.1 %pose.1 = (f32[256,128]{1,0:T(8,128)}, f32[1536,384]{1,0:T(8,128)}, f32[192,1536]{1,0:T(8,128)}) custom-call(s32[4]{0:T(128)} %pad_add_fusion.where_ref, f32[3,1024]{1,0:T(4,128)} %rotvec_ref.1, f32[3,1024]{1,0:T(4,128)} %trans_ref.1), custom_call_target="tpu_custom_call" | custom-call | tf_op jit(solution)/shard_map/pose/pallas_call | solution.py:792
  23.6 12.3 %early.1 = (f32[1280,768]{1,0:T(8,128)}, f32[128,768]{1,0:T(8,128)}, f32[128,768]{1,0:T(8,128)}, f32[1536,128]{1,0:T(8,128)}) custom-call(s32[4]{0:T(128)} %pad_add_fusion.where_ref, s32[2,192]{1,0:T(2,128)} %ef_ref.3, f32[2,192,768]{2,1,0:T(8,128)} %get-tuple-element.45.flow_ref, f32[2,192,768]{2,1,0:T(8,128)} %get-tuple-element.44.weight_ref, ...), custom_call_target="tpu_custom_call" | custom-call | tf_op jit(solution)/shard_map/early/pallas_call | solution.py:792
  35.9 1.0 collective-permute-done.1.rup_ref
  36.9 0.0 collective-permute-done.rdown_ref
  36.9 0.8 copy-done.1
  37.7 0.2 copy-done
  37.8 15.0 %main.1 = (f32[96,256]{1,0:T(8,128)}, f32[96,256]{1,0:T(8,128)}, f32[128,768]{1,0:T(8,128)}, f32[128,768]{1,0:T(8,128)}, f32[1536,768]{1,0:T(8,128)}) custom-call(s32[4]{0:T(128)} %pad_add_fusion.where_ref, f32[152,768]{1,0:T(8,128)} %copy-done, f32[144,768]{1,0:T(8,128)} %copy-done.1, f32[128,768]{1,0:T(8,128)} %get-tuple-element.25.curv_ref, ...), custom_call_target="tpu_custom_call" | custom-call | tf_op jit(solution)/shard_map/main/pallas_call | solution.py:792
  52.9 0.1 collective-permute-start.2
  53.0 1.5 %collective-permute-done.2 = f32[96,256]{1,0:T(8,128)S(1)} collective-permute-done((f32[96,256]{1,0:T(8,128)}, f32[96,256]{1,0:T(8,128)S(1)}, u32[]{:S(2)}, u32[]{:S(2)}) %collective-permute-start.2) | collective-permute-done | bytes 98336 | tf_op jit(solution)/shard_map/ppermute | solution.py:857
  54.5 0.9 add.21
  55.4 5.3 %collective-permute-start.3 = (f32[48,256]{1,0:T(8,128)S(1)}, f32[48,256]{1,0:T(8,128)S(1)}, u32[]{:S(2)}, u32[]{:S(2)}) collective-permute-start(f32[48,256]{1,0:T(8,128)S(1)} %get-tuple-element.42), channel_id=1, source_target_pairs={{0,2},{1,3},{2,0},{3,1},{4,6},{5,7},{6,4},{7,5},{8,10},{9,11},{10,... | collective-permute-start | bytes 147464 | tf_op jit(solution)/shard_map/ppermute | solution.py:871
  60.7 2.9 %collective-permute-start.5 = (f32[48,256]{1,0:T(8,128)S(1)}, f32[48,256]{1,0:T(8,128)S(1)}, u32[]{:S(2)}, u32[]{:S(2)}) collective-permute-start(f32[48,256]{1,0:T(8,128)S(1)} %get-tuple-element.43), channel_id=1, source_target_pairs={{0,6},{2,4},{4,10},{5,3},{6,8},{7,1},{8,14},{9,7},{10,12},{11,5},{... | collective-permute-start | bytes 147464 | tf_op jit(solution)/shard_map/ppermute | solution.py:869
  63.6 1.9 %collective-permute-start.4 = (f32[48,256]{1,0:T(8,128)S(1)}, f32[48,256]{1,0:T(8,128)S(1)}, u32[]{:S(2)}, u32[]{:S(2)}) collective-permute-start(f32[48,256]{1,0:T(8,128)S(1)} %get-tuple-element.43), channel_id=1, source_target_pairs={{0,4},{2,6},{4,8},{5,1},{6,10},{7,3},{8,12},{9,5},{10,14},{11,7},{... | collective-permute-start | bytes 147464 | tf_op jit(solution)/shard_map/ppermute | solution.py:869
  65.6 0.0 collective-permute-done.3
  65.6 5.3 %collective-permute-done.5 = f32[48,256]{1,0:T(8,128)S(1)} collective-permute-done((f32[48,256]{1,0:T(8,128)S(1)}, f32[48,256]{1,0:T(8,128)S(1)}, u32[]{:S(2)}, u32[]{:S(2)}) %collective-permute-start.5) | collective-permute-done | bytes 49184 | tf_op jit(solution)/shard_map/ppermute | solution.py:869
  70.9 3.6 %collective-permute-done.4 = f32[48,256]{1,0:T(8,128)S(1)} collective-permute-done((f32[48,256]{1,0:T(8,128)S(1)}, f32[48,256]{1,0:T(8,128)S(1)}, u32[]{:S(2)}, u32[]{:S(2)}) %collective-permute-start.4) | collective-permute-done | bytes 49184 | tf_op jit(solution)/shard_map/ppermute | solution.py:869
  74.4 0.0 copy-start.2
  74.4 0.1 collective-permute-start.8
  74.5 0.1 collective-permute-start.7
  74.7 4.3 %collective-permute-start.6 = (f32[48,256]{1,0:T(8,128)S(1)}, f32[48,256]{1,0:T(8,128)S(1)}, u32[]{:S(2)}, u32[]{:S(2)}) collective-permute-start(f32[48,256]{1,0:T(8,128)S(1)} %add_add_fusion.a_ref), channel_id=1, source_target_pairs={{0,4},{4,0},{8,12},{12,8},{16,20},{20,16},{24,28},{28,24},{32,36},... | collective-permute-start | bytes 147464 | tf_op jit(solution)/shard_map/ppermute | solution.py:878
  78.9 1.5 %collective-permute-done.8.d_ref = f32[48,256]{1,0:T(8,128)S(1)} collective-permute-done((f32[48,256]{1,0:T(8,128)S(1)}, f32[48,256]{1,0:T(8,128)S(1)}, u32[]{:S(2)}, u32[]{:S(2)}) %collective-permute-start.8) | collective-permute-done | bytes 49184 | tf_op jit(solution)/shard_map/ppermute | solution.py:878
  80.4 0.0 collective-permute-done.7.c_ref
  80.4 0.6 collective-permute-done.6.b_ref
  81.0 0.0 copy-done.8
  81.0 0.0 copy-done.9
  81.1 0.6 copy-done.10
  81.7 1.6 %place.1.c_ref = f32[192,256]{1,0:T(8,128)} custom-call(s32[4]{0:T(128)} %pad_add_fusion.where_ref, f32[48,256]{1,0:T(8,128)} %copy-done.2, f32[48,256]{1,0:T(8,128)} %copy-done.10, f32[48,256]{1,0:T(8,128)} %copy-done.9, f32[48,256]{1,0:T(8,128)} %copy-done.8), custom_call_target="tpu_custom_call" | custom-call | tf_op jit(solution)/shard_map/place/pallas_call | solution.py:792
  83.2 2.7 %collective-permute-start.10 = (f32[192,256]{1,0:T(8,128)}, f32[192,256]{1,0:T(8,128)S(1)}, u32[]{:S(2)}, u32[]{:S(2)}) collective-permute-start(f32[192,256]{1,0:T(8,128)} %place.1.c_ref), channel_id=1, source_target_pairs={{16,0},{20,4},{24,8},{28,12},{32,16},{36,20},{40,24},{44,28},{48,3... | collective-permute-start | bytes 589832 | tf_op jit(solution)/shard_map/ppermute | solution.py:811
  86.0 3.1 %collective-permute-start.9 = (f32[192,256]{1,0:T(8,128)}, f32[192,256]{1,0:T(8,128)S(1)}, u32[]{:S(2)}, u32[]{:S(2)}) collective-permute-start(f32[192,256]{1,0:T(8,128)} %place.1.c_ref), channel_id=1, source_target_pairs={{0,16},{4,20},{8,24},{12,28},{16,32},{20,36},{24,40},{28,44},{32,4... | collective-permute-start | bytes 589832 | tf_op jit(solution)/shard_map/ppermute | solution.py:811
  89.1 0.1 collective-permute-start.12
  89.2 1.8 %collective-permute-done.10.n_ref = f32[192,256]{1,0:T(8,128)S(1)} collective-permute-done((f32[192,256]{1,0:T(8,128)}, f32[192,256]{1,0:T(8,128)S(1)}, u32[]{:S(2)}, u32[]{:S(2)}) %collective-permute-start.10) | collective-permute-done | bytes 196640 | tf_op jit(solution)/shard_map/ppermute | solution.py:811
  91.0 0.0 collective-permute-start.13
  91.0 6.0 %collective-permute-done.9.p_ref = f32[192,256]{1,0:T(8,128)S(1)} collective-permute-done((f32[192,256]{1,0:T(8,128)}, f32[192,256]{1,0:T(8,128)S(1)}, u32[]{:S(2)}, u32[]{:S(2)}) %collective-permute-start.9) | collective-permute-done | bytes 196640 | tf_op jit(solution)/shard_map/ppermute | solution.py:811
  97.0 0.0 collective-permute-start.11
  97.0 0.0 collective-permute-done.12.c2_ref
  97.0 0.0 collective-permute-done.13.n2_ref
  97.1 1.4 collective-permute-done.11.p2_ref
  98.5 0.7 copy-done.7
  99.2 10.5 %first.1 = (f32[1152,256]{1,0:T(8,128)}, f32[1152,128]{1,0:T(8,128)}, f32[480,128]{1,0:T(8,128)}, f32[8,128]{1,0:T(8,128)}) custom-call(s32[4]{0:T(128)} %pad_add_fusion.where_ref, f32[192,256]{1,0:T(8,128)} %copy-done.4, f32[192,256]{1,0:T(8,128)} %place.1.c_ref, f32[192,256]{1,0:T(8,128)} %copy-done.3, f32[192,256]{1,0:T(8,128)} %copy-done.7, ...), custom_call_target="tpu_custom_call" | custom-call | tf_op jit(solution)/shard_map/first/pallas_call | solution.py:792
  109.6 1.9 %collective-permute-start.15 = (f32[8,128]{1,0:T(8,128)}, f32[8,128]{1,0:T(8,128)S(1)}, u32[]{:S(2)}, u32[]{:S(2)}) collective-permute-start(f32[8,128]{1,0:T(8,128)} %get-tuple-element.36.own_ref), channel_id=1, source_target_pairs={{16,0},{20,4},{24,8},{28,12},{32,16},{36,20},{40,24},{44,28},{48,3... | collective-permute-start | bytes 12296 | tf_op jit(solution)/shard_map/ppermute | solution.py:811
  111.5 3.9 %collective-permute-start.14 = (f32[8,128]{1,0:T(8,128)}, f32[8,128]{1,0:T(8,128)S(1)}, u32[]{:S(2)}, u32[]{:S(2)}) collective-permute-start(f32[8,128]{1,0:T(8,128)} %get-tuple-element.36.own_ref), channel_id=1, source_target_pairs={{0,16},{4,20},{8,24},{12,28},{16,32},{20,36},{24,40},{28,44},{32,4... | collective-permute-start | bytes 12296 | tf_op jit(solution)/shard_map/ppermute | solution.py:811
  115.5 0.0 collective-permute-done.15.above_ref
  115.5 3.9 %collective-permute-done.14.below_ref = f32[8,128]{1,0:T(8,128)S(1)} collective-permute-done((f32[8,128]{1,0:T(8,128)}, f32[8,128]{1,0:T(8,128)S(1)}, u32[]{:S(2)}, u32[]{:S(2)}) %collective-permute-start.14) | collective-permute-done | bytes 4128 | tf_op jit(solution)/shard_map/ppermute | solution.py:811
  119.4 0.6 copy-done.15
  120.0 5.4 %second.1 = (f32[8,128]{1,0:T(8,128)}, f32[288,128]{1,0:T(8,128)}) custom-call(f32[1152,256]{1,0:T(8,128)} %get-tuple-element.33.s_ref, f32[1152,128]{1,0:T(8,128)} %get-tuple-element.34.up_ref, f32[480,128]{1,0:T(8,128)} %get-tuple-element.35.v_ref, f32[8,128]{1,0:T(8,128)} %copy-done.15, f32[8,128]{1,0:T(8,128)} %get-tuple-element.36.own_ref, ...), custom_call_target="tpu_custom_call" | custom-call | tf_op jit(solution)/shard_map/second/pallas_call | solution.py:792
  125.3 2.0 %collective-permute-start.17 = (f32[8,128]{1,0:T(8,128)}, f32[8,128]{1,0:T(8,128)S(1)}, u32[]{:S(2)}, u32[]{:S(2)}) collective-permute-start(f32[8,128]{1,0:T(8,128)} %get-tuple-element.37.a_ref), channel_id=1, source_target_pairs={{0,32},{4,36},{8,40},{12,44},{16,48},{20,52},{24,56},{28,60},{32,0... | collective-permute-start | bytes 12296 | tf_op jit(solution)/shard_map/ppermute | solution.py:878
  127.3 2.1 %collective-permute-start.16 = (f32[8,128]{1,0:T(8,128)}, f32[8,128]{1,0:T(8,128)S(1)}, u32[]{:S(2)}, u32[]{:S(2)}) collective-permute-start(f32[8,128]{1,0:T(8,128)} %get-tuple-element.37.a_ref), channel_id=1, source_target_pairs={{0,16},{4,20},{8,24},{12,28},{16,0},{20,4},{24,8},{28,12},{32,48},... | collective-permute-start | bytes 12296 | tf_op jit(solution)/shard_map/ppermute | solution.py:878
  129.4 0.9 collective-permute-done.18.d_ref
  130.3 0.3 collective-permute-done.17.c_ref
  130.6 0.6 collective-permute-done.16.b_ref
  131.3 0.6 copy-done.18
  131.8 1.4 sum.1.a_ref
  133.2 1.6 %collective-permute-start.21 = (f32[8,128]{1,0:T(8,128)}, f32[8,128]{1,0:T(8,128)S(1)}, u32[]{:S(2)}, u32[]{:S(2)}) collective-permute-start(f32[8,128]{1,0:T(8,128)} %sum.1.a_ref), channel_id=1, source_target_pairs={{0,192},{4,196},{8,200},{12,204},{16,208},{20,212},{24,216},{28,22... | collective-permute-start | bytes 12296 | tf_op jit(solution)/shard_map/ppermute | solution.py:878
  134.8 1.0 collective-permute-start.20
  135.8 1.5 %collective-permute-start.19 = (f32[8,128]{1,0:T(8,128)}, f32[8,128]{1,0:T(8,128)S(1)}, u32[]{:S(2)}, u32[]{:S(2)}) collective-permute-start(f32[8,128]{1,0:T(8,128)} %sum.1.a_ref), channel_id=1, source_target_pairs={{0,64},{4,68},{8,72},{12,76},{16,80},{20,84},{24,88},{28,92},{32,9... | collective-permute-start | bytes 12296 | tf_op jit(solution)/shard_map/ppermute | solution.py:878
  137.3 0.0 collective-permute-done.21.d_ref
  137.3 2.8 %collective-permute-done.20.c_ref = f32[8,128]{1,0:T(8,128)S(1)} collective-permute-done((f32[8,128]{1,0:T(8,128)}, f32[8,128]{1,0:T(8,128)S(1)}, u32[]{:S(2)}, u32[]{:S(2)}) %collective-permute-start.20) | collective-permute-done | bytes 4128 | tf_op jit(solution)/shard_map/ppermute | solution.py:878
  140.1 0.6 copy-done.12
  140.7 7.4 %solve.1 = (f32[6,16]{1,0:T(8,128)}, f32[16,768]{1,0:T(8,128)}) custom-call(s32[4]{0:T(128)} %pad_add_fusion.where_ref, f32[8,128]{1,0:T(8,128)} %sum.1.a_ref, f32[8,128]{1,0:T(8,128)} %copy-done.13, f32[8,128]{1,0:T(8,128)} %copy-done.12, f32[8,128]{1,0:T(8,128)} %copy-done.11, f32[480,128]{1,0:T(8,128)} %get-tuple-element.35.v_ref, ...), custom_call_target="tpu_custom_call" | custom-call | tf_op jit(solution)/shard_map/solve/pallas_call | solution.py:792
  (32 shorter events, 0.1 us)
Async XLA Ops:
  7.9 29.0 %collective-permute-start = (f32[152,768]{1,0:T(8,128)}, f32[152,768]{1,0:T(8,128)S(1)}, u32[]{:S(2)}, u32[]{:S(2)}) collective-permute-start(f32[152,768]{1,0:T(8,128)} %get-tuple-element.22), channel_id=1, source_target_pairs={{4,0},{8,4},{12,8},{16,12},{20,16},{24,20},{28,24},{32,28},{36,32}... | collective-permute-start | bytes 1400840 | tf_op jit(solution)/shard_map/ppermute | solution.py:811
  16.5 20.4 %collective-permute-start.1 = (f32[144,768]{1,0:T(8,128)}, f32[144,768]{1,0:T(8,128)S(1)}, u32[]{:S(2)}, u32[]{:S(2)}) collective-permute-start(f32[144,768]{1,0:T(8,128)} %get-tuple-element.23), channel_id=1, source_target_pairs={{0,4},{4,8},{8,12},{12,16},{16,20},{20,24},{24,28},{28,32},{32,36}... | collective-permute-start | bytes 1327112 | tf_op jit(solution)/shard_map/ppermute | solution.py:811
  36.9 0.8 copy-start.1
  36.9 0.9 copy-start
  52.9 1.6 %collective-permute-start.2 = (f32[96,256]{1,0:T(8,128)}, f32[96,256]{1,0:T(8,128)S(1)}, u32[]{:S(2)}, u32[]{:S(2)}) collective-permute-start(f32[96,256]{1,0:T(8,128)} %get-tuple-element.32), channel_id=1, source_target_pairs={{0,1},{1,0},{2,3},{3,2},{4,5},{5,4},{6,7},{7,6},{8,9},{9,8},{10,11... | collective-permute-start | bytes 294920 | tf_op jit(solution)/shard_map/ppermute | solution.py:857
  55.4 10.2 %collective-permute-start.3 = (f32[48,256]{1,0:T(8,128)S(1)}, f32[48,256]{1,0:T(8,128)S(1)}, u32[]{:S(2)}, u32[]{:S(2)}) collective-permute-start(f32[48,256]{1,0:T(8,128)S(1)} %get-tuple-element.42), channel_id=1, source_target_pairs={{0,2},{1,3},{2,0},{3,1},{4,6},{5,7},{6,4},{7,5},{8,10},{9,11},{10,... | collective-permute-start | bytes 147464 | tf_op jit(solution)/shard_map/ppermute | solution.py:871
  60.7 10.2 %collective-permute-start.5 = (f32[48,256]{1,0:T(8,128)S(1)}, f32[48,256]{1,0:T(8,128)S(1)}, u32[]{:S(2)}, u32[]{:S(2)}) collective-permute-start(f32[48,256]{1,0:T(8,128)S(1)} %get-tuple-element.43), channel_id=1, source_target_pairs={{0,6},{2,4},{4,10},{5,3},{6,8},{7,1},{8,14},{9,7},{10,12},{11,5},{... | collective-permute-start | bytes 147464 | tf_op jit(solution)/shard_map/ppermute | solution.py:869
  63.6 10.8 %collective-permute-start.4 = (f32[48,256]{1,0:T(8,128)S(1)}, f32[48,256]{1,0:T(8,128)S(1)}, u32[]{:S(2)}, u32[]{:S(2)}) collective-permute-start(f32[48,256]{1,0:T(8,128)S(1)} %get-tuple-element.43), channel_id=1, source_target_pairs={{0,4},{2,6},{4,8},{5,1},{6,10},{7,3},{8,12},{9,5},{10,14},{11,7},{... | collective-permute-start | bytes 147464 | tf_op jit(solution)/shard_map/ppermute | solution.py:869
  74.4 6.6 %copy-start.2 = (f32[48,256]{1,0:T(8,128)}, f32[48,256]{1,0:T(8,128)S(1)}, u32[]{:S(2)}) copy-start(f32[48,256]{1,0:T(8,128)S(1)} %add_add_fusion.a_ref) | copy-start | bytes 147460
  74.4 6.0 %collective-permute-start.8 = (f32[48,256]{1,0:T(8,128)S(1)}, f32[48,256]{1,0:T(8,128)S(1)}, u32[]{:S(2)}, u32[]{:S(2)}) collective-permute-start(f32[48,256]{1,0:T(8,128)S(1)} %add_add_fusion.a_ref), channel_id=1, source_target_pairs={{0,12},{4,8},{8,4},{12,0},{16,28},{20,24},{24,20},{28,16},{32,44},... | collective-permute-start | bytes 147464 | tf_op jit(solution)/shard_map/ppermute | solution.py:878
  74.5 5.9 %collective-permute-start.7 = (f32[48,256]{1,0:T(8,128)S(1)}, f32[48,256]{1,0:T(8,128)S(1)}, u32[]{:S(2)}, u32[]{:S(2)}) collective-permute-start(f32[48,256]{1,0:T(8,128)S(1)} %add_add_fusion.a_ref), channel_id=1, source_target_pairs={{0,8},{4,12},{8,0},{12,4},{16,24},{20,28},{24,16},{28,20},{32,40},... | collective-permute-start | bytes 147464 | tf_op jit(solution)/shard_map/ppermute | solution.py:878
  74.7 6.3 %collective-permute-start.6 = (f32[48,256]{1,0:T(8,128)S(1)}, f32[48,256]{1,0:T(8,128)S(1)}, u32[]{:S(2)}, u32[]{:S(2)}) collective-permute-start(f32[48,256]{1,0:T(8,128)S(1)} %add_add_fusion.a_ref), channel_id=1, source_target_pairs={{0,4},{4,0},{8,12},{12,8},{16,20},{20,16},{24,28},{28,24},{32,36},... | collective-permute-start | bytes 147464 | tf_op jit(solution)/shard_map/ppermute | solution.py:878
  80.4 0.6 copy-start.8
  80.4 0.6 copy-start.9
  81.1 0.6 copy-start.10
  83.2 7.8 %collective-permute-start.10 = (f32[192,256]{1,0:T(8,128)}, f32[192,256]{1,0:T(8,128)S(1)}, u32[]{:S(2)}, u32[]{:S(2)}) collective-permute-start(f32[192,256]{1,0:T(8,128)} %place.1.c_ref), channel_id=1, source_target_pairs={{16,0},{20,4},{24,8},{28,12},{32,16},{36,20},{40,24},{44,28},{48,3... | collective-permute-start | bytes 589832 | tf_op jit(solution)/shard_map/ppermute | solution.py:811
  86.0 11.1 %collective-permute-start.9 = (f32[192,256]{1,0:T(8,128)}, f32[192,256]{1,0:T(8,128)S(1)}, u32[]{:S(2)}, u32[]{:S(2)}) collective-permute-start(f32[192,256]{1,0:T(8,128)} %place.1.c_ref), channel_id=1, source_target_pairs={{0,16},{4,20},{8,24},{12,28},{16,32},{20,36},{24,40},{28,44},{32,4... | collective-permute-start | bytes 589832 | tf_op jit(solution)/shard_map/ppermute | solution.py:811
  89.1 8.0 %collective-permute-start.12 = (f32[192,256]{1,0:T(8,128)}, f32[192,256]{1,0:T(8,128)S(1)}, u32[]{:S(2)}, u32[]{:S(2)}) collective-permute-start(f32[192,256]{1,0:T(8,128)} %place.1.c_ref), channel_id=1, source_target_pairs={{0,1},{1,0},{2,3},{3,2},{4,5},{5,4},{6,7},{7,6},{8,9},{9,8},{10,11... | collective-permute-start | bytes 589832 | tf_op jit(solution)/shard_map/ppermute | solution.py:882
  91.0 7.5 %copy-start.3 = (f32[192,256]{1,0:T(8,128)}, f32[192,256]{1,0:T(8,128)S(1)}, u32[]{:S(2)}) copy-start(f32[192,256]{1,0:T(8,128)S(1)} %collective-permute-done.10.n_ref) | copy-start | bytes 589828
  91.0 6.1 %collective-permute-start.13 = (f32[192,256]{1,0:T(8,128)S(1)}, f32[192,256]{1,0:T(8,128)S(1)}, u32[]{:S(2)}, u32[]{:S(2)}) collective-permute-start(f32[192,256]{1,0:T(8,128)S(1)} %collective-permute-done.10.n_ref), channel_id=1, source_target_pairs={{0,1},{1,0},{2,3},{3,2},{4,5},{5,4},{6,7},{7,6},{8,9},{9,8},{10,11... | collective-permute-start | bytes 589832 | tf_op jit(solution)/shard_map/ppermute | solution.py:882
  97.0 1.4 copy-start.4
  97.0 1.4 collective-permute-start.11
  97.0 1.4 copy-start.5
  97.1 1.4 copy-start.6
  98.5 0.7 copy-start.7
  109.6 5.8 %collective-permute-start.15 = (f32[8,128]{1,0:T(8,128)}, f32[8,128]{1,0:T(8,128)S(1)}, u32[]{:S(2)}, u32[]{:S(2)}) collective-permute-start(f32[8,128]{1,0:T(8,128)} %get-tuple-element.36.own_ref), channel_id=1, source_target_pairs={{16,0},{20,4},{24,8},{28,12},{32,16},{36,20},{40,24},{44,28},{48,3... | collective-permute-start | bytes 12296 | tf_op jit(solution)/shard_map/ppermute | solution.py:811
  111.5 7.8 %collective-permute-start.14 = (f32[8,128]{1,0:T(8,128)}, f32[8,128]{1,0:T(8,128)S(1)}, u32[]{:S(2)}, u32[]{:S(2)}) collective-permute-start(f32[8,128]{1,0:T(8,128)} %get-tuple-element.36.own_ref), channel_id=1, source_target_pairs={{0,16},{4,20},{8,24},{12,28},{16,32},{20,36},{24,40},{28,44},{32,4... | collective-permute-start | bytes 12296 | tf_op jit(solution)/shard_map/ppermute | solution.py:811
  115.5 3.9 %copy-start.14 = (f32[8,128]{1,0:T(8,128)}, f32[8,128]{1,0:T(8,128)S(1)}, u32[]{:S(2)}) copy-start(f32[8,128]{1,0:T(8,128)S(1)} %collective-permute-done.15.above_ref) | copy-start | bytes 12292
  119.4 0.6 copy-start.15
  125.3 5.0 %collective-permute-start.18 = (f32[8,128]{1,0:T(8,128)}, f32[8,128]{1,0:T(8,128)S(1)}, u32[]{:S(2)}, u32[]{:S(2)}) collective-permute-start(f32[8,128]{1,0:T(8,128)} %get-tuple-element.37.a_ref), channel_id=1, source_target_pairs={{0,48},{4,52},{8,56},{12,60},{16,32},{20,36},{24,40},{28,44},{32,1... | collective-permute-start | bytes 12296 | tf_op jit(solution)/shard_map/ppermute | solution.py:878
  125.3 5.3 %collective-permute-start.17 = (f32[8,128]{1,0:T(8,128)}, f32[8,128]{1,0:T(8,128)S(1)}, u32[]{:S(2)}, u32[]{:S(2)}) collective-permute-start(f32[8,128]{1,0:T(8,128)} %get-tuple-element.37.a_ref), channel_id=1, source_target_pairs={{0,32},{4,36},{8,40},{12,44},{16,48},{20,52},{24,56},{28,60},{32,0... | collective-permute-start | bytes 12296 | tf_op jit(solution)/shard_map/ppermute | solution.py:878
  127.3 4.0 %collective-permute-start.16 = (f32[8,128]{1,0:T(8,128)}, f32[8,128]{1,0:T(8,128)S(1)}, u32[]{:S(2)}, u32[]{:S(2)}) collective-permute-start(f32[8,128]{1,0:T(8,128)} %get-tuple-element.37.a_ref), channel_id=1, source_target_pairs={{0,16},{4,20},{8,24},{12,28},{16,0},{20,4},{24,8},{28,12},{32,48},... | collective-permute-start | bytes 12296 | tf_op jit(solution)/shard_map/ppermute | solution.py:878
  130.3 0.9 copy-start.16
  130.6 0.6 copy-start.17
  131.3 0.6 copy-start.18
  133.2 4.1 %collective-permute-start.21 = (f32[8,128]{1,0:T(8,128)}, f32[8,128]{1,0:T(8,128)S(1)}, u32[]{:S(2)}, u32[]{:S(2)}) collective-permute-start(f32[8,128]{1,0:T(8,128)} %sum.1.a_ref), channel_id=1, source_target_pairs={{0,192},{4,196},{8,200},{12,204},{16,208},{20,212},{24,216},{28,22... | collective-permute-start | bytes 12296 | tf_op jit(solution)/shard_map/ppermute | solution.py:878
  134.8 5.3 %collective-permute-start.20 = (f32[8,128]{1,0:T(8,128)}, f32[8,128]{1,0:T(8,128)S(1)}, u32[]{:S(2)}, u32[]{:S(2)}) collective-permute-start(f32[8,128]{1,0:T(8,128)} %sum.1.a_ref), channel_id=1, source_target_pairs={{0,128},{4,132},{8,136},{12,140},{16,144},{20,148},{24,152},{28,15... | collective-permute-start | bytes 12296 | tf_op jit(solution)/shard_map/ppermute | solution.py:878
  135.8 4.3 %collective-permute-start.19 = (f32[8,128]{1,0:T(8,128)}, f32[8,128]{1,0:T(8,128)S(1)}, u32[]{:S(2)}, u32[]{:S(2)}) collective-permute-start(f32[8,128]{1,0:T(8,128)} %sum.1.a_ref), channel_id=1, source_target_pairs={{0,64},{4,68},{8,72},{12,76},{16,80},{20,84},{24,88},{28,92},{32,9... | collective-permute-start | bytes 12296 | tf_op jit(solution)/shard_map/ppermute | solution.py:878
  137.3 2.8 %copy-start.11 = (f32[8,128]{1,0:T(8,128)}, f32[8,128]{1,0:T(8,128)S(1)}, u32[]{:S(2)}) copy-start(f32[8,128]{1,0:T(8,128)S(1)} %collective-permute-done.21.d_ref) | copy-start | bytes 12292
  140.1 0.6 copy-start.12
  140.1 0.6 copy-start.13
